TPU v7x, 128 devices: a whole 4x4x4 slice. The times are simulated.
128 devices in a mesh: dp: 32 (over x, z_hi, y), expert: 4 (over z_lo, core).
Axes of the slice: x: 4, y: 4, z: 4 (z_hi: 2, z_lo: 2; z = z_hi * 2 + z_lo), core: 2. Of those that a mesh axis runs over, the one named last changes fastest.
Arguments:
- tokens: bfloat16 [16384, 2048], P(('dp', 'expert')), may hold values from -6 to 6
- cotangent: bfloat16 [16384, 2048], P(('dp', 'expert')), may hold values from -6 to 6
- expert_ids: int32 [16384, 2], P(('dp', 'expert')), may hold values from 0 to 3, all different within a row; in each aligned block of 128 rows (0 to 127, 128 to 255, ...) at most 128 rows name the same one
- combine: float32 [16384, 2], P(('dp', 'expert')), may hold values from 0.1 to 1
- w_gate: bfloat16 [4, 2048, 768], P('expert'), may hold values from -0.125 to 0.125
- w_up: bfloat16 [4, 2048, 768], P('expert'), may hold values from -0.125 to 0.125
- w_down: bfloat16 [4, 768, 2048], P('expert'), may hold values from -0.21875 to 0.21875
Outputs:
- input_grad: bfloat16 [16384, 2048], P(('dp', 'expert'))
- combine_grad: float32 [16384, 2], P(('dp', 'expert'))
- gate_grad: bfloat16 [4, 2048, 768], P('expert', 'dp')
- up_grad: bfloat16 [4, 2048, 768], P('expert', 'dp')
- down_grad: bfloat16 [4, 768, 2048], P('expert', 'dp')
Inputs may be any that keep to these rules, and one draw needn't show every extreme that they name: `expert_ids`: each token names 2 different experts. In the rows of one device no expert is named by more than 128 tokens, and in some devices' rows some expert is named by exactly 128.
All inputs are finite; a program needn't handle non-finite values.
Results may differ from a plain program's by a relative error of at most 0.02.
Values may be sent and summed in bfloat16 or wider, within the bound.
No kernel may reach another device: no remote copies, remote signals or barrier semaphores. Data moves between devices by JAX's collectives and lax.ppermute only.
A program may use at most 128 MiB of HBM per device.

v0:
```python
import jax
import jax.numpy as jnp
from jax import lax
from jax.experimental import pallas as pl
from jax.experimental.pallas import tpu as pltpu
from jax.sharding import Mesh
from jax.sharding import PartitionSpec as P


F32 = jnp.float32
BF16 = jnp.bfloat16
GROUP = ("zl", "c")
REPLICA = ("x", "zh", "y")
EVERY = ("x", "zh", "y", "zl", "c")
XA, XB, YA, YB, Z = ("x", 1), ("x", 3), ("y", 1), ("y", 3), ("zh", 1)
ORDERS = ((XA, XB, YA, YB, Z), (YA, YB, XA, XB, Z), (XB, XA, YB, YA, Z), (YB, YA, XB, XA, Z))
DOWN_ORDERS = ORDERS[:2] + ((Z, XA, YB, YA, XB), (Z, YA, XB, XA, YB))
BLOCKS = 32
HALF = BLOCKS // 2
PIECE = 128
LANES = 128
ROW = ((8, LANES), F32)


def moved(array, axis, mask):
    return lax.ppermute(array, axis, [(i, i ^ mask) for i in range(lax.axis_size(axis))])


def block_at(order, pos):
    masks = dict.fromkeys(REPLICA, 0)
    for step, (axis, mask) in enumerate(order):
        if pos >> (4 - step) & 1:
            masks[axis] ^= mask
    x, z, y = (lax.axis_index(axis) ^ masks[axis] for axis in REPLICA)
    return (x * 2 + z) * 4 + y


def group_index():
    return lax.axis_index("zl") * 2 + lax.axis_index("c")


def as_row(column):
    return jnp.broadcast_to(column, (column.shape[0], LANES)).T[:8]


def as_column(row):
    return jnp.broadcast_to(row[0:1, :], (LANES, LANES)).T[:, 0:1]


def nt(a, b):
    return lax.dot_general(a, b, (((1,), (1,)), ((), ())), preferred_element_type=F32)


def nn(a, b):
    return jnp.dot(a, b, preferred_element_type=F32)


def kernel(body, ins, outs, limit, flops, scratch=()):
    vmem = pl.BlockSpec(memory_space=pltpu.VMEM)
    return pl.pallas_call(
        body,
        in_specs=[vmem] * len(ins),
        out_specs=[vmem] * len(outs),
        out_shape=[jax.ShapeDtypeStruct(s, t) for s, t in outs],
        scratch_shapes=list(scratch),
        compiler_params=pltpu.CompilerParams(vmem_limit_bytes=limit << 20),
        cost_estimate=pl.CostEstimate(flops=flops, transcendentals=0, bytes_accessed=1 << 20),
    )(*ins)


def route_body(ids, combine, *outs):
    mine = group_index()
    for m, out in enumerate(outs):
        chosen = ids[...] == (mine ^ m)
        row = jnp.sum(jnp.where(chosen, combine[...], 0.0), axis=0, keepdims=True)
        out[...] = jnp.broadcast_to(row, out.shape)


def combine_body(ids, c0, c1, c2, c3, out):
    mine = group_index()
    total = jnp.zeros(out.shape, F32)
    for m, c in enumerate((c0, c1, c2, c3)):
        total = total + jnp.where(ids[...] == (mine ^ m), c[0:1, :], 0.0)
    out[...] = total


def forward_body(x0, x1, c0, c1, wg, wu, slope, act_out, hid, cht, xt, xs):
    cw = jnp.concatenate([as_column(c0[...]), as_column(c1[...])], axis=0)
    for j, x in enumerate((x0, x1)):
        xs[pl.ds(j * PIECE, PIECE), :] = x[...]
    tile = 256
    for f in range(wg.shape[1] // tile):
        at = pl.ds(f * tile, tile)
        gate = nn(xs[...], wg[:, at])
        up = nn(xs[...], wu[:, at])
        sig = jax.nn.sigmoid(gate)
        act = gate * sig
        slope[:, at] = up * (sig * (1.0 + gate * (1.0 - sig)))
        act_out[:, at] = act
        hidden = act * up
        hid[:, at] = hidden.astype(BF16)
        cht[at, :] = (cw * hidden).T
    for j in range(2):
        xt[:, pl.ds(j * PIECE, PIECE)] = xs[pl.ds(j * PIECE, PIECE), :].T


def forward(x0, x1, cws, wg, wu):
    d, ff = wg.shape
    rows = 2 * PIECE
    outs = [((rows, ff), F32), ((rows, ff), F32), ((rows, ff), BF16), ((ff, rows), F32), ((d, rows), BF16)]
    return kernel(
        forward_body,
        (x0, x1, *cws, wg, wu),
        outs,
        12,
        4 * rows * d * ff,
        scratch=(pltpu.VMEM((rows, d), BF16),),
    )


def down_body(first, chunk, hta, htb, g0, g1, g2, g3, *refs):
    outs, (mixed, gs) = refs[:-2], refs[-2:]
    cols = g2.shape[1] // 2
    for j, g in enumerate((g0, g1)):
        gs[pl.ds(j * PIECE, PIECE), :] = g[:, pl.ds(chunk * 2 * cols, 2 * cols)]
    for j, g in enumerate((g2, g3)):
        gs[pl.ds((2 + j) * PIECE, PIECE), :] = g[...]
    size = hta.shape[0] // BLOCKS
    rows = hta.shape[1]
    for q in range(2):
        out = outs[q % len(outs)]
        base = q * (out.shape[0] // 2) if len(outs) == 1 else 0
        for b in range(HALF):
            start = pl.multiple_of(block_at(DOWN_ORDERS[2 * chunk + q], first + b) * size, 8)
            mixed[q, pl.ds(b * size, size), pl.ds(0, rows)] = hta[pl.ds(start, size), :]
            mixed[q, pl.ds(b * size, size), pl.ds(rows, rows)] = htb[pl.ds(start, size), :]
        part = nn(mixed[q].astype(BF16), gs[:, pl.ds(q * cols, cols)])
        for b in range(HALF):
            block = part[b * size : (b + 1) * size]
            stack = [block[:, k * LANES : (k + 1) * LANES] for k in range(cols // LANES)]
            tall = size * len(stack)
            out[pl.ds(base + b * tall, tall), :] = jnp.concatenate(stack, axis=0).astype(BF16)


def down_half(first, chunk, hts, pieces, joint=False):
    ff, rows = hts[0].shape
    width = pieces[2].shape[1]
    count = 1 if joint else 2
    out = ((2 // count * HALF * ff // BLOCKS * (width // 2 // LANES), LANES), BF16)

    def body(*refs):
        down_body(first, chunk, *refs)

    return kernel(
        body,
        (*hts, *pieces),
        [out] * count,
        12,
        2 * rows * ff * width,
        scratch=(pltpu.VMEM((2, ff // 2, 2 * rows), F32), pltpu.VMEM((2 * rows, width), BF16)),
    )


def hidden_body(pieces, c0, c1, wd, slope, act, hid, gd, ud, comb0, comb1, gs):
    cw = jnp.concatenate([as_column(c0[...]), as_column(c1[...])], axis=0)
    for j, chunks in enumerate(pieces):
        at = 0
        for g in chunks:
            gs[pl.ds(j * PIECE, PIECE), pl.ds(at, g.shape[1])] = g[...]
            at += g.shape[1]
    tile = 256
    total = jnp.zeros((gs.shape[0], 1), F32)
    for f in range(wd.shape[0] // tile):
        at = pl.ds(f * tile, tile)
        back = nt(gs[...], wd[at, :])
        total = total + jnp.sum(hid[:, at].astype(F32) * back, axis=1, keepdims=True)
        back = cw * back
        gd[:, at] = (back * slope[:, at]).astype(BF16)
        ud[:, at] = (back * act[:, at]).astype(BF16)
    comb0[...] = as_row(total[:PIECE])
    comb1[...] = as_row(total[PIECE:])


def hidden_part(pieces, cws, wd, slope, act, hid):
    ff, d = wd.shape
    rows = 2 * PIECE
    counts = [len(chunks) for chunks in pieces]

    def body(*refs):
        first, second = refs[: counts[0]], refs[counts[0] : sum(counts)]
        hidden_body((first, second), *refs[sum(counts) :])

    return kernel(
        body,
        (*pieces[0], *pieces[1], *cws, wd, slope, act, hid),
        [((rows, ff), BF16), ((rows, ff), BF16), ROW, ROW],
        10,
        2 * rows * d * ff,
        scratch=(pltpu.VMEM((rows, d), BF16),),
    )


def gate_body(first, xta, xtb, gda, gdb, uda, udb, *refs):
    outs, mixed = refs[:4], refs[4]
    size = xta.shape[0] // BLOCKS // 2
    rows = xta.shape[1]
    for p in range(4):
        for b in range(HALF):
            start = pl.multiple_of(block_at(ORDERS[p], first + b) * (2 * size) + (p % 2) * size, size)
            mixed[p, pl.ds(b * size, size), pl.ds(0, rows)] = xta[pl.ds(start, size), :]
            mixed[p, pl.ds(b * size, size), pl.ds(rows, rows)] = xtb[pl.ds(start, size), :]
        ga, gb = (gda, gdb) if p < 2 else (uda, udb)
        cols = ga.shape[1]
        tile = 256
        per = tile // LANES
        tall = size * (cols // LANES)
        for n in range(cols // tile):
            at = pl.ds(n * tile, tile)
            part = nn(mixed[p, :, pl.ds(0, rows)], ga[:, at]) + nn(mixed[p, :, pl.ds(rows, rows)], gb[:, at])
            part = part.astype(BF16)
            for b in range(HALF):
                for k in range(per):
                    to = b * tall + (n * per + k) * size
                    outs[p][pl.ds(to, size), :] = part[b * size : (b + 1) * size, k * LANES : (k + 1) * LANES]


def gate_half(first, xts, gds, uds):
    d, rows = xts[0].shape
    ff = gds[0].shape[1]
    out = ((HALF * (d // BLOCKS // 2) * (ff // LANES), LANES), BF16)

    def body(*refs):
        gate_body(first, *refs)

    return kernel(
        body,
        (*xts, *gds, *uds),
        [out] * 4,
        12,
        4 * rows * ff * d,
        scratch=(pltpu.VMEM((4, d // 4, 2 * rows), BF16),),
    )


def rows_body(gda, gdb, uda, udb, wg, wu, r0, r1, r2, r3, gd, ud):
    half = gda.shape[0]
    for scratch, pair in ((gd, (gda, gdb)), (ud, (uda, udb))):
        for j, ref in enumerate(pair):
            scratch[pl.ds(j * half, half), :] = ref[...]
    tile = 512
    for n in range(wg.shape[0] // tile):
        at = pl.ds(n * tile, tile)
        total = (nt(gd[...], wg[at, :]) + nt(ud[...], wu[at, :])).astype(BF16)
        for j, r in enumerate((r0, r1, r2, r3)):
            r[:, at] = total[j * PIECE : (j + 1) * PIECE, :]


def finish_body(base, last, end2, end3, gate, up, down):
    recv = [r[...].astype(F32) for r in (last, end2, end3)]
    total = base[...] + jnp.concatenate(recv, axis=0)
    half, low = gate.shape[0] // 2, down.shape[0]
    cols = down.shape[1] // 4
    at = 0
    for p in range(4):
        out = gate if p < 2 else up
        for k in range(gate.shape[1] // LANES):
            block = total[at : at + half].astype(BF16)
            out[pl.ds(p % 2 * half, half), pl.ds(k * LANES, LANES)] = block
            at += half
    for p in range(4):
        for k in range(cols // LANES):
            block = total[at : at + low].astype(BF16)
            down[:, pl.ds(p * cols + k * LANES, LANES)] = block
            at += low


def summed(arrays, start, stop, kind=BF16):
    total = 0.0
    for blocks, a in arrays:
        size = a.shape[0] // blocks
        total = total + a[start * size : stop * size].astype(F32)
    return total.astype(kind)


def shards(tokens, cotangent, expert_ids, combine, w_gate, w_up, w_down):
    wg, wu, wd = w_gate[0], w_up[0], w_down[0]
    d, ff = wg.shape
    rows = 4 * PIECE

    tok_far = moved(tokens, "zl", 1)
    tok_near = moved(tokens, "c", 1)
    own = kernel(route_body, (expert_ids.T, combine.T), [ROW] * 4, 2, 1 << 10)
    cws = [own[0]] + [moved(own[m], GROUP, m) for m in (1, 2, 3)]
    cwa, cwb = cws[:2], cws[2:]
    cot_near = moved(cotangent, "c", 1)
    cot_far = [moved(cotangent[:, k * d // 2 : (k + 1) * d // 2], "zl", 1) for k in range(2)]
    tok_both = moved(tok_far, "c", 1)
    cot_both = [moved(cot_far[k], "c", 1) for k in range(2)]

    fa = forward(tokens, tok_near, cwa, wg, wu)
    fb = forward(tok_far, tok_both, cwb, wg, wu)
    hts, xts = (fa[3], fb[3]), (fa[4], fb[4])
    pieces = [(cotangent, cot_near, cot_far[k], cot_both[k]) for k in range(2)]
    down_send = down_half(HALF, 0, hts, pieces[0])
    down_z = down_half(HALF, 1, hts, pieces[1], joint=True)[0]
    ha = hidden_part(((cotangent,), (cot_near,)), cwa, wd, *fa[:3])
    hb = hidden_part((cot_far, cot_both), cwb, wd, *fb[:3])
    gds, uds = (ha[0], hb[0]), (ha[1], hb[1])
    gate_send = gate_half(HALF, xts, gds, uds)
    down_keep = [a for k in range(2) for a in down_half(0, k, hts, pieces[k])]
    gate_keep = gate_half(0, xts, gds, uds)
    grads = kernel(
        rows_body,
        (*gds, *uds, wg, wu),
        [((PIECE, d), BF16)] * 4,
        12,
        4 * rows * d * ff,
        scratch=(pltpu.VMEM((rows, ff), BF16),) * 2,
    )

    down_z = moved(down_z, *Z)
    size = down_z.shape[0] // 2
    down_got = [moved(down_send[p], *ORDERS[p][0]) for p in (0, 1)]
    down_got += [lax.optimization_barrier(a) for a in (down_z[:size], down_z[size:])]
    have = [
        [
            [(HALF, gate_keep[p]), (HALF, moved(gate_send[p], *ORDERS[p][0]))],
            [(HALF, down_keep[p]), (HALF, down_got[p])],
        ]
        for p in range(4)
    ]

    def joined(p, start, stop, kind=BF16):
        return jnp.concatenate([summed(held, start, stop, kind) for held in have[p]], axis=0)

    def shared(array, p, blocks):
        at = 0
        for held in have[p]:
            size = held[0][1].shape[0] // HALF * blocks
            held.append((blocks, array[at : at + size]))
            at += size

    for step, left in ((1, 16), (2, 8), (3, 4)):
        for p in range(4):
            shared(moved(joined(p, left // 2, left), *ORDERS[p][step]), p, left // 2)
    gates, downs = ([have[p][k] for p in range(4)] for k in (0, 1))
    last = moved(jnp.concatenate([summed(h, 1, 2) for h in gates + downs[:2]], axis=0), *Z)
    others = [moved(summed(downs[p], 1, 2), *DOWN_ORDERS[p][4]) for p in (2, 3)]
    base = jnp.concatenate([summed(h, 0, 1, F32) for h in gates + downs], axis=0)
    gate_grad, up_grad, down_grad = kernel(
        finish_body,
        (base, last, *others),
        [((d // BLOCKS, ff), BF16), ((d // BLOCKS, ff), BF16), ((ff // BLOCKS, d), BF16)],
        4,
        1 << 20,
    )

    near = moved(grads[1], "c", 1)
    far = (grads[2].astype(F32) + moved(grads[3], "c", 1).astype(F32)).astype(BF16)
    far = moved(far, "zl", 1)
    input_grad = (grads[0].astype(F32) + near.astype(F32) + far.astype(F32)).astype(BF16)

    comb = [ha[2], ha[3], hb[2], hb[3]]
    given = [comb[0]] + [moved(comb[m], GROUP, m) for m in (1, 2, 3)]
    combine_grad = kernel(combine_body, (expert_ids.T, *given), [((2, PIECE), F32)], 2, 1 << 10)[0].T
    return (input_grad, combine_grad, gate_grad[None], up_grad[None], down_grad[None])


def solution(mesh):
    torus = Mesh(mesh.devices.reshape(4, 2, 4, 2, 2), EVERY)
    tokens, weights, grads = P(EVERY, None), P(GROUP, None, None), P(GROUP, REPLICA, None)

    return jax.shard_map(
        shards,
        mesh=torus,
        in_specs=(tokens, tokens, tokens, tokens, weights, weights, weights),
        out_specs=(tokens, tokens, grads, grads, grads),
        check_vma=False,
    )
```

profile of v0, /device:TPU:0, one launch (start us, length us, event | category | flops | bytes accessed | tf_op | source)
XLA Modules:
  0.0 146.5 jit_solution(11396868539099545973)
XLA Ops:
  0.6 2.1 %collective-permute-start.9 = (bf16[128,2048]{1,0:T(8,128)(2,1)}, bf16[128,2048]{1,0:T(8,128)(2,1)S(1)}, u32[]{:S(2)}, u32[]{:S(2)}) collective-permute-start(bf16[128,2048]{1,0:T(8,128)(2,1)} %x0.1), channel_id=1, source_target_pairs={{0,2},{2,0},{1,3},{3,1},{4,6},{6,4},{5,7},{7,5},{8,10},{10,8},{9,1... | collective-permute-start | bytes 1572872 | tf_op jit(solution)/shard_map/ppermute | solution.py:26
  3.3 11.6 %collective-permute-done.9.x0 = bf16[128,2048]{1,0:T(8,128)(2,1)S(1)} collective-permute-done((bf16[128,2048]{1,0:T(8,128)(2,1)}, bf16[128,2048]{1,0:T(8,128)(2,1)S(1)}, u32[]{:S(2)}, u32[]{:S(2)}) %collective-permute-start.9) | collective-permute-done | bytes 524320 | tf_op jit(solution)/shard_map/ppermute | solution.py:26
  14.9 1.1 fusion.5
  16.0 1.8 %collective-permute-start.3 = (bf16[128,1024]{1,0:T(8,128)(2,1)S(1)}, bf16[128,1024]{1,0:T(8,128)(2,1)S(1)}, u32[]{:S(2)}, u32[]{:S(2)}) collective-permute-start(bf16[128,1024]{1,0:T(8,128)(2,1)S(1)} %get-tuple-element.98), channel_id=1, source_target_pairs={{0,2},{2,0},{1,3},{3,1},{4,6},{6,4},{5,7},{7,5},{8,10},{10,8},{9,1... | collective-permute-start | bytes 786440 | tf_op jit(solution)/shard_map/ppermute | solution.py:26
  17.8 0.7 copy-done.7
  18.5 0.7 copy-done.9
  19.5 0.9 collective-permute-done.1.c1.refs_3_
  20.7 4.5 %collective-permute-done.3.refs_0_.refs_4_ = bf16[128,1024]{1,0:T(8,128)(2,1)S(1)} collective-permute-done((bf16[128,1024]{1,0:T(8,128)(2,1)S(1)}, bf16[128,1024]{1,0:T(8,128)(2,1)S(1)}, u32[]{:S(2)}, u32[]{:S(2)}) %collective-permute-start.3) | collective-permute-done | bytes 262176 | tf_op jit(solution)/shard_map/ppermute | solution.py:26
  25.2 1.7 %collective-permute-start.7 = (f32[8,128]{1,0:T(8,128)S(1)}, f32[8,128]{1,0:T(8,128)S(1)}, u32[]{:S(2)}, u32[]{:S(2)}) collective-permute-start(f32[8,128]{1,0:T(8,128)S(1)} %get-tuple-element.54), channel_id=1, source_target_pairs={{0,2},{1,3},{2,0},{3,1},{4,6},{5,7},{6,4},{7,5},{8,10},{9,11},{10,... | collective-permute-start | bytes 12296 | tf_op jit(solution)/shard_map/ppermute | solution.py:26
  27.0 1.9 %copy-done.2 = bf16[1,2048,768]{2,1,0:T(8,128)(2,1)S(1)} copy-done((bf16[1,2048,768]{2,1,0:T(8,128)(2,1)S(1)}, bf16[1,2048,768]{2,1,0:T(8,128)(2,1)}, u32[]{:S(2)}) %copy-start.2) | copy-done | bytes 3145752
  28.9 1.9 %copy-done.4 = bf16[1,2048,768]{2,1,0:T(8,128)(2,1)S(1)} copy-done((bf16[1,2048,768]{2,1,0:T(8,128)(2,1)S(1)}, bf16[1,2048,768]{2,1,0:T(8,128)(2,1)}, u32[]{:S(2)}) %copy-start.4) | copy-done | bytes 3145752
  30.8 2.0 %shard_map.111 = (f32[256,768]{1,0:T(8,128)S(1)}, f32[256,768]{1,0:T(8,128)S(1)}, bf16[256,768]{1,0:T(8,128)(2,1)S(1)}, f32[768,256]{1,0:T(8,128)S(1)}, bf16[2048,256]{1,0:T(8,128)(2,1)S(1)}) custom-call(bf16[128,2048]{1,0:T(8,128)(2,1)S(1)} %copy-done.6, bf16[128,2048]{1,0:T(8,128)(2,1)S(1)} %collective-permute-done.2.x1, ...), custom_call_target="tpu_custom_call" | custom-call | flops 1610612736 | bytes 1048576 | tf_op jit(solution)/shard_map/pallas_call | solution.py:60
  33.4 1.2 shard_map.112
  35.0 0.9 collective-permute-done.8.c1.refs_5_
  35.9 2.0 %shard_map.113 = (f32[256,768]{1,0:T(8,128)S(1)}, f32[256,768]{1,0:T(8,128)S(1)}, bf16[256,768]{1,0:T(8,128)(2,1)S(1)}, f32[768,256]{1,0:T(8,128)S(1)}, bf16[2048,256]{1,0:T(8,128)(2,1)S(1)}) custom-call(bf16[128,2048]{1,0:T(8,128)(2,1)S(1)} %collective-permute-done.9.x0, bf16[128,2048]{1,0:T(8,128)(2,1)S(1)} %collective-permute-done.10.x1, ...), custom_call_target="tpu_custom_call" | custom-call | flops 1610612736 | bytes 1048576 | tf_op jit(solution)/shard_map/pallas_call | solution.py:60
  38.5 1.6 %collective-permute-start.18 = (bf16[1536,128]{1,0:T(8,128)(2,1)S(1)}, bf16[1536,128]{1,0:T(8,128)(2,1)S(1)}, u32[]{:S(2)}, u32[]{:S(2)}) collective-permute-start(bf16[1536,128]{1,0:T(8,128)(2,1)S(1)} %get-tuple-element.77), channel_id=1, source_target_pairs={{0,32},{32,0},{64,96},{96,64},{1,33},{33,1},{65,97},{97,65},{2,34}... | collective-permute-start | bytes 1179656 | tf_op jit(solution)/shard_map/ppermute | solution.py:26
  40.0 1.6 %collective-permute-start.23 = (bf16[1536,128]{1,0:T(8,128)(2,1)S(1)}, bf16[1536,128]{1,0:T(8,128)(2,1)S(1)}, u32[]{:S(2)}, u32[]{:S(2)}) collective-permute-start(bf16[1536,128]{1,0:T(8,128)(2,1)S(1)} %get-tuple-element.81), channel_id=1, source_target_pairs={{0,4},{4,0},{8,12},{12,8},{1,5},{5,1},{9,13},{13,9},{2,6},{6,2},{1... | collective-permute-start | bytes 1179656 | tf_op jit(solution)/shard_map/ppermute | solution.py:26
  41.6 1.2 shard_map.114
  42.8 3.4 %shard_map.115 = (bf16[128,2048]{1,0:T(8,128)(2,1)S(1)}, bf16[128,2048]{1,0:T(8,128)(2,1)S(1)}, bf16[128,2048]{1,0:T(8,128)(2,1)S(1)}, bf16[128,2048]{1,0:T(8,128)(2,1)S(1)}) custom-call(bf16[256,768]{1,0:T(8,128)(2,1)S(1)} %get-tuple-element.53.gda.refs_2_, bf16[256,768]{1,0:T(8,128)(2,1)S(1)} %get-tuple-element.59.gdb.refs_3_, ...), custom_call_target="tpu_custom_call" | custom-call | flops 3221225472 | bytes 1048576 | tf_op jit(solution)/shard_map/pallas_call | solution.py:60
  46.3 1.8 %shard_map.118 = (bf16[3072,128]{1,0:T(8,128)(2,1)S(1)}, bf16[3072,128]{1,0:T(8,128)(2,1)S(1)}, bf16[3072,128]{1,0:T(8,128)(2,1)S(1)}, bf16[3072,128]{1,0:T(8,128)(2,1)S(1)}) custom-call(bf16[2048,256]{1,0:T(8,128)(2,1)S(1)} %get-tuple-element.70.refs_0_, bf16[2048,256]{1,0:T(8,128)(2,1)S(1)} %get-tuple-element.71.refs_1_, ...), custom_call_target="tpu_custom_call" | custom-call | flops 1610612736 | bytes 1048576 | tf_op jit(solution)/shard_map/pallas_call | solution.py:60
  48.1 1.8 %shard_map.117 = (bf16[3072,128]{1,0:T(8,128)(2,1)S(1)}, bf16[3072,128]{1,0:T(8,128)(2,1)S(1)}, bf16[3072,128]{1,0:T(8,128)(2,1)S(1)}, bf16[3072,128]{1,0:T(8,128)(2,1)S(1)}) custom-call(bf16[2048,256]{1,0:T(8,128)(2,1)S(1)} %get-tuple-element.70.refs_0_, bf16[2048,256]{1,0:T(8,128)(2,1)S(1)} %get-tuple-element.71.refs_1_, ...), custom_call_target="tpu_custom_call" | custom-call | flops 1610612736 | bytes 1048576 | tf_op jit(solution)/shard_map/pallas_call | solution.py:60
  49.9 1.1 collective-permute-start.15
  52.2 1.2 collective-permute-start.16
  54.0 3.7 %collective-permute-start.28 = (bf16[3072,128]{1,0:T(8,128)(2,1)S(1)}, bf16[3072,128]{1,0:T(8,128)(2,1)S(1)}, u32[]{:S(2)}, u32[]{:S(2)}) collective-permute-start(bf16[3072,128]{1,0:T(8,128)(2,1)S(1)} %shard_map.122), channel_id=1, source_target_pairs={{0,16},{16,0},{1,17},{17,1},{2,18},{18,2},{3,19},{19,3},{4,20},{20... | collective-permute-start | bytes 2359304 | tf_op jit(solution)/shard_map/ppermute | solution.py:26
  59.5 2.8 %collective-permute-start.27 = (bf16[3072,128]{1,0:T(8,128)(2,1)S(1)}, bf16[3072,128]{1,0:T(8,128)(2,1)S(1)}, u32[]{:S(2)}, u32[]{:S(2)}) collective-permute-start(bf16[3072,128]{1,0:T(8,128)(2,1)S(1)} %get-tuple-element.83), channel_id=1, source_target_pairs={{0,96},{32,64},{64,32},{96,0},{1,97},{33,65},{65,33},{97,1},{2,98}... | collective-permute-start | bytes 2359304 | tf_op jit(solution)/shard_map/ppermute | solution.py:26
  62.4 13.0 %collective-permute-done.28 = bf16[3072,128]{1,0:T(8,128)(2,1)S(1)} collective-permute-done((bf16[3072,128]{1,0:T(8,128)(2,1)S(1)}, bf16[3072,128]{1,0:T(8,128)(2,1)S(1)}, u32[]{:S(2)}, u32[]{:S(2)}) %collective-permute-start.28) | collective-permute-done | bytes 786464 | tf_op jit(solution)/shard_map/ppermute | solution.py:26
  75.4 2.2 %collective-permute-start.32 = (bf16[3072,128]{1,0:T(8,128)(2,1)S(1)}, bf16[3072,128]{1,0:T(8,128)(2,1)S(1)}, u32[]{:S(2)}, u32[]{:S(2)}) collective-permute-start(bf16[3072,128]{1,0:T(8,128)(2,1)S(1)} %get-tuple-element.86), channel_id=1, source_target_pairs={{0,12},{4,8},{8,4},{12,0},{1,13},{5,9},{9,5},{13,1},{2,14},{6,10},... | collective-permute-start | bytes 2359304 | tf_op jit(solution)/shard_map/ppermute | solution.py:26
  78.7 2.6 %collective-permute-start.19 = (bf16[2304,128]{1,0:T(8,128)(2,1)S(1)}, bf16[2304,128]{1,0:T(8,128)(2,1)S(1)}, u32[]{:S(2)}, u32[]{:S(2)}) collective-permute-start(bf16[2304,128]{1,0:T(8,128)(2,1)S(1)} %pad_maximum_fusion), channel_id=1, source_target_pairs={{0,96},{32,64},{64,32},{96,0},{1,97},{33,65},{65,33},{97,1},{2,98}... | collective-permute-start | bytes 1769480 | tf_op jit(solution)/shard_map/ppermute | solution.py:26
  81.5 2.3 %collective-permute-start.24 = (bf16[2304,128]{1,0:T(8,128)(2,1)S(1)}, bf16[2304,128]{1,0:T(8,128)(2,1)S(1)}, u32[]{:S(2)}, u32[]{:S(2)}) collective-permute-start(bf16[2304,128]{1,0:T(8,128)(2,1)S(1)} %pad_maximum_fusion.1), channel_id=1, source_target_pairs={{0,12},{4,8},{8,4},{12,0},{1,13},{5,9},{9,5},{13,1},{2,14},{6,10},... | collective-permute-start | bytes 1769480 | tf_op jit(solution)/shard_map/ppermute | solution.py:26
  84.0 13.1 %collective-permute-done.32 = bf16[3072,128]{1,0:T(8,128)(2,1)S(1)} collective-permute-done((bf16[3072,128]{1,0:T(8,128)(2,1)S(1)}, bf16[3072,128]{1,0:T(8,128)(2,1)S(1)}, u32[]{:S(2)}, u32[]{:S(2)}) %collective-permute-start.32) | collective-permute-done | bytes 786464 | tf_op jit(solution)/shard_map/ppermute | solution.py:26
  98.3 9.9 %collective-permute-done.24 = bf16[2304,128]{1,0:T(8,128)(2,1)S(1)} collective-permute-done((bf16[2304,128]{1,0:T(8,128)(2,1)S(1)}, bf16[2304,128]{1,0:T(8,128)(2,1)S(1)}, u32[]{:S(2)}, u32[]{:S(2)}) %collective-permute-start.24) | collective-permute-done | bytes 589856 | tf_op jit(solution)/shard_map/ppermute | solution.py:26
  108.3 1.0 collective-permute-done.29
  110.1 0.9 collective-permute-done.33
  110.9 2.2 %collective-permute-start.30 = (bf16[1152,128]{1,0:T(8,128)(2,1)S(1)}, bf16[1152,128]{1,0:T(8,128)(2,1)S(1)}, u32[]{:S(2)}, u32[]{:S(2)}) collective-permute-start(bf16[1152,128]{1,0:T(8,128)(2,1)S(1)} %pad_maximum_fusion.6), channel_id=1, source_target_pairs={{0,12},{4,8},{8,4},{12,0},{1,13},{5,9},{9,5},{13,1},{2,14},{6,10},... | collective-permute-start | bytes 884744 | tf_op jit(solution)/shard_map/ppermute | solution.py:26
  113.3 3.2 %collective-permute-done.20 = bf16[1152,128]{1,0:T(8,128)(2,1)S(1)} collective-permute-done((bf16[1152,128]{1,0:T(8,128)(2,1)S(1)}, bf16[1152,128]{1,0:T(8,128)(2,1)S(1)}, u32[]{:S(2)}, u32[]{:S(2)}) %collective-permute-start.20) | collective-permute-done | bytes 294944 | tf_op jit(solution)/shard_map/ppermute | solution.py:26
  116.5 2.8 %collective-permute-start.34 = (bf16[1152,128]{1,0:T(8,128)(2,1)S(1)}, bf16[1152,128]{1,0:T(8,128)(2,1)S(1)}, u32[]{:S(2)}, u32[]{:S(2)}) collective-permute-start(bf16[1152,128]{1,0:T(8,128)(2,1)S(1)} %pad_maximum_fusion.7), channel_id=1, source_target_pairs={{0,96},{32,64},{64,32},{96,0},{1,97},{33,65},{65,33},{97,1},{2,98}... | collective-permute-start | bytes 884744 | tf_op jit(solution)/shard_map/ppermute | solution.py:26
  119.4 2.3 %collective-permute-start.21 = (bf16[576,128]{1,0:T(8,128)(2,1)S(1)}, bf16[576,128]{1,0:T(8,128)(2,1)S(1)}, u32[]{:S(2)}, u32[]{:S(2)}) collective-permute-start(bf16[576,128]{1,0:T(8,128)(2,1)S(1)} %pad_maximum_fusion.8), channel_id=1, source_target_pairs={{0,12},{4,8},{8,4},{12,0},{1,13},{5,9},{9,5},{13,1},{2,14},{6,10},... | collective-permute-start | bytes 442376 | tf_op jit(solution)/shard_map/ppermute | solution.py:26
  121.8 0.9 collective-permute-start.26
  122.8 3.7 %collective-permute-done.34 = bf16[1152,128]{1,0:T(8,128)(2,1)S(1)} collective-permute-done((bf16[1152,128]{1,0:T(8,128)(2,1)S(1)}, bf16[1152,128]{1,0:T(8,128)(2,1)S(1)}, u32[]{:S(2)}, u32[]{:S(2)}) %collective-permute-start.34) | collective-permute-done | bytes 294944 | tf_op jit(solution)/shard_map/ppermute | solution.py:26
  126.5 0.8 collective-permute-start.31
  128.3 3.3 %collective-permute-done.31 = bf16[576,128]{1,0:T(8,128)(2,1)S(1)} collective-permute-done((bf16[576,128]{1,0:T(8,128)(2,1)S(1)}, bf16[576,128]{1,0:T(8,128)(2,1)S(1)}, u32[]{:S(2)}, u32[]{:S(2)}) %collective-permute-start.31) | collective-permute-done | bytes 147488 | tf_op jit(solution)/shard_map/ppermute | solution.py:26
  131.6 1.0 collective-permute-done.35
  132.8 2.2 %collective-permute-start.38 = (bf16[96,128]{1,0:T(8,128)(2,1)S(1)}, bf16[96,128]{1,0:T(8,128)(2,1)S(1)}, u32[]{:S(2)}, u32[]{:S(2)}) collective-permute-start(bf16[96,128]{1,0:T(8,128)(2,1)S(1)} %get-tuple-element.91), channel_id=1, source_target_pairs={{0,12},{4,8},{8,4},{12,0},{1,13},{5,9},{9,5},{13,1},{2,14},{6,10},... | collective-permute-start | bytes 73736 | tf_op jit(solution)/shard_map/ppermute | solution.py:26
  135.0 2.7 %collective-permute-start.37 = (bf16[96,128]{1,0:T(8,128)(2,1)S(1)}, bf16[96,128]{1,0:T(8,128)(2,1)S(1)}, u32[]{:S(2)}, u32[]{:S(2)}) collective-permute-start(bf16[96,128]{1,0:T(8,128)(2,1)S(1)} %get-tuple-element.93), channel_id=1, source_target_pairs={{0,96},{32,64},{64,32},{96,0},{1,97},{33,65},{65,33},{97,1},{2,98}... | collective-permute-start | bytes 73736 | tf_op jit(solution)/shard_map/ppermute | solution.py:26
  138.0 2.6 %collective-permute-start.36 = (bf16[960,128]{1,0:T(8,128)(2,1)S(1)}, bf16[960,128]{1,0:T(8,128)(2,1)S(1)}, u32[]{:S(2)}, u32[]{:S(2)}) collective-permute-start(bf16[960,128]{1,0:T(8,128)(2,1)S(1)} %constant_dynamic-update-slice_fusion), channel_id=1, source_target_pairs={{0,16},{16,0},{1,17},{17,1},{2,18},{18,2},{3,19},{19,3},{4,20},{20... | collective-permute-start | bytes 737288 | tf_op jit(solution)/shard_map/ppermute | solution.py:26
  140.6 1.0 add_convert_fusion
  141.7 4.1 %collective-permute-done.36.last = bf16[960,128]{1,0:T(8,128)(2,1)S(1)} collective-permute-done((bf16[960,128]{1,0:T(8,128)(2,1)S(1)}, bf16[960,128]{1,0:T(8,128)(2,1)S(1)}, u32[]{:S(2)}, u32[]{:S(2)}) %collective-permute-start.36) | collective-permute-done | bytes 245792 | tf_op jit(solution)/shard_map/ppermute | solution.py:26
  145.7 0.7 shard_map.123
  (118 shorter events, 11.8 us)
Async XLA Ops:
  0.6 26.3 %copy-start.6 = (bf16[128,2048]{1,0:T(8,128)(2,1)S(1)}, bf16[128,2048]{1,0:T(8,128)(2,1)}, u32[]{:S(2)}) copy-start(bf16[128,2048]{1,0:T(8,128)(2,1)} %x0.1) | copy-start | bytes 1572868
  0.6 14.2 %collective-permute-start.9 = (bf16[128,2048]{1,0:T(8,128)(2,1)}, bf16[128,2048]{1,0:T(8,128)(2,1)S(1)}, u32[]{:S(2)}, u32[]{:S(2)}) collective-permute-start(bf16[128,2048]{1,0:T(8,128)(2,1)} %x0.1), channel_id=1, source_target_pairs={{0,2},{2,0},{1,3},{3,1},{4,6},{6,4},{5,7},{7,5},{8,10},{10,8},{9,1... | collective-permute-start | bytes 1572872 | tf_op jit(solution)/shard_map/ppermute | solution.py:26
  2.7 24.2 %collective-permute-start.2 = (bf16[128,2048]{1,0:T(8,128)(2,1)}, bf16[128,2048]{1,0:T(8,128)(2,1)S(1)}, u32[]{:S(2)}, u32[]{:S(2)}) collective-permute-start(bf16[128,2048]{1,0:T(8,128)(2,1)} %x0.1), channel_id=1, source_target_pairs={{0,1},{1,0},{2,3},{3,2},{4,5},{5,4},{6,7},{7,6},{8,9},{9,8},{10,11... | collective-permute-start | bytes 1572872 | tf_op jit(solution)/shard_map/ppermute | solution.py:26
  2.8 30.5 %collective-permute-start = (bf16[128,2048]{1,0:T(8,128)(2,1)}, bf16[128,2048]{1,0:T(8,128)(2,1)S(1)}, u32[]{:S(2)}, u32[]{:S(2)}) collective-permute-start(bf16[128,2048]{1,0:T(8,128)(2,1)} %refs_2_.7), channel_id=1, source_target_pairs={{0,1},{1,0},{2,3},{3,2},{4,5},{5,4},{6,7},{7,6},{8,9},{9,8},{10,11... | collective-permute-start | bytes 1572872 | tf_op jit(solution)/shard_map/ppermute | solution.py:26
  14.9 21.0 %collective-permute-start.10 = (bf16[128,2048]{1,0:T(8,128)(2,1)S(1)}, bf16[128,2048]{1,0:T(8,128)(2,1)S(1)}, u32[]{:S(2)}, u32[]{:S(2)}) collective-permute-start(bf16[128,2048]{1,0:T(8,128)(2,1)S(1)} %collective-permute-done.9.x0), channel_id=1, source_target_pairs={{0,1},{1,0},{2,3},{3,2},{4,5},{5,4},{6,7},{7,6},{8,9},{9,8},{10,11... | collective-permute-start | bytes 1572872 | tf_op jit(solution)/shard_map/ppermute | solution.py:26
  16.0 9.3 %collective-permute-start.3 = (bf16[128,1024]{1,0:T(8,128)(2,1)S(1)}, bf16[128,1024]{1,0:T(8,128)(2,1)S(1)}, u32[]{:S(2)}, u32[]{:S(2)}) collective-permute-start(bf16[128,1024]{1,0:T(8,128)(2,1)S(1)} %get-tuple-element.98), channel_id=1, source_target_pairs={{0,2},{2,0},{1,3},{3,1},{4,6},{6,4},{5,7},{7,5},{8,10},{10,8},{9,1... | collective-permute-start | bytes 786440 | tf_op jit(solution)/shard_map/ppermute | solution.py:26
  17.8 0.7 copy-start.7
  19.1 1.2 collective-permute-start.1
  20.4 12.4 %collective-permute-start.4 = (bf16[128,1024]{1,0:T(8,128)(2,1)S(1)}, bf16[128,1024]{1,0:T(8,128)(2,1)S(1)}, u32[]{:S(2)}, u32[]{:S(2)}) collective-permute-start(bf16[128,1024]{1,0:T(8,128)(2,1)S(1)} %get-tuple-element.97), channel_id=1, source_target_pairs={{0,2},{2,0},{1,3},{3,1},{4,6},{6,4},{5,7},{7,5},{8,10},{10,8},{9,1... | collective-permute-start | bytes 786440 | tf_op jit(solution)/shard_map/ppermute | solution.py:26
  25.2 9.4 %collective-permute-start.7 = (f32[8,128]{1,0:T(8,128)S(1)}, f32[8,128]{1,0:T(8,128)S(1)}, u32[]{:S(2)}, u32[]{:S(2)}) collective-permute-start(f32[8,128]{1,0:T(8,128)S(1)} %get-tuple-element.54), channel_id=1, source_target_pairs={{0,2},{1,3},{2,0},{3,1},{4,6},{5,7},{6,4},{7,5},{8,10},{9,11},{10,... | collective-permute-start | bytes 12296 | tf_op jit(solution)/shard_map/ppermute | solution.py:26
  27.0 10.9 %collective-permute-start.5 = (bf16[128,1024]{1,0:T(8,128)(2,1)S(1)}, bf16[128,1024]{1,0:T(8,128)(2,1)S(1)}, u32[]{:S(2)}, u32[]{:S(2)}) collective-permute-start(bf16[128,1024]{1,0:T(8,128)(2,1)S(1)} %collective-permute-done.3.refs_0_.refs_4_), channel_id=1, source_target_pairs={{0,1},{1,0},{2,3},{3,2},{4,5},{5,4},{6,7},{7,6},{8,9},{9,8},{10,11... | collective-permute-start | bytes 786440 | tf_op jit(solution)/shard_map/ppermute | solution.py:26
  27.0 1.9 %copy-start.2 = (bf16[1,2048,768]{2,1,0:T(8,128)(2,1)S(1)}, bf16[1,2048,768]{2,1,0:T(8,128)(2,1)}, u32[]{:S(2)}) copy-start(bf16[1,2048,768]{2,1,0:T(8,128)(2,1)} %param.11) | copy-start | bytes 9437188
  28.9 1.9 %copy-start.4 = (bf16[1,2048,768]{2,1,0:T(8,128)(2,1)S(1)}, bf16[1,2048,768]{2,1,0:T(8,128)(2,1)}, u32[]{:S(2)}) copy-start(bf16[1,2048,768]{2,1,0:T(8,128)(2,1)} %param.12) | copy-start | bytes 9437188
  30.7 2.7 %copy-start = (bf16[128,2048]{1,0:T(8,128)(2,1)S(1)}, bf16[128,2048]{1,0:T(8,128)(2,1)}, u32[]{:S(2)}) copy-start(bf16[128,2048]{1,0:T(8,128)(2,1)} %refs_2_.7) | copy-start | bytes 1572868
  30.7 2.7 %copy-start.1 = (bf16[1,768,2048]{2,1,0:T(8,128)(2,1)S(1)}, bf16[1,768,2048]{2,1,0:T(8,128)(2,1)}, u32[]{:S(2)}) copy-start(bf16[1,768,2048]{2,1,0:T(8,128)(2,1)} %param.13) | copy-start | bytes 9437188
  30.8 5.1 %copy-start.5 = (bf16[1,2048,768]{2,1,0:T(8,128)(2,1)S(1)}, bf16[1,2048,768]{2,1,0:T(8,128)(2,1)}, u32[]{:S(2)}) copy-start(bf16[1,2048,768]{2,1,0:T(8,128)(2,1)} %param.12) | copy-start | bytes 9437188
  32.8 3.1 %collective-permute-start.8 = (f32[8,128]{1,0:T(8,128)S(1)}, f32[8,128]{1,0:T(8,128)S(1)}, u32[]{:S(2)}, u32[]{:S(2)}) collective-permute-start(f32[8,128]{1,0:T(8,128)S(1)} %get-tuple-element.55), channel_id=1, source_target_pairs={{0,3},{1,2},{2,1},{3,0},{4,7},{5,6},{6,5},{7,4},{8,11},{9,10},{10,... | collective-permute-start | bytes 12296 | tf_op jit(solution)/shard_map/ppermute | solution.py:26
  33.2 8.4 %collective-permute-start.6 = (bf16[128,1024]{1,0:T(8,128)(2,1)S(1)}, bf16[128,1024]{1,0:T(8,128)(2,1)S(1)}, u32[]{:S(2)}, u32[]{:S(2)}) collective-permute-start(bf16[128,1024]{1,0:T(8,128)(2,1)S(1)} %collective-permute-done.4.refs_1_.refs_4_), channel_id=1, source_target_pairs={{0,1},{1,0},{2,3},{3,2},{4,5},{5,4},{6,7},{7,6},{8,9},{9,8},{10,11... | collective-permute-start | bytes 786440 | tf_op jit(solution)/shard_map/ppermute | solution.py:26
  33.4 2.4 %copy-start.3 = (bf16[1,2048,768]{2,1,0:T(8,128)(2,1)S(1)}, bf16[1,2048,768]{2,1,0:T(8,128)(2,1)}, u32[]{:S(2)}) copy-start(bf16[1,2048,768]{2,1,0:T(8,128)(2,1)} %param.11) | copy-start | bytes 9437188
  34.7 17.5 %collective-permute-start.14 = (f32[8,128]{1,0:T(8,128)S(1)}, f32[8,128]{1,0:T(8,128)S(1)}, u32[]{:S(2)}, u32[]{:S(2)}) collective-permute-start(f32[8,128]{1,0:T(8,128)S(1)} %get-tuple-element.67), channel_id=1, source_target_pairs={{0,1},{1,0},{2,3},{3,2},{4,5},{5,4},{6,7},{7,6},{8,9},{9,8},{10,11... | collective-permute-start | bytes 12296 | tf_op jit(solution)/shard_map/ppermute | solution.py:26
  38.5 19.8 %collective-permute-start.18 = (bf16[1536,128]{1,0:T(8,128)(2,1)S(1)}, bf16[1536,128]{1,0:T(8,128)(2,1)S(1)}, u32[]{:S(2)}, u32[]{:S(2)}) collective-permute-start(bf16[1536,128]{1,0:T(8,128)(2,1)S(1)} %get-tuple-element.77), channel_id=1, source_target_pairs={{0,32},{32,0},{64,96},{96,64},{1,33},{33,1},{65,97},{97,65},{2,34}... | collective-permute-start | bytes 1179656 | tf_op jit(solution)/shard_map/ppermute | solution.py:26
  40.0 18.8 %collective-permute-start.23 = (bf16[1536,128]{1,0:T(8,128)(2,1)S(1)}, bf16[1536,128]{1,0:T(8,128)(2,1)S(1)}, u32[]{:S(2)}, u32[]{:S(2)}) collective-permute-start(bf16[1536,128]{1,0:T(8,128)(2,1)S(1)} %get-tuple-element.81), channel_id=1, source_target_pairs={{0,4},{4,0},{8,12},{12,8},{1,5},{5,1},{9,13},{13,9},{2,6},{6,2},{1... | collective-permute-start | bytes 1179656 | tf_op jit(solution)/shard_map/ppermute | solution.py:26
  49.9 4.1 %collective-permute-start.15 = (f32[8,128]{1,0:T(8,128)S(1)}, f32[8,128]{1,0:T(8,128)S(1)}, u32[]{:S(2)}, u32[]{:S(2)}) collective-permute-start(f32[8,128]{1,0:T(8,128)S(1)} %get-tuple-element.68), channel_id=1, source_target_pairs={{0,2},{1,3},{2,0},{3,1},{4,6},{5,7},{6,4},{7,5},{8,10},{9,11},{10,... | collective-permute-start | bytes 12296 | tf_op jit(solution)/shard_map/ppermute | solution.py:26
  51.0 8.5 %collective-permute-start.12 = (bf16[128,2048]{1,0:T(8,128)(2,1)S(1)}, bf16[128,2048]{1,0:T(8,128)(2,1)S(1)}, u32[]{:S(2)}, u32[]{:S(2)}) collective-permute-start(bf16[128,2048]{1,0:T(8,128)(2,1)S(1)} %get-tuple-element.65), channel_id=1, source_target_pairs={{0,1},{1,0},{2,3},{3,2},{4,5},{5,4},{6,7},{7,6},{8,9},{9,8},{10,11... | collective-permute-start | bytes 1572872 | tf_op jit(solution)/shard_map/ppermute | solution.py:26
  52.2 5.5 %copy-start.8 = (s32[128,2]{0,1:T(2,128)S(1)}, s32[128,2]{0,1:T(2,128)}, u32[]{:S(2)}) copy-start(s32[128,2]{0,1:T(2,128)} %param.9) | copy-start | bytes 3076
  52.2 5.5 %collective-permute-start.16 = (f32[8,128]{1,0:T(8,128)S(1)}, f32[8,128]{1,0:T(8,128)S(1)}, u32[]{:S(2)}, u32[]{:S(2)}) collective-permute-start(f32[8,128]{1,0:T(8,128)S(1)} %get-tuple-element.69), channel_id=1, source_target_pairs={{0,3},{1,2},{2,1},{3,0},{4,7},{5,6},{6,5},{7,4},{8,11},{9,10},{10,... | collective-permute-start | bytes 12296 | tf_op jit(solution)/shard_map/ppermute | solution.py:26
  54.0 21.4 %collective-permute-start.28 = (bf16[3072,128]{1,0:T(8,128)(2,1)S(1)}, bf16[3072,128]{1,0:T(8,128)(2,1)S(1)}, u32[]{:S(2)}, u32[]{:S(2)}) collective-permute-start(bf16[3072,128]{1,0:T(8,128)(2,1)S(1)} %shard_map.122), channel_id=1, source_target_pairs={{0,16},{16,0},{1,17},{17,1},{2,18},{18,2},{3,19},{19,3},{4,20},{20... | collective-permute-start | bytes 2359304 | tf_op jit(solution)/shard_map/ppermute | solution.py:26
  57.7 83.0 %collective-permute-start.11 = (bf16[128,2048]{1,0:T(8,128)(2,1)S(1)}, bf16[128,2048]{1,0:T(8,128)(2,1)S(1)}, u32[]{:S(2)}, u32[]{:S(2)}) collective-permute-start(bf16[128,2048]{1,0:T(8,128)(2,1)S(1)} %get-tuple-element.63), channel_id=1, source_target_pairs={{0,1},{1,0},{2,3},{3,2},{4,5},{5,4},{6,7},{7,6},{8,9},{9,8},{10,11... | collective-permute-start | bytes 1572872 | tf_op jit(solution)/shard_map/ppermute | solution.py:26
  58.2 19.9 %collective-permute-start.17 = (bf16[3072,128]{1,0:T(8,128)(2,1)S(1)}, bf16[3072,128]{1,0:T(8,128)(2,1)S(1)}, u32[]{:S(2)}, u32[]{:S(2)}) collective-permute-start(bf16[3072,128]{1,0:T(8,128)(2,1)S(1)} %get-tuple-element.73), channel_id=1, source_target_pairs={{0,32},{32,0},{64,96},{96,64},{1,33},{33,1},{65,97},{97,65},{2,34}... | collective-permute-start | bytes 2359304 | tf_op jit(solution)/shard_map/ppermute | solution.py:26
  58.8 19.9 %collective-permute-start.22 = (bf16[3072,128]{1,0:T(8,128)(2,1)S(1)}, bf16[3072,128]{1,0:T(8,128)(2,1)S(1)}, u32[]{:S(2)}, u32[]{:S(2)}) collective-permute-start(bf16[3072,128]{1,0:T(8,128)(2,1)S(1)} %get-tuple-element.79), channel_id=1, source_target_pairs={{0,4},{4,0},{8,12},{12,8},{1,5},{5,1},{9,13},{13,9},{2,6},{6,2},{1... | collective-permute-start | bytes 2359304 | tf_op jit(solution)/shard_map/ppermute | solution.py:26
  59.5 22.1 %collective-permute-start.27 = (bf16[3072,128]{1,0:T(8,128)(2,1)S(1)}, bf16[3072,128]{1,0:T(8,128)(2,1)S(1)}, u32[]{:S(2)}, u32[]{:S(2)}) collective-permute-start(bf16[3072,128]{1,0:T(8,128)(2,1)S(1)} %get-tuple-element.83), channel_id=1, source_target_pairs={{0,96},{32,64},{64,32},{96,0},{1,97},{33,65},{65,33},{97,1},{2,98}... | collective-permute-start | bytes 2359304 | tf_op jit(solution)/shard_map/ppermute | solution.py:26
  75.4 21.6 %collective-permute-start.32 = (bf16[3072,128]{1,0:T(8,128)(2,1)S(1)}, bf16[3072,128]{1,0:T(8,128)(2,1)S(1)}, u32[]{:S(2)}, u32[]{:S(2)}) collective-permute-start(bf16[3072,128]{1,0:T(8,128)(2,1)S(1)} %get-tuple-element.86), channel_id=1, source_target_pairs={{0,12},{4,8},{8,4},{12,0},{1,13},{5,9},{9,5},{13,1},{2,14},{6,10},... | collective-permute-start | bytes 2359304 | tf_op jit(solution)/shard_map/ppermute | solution.py:26
  78.2 62.4 %collective-permute-start.13 = (bf16[128,2048]{1,0:T(8,128)(2,1)S(1)}, bf16[128,2048]{1,0:T(8,128)(2,1)S(1)}, u32[]{:S(2)}, u32[]{:S(2)}) collective-permute-start(bf16[128,2048]{1,0:T(8,128)(2,1)S(1)} %add_convert_fusion.1), channel_id=1, source_target_pairs={{0,2},{2,0},{1,3},{3,1},{4,6},{6,4},{5,7},{7,5},{8,10},{10,8},{9,1... | collective-permute-start | bytes 1572872 | tf_op jit(solution)/shard_map/ppermute | solution.py:26
  78.7 19.0 %collective-permute-start.19 = (bf16[2304,128]{1,0:T(8,128)(2,1)S(1)}, bf16[2304,128]{1,0:T(8,128)(2,1)S(1)}, u32[]{:S(2)}, u32[]{:S(2)}) collective-permute-start(bf16[2304,128]{1,0:T(8,128)(2,1)S(1)} %pad_maximum_fusion), channel_id=1, source_target_pairs={{0,96},{32,64},{64,32},{96,0},{1,97},{33,65},{65,33},{97,1},{2,98}... | collective-permute-start | bytes 1769480 | tf_op jit(solution)/shard_map/ppermute | solution.py:26
  81.5 26.6 %collective-permute-start.24 = (bf16[2304,128]{1,0:T(8,128)(2,1)S(1)}, bf16[2304,128]{1,0:T(8,128)(2,1)S(1)}, u32[]{:S(2)}, u32[]{:S(2)}) collective-permute-start(bf16[2304,128]{1,0:T(8,128)(2,1)S(1)} %pad_maximum_fusion.1), channel_id=1, source_target_pairs={{0,12},{4,8},{8,4},{12,0},{1,13},{5,9},{9,5},{13,1},{2,14},{6,10},... | collective-permute-start | bytes 1769480 | tf_op jit(solution)/shard_map/ppermute | solution.py:26
  97.0 12.3 %collective-permute-start.29 = (bf16[2304,128]{1,0:T(8,128)(2,1)S(1)}, bf16[2304,128]{1,0:T(8,128)(2,1)S(1)}, u32[]{:S(2)}, u32[]{:S(2)}) collective-permute-start(bf16[2304,128]{1,0:T(8,128)(2,1)S(1)} %pad_maximum_fusion.2), channel_id=1, source_target_pairs={{0,32},{32,0},{64,96},{96,64},{1,33},{33,1},{65,97},{97,65},{2,34}... | collective-permute-start | bytes 1769480 | tf_op jit(solution)/shard_map/ppermute | solution.py:26
  97.8 13.1 %collective-permute-start.33 = (bf16[2304,128]{1,0:T(8,128)(2,1)S(1)}, bf16[2304,128]{1,0:T(8,128)(2,1)S(1)}, u32[]{:S(2)}, u32[]{:S(2)}) collective-permute-start(bf16[2304,128]{1,0:T(8,128)(2,1)S(1)} %pad_maximum_fusion.3), channel_id=1, source_target_pairs={{0,4},{4,0},{8,12},{12,8},{1,5},{5,1},{9,13},{13,9},{2,6},{6,2},{1... | collective-permute-start | bytes 1769480 | tf_op jit(solution)/shard_map/ppermute | solution.py:26
  108.2 8.3 %collective-permute-start.20 = (bf16[1152,128]{1,0:T(8,128)(2,1)S(1)}, bf16[1152,128]{1,0:T(8,128)(2,1)S(1)}, u32[]{:S(2)}, u32[]{:S(2)}) collective-permute-start(bf16[1152,128]{1,0:T(8,128)(2,1)S(1)} %pad_maximum_fusion.4), channel_id=1, source_target_pairs={{0,4},{4,0},{8,12},{12,8},{1,5},{5,1},{9,13},{13,9},{2,6},{6,2},{1... | collective-permute-start | bytes 884744 | tf_op jit(solution)/shard_map/ppermute | solution.py:26
  109.4 10.0 %collective-permute-start.25 = (bf16[1152,128]{1,0:T(8,128)(2,1)S(1)}, bf16[1152,128]{1,0:T(8,128)(2,1)S(1)}, u32[]{:S(2)}, u32[]{:S(2)}) collective-permute-start(bf16[1152,128]{1,0:T(8,128)(2,1)S(1)} %pad_maximum_fusion.5), channel_id=1, source_target_pairs={{0,32},{32,0},{64,96},{96,64},{1,33},{33,1},{65,97},{97,65},{2,34}... | collective-permute-start | bytes 884744 | tf_op jit(solution)/shard_map/ppermute | solution.py:26
  110.9 10.8 %collective-permute-start.30 = (bf16[1152,128]{1,0:T(8,128)(2,1)S(1)}, bf16[1152,128]{1,0:T(8,128)(2,1)S(1)}, u32[]{:S(2)}, u32[]{:S(2)}) collective-permute-start(bf16[1152,128]{1,0:T(8,128)(2,1)S(1)} %pad_maximum_fusion.6), channel_id=1, source_target_pairs={{0,12},{4,8},{8,4},{12,0},{1,13},{5,9},{9,5},{13,1},{2,14},{6,10},... | collective-permute-start | bytes 884744 | tf_op jit(solution)/shard_map/ppermute | solution.py:26
  116.5 10.0 %collective-permute-start.34 = (bf16[1152,128]{1,0:T(8,128)(2,1)S(1)}, bf16[1152,128]{1,0:T(8,128)(2,1)S(1)}, u32[]{:S(2)}, u32[]{:S(2)}) collective-permute-start(bf16[1152,128]{1,0:T(8,128)(2,1)S(1)} %pad_maximum_fusion.7), channel_id=1, source_target_pairs={{0,96},{32,64},{64,32},{96,0},{1,97},{33,65},{65,33},{97,1},{2,98}... | collective-permute-start | bytes 884744 | tf_op jit(solution)/shard_map/ppermute | solution.py:26
  119.4 8.0 %collective-permute-start.21 = (bf16[576,128]{1,0:T(8,128)(2,1)S(1)}, bf16[576,128]{1,0:T(8,128)(2,1)S(1)}, u32[]{:S(2)}, u32[]{:S(2)}) collective-permute-start(bf16[576,128]{1,0:T(8,128)(2,1)S(1)} %pad_maximum_fusion.8), channel_id=1, source_target_pairs={{0,12},{4,8},{8,4},{12,0},{1,13},{5,9},{9,5},{13,1},{2,14},{6,10},... | collective-permute-start | bytes 442376 | tf_op jit(solution)/shard_map/ppermute | solution.py:26
  121.8 6.5 %collective-permute-start.26 = (bf16[576,128]{1,0:T(8,128)(2,1)S(1)}, bf16[576,128]{1,0:T(8,128)(2,1)S(1)}, u32[]{:S(2)}, u32[]{:S(2)}) collective-permute-start(bf16[576,128]{1,0:T(8,128)(2,1)S(1)} %pad_maximum_fusion.9), channel_id=1, source_target_pairs={{0,96},{32,64},{64,32},{96,0},{1,97},{33,65},{65,33},{97,1},{2,98}... | collective-permute-start | bytes 442376 | tf_op jit(solution)/shard_map/ppermute | solution.py:26
  126.5 5.1 %collective-permute-start.31 = (bf16[576,128]{1,0:T(8,128)(2,1)S(1)}, bf16[576,128]{1,0:T(8,128)(2,1)S(1)}, u32[]{:S(2)}, u32[]{:S(2)}) collective-permute-start(bf16[576,128]{1,0:T(8,128)(2,1)S(1)} %pad_maximum_fusion.10), channel_id=1, source_target_pairs={{0,4},{4,0},{8,12},{12,8},{1,5},{5,1},{9,13},{13,9},{2,6},{6,2},{1... | collective-permute-start | bytes 442376 | tf_op jit(solution)/shard_map/ppermute | solution.py:26
  127.4 5.2 %collective-permute-start.35 = (bf16[576,128]{1,0:T(8,128)(2,1)S(1)}, bf16[576,128]{1,0:T(8,128)(2,1)S(1)}, u32[]{:S(2)}, u32[]{:S(2)}) collective-permute-start(bf16[576,128]{1,0:T(8,128)(2,1)S(1)} %pad_maximum_fusion.11), channel_id=1, source_target_pairs={{0,32},{32,0},{64,96},{96,64},{1,33},{33,1},{65,97},{97,65},{2,34}... | collective-permute-start | bytes 442376 | tf_op jit(solution)/shard_map/ppermute | solution.py:26
  132.8 8.9 %collective-permute-start.38 = (bf16[96,128]{1,0:T(8,128)(2,1)S(1)}, bf16[96,128]{1,0:T(8,128)(2,1)S(1)}, u32[]{:S(2)}, u32[]{:S(2)}) collective-permute-start(bf16[96,128]{1,0:T(8,128)(2,1)S(1)} %get-tuple-element.91), channel_id=1, source_target_pairs={{0,12},{4,8},{8,4},{12,0},{1,13},{5,9},{9,5},{13,1},{2,14},{6,10},... | collective-permute-start | bytes 73736 | tf_op jit(solution)/shard_map/ppermute | solution.py:26
  135.0 6.6 %collective-permute-start.37 = (bf16[96,128]{1,0:T(8,128)(2,1)S(1)}, bf16[96,128]{1,0:T(8,128)(2,1)S(1)}, u32[]{:S(2)}, u32[]{:S(2)}) collective-permute-start(bf16[96,128]{1,0:T(8,128)(2,1)S(1)} %get-tuple-element.93), channel_id=1, source_target_pairs={{0,96},{32,64},{64,32},{96,0},{1,97},{33,65},{65,33},{97,1},{2,98}... | collective-permute-start | bytes 73736 | tf_op jit(solution)/shard_map/ppermute | solution.py:26
  138.0 7.8 %collective-permute-start.36 = (bf16[960,128]{1,0:T(8,128)(2,1)S(1)}, bf16[960,128]{1,0:T(8,128)(2,1)S(1)}, u32[]{:S(2)}, u32[]{:S(2)}) collective-permute-start(bf16[960,128]{1,0:T(8,128)(2,1)S(1)} %constant_dynamic-update-slice_fusion), channel_id=1, source_target_pairs={{0,16},{16,0},{1,17},{17,1},{2,18},{18,2},{3,19},{19,3},{4,20},{20... | collective-permute-start | bytes 737288 | tf_op jit(solution)/shard_map/ppermute | solution.py:26
  (1 other events, 0.7 us)
where the time goes:
time: 147 us; the launch traced here: 146 us
  waiting for transfers between devices  72 us (49%)
  starting transfers between devices  46.5 us (32%)
  Pallas kernels  17.1 us (12%)
  local copies, waits for them, and re-layouts  6.27 us (4%)
  other arithmetic  3.46 us (2%)
    ppermute x39, waiting for transfers between devices, moved(): lax.ppermute(array, axis, [(i, i ^ mask) for i in range(lax.axis_size(axi...  72 us
    ppermute x39, starting transfers between devices, moved(): lax.ppermute(array, axis, [(i, i ^ mask) for i in range(lax.axis_size(axi...  46.5 us
    pallas_call x14, Pallas kernels, kernel(): pl.pallas_call(body, in_specs=[vmem] * len(ins), out_specs=[vmem] * len(o...  17.1 us
    unnamed x20, local copies, waits for them, and re-layouts  5.16 us
  transfers between devices with their start and end apart: 39, of which 16 were waited for; matrix products, arithmetic and copies ran while one was open for 3% of the time, Pallas kernels for 11%

commit v1 on v0

--- a/solution.py
+++ b/solution.py
@@ -15,6 +15,7 @@
 XA, XB, YA, YB, Z = ("x", 1), ("x", 3), ("y", 1), ("y", 3), ("zh", 1)
 ORDERS = ((XA, XB, YA, YB, Z), (YA, YB, XA, XB, Z), (XB, XA, YB, YA, Z), (YB, YA, XB, XA, Z))
 DOWN_ORDERS = ORDERS[:2] + ((Z, XA, YB, YA, XB), (Z, YA, XB, XA, YB))
+CHAINS = (2, 3, 0, 1)
 BLOCKS = 32
 HALF = BLOCKS // 2
 PIECE = 128
@@ -255,9 +256,14 @@
             r[:, at] = total[j * PIECE : (j + 1) * PIECE, :]
 
 
-def finish_body(base, last, end2, end3, gate, up, down):
-    recv = [r[...].astype(F32) for r in (last, end2, end3)]
-    total = base[...] + jnp.concatenate(recv, axis=0)
+def finish_body(*refs):
+    bases, (last_a, end2, end3, last_b), (gate, up, down) = refs[:8], refs[8:12], refs[12:]
+    first, second = last_a[...].astype(F32), last_b[...].astype(F32)
+    tall, low = bases[0].shape[0], bases[4].shape[0]
+    recvs = [second[:tall], second[tall : 2 * tall], first[:tall], first[tall:]]
+    recvs += [second[2 * tall : 2 * tall + low], second[2 * tall + low :]]
+    recvs += [end2[...].astype(F32), end3[...].astype(F32)]
+    total = jnp.concatenate([b[...] + r for b, r in zip(bases, recvs)], axis=0)
     half, low = gate.shape[0] // 2, down.shape[0]
     cols = down.shape[1] // 4
     at = 0
@@ -330,26 +336,34 @@
         for p in range(4)
     ]
 
-    def joined(p, start, stop, kind=BF16):
-        return jnp.concatenate([summed(held, start, stop, kind) for held in have[p]], axis=0)
-
-    def shared(array, p, blocks):
+    gates, downs = ([have[p][k] for p in range(4)] for k in (0, 1))
+    left = {id(h): HALF for h in gates + downs}
+
+    def exchange(held, step):
+        sends = [summed(h, left[id(h)] // 2, left[id(h)]) for h in held]
+        sent = jnp.concatenate(sends, axis=0)
+        got = moved(sent, *step)
         at = 0
-        for held in have[p]:
-            size = held[0][1].shape[0] // HALF * blocks
-            held.append((blocks, array[at : at + size]))
-            at += size
-
-    for step, left in ((1, 16), (2, 8), (3, 4)):
-        for p in range(4):
-            shared(moved(joined(p, left // 2, left), *ORDERS[p][step]), p, left // 2)
-    gates, downs = ([have[p][k] for p in range(4)] for k in (0, 1))
-    last = moved(jnp.concatenate([summed(h, 1, 2) for h in gates + downs[:2]], axis=0), *Z)
-    others = [moved(summed(downs[p], 1, 2), *DOWN_ORDERS[p][4]) for p in (2, 3)]
-    base = jnp.concatenate([summed(h, 0, 1, F32) for h in gates + downs], axis=0)
+        for h, send in zip(held, sends):
+            left[id(h)] //= 2
+            h.append((left[id(h)], got[at : at + send.shape[0]]))
+            at += send.shape[0]
+        return got
+
+    for p in CHAINS:
+        exchange(have[p][: 2 if p < 2 else 1], ORDERS[p][1])
+    for p in (2, 3):
+        exchange(downs[p : p + 1], DOWN_ORDERS[p][1])
+    for step in (2, 3):
+        for p in CHAINS:
+            exchange(have[p], ORDERS[p][step])
+    last_a = exchange(gates[2:], Z)
+    ends = [exchange(downs[p : p + 1], DOWN_ORDERS[p][4]) for p in (2, 3)]
+    last_b = exchange(gates[:2] + downs[:2], Z)
+    bases = [summed(h[:-1], 0, 1, F32) for h in gates + downs]
     gate_grad, up_grad, down_grad = kernel(
         finish_body,
-        (base, last, *others),
+        (*bases, last_a, *ends, last_b),
         [((d // BLOCKS, ff), BF16), ((d // BLOCKS, ff), BF16), ((ff // BLOCKS, d), BF16)],
         4,
         1 << 20,

time: 147 us -> 164 us (1.12)
  waiting for transfers between devices: 72 us -> 85.5 us
  starting transfers between devices: 46.5 us -> 50.1 us
    ppermute x39 -> x42, waiting for transfers between devices: 72 us -> 85.5 us  [moved(): lax.ppermute(array, axis, [(i, i ^ mask) for i in range(lax.axis_size(axi...]
    ppermute x39 -> x42, starting transfers between devices: 46.5 us -> 50.1 us  [moved(): lax.ppermute(array, axis, [(i, i ^ mask) for i in range(lax.axis_size(axi...]
  transfers between devices with their start and end apart: 39 -> 42, of which waited for: 16 -> 18; matrix products, arithmetic and copies ran while one was open for 3% -> 3% of each run, Pallas kernels for 11% -> 10%
where the time goes in v1:
time: 164 us; the launch traced here: 163 us
  waiting for transfers between devices  85.5 us (52%)
  starting transfers between devices  50.1 us (31%)
  Pallas kernels  17 us (10%)
  local copies, waits for them, and re-layouts  6.27 us (4%)
  other arithmetic  3.3 us (2%)
    ppermute x42, waiting for transfers between devices, moved(): lax.ppermute(array, axis, [(i, i ^ mask) for i in range(lax.axis_size(axi...  85.5 us
    ppermute x42, starting transfers between devices, moved(): lax.ppermute(array, axis, [(i, i ^ mask) for i in range(lax.axis_size(axi...  50.1 us
    pallas_call x14, Pallas kernels, kernel(): pl.pallas_call(body, in_specs=[vmem] * len(ins), out_specs=[vmem] * len(o...  17 us
    unnamed x20, local copies, waits for them, and re-layouts  5.16 us
  transfers between devices with their start and end apart: 42, of which 18 were waited for; matrix products, arithmetic and copies ran while one was open for 3% of the time, Pallas kernels for 10%

profile of v1, /device:TPU:0, one launch (start us, length us, event | category | flops | bytes accessed | tf_op | source)
XLA Modules:
  0.0 163.4 jit_solution(14772988321416821822)
XLA Ops:
  0.6 2.1 %collective-permute-start.9 = (bf16[128,2048]{1,0:T(8,128)(2,1)}, bf16[128,2048]{1,0:T(8,128)(2,1)S(1)}, u32[]{:S(2)}, u32[]{:S(2)}) collective-permute-start(bf16[128,2048]{1,0:T(8,128)(2,1)} %x0.1), channel_id=1, source_target_pairs={{0,2},{2,0},{1,3},{3,1},{4,6},{6,4},{5,7},{7,5},{8,10},{10,8},{9,1... | collective-permute-start | bytes 1572872 | tf_op jit(solution)/shard_map/ppermute | solution.py:27
  3.3 11.6 %collective-permute-done.9.x0 = bf16[128,2048]{1,0:T(8,128)(2,1)S(1)} collective-permute-done((bf16[128,2048]{1,0:T(8,128)(2,1)}, bf16[128,2048]{1,0:T(8,128)(2,1)S(1)}, u32[]{:S(2)}, u32[]{:S(2)}) %collective-permute-start.9) | collective-permute-done | bytes 524320 | tf_op jit(solution)/shard_map/ppermute | solution.py:27
  14.9 1.1 fusion.1
  16.0 1.8 %collective-permute-start.3 = (bf16[128,1024]{1,0:T(8,128)(2,1)S(1)}, bf16[128,1024]{1,0:T(8,128)(2,1)S(1)}, u32[]{:S(2)}, u32[]{:S(2)}) collective-permute-start(bf16[128,1024]{1,0:T(8,128)(2,1)S(1)} %get-tuple-element.110), channel_id=1, source_target_pairs={{0,2},{2,0},{1,3},{3,1},{4,6},{6,4},{5,7},{7,5},{8,10},{10,8},{9,1... | collective-permute-start | bytes 786440 | tf_op jit(solution)/shard_map/ppermute | solution.py:27
  19.5 0.9 collective-permute-done.1.c1.refs_3_
  20.7 4.5 %collective-permute-done.3.refs_0_.refs_4_ = bf16[128,1024]{1,0:T(8,128)(2,1)S(1)} collective-permute-done((bf16[128,1024]{1,0:T(8,128)(2,1)S(1)}, bf16[128,1024]{1,0:T(8,128)(2,1)S(1)}, u32[]{:S(2)}, u32[]{:S(2)}) %collective-permute-start.3) | collective-permute-done | bytes 262176 | tf_op jit(solution)/shard_map/ppermute | solution.py:27
  25.2 1.7 %collective-permute-start.7 = (f32[8,128]{1,0:T(8,128)S(1)}, f32[8,128]{1,0:T(8,128)S(1)}, u32[]{:S(2)}, u32[]{:S(2)}) collective-permute-start(f32[8,128]{1,0:T(8,128)S(1)} %get-tuple-element.54), channel_id=1, source_target_pairs={{0,2},{1,3},{2,0},{3,1},{4,6},{5,7},{6,4},{7,5},{8,10},{9,11},{10,... | collective-permute-start | bytes 12296 | tf_op jit(solution)/shard_map/ppermute | solution.py:27
  27.0 1.9 %copy-done.2 = bf16[1,2048,768]{2,1,0:T(8,128)(2,1)S(1)} copy-done((bf16[1,2048,768]{2,1,0:T(8,128)(2,1)S(1)}, bf16[1,2048,768]{2,1,0:T(8,128)(2,1)}, u32[]{:S(2)}) %copy-start.2) | copy-done | bytes 3145752
  28.9 1.9 %copy-done.4 = bf16[1,2048,768]{2,1,0:T(8,128)(2,1)S(1)} copy-done((bf16[1,2048,768]{2,1,0:T(8,128)(2,1)S(1)}, bf16[1,2048,768]{2,1,0:T(8,128)(2,1)}, u32[]{:S(2)}) %copy-start.4) | copy-done | bytes 3145752
  30.8 2.0 %shard_map.111 = (f32[256,768]{1,0:T(8,128)S(1)}, f32[256,768]{1,0:T(8,128)S(1)}, bf16[256,768]{1,0:T(8,128)(2,1)S(1)}, f32[768,256]{1,0:T(8,128)S(1)}, bf16[2048,256]{1,0:T(8,128)(2,1)S(1)}) custom-call(bf16[128,2048]{1,0:T(8,128)(2,1)S(1)} %copy-done.6, bf16[128,2048]{1,0:T(8,128)(2,1)S(1)} %collective-permute-done.2.x1, ...), custom_call_target="tpu_custom_call" | custom-call | flops 1610612736 | bytes 1048576 | tf_op jit(solution)/shard_map/pallas_call | solution.py:61
  33.4 1.2 shard_map.112
  35.9 2.0 %shard_map.113 = (f32[256,768]{1,0:T(8,128)S(1)}, f32[256,768]{1,0:T(8,128)S(1)}, bf16[256,768]{1,0:T(8,128)(2,1)S(1)}, f32[768,256]{1,0:T(8,128)S(1)}, bf16[2048,256]{1,0:T(8,128)(2,1)S(1)}) custom-call(bf16[128,2048]{1,0:T(8,128)(2,1)S(1)} %collective-permute-done.9.x0, bf16[128,2048]{1,0:T(8,128)(2,1)S(1)} %collective-permute-done.10.x1, ...), custom_call_target="tpu_custom_call" | custom-call | flops 1610612736 | bytes 1048576 | tf_op jit(solution)/shard_map/pallas_call | solution.py:61
  38.5 1.6 %collective-permute-start.23 = (bf16[1536,128]{1,0:T(8,128)(2,1)S(1)}, bf16[1536,128]{1,0:T(8,128)(2,1)S(1)}, u32[]{:S(2)}, u32[]{:S(2)}) collective-permute-start(bf16[1536,128]{1,0:T(8,128)(2,1)S(1)} %get-tuple-element.81), channel_id=1, source_target_pairs={{0,4},{4,0},{8,12},{12,8},{1,5},{5,1},{9,13},{13,9},{2,6},{6,2},{1... | collective-permute-start | bytes 1179656 | tf_op jit(solution)/shard_map/ppermute | solution.py:27
  40.1 1.5 collective-permute-start.18
  41.6 1.2 shard_map.114
  42.8 3.4 %shard_map.115 = (bf16[128,2048]{1,0:T(8,128)(2,1)S(1)}, bf16[128,2048]{1,0:T(8,128)(2,1)S(1)}, bf16[128,2048]{1,0:T(8,128)(2,1)S(1)}, bf16[128,2048]{1,0:T(8,128)(2,1)S(1)}) custom-call(bf16[256,768]{1,0:T(8,128)(2,1)S(1)} %get-tuple-element.53.gda.refs_2_, bf16[256,768]{1,0:T(8,128)(2,1)S(1)} %get-tuple-element.59.gdb.refs_3_, ...), custom_call_target="tpu_custom_call" | custom-call | flops 3221225472 | bytes 1048576 | tf_op jit(solution)/shard_map/pallas_call | solution.py:61
  46.3 1.8 %shard_map.117 = (bf16[3072,128]{1,0:T(8,128)(2,1)S(1)}, bf16[3072,128]{1,0:T(8,128)(2,1)S(1)}, bf16[3072,128]{1,0:T(8,128)(2,1)S(1)}, bf16[3072,128]{1,0:T(8,128)(2,1)S(1)}) custom-call(bf16[2048,256]{1,0:T(8,128)(2,1)S(1)} %get-tuple-element.70.refs_0_, bf16[2048,256]{1,0:T(8,128)(2,1)S(1)} %get-tuple-element.71.refs_1_, ...), custom_call_target="tpu_custom_call" | custom-call | flops 1610612736 | bytes 1048576 | tf_op jit(solution)/shard_map/pallas_call | solution.py:61
  48.1 1.8 %shard_map.118 = (bf16[3072,128]{1,0:T(8,128)(2,1)S(1)}, bf16[3072,128]{1,0:T(8,128)(2,1)S(1)}, bf16[3072,128]{1,0:T(8,128)(2,1)S(1)}, bf16[3072,128]{1,0:T(8,128)(2,1)S(1)}) custom-call(bf16[2048,256]{1,0:T(8,128)(2,1)S(1)} %get-tuple-element.70.refs_0_, bf16[2048,256]{1,0:T(8,128)(2,1)S(1)} %get-tuple-element.71.refs_1_, ...), custom_call_target="tpu_custom_call" | custom-call | flops 1610612736 | bytes 1048576 | tf_op jit(solution)/shard_map/pallas_call | solution.py:61
  49.9 1.1 collective-permute-start.15
  52.2 1.2 collective-permute-start.16
  56.4 3.6 %collective-permute-start.29 = (bf16[3072,128]{1,0:T(8,128)(2,1)S(1)}, bf16[3072,128]{1,0:T(8,128)(2,1)S(1)}, u32[]{:S(2)}, u32[]{:S(2)}) collective-permute-start(bf16[3072,128]{1,0:T(8,128)(2,1)S(1)} %shard_map.122), channel_id=1, source_target_pairs={{0,16},{16,0},{1,17},{17,1},{2,18},{18,2},{3,19},{19,3},{4,20},{20... | collective-permute-start | bytes 2359304 | tf_op jit(solution)/shard_map/ppermute | solution.py:27
  60.0 2.3 %collective-permute-start.33 = (bf16[3072,128]{1,0:T(8,128)(2,1)S(1)}, bf16[3072,128]{1,0:T(8,128)(2,1)S(1)}, u32[]{:S(2)}, u32[]{:S(2)}) collective-permute-start(bf16[3072,128]{1,0:T(8,128)(2,1)S(1)} %get-tuple-element.86), channel_id=1, source_target_pairs={{0,12},{4,8},{8,4},{12,0},{1,13},{5,9},{9,5},{13,1},{2,14},{6,10},... | collective-permute-start | bytes 2359304 | tf_op jit(solution)/shard_map/ppermute | solution.py:27
  62.4 2.8 %collective-permute-start.27 = (bf16[3072,128]{1,0:T(8,128)(2,1)S(1)}, bf16[3072,128]{1,0:T(8,128)(2,1)S(1)}, u32[]{:S(2)}, u32[]{:S(2)}) collective-permute-start(bf16[3072,128]{1,0:T(8,128)(2,1)S(1)} %get-tuple-element.83), channel_id=1, source_target_pairs={{0,96},{32,64},{64,32},{96,0},{1,97},{33,65},{65,33},{97,1},{2,98}... | collective-permute-start | bytes 2359304 | tf_op jit(solution)/shard_map/ppermute | solution.py:27
  65.4 12.5 %collective-permute-done.29 = bf16[3072,128]{1,0:T(8,128)(2,1)S(1)} collective-permute-done((bf16[3072,128]{1,0:T(8,128)(2,1)S(1)}, bf16[3072,128]{1,0:T(8,128)(2,1)S(1)}, u32[]{:S(2)}, u32[]{:S(2)}) %collective-permute-start.29) | collective-permute-done | bytes 786464 | tf_op jit(solution)/shard_map/ppermute | solution.py:27
  79.0 1.8 %collective-permute-done.33 = bf16[3072,128]{1,0:T(8,128)(2,1)S(1)} collective-permute-done((bf16[3072,128]{1,0:T(8,128)(2,1)S(1)}, bf16[3072,128]{1,0:T(8,128)(2,1)S(1)}, u32[]{:S(2)}, u32[]{:S(2)}) %collective-permute-start.33) | collective-permute-done | bytes 786464 | tf_op jit(solution)/shard_map/ppermute | solution.py:27
  80.7 2.2 %collective-permute-start.24 = (bf16[2304,128]{1,0:T(8,128)(2,1)S(1)}, bf16[2304,128]{1,0:T(8,128)(2,1)S(1)}, u32[]{:S(2)}, u32[]{:S(2)}) collective-permute-start(bf16[2304,128]{1,0:T(8,128)(2,1)S(1)} %pad_maximum_fusion.1), channel_id=1, source_target_pairs={{0,12},{4,8},{8,4},{12,0},{1,13},{5,9},{9,5},{13,1},{2,14},{6,10},... | collective-permute-start | bytes 1769480 | tf_op jit(solution)/shard_map/ppermute | solution.py:27
  83.3 2.1 %collective-permute-start.35 = (bf16[768,128]{1,0:T(8,128)(2,1)S(1)}, bf16[768,128]{1,0:T(8,128)(2,1)S(1)}, u32[]{:S(2)}, u32[]{:S(2)}) collective-permute-start(bf16[768,128]{1,0:T(8,128)(2,1)S(1)} %add_convert_fusion.6), channel_id=1, source_target_pairs={{0,4},{4,0},{8,12},{12,8},{1,5},{5,1},{9,13},{13,9},{2,6},{6,2},{1... | collective-permute-start | bytes 589832 | tf_op jit(solution)/shard_map/ppermute | solution.py:27
  85.6 11.5 %collective-permute-done.35 = bf16[768,128]{1,0:T(8,128)(2,1)S(1)} collective-permute-done((bf16[768,128]{1,0:T(8,128)(2,1)S(1)}, bf16[768,128]{1,0:T(8,128)(2,1)S(1)}, u32[]{:S(2)}, u32[]{:S(2)}) %collective-permute-start.35) | collective-permute-done | bytes 196640 | tf_op jit(solution)/shard_map/ppermute | solution.py:27
  97.1 1.5 collective-permute-start.30
  98.6 4.1 %collective-permute-done.30 = bf16[768,128]{1,0:T(8,128)(2,1)S(1)} collective-permute-done((bf16[768,128]{1,0:T(8,128)(2,1)S(1)}, bf16[768,128]{1,0:T(8,128)(2,1)S(1)}, u32[]{:S(2)}, u32[]{:S(2)}) %collective-permute-start.30) | collective-permute-done | bytes 196640 | tf_op jit(solution)/shard_map/ppermute | solution.py:27
  102.8 3.1 %collective-permute-start.19 = (bf16[2304,128]{1,0:T(8,128)(2,1)S(1)}, bf16[2304,128]{1,0:T(8,128)(2,1)S(1)}, u32[]{:S(2)}, u32[]{:S(2)}) collective-permute-start(bf16[2304,128]{1,0:T(8,128)(2,1)S(1)} %pad_maximum_fusion), channel_id=1, source_target_pairs={{0,96},{32,64},{64,32},{96,0},{1,97},{33,65},{65,33},{97,1},{2,98}... | collective-permute-start | bytes 1769480 | tf_op jit(solution)/shard_map/ppermute | solution.py:27
  106.2 7.5 %collective-permute-done.28 = bf16[1536,128]{1,0:T(8,128)(2,1)S(1)} collective-permute-done((bf16[1536,128]{1,0:T(8,128)(2,1)S(1)}, bf16[1536,128]{1,0:T(8,128)(2,1)S(1)}, u32[]{:S(2)}, u32[]{:S(2)}) %collective-permute-start.28) | collective-permute-done | bytes 393248 | tf_op jit(solution)/shard_map/ppermute | solution.py:27
  114.1 1.2 collective-permute-start.31
  115.4 3.6 %collective-permute-done.19 = bf16[2304,128]{1,0:T(8,128)(2,1)S(1)} collective-permute-done((bf16[2304,128]{1,0:T(8,128)(2,1)S(1)}, bf16[2304,128]{1,0:T(8,128)(2,1)S(1)}, u32[]{:S(2)}, u32[]{:S(2)}) %collective-permute-start.19) | collective-permute-done | bytes 589856 | tf_op jit(solution)/shard_map/ppermute | solution.py:27
  119.6 2.7 %collective-permute-done.36 = bf16[1152,128]{1,0:T(8,128)(2,1)S(1)} collective-permute-done((bf16[1152,128]{1,0:T(8,128)(2,1)S(1)}, bf16[1152,128]{1,0:T(8,128)(2,1)S(1)}, u32[]{:S(2)}, u32[]{:S(2)}) %collective-permute-start.36) | collective-permute-done | bytes 294944 | tf_op jit(solution)/shard_map/ppermute | solution.py:27
  123.4 5.2 %collective-permute-done.37 = bf16[576,128]{1,0:T(8,128)(2,1)S(1)} collective-permute-done((bf16[576,128]{1,0:T(8,128)(2,1)S(1)}, bf16[576,128]{1,0:T(8,128)(2,1)S(1)}, u32[]{:S(2)}, u32[]{:S(2)}) %collective-permute-start.37) | collective-permute-done | bytes 147488 | tf_op jit(solution)/shard_map/ppermute | solution.py:27
  128.7 1.0 collective-permute-start.32
  129.7 4.1 %collective-permute-done.32 = bf16[576,128]{1,0:T(8,128)(2,1)S(1)} collective-permute-done((bf16[576,128]{1,0:T(8,128)(2,1)S(1)}, bf16[576,128]{1,0:T(8,128)(2,1)S(1)}, u32[]{:S(2)}, u32[]{:S(2)}) %collective-permute-start.32) | collective-permute-done | bytes 147488 | tf_op jit(solution)/shard_map/ppermute | solution.py:27
  133.9 4.5 %collective-permute-start.38 = (bf16[384,128]{1,0:T(8,128)(2,1)S(1)}, bf16[384,128]{1,0:T(8,128)(2,1)S(1)}, u32[]{:S(2)}, u32[]{:S(2)}) collective-permute-start(bf16[384,128]{1,0:T(8,128)(2,1)S(1)} %pad_maximum_fusion.11), channel_id=1, source_target_pairs={{0,16},{16,0},{1,17},{17,1},{2,18},{18,2},{3,19},{19,3},{4,20},{20... | collective-permute-start | bytes 294920 | tf_op jit(solution)/shard_map/ppermute | solution.py:27
  138.5 1.5 collective-permute-start.40
  140.2 2.8 %collective-permute-start.26 = (bf16[576,128]{1,0:T(8,128)(2,1)S(1)}, bf16[576,128]{1,0:T(8,128)(2,1)S(1)}, u32[]{:S(2)}, u32[]{:S(2)}) collective-permute-start(bf16[576,128]{1,0:T(8,128)(2,1)S(1)} %pad_maximum_fusion.7), channel_id=1, source_target_pairs={{0,96},{32,64},{64,32},{96,0},{1,97},{33,65},{65,33},{97,1},{2,98}... | collective-permute-start | bytes 442376 | tf_op jit(solution)/shard_map/ppermute | solution.py:27
  143.1 3.5 %collective-permute-done.26 = bf16[576,128]{1,0:T(8,128)(2,1)S(1)} collective-permute-done((bf16[576,128]{1,0:T(8,128)(2,1)S(1)}, bf16[576,128]{1,0:T(8,128)(2,1)S(1)}, u32[]{:S(2)}, u32[]{:S(2)}) %collective-permute-start.26) | collective-permute-done | bytes 147488 | tf_op jit(solution)/shard_map/ppermute | solution.py:27
  146.6 1.8 %collective-permute-start.21 = (bf16[576,128]{1,0:T(8,128)(2,1)S(1)}, bf16[576,128]{1,0:T(8,128)(2,1)S(1)}, u32[]{:S(2)}, u32[]{:S(2)}) collective-permute-start(bf16[576,128]{1,0:T(8,128)(2,1)S(1)} %pad_maximum_fusion.6), channel_id=1, source_target_pairs={{0,12},{4,8},{8,4},{12,0},{1,13},{5,9},{9,5},{13,1},{2,14},{6,10},... | collective-permute-start | bytes 442376 | tf_op jit(solution)/shard_map/ppermute | solution.py:27
  148.5 4.5 %collective-permute-done.21 = bf16[576,128]{1,0:T(8,128)(2,1)S(1)} collective-permute-done((bf16[576,128]{1,0:T(8,128)(2,1)S(1)}, bf16[576,128]{1,0:T(8,128)(2,1)S(1)}, u32[]{:S(2)}, u32[]{:S(2)}) %collective-permute-start.21) | collective-permute-done | bytes 147488 | tf_op jit(solution)/shard_map/ppermute | solution.py:27
  153.0 2.7 %collective-permute-start.39 = (bf16[96,128]{1,0:T(8,128)(2,1)S(1)}, bf16[96,128]{1,0:T(8,128)(2,1)S(1)}, u32[]{:S(2)}, u32[]{:S(2)}) collective-permute-start(bf16[96,128]{1,0:T(8,128)(2,1)S(1)} %get-tuple-element.105), channel_id=1, source_target_pairs={{0,96},{32,64},{64,32},{96,0},{1,97},{33,65},{65,33},{97,1},{2,98}... | collective-permute-start | bytes 73736 | tf_op jit(solution)/shard_map/ppermute | solution.py:27
  156.0 1.0 add_convert_fusion
  157.0 1.0 collective-permute-done.39.refs_9_
  158.0 4.6 %collective-permute-done.41.refs_11_ = bf16[576,128]{1,0:T(8,128)(2,1)S(1)} collective-permute-done((bf16[576,128]{1,0:T(8,128)(2,1)S(1)}, bf16[576,128]{1,0:T(8,128)(2,1)S(1)}, u32[]{:S(2)}, u32[]{:S(2)}) %collective-permute-start.41) | collective-permute-done | bytes 147488 | tf_op jit(solution)/shard_map/ppermute | solution.py:27
  (118 shorter events, 14.9 us)
Async XLA Ops:
  0.6 26.3 %copy-start.6 = (bf16[128,2048]{1,0:T(8,128)(2,1)S(1)}, bf16[128,2048]{1,0:T(8,128)(2,1)}, u32[]{:S(2)}) copy-start(bf16[128,2048]{1,0:T(8,128)(2,1)} %x0.1) | copy-start | bytes 1572868
  0.6 14.2 %collective-permute-start.9 = (bf16[128,2048]{1,0:T(8,128)(2,1)}, bf16[128,2048]{1,0:T(8,128)(2,1)S(1)}, u32[]{:S(2)}, u32[]{:S(2)}) collective-permute-start(bf16[128,2048]{1,0:T(8,128)(2,1)} %x0.1), channel_id=1, source_target_pairs={{0,2},{2,0},{1,3},{3,1},{4,6},{6,4},{5,7},{7,5},{8,10},{10,8},{9,1... | collective-permute-start | bytes 1572872 | tf_op jit(solution)/shard_map/ppermute | solution.py:27
  2.7 24.2 %collective-permute-start.2 = (bf16[128,2048]{1,0:T(8,128)(2,1)}, bf16[128,2048]{1,0:T(8,128)(2,1)S(1)}, u32[]{:S(2)}, u32[]{:S(2)}) collective-permute-start(bf16[128,2048]{1,0:T(8,128)(2,1)} %x0.1), channel_id=1, source_target_pairs={{0,1},{1,0},{2,3},{3,2},{4,5},{5,4},{6,7},{7,6},{8,9},{9,8},{10,11... | collective-permute-start | bytes 1572872 | tf_op jit(solution)/shard_map/ppermute | solution.py:27
  2.8 30.5 %collective-permute-start = (bf16[128,2048]{1,0:T(8,128)(2,1)}, bf16[128,2048]{1,0:T(8,128)(2,1)S(1)}, u32[]{:S(2)}, u32[]{:S(2)}) collective-permute-start(bf16[128,2048]{1,0:T(8,128)(2,1)} %refs_2_.7), channel_id=1, source_target_pairs={{0,1},{1,0},{2,3},{3,2},{4,5},{5,4},{6,7},{7,6},{8,9},{9,8},{10,11... | collective-permute-start | bytes 1572872 | tf_op jit(solution)/shard_map/ppermute | solution.py:27
  14.9 21.0 %collective-permute-start.10 = (bf16[128,2048]{1,0:T(8,128)(2,1)S(1)}, bf16[128,2048]{1,0:T(8,128)(2,1)S(1)}, u32[]{:S(2)}, u32[]{:S(2)}) collective-permute-start(bf16[128,2048]{1,0:T(8,128)(2,1)S(1)} %collective-permute-done.9.x0), channel_id=1, source_target_pairs={{0,1},{1,0},{2,3},{3,2},{4,5},{5,4},{6,7},{7,6},{8,9},{9,8},{10,11... | collective-permute-start | bytes 1572872 | tf_op jit(solution)/shard_map/ppermute | solution.py:27
  16.0 9.3 %collective-permute-start.3 = (bf16[128,1024]{1,0:T(8,128)(2,1)S(1)}, bf16[128,1024]{1,0:T(8,128)(2,1)S(1)}, u32[]{:S(2)}, u32[]{:S(2)}) collective-permute-start(bf16[128,1024]{1,0:T(8,128)(2,1)S(1)} %get-tuple-element.110), channel_id=1, source_target_pairs={{0,2},{2,0},{1,3},{3,1},{4,6},{6,4},{5,7},{7,5},{8,10},{10,8},{9,1... | collective-permute-start | bytes 786440 | tf_op jit(solution)/shard_map/ppermute | solution.py:27
  19.1 1.2 collective-permute-start.1
  20.4 12.4 %collective-permute-start.4 = (bf16[128,1024]{1,0:T(8,128)(2,1)S(1)}, bf16[128,1024]{1,0:T(8,128)(2,1)S(1)}, u32[]{:S(2)}, u32[]{:S(2)}) collective-permute-start(bf16[128,1024]{1,0:T(8,128)(2,1)S(1)} %get-tuple-element.109), channel_id=1, source_target_pairs={{0,2},{2,0},{1,3},{3,1},{4,6},{6,4},{5,7},{7,5},{8,10},{10,8},{9,1... | collective-permute-start | bytes 786440 | tf_op jit(solution)/shard_map/ppermute | solution.py:27
  25.2 9.4 %collective-permute-start.7 = (f32[8,128]{1,0:T(8,128)S(1)}, f32[8,128]{1,0:T(8,128)S(1)}, u32[]{:S(2)}, u32[]{:S(2)}) collective-permute-start(f32[8,128]{1,0:T(8,128)S(1)} %get-tuple-element.54), channel_id=1, source_target_pairs={{0,2},{1,3},{2,0},{3,1},{4,6},{5,7},{6,4},{7,5},{8,10},{9,11},{10,... | collective-permute-start | bytes 12296 | tf_op jit(solution)/shard_map/ppermute | solution.py:27
  27.0 10.9 %collective-permute-start.5 = (bf16[128,1024]{1,0:T(8,128)(2,1)S(1)}, bf16[128,1024]{1,0:T(8,128)(2,1)S(1)}, u32[]{:S(2)}, u32[]{:S(2)}) collective-permute-start(bf16[128,1024]{1,0:T(8,128)(2,1)S(1)} %collective-permute-done.3.refs_0_.refs_4_), channel_id=1, source_target_pairs={{0,1},{1,0},{2,3},{3,2},{4,5},{5,4},{6,7},{7,6},{8,9},{9,8},{10,11... | collective-permute-start | bytes 786440 | tf_op jit(solution)/shard_map/ppermute | solution.py:27
  30.7 2.7 %copy-start = (bf16[128,2048]{1,0:T(8,128)(2,1)S(1)}, bf16[128,2048]{1,0:T(8,128)(2,1)}, u32[]{:S(2)}) copy-start(bf16[128,2048]{1,0:T(8,128)(2,1)} %refs_2_.7) | copy-start | bytes 1572868
  30.7 2.7 %copy-start.1 = (bf16[1,768,2048]{2,1,0:T(8,128)(2,1)S(1)}, bf16[1,768,2048]{2,1,0:T(8,128)(2,1)}, u32[]{:S(2)}) copy-start(bf16[1,768,2048]{2,1,0:T(8,128)(2,1)} %param.13) | copy-start | bytes 9437188
  30.8 5.1 %copy-start.5 = (bf16[1,2048,768]{2,1,0:T(8,128)(2,1)S(1)}, bf16[1,2048,768]{2,1,0:T(8,128)(2,1)}, u32[]{:S(2)}) copy-start(bf16[1,2048,768]{2,1,0:T(8,128)(2,1)} %param.12) | copy-start | bytes 9437188
  32.8 3.1 %collective-permute-start.8 = (f32[8,128]{1,0:T(8,128)S(1)}, f32[8,128]{1,0:T(8,128)S(1)}, u32[]{:S(2)}, u32[]{:S(2)}) collective-permute-start(f32[8,128]{1,0:T(8,128)S(1)} %get-tuple-element.55), channel_id=1, source_target_pairs={{0,3},{1,2},{2,1},{3,0},{4,7},{5,6},{6,5},{7,4},{8,11},{9,10},{10,... | collective-permute-start | bytes 12296 | tf_op jit(solution)/shard_map/ppermute | solution.py:27
  33.2 8.4 %collective-permute-start.6 = (bf16[128,1024]{1,0:T(8,128)(2,1)S(1)}, bf16[128,1024]{1,0:T(8,128)(2,1)S(1)}, u32[]{:S(2)}, u32[]{:S(2)}) collective-permute-start(bf16[128,1024]{1,0:T(8,128)(2,1)S(1)} %collective-permute-done.4.refs_1_.refs_4_), channel_id=1, source_target_pairs={{0,1},{1,0},{2,3},{3,2},{4,5},{5,4},{6,7},{7,6},{8,9},{9,8},{10,11... | collective-permute-start | bytes 786440 | tf_op jit(solution)/shard_map/ppermute | solution.py:27
  33.4 2.4 %copy-start.3 = (bf16[1,2048,768]{2,1,0:T(8,128)(2,1)S(1)}, bf16[1,2048,768]{2,1,0:T(8,128)(2,1)}, u32[]{:S(2)}) copy-start(bf16[1,2048,768]{2,1,0:T(8,128)(2,1)} %param.11) | copy-start | bytes 9437188
  34.7 17.5 %collective-permute-start.14 = (f32[8,128]{1,0:T(8,128)S(1)}, f32[8,128]{1,0:T(8,128)S(1)}, u32[]{:S(2)}, u32[]{:S(2)}) collective-permute-start(f32[8,128]{1,0:T(8,128)S(1)} %get-tuple-element.67), channel_id=1, source_target_pairs={{0,1},{1,0},{2,3},{3,2},{4,5},{5,4},{6,7},{7,6},{8,9},{9,8},{10,11... | collective-permute-start | bytes 12296 | tf_op jit(solution)/shard_map/ppermute | solution.py:27
  38.5 17.9 %collective-permute-start.23 = (bf16[1536,128]{1,0:T(8,128)(2,1)S(1)}, bf16[1536,128]{1,0:T(8,128)(2,1)S(1)}, u32[]{:S(2)}, u32[]{:S(2)}) collective-permute-start(bf16[1536,128]{1,0:T(8,128)(2,1)S(1)} %get-tuple-element.81), channel_id=1, source_target_pairs={{0,4},{4,0},{8,12},{12,8},{1,5},{5,1},{9,13},{13,9},{2,6},{6,2},{1... | collective-permute-start | bytes 1179656 | tf_op jit(solution)/shard_map/ppermute | solution.py:27
  40.1 19.9 %collective-permute-start.18 = (bf16[1536,128]{1,0:T(8,128)(2,1)S(1)}, bf16[1536,128]{1,0:T(8,128)(2,1)S(1)}, u32[]{:S(2)}, u32[]{:S(2)}) collective-permute-start(bf16[1536,128]{1,0:T(8,128)(2,1)S(1)} %get-tuple-element.77), channel_id=1, source_target_pairs={{0,32},{32,0},{64,96},{96,64},{1,33},{33,1},{65,97},{97,65},{2,34}... | collective-permute-start | bytes 1179656 | tf_op jit(solution)/shard_map/ppermute | solution.py:27
  49.9 4.1 %collective-permute-start.15 = (f32[8,128]{1,0:T(8,128)S(1)}, f32[8,128]{1,0:T(8,128)S(1)}, u32[]{:S(2)}, u32[]{:S(2)}) collective-permute-start(f32[8,128]{1,0:T(8,128)S(1)} %get-tuple-element.68), channel_id=1, source_target_pairs={{0,2},{1,3},{2,0},{3,1},{4,6},{5,7},{6,4},{7,5},{8,10},{9,11},{10,... | collective-permute-start | bytes 12296 | tf_op jit(solution)/shard_map/ppermute | solution.py:27
  51.0 11.5 %collective-permute-start.12 = (bf16[128,2048]{1,0:T(8,128)(2,1)S(1)}, bf16[128,2048]{1,0:T(8,128)(2,1)S(1)}, u32[]{:S(2)}, u32[]{:S(2)}) collective-permute-start(bf16[128,2048]{1,0:T(8,128)(2,1)S(1)} %get-tuple-element.65), channel_id=1, source_target_pairs={{0,1},{1,0},{2,3},{3,2},{4,5},{5,4},{6,7},{7,6},{8,9},{9,8},{10,11... | collective-permute-start | bytes 1572872 | tf_op jit(solution)/shard_map/ppermute | solution.py:27
  52.1 3.7 %copy-start.8 = (s32[128,2]{0,1:T(2,128)S(1)}, s32[128,2]{0,1:T(2,128)}, u32[]{:S(2)}) copy-start(s32[128,2]{0,1:T(2,128)} %param.9) | copy-start | bytes 3076
  52.2 3.1 %collective-permute-start.16 = (f32[8,128]{1,0:T(8,128)S(1)}, f32[8,128]{1,0:T(8,128)S(1)}, u32[]{:S(2)}, u32[]{:S(2)}) collective-permute-start(f32[8,128]{1,0:T(8,128)S(1)} %get-tuple-element.69), channel_id=1, source_target_pairs={{0,3},{1,2},{2,1},{3,0},{4,7},{5,6},{6,5},{7,4},{8,11},{9,10},{10,... | collective-permute-start | bytes 12296 | tf_op jit(solution)/shard_map/ppermute | solution.py:27
  54.0 24.1 %collective-permute-start.22 = (bf16[3072,128]{1,0:T(8,128)(2,1)S(1)}, bf16[3072,128]{1,0:T(8,128)(2,1)S(1)}, u32[]{:S(2)}, u32[]{:S(2)}) collective-permute-start(bf16[3072,128]{1,0:T(8,128)(2,1)S(1)} %get-tuple-element.79), channel_id=1, source_target_pairs={{0,4},{4,0},{8,12},{12,8},{1,5},{5,1},{9,13},{13,9},{2,6},{6,2},{1... | collective-permute-start | bytes 2359304 | tf_op jit(solution)/shard_map/ppermute | solution.py:27
  55.3 27.8 %collective-permute-start.17 = (bf16[3072,128]{1,0:T(8,128)(2,1)S(1)}, bf16[3072,128]{1,0:T(8,128)(2,1)S(1)}, u32[]{:S(2)}, u32[]{:S(2)}) collective-permute-start(bf16[3072,128]{1,0:T(8,128)(2,1)S(1)} %get-tuple-element.73), channel_id=1, source_target_pairs={{0,32},{32,0},{64,96},{96,64},{1,33},{33,1},{65,97},{97,65},{2,34}... | collective-permute-start | bytes 2359304 | tf_op jit(solution)/shard_map/ppermute | solution.py:27
  56.4 21.5 %collective-permute-start.29 = (bf16[3072,128]{1,0:T(8,128)(2,1)S(1)}, bf16[3072,128]{1,0:T(8,128)(2,1)S(1)}, u32[]{:S(2)}, u32[]{:S(2)}) collective-permute-start(bf16[3072,128]{1,0:T(8,128)(2,1)S(1)} %shard_map.122), channel_id=1, source_target_pairs={{0,16},{16,0},{1,17},{17,1},{2,18},{18,2},{3,19},{19,3},{4,20},{20... | collective-permute-start | bytes 2359304 | tf_op jit(solution)/shard_map/ppermute | solution.py:27
  60.0 20.7 %collective-permute-start.33 = (bf16[3072,128]{1,0:T(8,128)(2,1)S(1)}, bf16[3072,128]{1,0:T(8,128)(2,1)S(1)}, u32[]{:S(2)}, u32[]{:S(2)}) collective-permute-start(bf16[3072,128]{1,0:T(8,128)(2,1)S(1)} %get-tuple-element.86), channel_id=1, source_target_pairs={{0,12},{4,8},{8,4},{12,0},{1,13},{5,9},{9,5},{13,1},{2,14},{6,10},... | collective-permute-start | bytes 2359304 | tf_op jit(solution)/shard_map/ppermute | solution.py:27
  62.4 20.8 %collective-permute-start.27 = (bf16[3072,128]{1,0:T(8,128)(2,1)S(1)}, bf16[3072,128]{1,0:T(8,128)(2,1)S(1)}, u32[]{:S(2)}, u32[]{:S(2)}) collective-permute-start(bf16[3072,128]{1,0:T(8,128)(2,1)S(1)} %get-tuple-element.83), channel_id=1, source_target_pairs={{0,96},{32,64},{64,32},{96,0},{1,97},{33,65},{65,33},{97,1},{2,98}... | collective-permute-start | bytes 2359304 | tf_op jit(solution)/shard_map/ppermute | solution.py:27
  77.9 78.0 %collective-permute-start.11 = (bf16[128,2048]{1,0:T(8,128)(2,1)S(1)}, bf16[128,2048]{1,0:T(8,128)(2,1)S(1)}, u32[]{:S(2)}, u32[]{:S(2)}) collective-permute-start(bf16[128,2048]{1,0:T(8,128)(2,1)S(1)} %get-tuple-element.63), channel_id=1, source_target_pairs={{0,1},{1,0},{2,3},{3,2},{4,5},{5,4},{6,7},{7,6},{8,9},{9,8},{10,11... | collective-permute-start | bytes 1572872 | tf_op jit(solution)/shard_map/ppermute | solution.py:27
  78.0 77.9 %collective-permute-start.13 = (bf16[128,2048]{1,0:T(8,128)(2,1)S(1)}, bf16[128,2048]{1,0:T(8,128)(2,1)S(1)}, u32[]{:S(2)}, u32[]{:S(2)}) collective-permute-start(bf16[128,2048]{1,0:T(8,128)(2,1)S(1)} %add_convert_fusion.1), channel_id=1, source_target_pairs={{0,2},{2,0},{1,3},{3,1},{4,6},{6,4},{5,7},{7,5},{8,10},{10,8},{9,1... | collective-permute-start | bytes 1572872 | tf_op jit(solution)/shard_map/ppermute | solution.py:27
  80.7 33.3 %collective-permute-start.24 = (bf16[2304,128]{1,0:T(8,128)(2,1)S(1)}, bf16[2304,128]{1,0:T(8,128)(2,1)S(1)}, u32[]{:S(2)}, u32[]{:S(2)}) collective-permute-start(bf16[2304,128]{1,0:T(8,128)(2,1)S(1)} %pad_maximum_fusion.1), channel_id=1, source_target_pairs={{0,12},{4,8},{8,4},{12,0},{1,13},{5,9},{9,5},{13,1},{2,14},{6,10},... | collective-permute-start | bytes 1769480 | tf_op jit(solution)/shard_map/ppermute | solution.py:27
  83.0 22.9 %collective-permute-start.34 = (bf16[1536,128]{1,0:T(8,128)(2,1)S(1)}, bf16[1536,128]{1,0:T(8,128)(2,1)S(1)}, u32[]{:S(2)}, u32[]{:S(2)}) collective-permute-start(bf16[1536,128]{1,0:T(8,128)(2,1)S(1)} %add_convert_fusion.2), channel_id=1, source_target_pairs={{0,4},{4,0},{8,12},{12,8},{1,5},{5,1},{9,13},{13,9},{2,6},{6,2},{1... | collective-permute-start | bytes 1179656 | tf_op jit(solution)/shard_map/ppermute | solution.py:27
  83.3 13.8 %collective-permute-start.35 = (bf16[768,128]{1,0:T(8,128)(2,1)S(1)}, bf16[768,128]{1,0:T(8,128)(2,1)S(1)}, u32[]{:S(2)}, u32[]{:S(2)}) collective-permute-start(bf16[768,128]{1,0:T(8,128)(2,1)S(1)} %add_convert_fusion.6), channel_id=1, source_target_pairs={{0,4},{4,0},{8,12},{12,8},{1,5},{5,1},{9,13},{13,9},{2,6},{6,2},{1... | collective-permute-start | bytes 589832 | tf_op jit(solution)/shard_map/ppermute | solution.py:27
  97.1 5.7 %collective-permute-start.30 = (bf16[768,128]{1,0:T(8,128)(2,1)S(1)}, bf16[768,128]{1,0:T(8,128)(2,1)S(1)}, u32[]{:S(2)}, u32[]{:S(2)}) collective-permute-start(bf16[768,128]{1,0:T(8,128)(2,1)S(1)} %add_convert_fusion.8), channel_id=1, source_target_pairs={{0,32},{32,0},{64,96},{96,64},{1,33},{33,1},{65,97},{97,65},{2,34}... | collective-permute-start | bytes 589832 | tf_op jit(solution)/shard_map/ppermute | solution.py:27
  102.8 16.3 %collective-permute-start.19 = (bf16[2304,128]{1,0:T(8,128)(2,1)S(1)}, bf16[2304,128]{1,0:T(8,128)(2,1)S(1)}, u32[]{:S(2)}, u32[]{:S(2)}) collective-permute-start(bf16[2304,128]{1,0:T(8,128)(2,1)S(1)} %pad_maximum_fusion), channel_id=1, source_target_pairs={{0,96},{32,64},{64,32},{96,0},{1,97},{33,65},{65,33},{97,1},{2,98}... | collective-permute-start | bytes 1769480 | tf_op jit(solution)/shard_map/ppermute | solution.py:27
  105.9 7.9 %collective-permute-start.28 = (bf16[1536,128]{1,0:T(8,128)(2,1)S(1)}, bf16[1536,128]{1,0:T(8,128)(2,1)S(1)}, u32[]{:S(2)}, u32[]{:S(2)}) collective-permute-start(bf16[1536,128]{1,0:T(8,128)(2,1)S(1)} %add_convert_fusion.3), channel_id=1, source_target_pairs={{0,32},{32,0},{64,96},{96,64},{1,33},{33,1},{65,97},{97,65},{2,34}... | collective-permute-start | bytes 1179656 | tf_op jit(solution)/shard_map/ppermute | solution.py:27
  113.8 8.5 %collective-permute-start.36 = (bf16[1152,128]{1,0:T(8,128)(2,1)S(1)}, bf16[1152,128]{1,0:T(8,128)(2,1)S(1)}, u32[]{:S(2)}, u32[]{:S(2)}) collective-permute-start(bf16[1152,128]{1,0:T(8,128)(2,1)S(1)} %pad_maximum_fusion.5), channel_id=1, source_target_pairs={{0,96},{32,64},{64,32},{96,0},{1,97},{33,65},{65,33},{97,1},{2,98}... | collective-permute-start | bytes 884744 | tf_op jit(solution)/shard_map/ppermute | solution.py:27
  114.1 8.9 %collective-permute-start.31 = (bf16[1152,128]{1,0:T(8,128)(2,1)S(1)}, bf16[1152,128]{1,0:T(8,128)(2,1)S(1)}, u32[]{:S(2)}, u32[]{:S(2)}) collective-permute-start(bf16[1152,128]{1,0:T(8,128)(2,1)S(1)} %pad_maximum_fusion.4), channel_id=1, source_target_pairs={{0,12},{4,8},{8,4},{12,0},{1,13},{5,9},{9,5},{13,1},{2,14},{6,10},... | collective-permute-start | bytes 884744 | tf_op jit(solution)/shard_map/ppermute | solution.py:27
  119.1 19.5 %collective-permute-start.25 = (bf16[1152,128]{1,0:T(8,128)(2,1)S(1)}, bf16[1152,128]{1,0:T(8,128)(2,1)S(1)}, u32[]{:S(2)}, u32[]{:S(2)}) collective-permute-start(bf16[1152,128]{1,0:T(8,128)(2,1)S(1)} %pad_maximum_fusion.3), channel_id=1, source_target_pairs={{0,32},{32,0},{64,96},{96,64},{1,33},{33,1},{65,97},{97,65},{2,34}... | collective-permute-start | bytes 884744 | tf_op jit(solution)/shard_map/ppermute | solution.py:27
  122.3 17.9 %collective-permute-start.20 = (bf16[1152,128]{1,0:T(8,128)(2,1)S(1)}, bf16[1152,128]{1,0:T(8,128)(2,1)S(1)}, u32[]{:S(2)}, u32[]{:S(2)}) collective-permute-start(bf16[1152,128]{1,0:T(8,128)(2,1)S(1)} %pad_maximum_fusion.2), channel_id=1, source_target_pairs={{0,4},{4,0},{8,12},{12,8},{1,5},{5,1},{9,13},{13,9},{2,6},{6,2},{1... | collective-permute-start | bytes 884744 | tf_op jit(solution)/shard_map/ppermute | solution.py:27
  123.0 5.7 %collective-permute-start.37 = (bf16[576,128]{1,0:T(8,128)(2,1)S(1)}, bf16[576,128]{1,0:T(8,128)(2,1)S(1)}, u32[]{:S(2)}, u32[]{:S(2)}) collective-permute-start(bf16[576,128]{1,0:T(8,128)(2,1)S(1)} %pad_maximum_fusion.9), channel_id=1, source_target_pairs={{0,32},{32,0},{64,96},{96,64},{1,33},{33,1},{65,97},{97,65},{2,34}... | collective-permute-start | bytes 442376 | tf_op jit(solution)/shard_map/ppermute | solution.py:27
  128.7 5.1 %collective-permute-start.32 = (bf16[576,128]{1,0:T(8,128)(2,1)S(1)}, bf16[576,128]{1,0:T(8,128)(2,1)S(1)}, u32[]{:S(2)}, u32[]{:S(2)}) collective-permute-start(bf16[576,128]{1,0:T(8,128)(2,1)S(1)} %pad_maximum_fusion.8), channel_id=1, source_target_pairs={{0,4},{4,0},{8,12},{12,8},{1,5},{5,1},{9,13},{13,9},{2,6},{6,2},{1... | collective-permute-start | bytes 442376 | tf_op jit(solution)/shard_map/ppermute | solution.py:27
  133.9 24.1 %collective-permute-start.38 = (bf16[384,128]{1,0:T(8,128)(2,1)S(1)}, bf16[384,128]{1,0:T(8,128)(2,1)S(1)}, u32[]{:S(2)}, u32[]{:S(2)}) collective-permute-start(bf16[384,128]{1,0:T(8,128)(2,1)S(1)} %pad_maximum_fusion.11), channel_id=1, source_target_pairs={{0,16},{16,0},{1,17},{17,1},{2,18},{18,2},{3,19},{19,3},{4,20},{20... | collective-permute-start | bytes 294920 | tf_op jit(solution)/shard_map/ppermute | solution.py:27
  138.5 18.5 %collective-permute-start.40 = (bf16[96,128]{1,0:T(8,128)(2,1)S(1)}, bf16[96,128]{1,0:T(8,128)(2,1)S(1)}, u32[]{:S(2)}, u32[]{:S(2)}) collective-permute-start(bf16[96,128]{1,0:T(8,128)(2,1)S(1)} %get-tuple-element.103), channel_id=1, source_target_pairs={{0,12},{4,8},{8,4},{12,0},{1,13},{5,9},{9,5},{13,1},{2,14},{6,10},... | collective-permute-start | bytes 73736 | tf_op jit(solution)/shard_map/ppermute | solution.py:27
  140.2 6.4 %collective-permute-start.26 = (bf16[576,128]{1,0:T(8,128)(2,1)S(1)}, bf16[576,128]{1,0:T(8,128)(2,1)S(1)}, u32[]{:S(2)}, u32[]{:S(2)}) collective-permute-start(bf16[576,128]{1,0:T(8,128)(2,1)S(1)} %pad_maximum_fusion.7), channel_id=1, source_target_pairs={{0,96},{32,64},{64,32},{96,0},{1,97},{33,65},{65,33},{97,1},{2,98}... | collective-permute-start | bytes 442376 | tf_op jit(solution)/shard_map/ppermute | solution.py:27
  146.6 6.4 %collective-permute-start.21 = (bf16[576,128]{1,0:T(8,128)(2,1)S(1)}, bf16[576,128]{1,0:T(8,128)(2,1)S(1)}, u32[]{:S(2)}, u32[]{:S(2)}) collective-permute-start(bf16[576,128]{1,0:T(8,128)(2,1)S(1)} %pad_maximum_fusion.6), channel_id=1, source_target_pairs={{0,12},{4,8},{8,4},{12,0},{1,13},{5,9},{9,5},{13,1},{2,14},{6,10},... | collective-permute-start | bytes 442376 | tf_op jit(solution)/shard_map/ppermute | solution.py:27
  153.0 5.0 %collective-permute-start.39 = (bf16[96,128]{1,0:T(8,128)(2,1)S(1)}, bf16[96,128]{1,0:T(8,128)(2,1)S(1)}, u32[]{:S(2)}, u32[]{:S(2)}) collective-permute-start(bf16[96,128]{1,0:T(8,128)(2,1)S(1)} %get-tuple-element.105), channel_id=1, source_target_pairs={{0,96},{32,64},{64,32},{96,0},{1,97},{33,65},{65,33},{97,1},{2,98}... | collective-permute-start | bytes 73736 | tf_op jit(solution)/shard_map/ppermute | solution.py:27
  155.9 6.7 %collective-permute-start.41 = (bf16[576,128]{1,0:T(8,128)(2,1)S(1)}, bf16[576,128]{1,0:T(8,128)(2,1)S(1)}, u32[]{:S(2)}, u32[]{:S(2)}) collective-permute-start(bf16[576,128]{1,0:T(8,128)(2,1)S(1)} %pad_maximum_fusion.10), channel_id=1, source_target_pairs={{0,16},{16,0},{1,17},{17,1},{2,18},{18,2},{3,19},{19,3},{4,20},{20... | collective-permute-start | bytes 442376 | tf_op jit(solution)/shard_map/ppermute | solution.py:27
  (4 other events, 5.1 us)

commit v2 on v1

--- a/solution.py
+++ b/solution.py
@@ -14,7 +14,7 @@
 EVERY = ("x", "zh", "y", "zl", "c")
 XA, XB, YA, YB, Z = ("x", 1), ("x", 3), ("y", 1), ("y", 3), ("zh", 1)
 ORDERS = ((XA, XB, YA, YB, Z), (YA, YB, XA, XB, Z), (XB, XA, YB, YA, Z), (YB, YA, XB, XA, Z))
-DOWN_ORDERS = ORDERS[:2] + ((Z, XA, YB, YA, XB), (Z, YA, XB, XA, YB))
+DOWN_ORDERS = ORDERS[:2] + ((Z, XB, XA, YB, YA), (Z, YB, YA, XB, XA))
 CHAINS = (2, 3, 0, 1)
 BLOCKS = 32
 HALF = BLOCKS // 2
@@ -110,12 +110,7 @@
     rows = 2 * PIECE
     outs = [((rows, ff), F32), ((rows, ff), F32), ((rows, ff), BF16), ((ff, rows), F32), ((d, rows), BF16)]
     return kernel(
-        forward_body,
-        (x0, x1, *cws, wg, wu),
-        outs,
-        12,
-        4 * rows * d * ff,
-        scratch=(pltpu.VMEM((rows, d), BF16),),
+        forward_body, (x0, x1, *cws, wg, wu), outs, 12, 4 * rows * d * ff, scratch=(pltpu.VMEM((rows, d), BF16),)
     )
 
 
@@ -201,45 +196,53 @@
     )
 
 
-def gate_body(first, xta, xtb, gda, gdb, uda, udb, *refs):
-    outs, mixed = refs[:4], refs[4]
+TILE = 256
+EARLY = ((2, 0, 3), (3, 0, 3))
+LATER = ((0, 0, 2), (1, 0, 2), (0, 2, 3), (1, 2, 3))
+
+
+def gate_body(first, specs, xta, xtb, gda, gdb, uda, udb, *refs):
+    outs, mixed = refs[:-1], refs[-1]
     size = xta.shape[0] // BLOCKS // 2
     rows = xta.shape[1]
-    for p in range(4):
-        for b in range(HALF):
-            start = pl.multiple_of(block_at(ORDERS[p], first + b) * (2 * size) + (p % 2) * size, size)
-            mixed[p, pl.ds(b * size, size), pl.ds(0, rows)] = xta[pl.ds(start, size), :]
-            mixed[p, pl.ds(b * size, size), pl.ds(rows, rows)] = xtb[pl.ds(start, size), :]
+    chains = []
+    for (p, low, high), out in zip(specs, outs):
+        if p not in chains:
+            chains.append(p)
+            at = chains.index(p)
+            for b in range(HALF):
+                start = pl.multiple_of(block_at(ORDERS[p], first + b) * (2 * size) + (p % 2) * size, size)
+                mixed[at, pl.ds(b * size, size), pl.ds(0, rows)] = xta[pl.ds(start, size), :]
+                mixed[at, pl.ds(b * size, size), pl.ds(rows, rows)] = xtb[pl.ds(start, size), :]
+        q = chains.index(p)
         ga, gb = (gda, gdb) if p < 2 else (uda, udb)
-        cols = ga.shape[1]
-        tile = 256
-        per = tile // LANES
-        tall = size * (cols // LANES)
-        for n in range(cols // tile):
-            at = pl.ds(n * tile, tile)
-            part = nn(mixed[p, :, pl.ds(0, rows)], ga[:, at]) + nn(mixed[p, :, pl.ds(rows, rows)], gb[:, at])
+        per = TILE // LANES
+        tall = size * per * (high - low)
+        for n in range(low, high):
+            at = pl.ds(n * TILE, TILE)
+            part = nn(mixed[q, :, pl.ds(0, rows)], ga[:, at]) + nn(mixed[q, :, pl.ds(rows, rows)], gb[:, at])
             part = part.astype(BF16)
             for b in range(HALF):
                 for k in range(per):
-                    to = b * tall + (n * per + k) * size
-                    outs[p][pl.ds(to, size), :] = part[b * size : (b + 1) * size, k * LANES : (k + 1) * LANES]
-
-
-def gate_half(first, xts, gds, uds):
+                    to = b * tall + ((n - low) * per + k) * size
+                    out[pl.ds(to, size), :] = part[b * size : (b + 1) * size, k * LANES : (k + 1) * LANES]
+
+
+def gate_half(first, specs, xts, gds, uds):
     d, rows = xts[0].shape
-    ff = gds[0].shape[1]
-    out = ((HALF * (d // BLOCKS // 2) * (ff // LANES), LANES), BF16)
+    tiles = [high - low for _, low, high in specs]
+    outs = [((HALF * (d // BLOCKS // 2) * t * (TILE // LANES), LANES), BF16) for t in tiles]
 
     def body(*refs):
-        gate_body(first, *refs)
+        gate_body(first, specs, *refs)
 
     return kernel(
         body,
         (*xts, *gds, *uds),
-        [out] * 4,
+        outs,
         12,
-        4 * rows * ff * d,
-        scratch=(pltpu.VMEM((4, d // 4, 2 * rows), BF16),),
+        d * rows * TILE * sum(tiles),
+        scratch=(pltpu.VMEM((len({p for p, _, _ in specs}), d // 4, 2 * rows), BF16),),
     )
 
 
@@ -257,27 +260,28 @@
 
 
 def finish_body(*refs):
-    bases, (last_a, end2, end3, last_b), (gate, up, down) = refs[:8], refs[8:12], refs[12:]
-    first, second = last_a[...].astype(F32), last_b[...].astype(F32)
-    tall, low = bases[0].shape[0], bases[4].shape[0]
-    recvs = [second[:tall], second[tall : 2 * tall], first[:tall], first[tall:]]
-    recvs += [second[2 * tall : 2 * tall + low], second[2 * tall + low :]]
-    recvs += [end2[...].astype(F32), end3[...].astype(F32)]
-    total = jnp.concatenate([b[...] + r for b, r in zip(bases, recvs)], axis=0)
+    bases, (last_a, last_b), (gate, up, down) = refs[:-5], refs[-5:-3], refs[-3:]
+    recv = {0: (last_b[...].astype(F32), 0), 2: (last_a[...].astype(F32), 0)}
     half, low = gate.shape[0] // 2, down.shape[0]
     cols = down.shape[1] // 4
-    at = 0
-    for p in range(4):
+    done = []
+    for n, base in enumerate(bases):
+        rows = base.shape[0]
+        p = (EARLY + LATER)[n][0] if n < 6 else n - 6
+        if n < 6 or p < 2:
+            array, at = recv[p // 2 * 2]
+            done.append(base[...] + array[at : at + rows])
+            recv[p // 2 * 2] = (array, at + rows)
+        else:
+            done.append(base[...])
+    for (p, first, _), total in zip(EARLY + LATER, done):
         out = gate if p < 2 else up
-        for k in range(gate.shape[1] // LANES):
-            block = total[at : at + half].astype(BF16)
-            out[pl.ds(p % 2 * half, half), pl.ds(k * LANES, LANES)] = block
-            at += half
-    for p in range(4):
+        for k in range(total.shape[0] // half):
+            to = first * TILE + k * LANES
+            out[pl.ds(p % 2 * half, half), pl.ds(to, LANES)] = total[k * half : (k + 1) * half].astype(BF16)
+    for p, total in enumerate(done[6:]):
         for k in range(cols // LANES):
-            block = total[at : at + low].astype(BF16)
-            down[:, pl.ds(p * cols + k * LANES, LANES)] = block
-            at += low
+            down[:, pl.ds(p * cols + k * LANES, LANES)] = total[k * low : (k + 1) * low].astype(BF16)
 
 
 def summed(arrays, start, stop, kind=BF16):
@@ -312,9 +316,10 @@
     ha = hidden_part(((cotangent,), (cot_near,)), cwa, wd, *fa[:3])
     hb = hidden_part((cot_far, cot_both), cwb, wd, *fb[:3])
     gds, uds = (ha[0], hb[0]), (ha[1], hb[1])
-    gate_send = gate_half(HALF, xts, gds, uds)
+    gate_send = list(gate_half(HALF, EARLY, xts, gds, uds))
+    gate_send += gate_half(HALF, LATER, xts, gds, uds)
     down_keep = [a for k in range(2) for a in down_half(0, k, hts, pieces[k])]
-    gate_keep = gate_half(0, xts, gds, uds)
+    gate_keep = gate_half(0, EARLY + LATER, xts, gds, uds)
     grads = kernel(
         rows_body,
         (*gds, *uds, wg, wu),
@@ -328,15 +333,10 @@
     size = down_z.shape[0] // 2
     down_got = [moved(down_send[p], *ORDERS[p][0]) for p in (0, 1)]
     down_got += [lax.optimization_barrier(a) for a in (down_z[:size], down_z[size:])]
-    have = [
-        [
-            [(HALF, gate_keep[p]), (HALF, moved(gate_send[p], *ORDERS[p][0]))],
-            [(HALF, down_keep[p]), (HALF, down_got[p])],
-        ]
-        for p in range(4)
-    ]
-
-    gates, downs = ([have[p][k] for p in range(4)] for k in (0, 1))
+    gates, downs = [], [[(HALF, down_keep[p]), (HALF, down_got[p])] for p in range(4)]
+    for spec, keep, send in zip(EARLY + LATER, gate_keep, gate_send):
+        gates.append([(HALF, keep), (HALF, moved(send, *ORDERS[spec[0]][0]))])
+    have = [[g for g, spec in zip(gates, EARLY + LATER) if spec[0] == p] + [downs[p]] for p in range(4)]
     left = {id(h): HALF for h in gates + downs}
 
     def exchange(held, step):
@@ -350,20 +350,25 @@
             at += send.shape[0]
         return got
 
-    for p in CHAINS:
-        exchange(have[p][: 2 if p < 2 else 1], ORDERS[p][1])
+    for p in (0, 1):
+        exchange(have[p][:1], ORDERS[p][1])
+    for p in (2, 3):
+        exchange(have[p][:1], ORDERS[p][1])
     for p in (2, 3):
         exchange(downs[p : p + 1], DOWN_ORDERS[p][1])
+    for p in (0, 1):
+        exchange(have[p][1:], ORDERS[p][1])
+    for p in (2, 3):
+        exchange(downs[p : p + 1], DOWN_ORDERS[p][2])
     for step in (2, 3):
         for p in CHAINS:
             exchange(have[p], ORDERS[p][step])
-    last_a = exchange(gates[2:], Z)
-    ends = [exchange(downs[p : p + 1], DOWN_ORDERS[p][4]) for p in (2, 3)]
-    last_b = exchange(gates[:2] + downs[:2], Z)
-    bases = [summed(h[:-1], 0, 1, F32) for h in gates + downs]
+    last_a = exchange(gates[:2], Z)
+    last_b = exchange(gates[2:] + downs[:2], Z)
+    bases = [summed(h[:-1], 0, 1, F32) for h in gates + downs[:2]] + [summed(h, 0, 1, F32) for h in downs[2:]]
     gate_grad, up_grad, down_grad = kernel(
         finish_body,
-        (*bases, last_a, *ends, last_b),
+        (*bases, last_a, last_b),
         [((d // BLOCKS, ff), BF16), ((d // BLOCKS, ff), BF16), ((ff // BLOCKS, d), BF16)],
         4,
         1 << 20,

time: 164 us -> 175 us (1.067)
  starting transfers between devices: 50.1 us -> 63.5 us
  waiting for transfers between devices: 85.5 us -> 82.5 us
    ppermute x42 -> x46, starting transfers between devices: 50.1 us -> 63.5 us  [moved(): lax.ppermute(array, axis, [(i, i ^ mask) for i in range(lax.axis_size(axi...]
    ppermute x42 -> x46, waiting for transfers between devices: 85.5 us -> 82.5 us  [moved(): lax.ppermute(array, axis, [(i, i ^ mask) for i in range(lax.axis_size(axi...]
    pallas_call x14 -> x15, Pallas kernels: 17 us -> 17.2 us  [kernel(): pl.pallas_call(body, in_specs=[vmem] * len(ins), out_specs=[vmem] * len(o...]
  transfers between devices with their start and end apart: 42 -> 46, of which waited for: 18 -> 17; matrix products, arithmetic and copies ran while one was open for 3% -> 3% of each run, Pallas kernels for 10% -> 9%
where the time goes in v2:
time: 175 us
  waiting for transfers between devices  82.5 us (47%)
  starting transfers between devices  63.5 us (36%)
  Pallas kernels  17.2 us (10%)
  local copies, waits for them, and re-layouts  7.32 us (4%)
  other arithmetic  3.39 us (2%)
    ppermute x46, waiting for transfers between devices, moved(): lax.ppermute(array, axis, [(i, i ^ mask) for i in range(lax.axis_size(axi...  82.5 us
    ppermute x46, starting transfers between devices, moved(): lax.ppermute(array, axis, [(i, i ^ mask) for i in range(lax.axis_size(axi...  63.5 us
    pallas_call x15, Pallas kernels, kernel(): pl.pallas_call(body, in_specs=[vmem] * len(ins), out_specs=[vmem] * len(o...  17.2 us
    unnamed x20, local copies, waits for them, and re-layouts  6.2 us
  transfers between devices with their start and end apart: 46, of which 17 were waited for; matrix products, arithmetic and copies ran while one was open for 3% of the time, Pallas kernels for 9%

profile of v2, /device:TPU:0, one launch (start us, length us, event | category | flops | bytes accessed | tf_op | source)
XLA Modules:
  0.0 175.2 jit_solution(964599058246655816)
XLA Ops:
  0.6 2.1 %collective-permute-start.9 = (bf16[128,2048]{1,0:T(8,128)(2,1)}, bf16[128,2048]{1,0:T(8,128)(2,1)S(1)}, u32[]{:S(2)}, u32[]{:S(2)}) collective-permute-start(bf16[128,2048]{1,0:T(8,128)(2,1)} %x0.1), channel_id=1, source_target_pairs={{0,2},{2,0},{1,3},{3,1},{4,6},{6,4},{5,7},{7,5},{8,10},{10,8},{9,1... | collective-permute-start | bytes 1572872 | tf_op jit(solution)/shard_map/ppermute | solution.py:27
  4.8 10.1 %collective-permute-done.9.x0 = bf16[128,2048]{1,0:T(8,128)(2,1)S(1)} collective-permute-done((bf16[128,2048]{1,0:T(8,128)(2,1)}, bf16[128,2048]{1,0:T(8,128)(2,1)S(1)}, u32[]{:S(2)}, u32[]{:S(2)}) %collective-permute-start.9) | collective-permute-done | bytes 524320 | tf_op jit(solution)/shard_map/ppermute | solution.py:27
  15.9 1.8 %collective-permute-start.4 = (bf16[128,1024]{1,0:T(8,128)(2,1)S(1)}, bf16[128,1024]{1,0:T(8,128)(2,1)S(1)}, u32[]{:S(2)}, u32[]{:S(2)}) collective-permute-start(bf16[128,1024]{1,0:T(8,128)(2,1)S(1)} %get-tuple-element.105), channel_id=1, source_target_pairs={{0,2},{2,0},{1,3},{3,1},{4,6},{6,4},{5,7},{7,5},{8,10},{10,8},{9,1... | collective-permute-start | bytes 786440 | tf_op jit(solution)/shard_map/ppermute | solution.py:27
  18.1 7.1 %collective-permute-done.4.refs_1_.refs_4_ = bf16[128,1024]{1,0:T(8,128)(2,1)S(1)} collective-permute-done((bf16[128,1024]{1,0:T(8,128)(2,1)S(1)}, bf16[128,1024]{1,0:T(8,128)(2,1)S(1)}, u32[]{:S(2)}, u32[]{:S(2)}) %collective-permute-start.4) | collective-permute-done | bytes 262176 | tf_op jit(solution)/shard_map/ppermute | solution.py:27
  25.2 1.7 collective-permute-start.7
  26.9 3.5 %collective-permute-done.3.refs_0_.refs_4_ = bf16[128,1024]{1,0:T(8,128)(2,1)S(1)} collective-permute-done((bf16[128,1024]{1,0:T(8,128)(2,1)S(1)}, bf16[128,1024]{1,0:T(8,128)(2,1)S(1)}, u32[]{:S(2)}, u32[]{:S(2)}) %collective-permute-start.3) | collective-permute-done | bytes 262176 | tf_op jit(solution)/shard_map/ppermute | solution.py:27
  30.9 1.9 %copy-done.2 = bf16[1,2048,768]{2,1,0:T(8,128)(2,1)S(1)} copy-done((bf16[1,2048,768]{2,1,0:T(8,128)(2,1)S(1)}, bf16[1,2048,768]{2,1,0:T(8,128)(2,1)}, u32[]{:S(2)}) %copy-start.2) | copy-done | bytes 3145752
  32.8 1.9 %copy-done.4 = bf16[1,2048,768]{2,1,0:T(8,128)(2,1)S(1)} copy-done((bf16[1,2048,768]{2,1,0:T(8,128)(2,1)S(1)}, bf16[1,2048,768]{2,1,0:T(8,128)(2,1)}, u32[]{:S(2)}) %copy-start.4) | copy-done | bytes 3145752
  35.7 2.0 %shard_map.111 = (f32[256,768]{1,0:T(8,128)S(1)}, f32[256,768]{1,0:T(8,128)S(1)}, bf16[256,768]{1,0:T(8,128)(2,1)S(1)}, f32[768,256]{1,0:T(8,128)S(1)}, bf16[2048,256]{1,0:T(8,128)(2,1)S(1)}) custom-call(bf16[128,2048]{1,0:T(8,128)(2,1)S(1)} %copy-done.6, bf16[128,2048]{1,0:T(8,128)(2,1)S(1)} %collective-permute-done.2.x1, ...), custom_call_target="tpu_custom_call" | custom-call | flops 1610612736 | bytes 1048576 | tf_op jit(solution)/shard_map/pallas_call | solution.py:61
  37.8 1.4 collective-permute-start.8
  41.0 2.0 %shard_map.113 = (f32[256,768]{1,0:T(8,128)S(1)}, f32[256,768]{1,0:T(8,128)S(1)}, bf16[256,768]{1,0:T(8,128)(2,1)S(1)}, f32[768,256]{1,0:T(8,128)S(1)}, bf16[2048,256]{1,0:T(8,128)(2,1)S(1)}) custom-call(bf16[128,2048]{1,0:T(8,128)(2,1)S(1)} %collective-permute-done.9.x0, bf16[128,2048]{1,0:T(8,128)(2,1)S(1)} %collective-permute-done.10.x1, ...), custom_call_target="tpu_custom_call" | custom-call | flops 1610612736 | bytes 1048576 | tf_op jit(solution)/shard_map/pallas_call | solution.py:61
  43.0 1.2 shard_map.114
  44.2 1.7 collective-permute-start.15
  45.9 3.4 %shard_map.115 = (bf16[128,2048]{1,0:T(8,128)(2,1)S(1)}, bf16[128,2048]{1,0:T(8,128)(2,1)S(1)}, bf16[128,2048]{1,0:T(8,128)(2,1)S(1)}, bf16[128,2048]{1,0:T(8,128)(2,1)S(1)}) custom-call(bf16[256,768]{1,0:T(8,128)(2,1)S(1)} %get-tuple-element.57.gda.refs_2_, bf16[256,768]{1,0:T(8,128)(2,1)S(1)} %get-tuple-element.63.gdb.refs_3_, ...), custom_call_target="tpu_custom_call" | custom-call | flops 3221225472 | bytes 1048576 | tf_op jit(solution)/shard_map/pallas_call | solution.py:61
  50.3 1.8 %collective-permute-start.32 = (bf16[1024,128]{1,0:T(8,128)(2,1)S(1)}, bf16[1024,128]{1,0:T(8,128)(2,1)S(1)}, u32[]{:S(2)}, u32[]{:S(2)}) collective-permute-start(bf16[1024,128]{1,0:T(8,128)(2,1)S(1)} %get-tuple-element.87), channel_id=1, source_target_pairs={{0,32},{32,0},{64,96},{96,64},{1,33},{33,1},{65,97},{97,65},{2,34}... | collective-permute-start | bytes 786440 | tf_op jit(solution)/shard_map/ppermute | solution.py:27
  52.1 1.6 collective-permute-start.39
  56.4 1.8 %shard_map.117 = (bf16[3072,128]{1,0:T(8,128)(2,1)S(1)}, bf16[3072,128]{1,0:T(8,128)(2,1)S(1)}, bf16[2048,128]{1,0:T(8,128)(2,1)S(1)}, bf16[2048,128]{1,0:T(8,12...) custom-call(bf16[2048,256]{1,0:T(8,128)(2,1)S(1)} %get-tuple-element.74.refs_0_, ...), custom_call_target="tpu_custom_call" | custom-call | flops 1610612736 | bytes 1048576 | tf_op jit(solution)/shard_map/pallas_call | solution.py:61
  59.9 3.6 %collective-permute-start.19 = (bf16[3072,128]{1,0:T(8,128)(2,1)S(1)}, bf16[3072,128]{1,0:T(8,128)(2,1)S(1)}, u32[]{:S(2)}, u32[]{:S(2)}) collective-permute-start(bf16[3072,128]{1,0:T(8,128)(2,1)S(1)} %shard_map.120), channel_id=1, source_target_pairs={{0,16},{16,0},{1,17},{17,1},{2,18},{18,2},{3,19},{19,3},{4,20},{20... | collective-permute-start | bytes 2359304 | tf_op jit(solution)/shard_map/ppermute | solution.py:27
  64.1 1.5 collective-permute-start.30
  65.6 1.6 collective-permute-start.37
  67.3 3.6 %collective-permute-done.33 = bf16[1536,128]{1,0:T(8,128)(2,1)S(1)} collective-permute-done((bf16[1536,128]{1,0:T(8,128)(2,1)S(1)}, bf16[1536,128]{1,0:T(8,128)(2,1)S(1)}, u32[]{:S(2)}, u32[]{:S(2)}) %collective-permute-start.33) | collective-permute-done | bytes 393248 | tf_op jit(solution)/shard_map/ppermute | solution.py:27
  71.5 2.7 %collective-permute-start.17 = (bf16[3072,128]{1,0:T(8,128)(2,1)S(1)}, bf16[3072,128]{1,0:T(8,128)(2,1)S(1)}, u32[]{:S(2)}, u32[]{:S(2)}) collective-permute-start(bf16[3072,128]{1,0:T(8,128)(2,1)S(1)} %get-tuple-element.77), channel_id=1, source_target_pairs={{0,96},{32,64},{64,32},{96,0},{1,97},{33,65},{65,33},{97,1},{2,98}... | collective-permute-start | bytes 2359304 | tf_op jit(solution)/shard_map/ppermute | solution.py:27
  74.3 2.3 %collective-permute-start.24 = (bf16[3072,128]{1,0:T(8,128)(2,1)S(1)}, bf16[3072,128]{1,0:T(8,128)(2,1)S(1)}, u32[]{:S(2)}, u32[]{:S(2)}) collective-permute-start(bf16[3072,128]{1,0:T(8,128)(2,1)S(1)} %get-tuple-element.82), channel_id=1, source_target_pairs={{0,12},{4,8},{8,4},{12,0},{1,13},{5,9},{9,5},{13,1},{2,14},{6,10},... | collective-permute-start | bytes 2359304 | tf_op jit(solution)/shard_map/ppermute | solution.py:27
  76.7 4.4 %collective-permute-done.30 = bf16[2048,128]{1,0:T(8,128)(2,1)S(1)} collective-permute-done((bf16[2048,128]{1,0:T(8,128)(2,1)S(1)}, bf16[2048,128]{1,0:T(8,128)(2,1)S(1)}, u32[]{:S(2)}, u32[]{:S(2)}) %collective-permute-start.30) | collective-permute-done | bytes 524320 | tf_op jit(solution)/shard_map/ppermute | solution.py:27
  81.1 2.2 %collective-permute-start.41 = (bf16[1280,128]{1,0:T(8,128)(2,1)S(1)}, bf16[1280,128]{1,0:T(8,128)(2,1)S(1)}, u32[]{:S(2)}, u32[]{:S(2)}) collective-permute-start(bf16[1280,128]{1,0:T(8,128)(2,1)S(1)} %pad_maximum_fusion.1), channel_id=1, source_target_pairs={{0,12},{4,8},{8,4},{12,0},{1,13},{5,9},{9,5},{13,1},{2,14},{6,10},... | collective-permute-start | bytes 983048 | tf_op jit(solution)/shard_map/ppermute | solution.py:27
  83.6 17.7 %collective-permute-done.41 = bf16[1280,128]{1,0:T(8,128)(2,1)S(1)} collective-permute-done((bf16[1280,128]{1,0:T(8,128)(2,1)S(1)}, bf16[1280,128]{1,0:T(8,128)(2,1)S(1)}, u32[]{:S(2)}, u32[]{:S(2)}) %collective-permute-start.41) | collective-permute-done | bytes 327712 | tf_op jit(solution)/shard_map/ppermute | solution.py:27
  101.3 1.5 collective-permute-start.34
  102.8 7.6 %collective-permute-done.34 = bf16[1280,128]{1,0:T(8,128)(2,1)S(1)} collective-permute-done((bf16[1280,128]{1,0:T(8,128)(2,1)S(1)}, bf16[1280,128]{1,0:T(8,128)(2,1)S(1)}, u32[]{:S(2)}, u32[]{:S(2)}) %collective-permute-start.34) | collective-permute-done | bytes 327712 | tf_op jit(solution)/shard_map/ppermute | solution.py:27
  110.5 2.2 %collective-permute-start.38 = (bf16[1024,128]{1,0:T(8,128)(2,1)S(1)}, bf16[1024,128]{1,0:T(8,128)(2,1)S(1)}, u32[]{:S(2)}, u32[]{:S(2)}) collective-permute-start(bf16[1024,128]{1,0:T(8,128)(2,1)S(1)} %add_convert_fusion.4), channel_id=1, source_target_pairs={{0,12},{4,8},{8,4},{12,0},{1,13},{5,9},{9,5},{13,1},{2,14},{6,10},... | collective-permute-start | bytes 786440 | tf_op jit(solution)/shard_map/ppermute | solution.py:27
  112.7 5.3 %collective-permute-done.38 = bf16[1024,128]{1,0:T(8,128)(2,1)S(1)} collective-permute-done((bf16[1024,128]{1,0:T(8,128)(2,1)S(1)}, bf16[1024,128]{1,0:T(8,128)(2,1)S(1)}, u32[]{:S(2)}, u32[]{:S(2)}) %collective-permute-start.38) | collective-permute-done | bytes 262176 | tf_op jit(solution)/shard_map/ppermute | solution.py:27
  118.0 2.7 %collective-permute-start.31 = (bf16[1024,128]{1,0:T(8,128)(2,1)S(1)}, bf16[1024,128]{1,0:T(8,128)(2,1)S(1)}, u32[]{:S(2)}, u32[]{:S(2)}) collective-permute-start(bf16[1024,128]{1,0:T(8,128)(2,1)S(1)} %add_convert_fusion.5), channel_id=1, source_target_pairs={{0,96},{32,64},{64,32},{96,0},{1,97},{33,65},{65,33},{97,1},{2,98}... | collective-permute-start | bytes 786440 | tf_op jit(solution)/shard_map/ppermute | solution.py:27
  120.8 4.8 %collective-permute-done.31 = bf16[1024,128]{1,0:T(8,128)(2,1)S(1)} collective-permute-done((bf16[1024,128]{1,0:T(8,128)(2,1)S(1)}, bf16[1024,128]{1,0:T(8,128)(2,1)S(1)}, u32[]{:S(2)}, u32[]{:S(2)}) %collective-permute-start.31) | collective-permute-done | bytes 262176 | tf_op jit(solution)/shard_map/ppermute | solution.py:27
  125.6 1.5 collective-permute-start.13
  127.6 2.3 %collective-permute-start.26 = (bf16[768,128]{1,0:T(8,128)(2,1)S(1)}, bf16[768,128]{1,0:T(8,128)(2,1)S(1)}, u32[]{:S(2)}, u32[]{:S(2)}) collective-permute-start(bf16[768,128]{1,0:T(8,128)(2,1)S(1)} %add_convert_fusion.8), channel_id=1, source_target_pairs={{0,12},{4,8},{8,4},{12,0},{1,13},{5,9},{9,5},{13,1},{2,14},{6,10},... | collective-permute-start | bytes 589832 | tf_op jit(solution)/shard_map/ppermute | solution.py:27
  130.1 4.5 %collective-permute-done.26 = bf16[768,128]{1,0:T(8,128)(2,1)S(1)} collective-permute-done((bf16[768,128]{1,0:T(8,128)(2,1)S(1)}, bf16[768,128]{1,0:T(8,128)(2,1)S(1)}, u32[]{:S(2)}, u32[]{:S(2)}) %collective-permute-start.26) | collective-permute-done | bytes 196640 | tf_op jit(solution)/shard_map/ppermute | solution.py:27
  134.6 2.7 %collective-permute-start.20 = (bf16[768,128]{1,0:T(8,128)(2,1)S(1)}, bf16[768,128]{1,0:T(8,128)(2,1)S(1)}, u32[]{:S(2)}, u32[]{:S(2)}) collective-permute-start(bf16[768,128]{1,0:T(8,128)(2,1)S(1)} %add_convert_fusion.10), channel_id=1, source_target_pairs={{0,96},{32,64},{64,32},{96,0},{1,97},{33,65},{65,33},{97,1},{2,98}... | collective-permute-start | bytes 589832 | tf_op jit(solution)/shard_map/ppermute | solution.py:27
  137.3 4.2 %collective-permute-done.20 = bf16[768,128]{1,0:T(8,128)(2,1)S(1)} collective-permute-done((bf16[768,128]{1,0:T(8,128)(2,1)S(1)}, bf16[768,128]{1,0:T(8,128)(2,1)S(1)}, u32[]{:S(2)}, u32[]{:S(2)}) %collective-permute-start.20) | collective-permute-done | bytes 196640 | tf_op jit(solution)/shard_map/ppermute | solution.py:27
  143.2 1.2 collective-permute-start.27
  145.5 1.2 collective-permute-start.21
  146.8 3.0 %collective-permute-start.43 = (bf16[576,128]{1,0:T(8,128)(2,1)S(1)}, bf16[576,128]{1,0:T(8,128)(2,1)S(1)}, u32[]{:S(2)}, u32[]{:S(2)}) collective-permute-start(bf16[576,128]{1,0:T(8,128)(2,1)S(1)} %pad_maximum_fusion.7), channel_id=1, source_target_pairs={{0,96},{32,64},{64,32},{96,0},{1,97},{33,65},{65,33},{97,1},{2,98}... | collective-permute-start | bytes 442376 | tf_op jit(solution)/shard_map/ppermute | solution.py:27
  150.3 2.2 %collective-permute-start.36 = (bf16[576,128]{1,0:T(8,128)(2,1)S(1)}, bf16[576,128]{1,0:T(8,128)(2,1)S(1)}, u32[]{:S(2)}, u32[]{:S(2)}) collective-permute-start(bf16[576,128]{1,0:T(8,128)(2,1)S(1)} %pad_maximum_fusion.6), channel_id=1, source_target_pairs={{0,12},{4,8},{8,4},{12,0},{1,13},{5,9},{9,5},{13,1},{2,14},{6,10},... | collective-permute-start | bytes 442376 | tf_op jit(solution)/shard_map/ppermute | solution.py:27
  152.7 2.7 %collective-permute-start.28 = (bf16[960,128]{1,0:T(8,128)(2,1)S(1)}, bf16[960,128]{1,0:T(8,128)(2,1)S(1)}, u32[]{:S(2)}, u32[]{:S(2)}) collective-permute-start(bf16[960,128]{1,0:T(8,128)(2,1)S(1)} %pad_maximum_fusion.5), channel_id=1, source_target_pairs={{0,96},{32,64},{64,32},{96,0},{1,97},{33,65},{65,33},{97,1},{2,98}... | collective-permute-start | bytes 737288 | tf_op jit(solution)/shard_map/ppermute | solution.py:27
  156.9 3.7 %collective-permute-start.45 = (bf16[576,128]{1,0:T(8,128)(2,1)S(1)}, bf16[576,128]{1,0:T(8,128)(2,1)S(1)}, u32[]{:S(2)}, u32[]{:S(2)}) collective-permute-start(bf16[576,128]{1,0:T(8,128)(2,1)S(1)} %fusion.3), channel_id=1, source_target_pairs={{0,16},{16,0},{1,17},{17,1},{2,18},{18,2},{3,19},{19,3},{4,20},{20... | collective-permute-start | bytes 442376 | tf_op jit(solution)/shard_map/ppermute | solution.py:27
  161.7 1.3 collective-permute-done.22
  163.2 2.6 %collective-permute-done.29 = bf16[480,128]{1,0:T(8,128)(2,1)S(1)} collective-permute-done((bf16[480,128]{1,0:T(8,128)(2,1)S(1)}, bf16[480,128]{1,0:T(8,128)(2,1)S(1)}, u32[]{:S(2)}, u32[]{:S(2)}) %collective-permute-start.29) | collective-permute-done | bytes 122912 | tf_op jit(solution)/shard_map/ppermute | solution.py:27
  165.8 2.2 %collective-permute-done.23 = bf16[480,128]{1,0:T(8,128)(2,1)S(1)} collective-permute-done((bf16[480,128]{1,0:T(8,128)(2,1)S(1)}, bf16[480,128]{1,0:T(8,128)(2,1)S(1)}, u32[]{:S(2)}, u32[]{:S(2)}) %collective-permute-start.23) | collective-permute-done | bytes 122912 | tf_op jit(solution)/shard_map/ppermute | solution.py:27
  168.2 3.7 %collective-permute-start.44 = (bf16[384,128]{1,0:T(8,128)(2,1)S(1)}, bf16[384,128]{1,0:T(8,128)(2,1)S(1)}, u32[]{:S(2)}, u32[]{:S(2)}) collective-permute-start(bf16[384,128]{1,0:T(8,128)(2,1)S(1)} %pad_maximum_fusion.10), channel_id=1, source_target_pairs={{0,16},{16,0},{1,17},{17,1},{2,18},{18,2},{3,19},{19,3},{4,20},{20... | collective-permute-start | bytes 294920 | tf_op jit(solution)/shard_map/ppermute | solution.py:27
  171.9 2.5 %collective-permute-done.44.refs_10_ = bf16[384,128]{1,0:T(8,128)(2,1)S(1)} collective-permute-done((bf16[384,128]{1,0:T(8,128)(2,1)S(1)}, bf16[384,128]{1,0:T(8,128)(2,1)S(1)}, u32[]{:S(2)}, u32[]{:S(2)}) %collective-permute-start.44) | collective-permute-done | bytes 98336 | tf_op jit(solution)/shard_map/ppermute | solution.py:27
  (142 shorter events, 21.8 us)
Async XLA Ops:
  0.6 14.2 %collective-permute-start.9 = (bf16[128,2048]{1,0:T(8,128)(2,1)}, bf16[128,2048]{1,0:T(8,128)(2,1)S(1)}, u32[]{:S(2)}, u32[]{:S(2)}) collective-permute-start(bf16[128,2048]{1,0:T(8,128)(2,1)} %x0.1), channel_id=1, source_target_pairs={{0,2},{2,0},{1,3},{3,1},{4,6},{6,4},{5,7},{7,5},{8,10},{10,8},{9,1... | collective-permute-start | bytes 1572872 | tf_op jit(solution)/shard_map/ppermute | solution.py:27
  2.7 27.7 %collective-permute-start.2 = (bf16[128,2048]{1,0:T(8,128)(2,1)}, bf16[128,2048]{1,0:T(8,128)(2,1)S(1)}, u32[]{:S(2)}, u32[]{:S(2)}) collective-permute-start(bf16[128,2048]{1,0:T(8,128)(2,1)} %x0.1), channel_id=1, source_target_pairs={{0,1},{1,0},{2,3},{3,2},{4,5},{5,4},{6,7},{7,6},{8,9},{9,8},{10,11... | collective-permute-start | bytes 1572872 | tf_op jit(solution)/shard_map/ppermute | solution.py:27
  4.1 13.6 %collective-permute-start.1 = (f32[8,128]{1,0:T(8,128)S(1)}, f32[8,128]{1,0:T(8,128)S(1)}, u32[]{:S(2)}, u32[]{:S(2)}) collective-permute-start(f32[8,128]{1,0:T(8,128)S(1)} %get-tuple-element.53), channel_id=1, source_target_pairs={{0,1},{1,0},{2,3},{3,2},{4,5},{5,4},{6,7},{7,6},{8,9},{9,8},{10,11... | collective-permute-start | bytes 12296 | tf_op jit(solution)/shard_map/ppermute | solution.py:27
  4.7 33.1 %collective-permute-start = (bf16[128,2048]{1,0:T(8,128)(2,1)}, bf16[128,2048]{1,0:T(8,128)(2,1)S(1)}, u32[]{:S(2)}, u32[]{:S(2)}) collective-permute-start(bf16[128,2048]{1,0:T(8,128)(2,1)} %refs_2_.7), channel_id=1, source_target_pairs={{0,1},{1,0},{2,3},{3,2},{4,5},{5,4},{6,7},{7,6},{8,9},{9,8},{10,11... | collective-permute-start | bytes 1572872 | tf_op jit(solution)/shard_map/ppermute | solution.py:27
  14.9 26.1 %collective-permute-start.10 = (bf16[128,2048]{1,0:T(8,128)(2,1)S(1)}, bf16[128,2048]{1,0:T(8,128)(2,1)S(1)}, u32[]{:S(2)}, u32[]{:S(2)}) collective-permute-start(bf16[128,2048]{1,0:T(8,128)(2,1)S(1)} %collective-permute-done.9.x0), channel_id=1, source_target_pairs={{0,1},{1,0},{2,3},{3,2},{4,5},{5,4},{6,7},{7,6},{8,9},{9,8},{10,11... | collective-permute-start | bytes 1572872 | tf_op jit(solution)/shard_map/ppermute | solution.py:27
  15.9 9.3 %collective-permute-start.4 = (bf16[128,1024]{1,0:T(8,128)(2,1)S(1)}, bf16[128,1024]{1,0:T(8,128)(2,1)S(1)}, u32[]{:S(2)}, u32[]{:S(2)}) collective-permute-start(bf16[128,1024]{1,0:T(8,128)(2,1)S(1)} %get-tuple-element.105), channel_id=1, source_target_pairs={{0,2},{2,0},{1,3},{3,1},{4,6},{6,4},{5,7},{7,5},{8,10},{10,8},{9,1... | collective-permute-start | bytes 786440 | tf_op jit(solution)/shard_map/ppermute | solution.py:27
  17.8 12.6 %collective-permute-start.3 = (bf16[128,1024]{1,0:T(8,128)(2,1)S(1)}, bf16[128,1024]{1,0:T(8,128)(2,1)S(1)}, u32[]{:S(2)}, u32[]{:S(2)}) collective-permute-start(bf16[128,1024]{1,0:T(8,128)(2,1)S(1)} %get-tuple-element.106), channel_id=1, source_target_pairs={{0,2},{2,0},{1,3},{3,1},{4,6},{6,4},{5,7},{7,5},{8,10},{10,8},{9,1... | collective-permute-start | bytes 786440 | tf_op jit(solution)/shard_map/ppermute | solution.py:27
  25.2 15.2 %collective-permute-start.7 = (f32[8,128]{1,0:T(8,128)S(1)}, f32[8,128]{1,0:T(8,128)S(1)}, u32[]{:S(2)}, u32[]{:S(2)}) collective-permute-start(f32[8,128]{1,0:T(8,128)S(1)} %get-tuple-element.58), channel_id=1, source_target_pairs={{0,2},{1,3},{2,0},{3,1},{4,6},{5,7},{6,4},{7,5},{8,10},{9,11},{10,... | collective-permute-start | bytes 12296 | tf_op jit(solution)/shard_map/ppermute | solution.py:27
  30.4 12.6 %collective-permute-start.6 = (bf16[128,1024]{1,0:T(8,128)(2,1)S(1)}, bf16[128,1024]{1,0:T(8,128)(2,1)S(1)}, u32[]{:S(2)}, u32[]{:S(2)}) collective-permute-start(bf16[128,1024]{1,0:T(8,128)(2,1)S(1)} %collective-permute-done.4.refs_1_.refs_4_), channel_id=1, source_target_pairs={{0,1},{1,0},{2,3},{3,2},{4,5},{5,4},{6,7},{7,6},{8,9},{9,8},{10,11... | collective-permute-start | bytes 786440 | tf_op jit(solution)/shard_map/ppermute | solution.py:27
  30.4 12.6 %collective-permute-start.5 = (bf16[128,1024]{1,0:T(8,128)(2,1)S(1)}, bf16[128,1024]{1,0:T(8,128)(2,1)S(1)}, u32[]{:S(2)}, u32[]{:S(2)}) collective-permute-start(bf16[128,1024]{1,0:T(8,128)(2,1)S(1)} %collective-permute-done.3.refs_0_.refs_4_), channel_id=1, source_target_pairs={{0,1},{1,0},{2,3},{3,2},{4,5},{5,4},{6,7},{7,6},{8,9},{9,8},{10,11... | collective-permute-start | bytes 786440 | tf_op jit(solution)/shard_map/ppermute | solution.py:27
  35.7 5.2 %copy-start.5 = (bf16[1,2048,768]{2,1,0:T(8,128)(2,1)S(1)}, bf16[1,2048,768]{2,1,0:T(8,128)(2,1)}, u32[]{:S(2)}) copy-start(bf16[1,2048,768]{2,1,0:T(8,128)(2,1)} %param.12) | copy-start | bytes 9437188
  37.8 3.2 %collective-permute-start.8 = (f32[8,128]{1,0:T(8,128)S(1)}, f32[8,128]{1,0:T(8,128)S(1)}, u32[]{:S(2)}, u32[]{:S(2)}) collective-permute-start(f32[8,128]{1,0:T(8,128)S(1)} %get-tuple-element.59), channel_id=1, source_target_pairs={{0,3},{1,2},{2,1},{3,0},{4,7},{5,6},{6,5},{7,4},{8,11},{9,10},{10,... | collective-permute-start | bytes 12296 | tf_op jit(solution)/shard_map/ppermute | solution.py:27
  40.4 18.4 %collective-permute-start.14 = (f32[8,128]{1,0:T(8,128)S(1)}, f32[8,128]{1,0:T(8,128)S(1)}, u32[]{:S(2)}, u32[]{:S(2)}) collective-permute-start(f32[8,128]{1,0:T(8,128)S(1)} %get-tuple-element.71), channel_id=1, source_target_pairs={{0,1},{1,0},{2,3},{3,2},{4,5},{5,4},{6,7},{7,6},{8,9},{9,8},{10,11... | collective-permute-start | bytes 12296 | tf_op jit(solution)/shard_map/ppermute | solution.py:27
  44.2 15.3 %collective-permute-start.15 = (f32[8,128]{1,0:T(8,128)S(1)}, f32[8,128]{1,0:T(8,128)S(1)}, u32[]{:S(2)}, u32[]{:S(2)}) collective-permute-start(f32[8,128]{1,0:T(8,128)S(1)} %get-tuple-element.72), channel_id=1, source_target_pairs={{0,2},{1,3},{2,0},{3,1},{4,6},{5,7},{6,4},{7,5},{8,10},{9,11},{10,... | collective-permute-start | bytes 12296 | tf_op jit(solution)/shard_map/ppermute | solution.py:27
  45.9 14.0 %collective-permute-start.16 = (f32[8,128]{1,0:T(8,128)S(1)}, f32[8,128]{1,0:T(8,128)S(1)}, u32[]{:S(2)}, u32[]{:S(2)}) collective-permute-start(f32[8,128]{1,0:T(8,128)S(1)} %get-tuple-element.73), channel_id=1, source_target_pairs={{0,3},{1,2},{2,1},{3,0},{4,7},{5,6},{6,5},{7,4},{8,11},{9,10},{10,... | collective-permute-start | bytes 12296 | tf_op jit(solution)/shard_map/ppermute | solution.py:27
  50.3 13.7 %collective-permute-start.32 = (bf16[1024,128]{1,0:T(8,128)(2,1)S(1)}, bf16[1024,128]{1,0:T(8,128)(2,1)S(1)}, u32[]{:S(2)}, u32[]{:S(2)}) collective-permute-start(bf16[1024,128]{1,0:T(8,128)(2,1)S(1)} %get-tuple-element.87), channel_id=1, source_target_pairs={{0,32},{32,0},{64,96},{96,64},{1,33},{33,1},{65,97},{97,65},{2,34}... | collective-permute-start | bytes 786440 | tf_op jit(solution)/shard_map/ppermute | solution.py:27
  52.1 13.5 %collective-permute-start.39 = (bf16[1024,128]{1,0:T(8,128)(2,1)S(1)}, bf16[1024,128]{1,0:T(8,128)(2,1)S(1)}, u32[]{:S(2)}, u32[]{:S(2)}) collective-permute-start(bf16[1024,128]{1,0:T(8,128)(2,1)S(1)} %get-tuple-element.93), channel_id=1, source_target_pairs={{0,4},{4,0},{8,12},{12,8},{1,5},{5,1},{9,13},{13,9},{2,6},{6,2},{1... | collective-permute-start | bytes 786440 | tf_op jit(solution)/shard_map/ppermute | solution.py:27
  56.4 7.1 %copy-start.8 = (s32[128,2]{0,1:T(2,128)S(1)}, s32[128,2]{0,1:T(2,128)}, u32[]{:S(2)}) copy-start(s32[128,2]{0,1:T(2,128)} %param.9) | copy-start | bytes 3076
  58.8 12.1 %collective-permute-start.33 = (bf16[1536,128]{1,0:T(8,128)(2,1)S(1)}, bf16[1536,128]{1,0:T(8,128)(2,1)S(1)}, u32[]{:S(2)}, u32[]{:S(2)}) collective-permute-start(bf16[1536,128]{1,0:T(8,128)(2,1)S(1)} %get-tuple-element.89), channel_id=1, source_target_pairs={{0,32},{32,0},{64,96},{96,64},{1,33},{33,1},{65,97},{97,65},{2,34}... | collective-permute-start | bytes 1179656 | tf_op jit(solution)/shard_map/ppermute | solution.py:27
  59.5 12.0 %collective-permute-start.40 = (bf16[1536,128]{1,0:T(8,128)(2,1)S(1)}, bf16[1536,128]{1,0:T(8,128)(2,1)S(1)}, u32[]{:S(2)}, u32[]{:S(2)}) collective-permute-start(bf16[1536,128]{1,0:T(8,128)(2,1)S(1)} %get-tuple-element.95), channel_id=1, source_target_pairs={{0,4},{4,0},{8,12},{12,8},{1,5},{5,1},{9,13},{13,9},{2,6},{6,2},{1... | collective-permute-start | bytes 1179656 | tf_op jit(solution)/shard_map/ppermute | solution.py:27
  59.9 67.2 %collective-permute-start.19 = (bf16[3072,128]{1,0:T(8,128)(2,1)S(1)}, bf16[3072,128]{1,0:T(8,128)(2,1)S(1)}, u32[]{:S(2)}, u32[]{:S(2)}) collective-permute-start(bf16[3072,128]{1,0:T(8,128)(2,1)S(1)} %shard_map.120), channel_id=1, source_target_pairs={{0,16},{16,0},{1,17},{17,1},{2,18},{18,2},{3,19},{19,3},{4,20},{20... | collective-permute-start | bytes 2359304 | tf_op jit(solution)/shard_map/ppermute | solution.py:27
  64.1 17.0 %collective-permute-start.30 = (bf16[2048,128]{1,0:T(8,128)(2,1)S(1)}, bf16[2048,128]{1,0:T(8,128)(2,1)S(1)}, u32[]{:S(2)}, u32[]{:S(2)}) collective-permute-start(bf16[2048,128]{1,0:T(8,128)(2,1)S(1)} %get-tuple-element.85), channel_id=1, source_target_pairs={{0,32},{32,0},{64,96},{96,64},{1,33},{33,1},{65,97},{97,65},{2,34}... | collective-permute-start | bytes 1572872 | tf_op jit(solution)/shard_map/ppermute | solution.py:27
  65.6 17.8 %collective-permute-start.37 = (bf16[2048,128]{1,0:T(8,128)(2,1)S(1)}, bf16[2048,128]{1,0:T(8,128)(2,1)S(1)}, u32[]{:S(2)}, u32[]{:S(2)}) collective-permute-start(bf16[2048,128]{1,0:T(8,128)(2,1)S(1)} %get-tuple-element.91), channel_id=1, source_target_pairs={{0,4},{4,0},{8,12},{12,8},{1,5},{5,1},{9,13},{13,9},{2,6},{6,2},{1... | collective-permute-start | bytes 1572872 | tf_op jit(solution)/shard_map/ppermute | solution.py:27
  70.9 3.4 %collective-permute-start.12 = (bf16[128,2048]{1,0:T(8,128)(2,1)S(1)}, bf16[128,2048]{1,0:T(8,128)(2,1)S(1)}, u32[]{:S(2)}, u32[]{:S(2)}) collective-permute-start(bf16[128,2048]{1,0:T(8,128)(2,1)S(1)} %get-tuple-element.69), channel_id=1, source_target_pairs={{0,1},{1,0},{2,3},{3,2},{4,5},{5,4},{6,7},{7,6},{8,9},{9,8},{10,11... | collective-permute-start | bytes 1572872 | tf_op jit(solution)/shard_map/ppermute | solution.py:27
  71.5 55.9 %collective-permute-start.17 = (bf16[3072,128]{1,0:T(8,128)(2,1)S(1)}, bf16[3072,128]{1,0:T(8,128)(2,1)S(1)}, u32[]{:S(2)}, u32[]{:S(2)}) collective-permute-start(bf16[3072,128]{1,0:T(8,128)(2,1)S(1)} %get-tuple-element.77), channel_id=1, source_target_pairs={{0,96},{32,64},{64,32},{96,0},{1,97},{33,65},{65,33},{97,1},{2,98}... | collective-permute-start | bytes 2359304 | tf_op jit(solution)/shard_map/ppermute | solution.py:27
  74.3 53.3 %collective-permute-start.24 = (bf16[3072,128]{1,0:T(8,128)(2,1)S(1)}, bf16[3072,128]{1,0:T(8,128)(2,1)S(1)}, u32[]{:S(2)}, u32[]{:S(2)}) collective-permute-start(bf16[3072,128]{1,0:T(8,128)(2,1)S(1)} %get-tuple-element.82), channel_id=1, source_target_pairs={{0,12},{4,8},{8,4},{12,0},{1,13},{5,9},{9,5},{13,1},{2,14},{6,10},... | collective-permute-start | bytes 2359304 | tf_op jit(solution)/shard_map/ppermute | solution.py:27
  81.1 20.2 %collective-permute-start.41 = (bf16[1280,128]{1,0:T(8,128)(2,1)S(1)}, bf16[1280,128]{1,0:T(8,128)(2,1)S(1)}, u32[]{:S(2)}, u32[]{:S(2)}) collective-permute-start(bf16[1280,128]{1,0:T(8,128)(2,1)S(1)} %pad_maximum_fusion.1), channel_id=1, source_target_pairs={{0,12},{4,8},{8,4},{12,0},{1,13},{5,9},{9,5},{13,1},{2,14},{6,10},... | collective-permute-start | bytes 983048 | tf_op jit(solution)/shard_map/ppermute | solution.py:27
  83.4 58.9 %collective-permute-start.11 = (bf16[128,2048]{1,0:T(8,128)(2,1)S(1)}, bf16[128,2048]{1,0:T(8,128)(2,1)S(1)}, u32[]{:S(2)}, u32[]{:S(2)}) collective-permute-start(bf16[128,2048]{1,0:T(8,128)(2,1)S(1)} %get-tuple-element.67), channel_id=1, source_target_pairs={{0,1},{1,0},{2,3},{3,2},{4,5},{5,4},{6,7},{7,6},{8,9},{9,8},{10,11... | collective-permute-start | bytes 1572872 | tf_op jit(solution)/shard_map/ppermute | solution.py:27
  101.3 9.2 %collective-permute-start.34 = (bf16[1280,128]{1,0:T(8,128)(2,1)S(1)}, bf16[1280,128]{1,0:T(8,128)(2,1)S(1)}, u32[]{:S(2)}, u32[]{:S(2)}) collective-permute-start(bf16[1280,128]{1,0:T(8,128)(2,1)S(1)} %pad_maximum_fusion), channel_id=1, source_target_pairs={{0,96},{32,64},{64,32},{96,0},{1,97},{33,65},{65,33},{97,1},{2,98}... | collective-permute-start | bytes 983048 | tf_op jit(solution)/shard_map/ppermute | solution.py:27
  110.5 7.6 %collective-permute-start.38 = (bf16[1024,128]{1,0:T(8,128)(2,1)S(1)}, bf16[1024,128]{1,0:T(8,128)(2,1)S(1)}, u32[]{:S(2)}, u32[]{:S(2)}) collective-permute-start(bf16[1024,128]{1,0:T(8,128)(2,1)S(1)} %add_convert_fusion.4), channel_id=1, source_target_pairs={{0,12},{4,8},{8,4},{12,0},{1,13},{5,9},{9,5},{13,1},{2,14},{6,10},... | collective-permute-start | bytes 786440 | tf_op jit(solution)/shard_map/ppermute | solution.py:27
  118.0 7.6 %collective-permute-start.31 = (bf16[1024,128]{1,0:T(8,128)(2,1)S(1)}, bf16[1024,128]{1,0:T(8,128)(2,1)S(1)}, u32[]{:S(2)}, u32[]{:S(2)}) collective-permute-start(bf16[1024,128]{1,0:T(8,128)(2,1)S(1)} %add_convert_fusion.5), channel_id=1, source_target_pairs={{0,96},{32,64},{64,32},{96,0},{1,97},{33,65},{65,33},{97,1},{2,98}... | collective-permute-start | bytes 786440 | tf_op jit(solution)/shard_map/ppermute | solution.py:27
  125.6 17.6 %collective-permute-start.13 = (bf16[128,2048]{1,0:T(8,128)(2,1)S(1)}, bf16[128,2048]{1,0:T(8,128)(2,1)S(1)}, u32[]{:S(2)}, u32[]{:S(2)}) collective-permute-start(bf16[128,2048]{1,0:T(8,128)(2,1)S(1)} %add_convert_fusion.1), channel_id=1, source_target_pairs={{0,2},{2,0},{1,3},{3,1},{4,6},{6,4},{5,7},{7,5},{8,10},{10,8},{9,1... | collective-permute-start | bytes 1572872 | tf_op jit(solution)/shard_map/ppermute | solution.py:27
  127.2 18.3 %collective-permute-start.42 = (bf16[1152,128]{1,0:T(8,128)(2,1)S(1)}, bf16[1152,128]{1,0:T(8,128)(2,1)S(1)}, u32[]{:S(2)}, u32[]{:S(2)}) collective-permute-start(bf16[1152,128]{1,0:T(8,128)(2,1)S(1)} %pad_maximum_fusion.3), channel_id=1, source_target_pairs={{0,32},{32,0},{64,96},{96,64},{1,33},{33,1},{65,97},{97,65},{2,34}... | collective-permute-start | bytes 884744 | tf_op jit(solution)/shard_map/ppermute | solution.py:27
  127.4 19.4 %collective-permute-start.35 = (bf16[1152,128]{1,0:T(8,128)(2,1)S(1)}, bf16[1152,128]{1,0:T(8,128)(2,1)S(1)}, u32[]{:S(2)}, u32[]{:S(2)}) collective-permute-start(bf16[1152,128]{1,0:T(8,128)(2,1)S(1)} %pad_maximum_fusion.2), channel_id=1, source_target_pairs={{0,4},{4,0},{8,12},{12,8},{1,5},{5,1},{9,13},{13,9},{2,6},{6,2},{1... | collective-permute-start | bytes 884744 | tf_op jit(solution)/shard_map/ppermute | solution.py:27
  127.6 7.0 %collective-permute-start.26 = (bf16[768,128]{1,0:T(8,128)(2,1)S(1)}, bf16[768,128]{1,0:T(8,128)(2,1)S(1)}, u32[]{:S(2)}, u32[]{:S(2)}) collective-permute-start(bf16[768,128]{1,0:T(8,128)(2,1)S(1)} %add_convert_fusion.8), channel_id=1, source_target_pairs={{0,12},{4,8},{8,4},{12,0},{1,13},{5,9},{9,5},{13,1},{2,14},{6,10},... | collective-permute-start | bytes 589832 | tf_op jit(solution)/shard_map/ppermute | solution.py:27
  134.6 6.9 %collective-permute-start.20 = (bf16[768,128]{1,0:T(8,128)(2,1)S(1)}, bf16[768,128]{1,0:T(8,128)(2,1)S(1)}, u32[]{:S(2)}, u32[]{:S(2)}) collective-permute-start(bf16[768,128]{1,0:T(8,128)(2,1)S(1)} %add_convert_fusion.10), channel_id=1, source_target_pairs={{0,96},{32,64},{64,32},{96,0},{1,97},{33,65},{65,33},{97,1},{2,98}... | collective-permute-start | bytes 589832 | tf_op jit(solution)/shard_map/ppermute | solution.py:27
  141.5 11.1 %collective-permute-start.25 = (bf16[1536,128]{1,0:T(8,128)(2,1)S(1)}, bf16[1536,128]{1,0:T(8,128)(2,1)S(1)}, u32[]{:S(2)}, u32[]{:S(2)}) collective-permute-start(bf16[1536,128]{1,0:T(8,128)(2,1)S(1)} %add_convert_fusion.2), channel_id=1, source_target_pairs={{0,4},{4,0},{8,12},{12,8},{1,5},{5,1},{9,13},{13,9},{2,6},{6,2},{1... | collective-permute-start | bytes 1179656 | tf_op jit(solution)/shard_map/ppermute | solution.py:27
  142.3 13.1 %collective-permute-start.18 = (bf16[1536,128]{1,0:T(8,128)(2,1)S(1)}, bf16[1536,128]{1,0:T(8,128)(2,1)S(1)}, u32[]{:S(2)}, u32[]{:S(2)}) collective-permute-start(bf16[1536,128]{1,0:T(8,128)(2,1)S(1)} %add_convert_fusion.3), channel_id=1, source_target_pairs={{0,32},{32,0},{64,96},{96,64},{1,33},{33,1},{65,97},{97,65},{2,34}... | collective-permute-start | bytes 1179656 | tf_op jit(solution)/shard_map/ppermute | solution.py:27
  143.2 7.1 %collective-permute-start.27 = (bf16[384,128]{1,0:T(8,128)(2,1)S(1)}, bf16[384,128]{1,0:T(8,128)(2,1)S(1)}, u32[]{:S(2)}, u32[]{:S(2)}) collective-permute-start(bf16[384,128]{1,0:T(8,128)(2,1)S(1)} %add_convert_fusion.19), channel_id=1, source_target_pairs={{0,4},{4,0},{8,12},{12,8},{1,5},{5,1},{9,13},{13,9},{2,6},{6,2},{1... | collective-permute-start | bytes 294920 | tf_op jit(solution)/shard_map/ppermute | solution.py:27
  145.5 7.0 %collective-permute-start.21 = (bf16[384,128]{1,0:T(8,128)(2,1)S(1)}, bf16[384,128]{1,0:T(8,128)(2,1)S(1)}, u32[]{:S(2)}, u32[]{:S(2)}) collective-permute-start(bf16[384,128]{1,0:T(8,128)(2,1)S(1)} %add_convert_fusion.21), channel_id=1, source_target_pairs={{0,32},{32,0},{64,96},{96,64},{1,33},{33,1},{65,97},{97,65},{2,34}... | collective-permute-start | bytes 294920 | tf_op jit(solution)/shard_map/ppermute | solution.py:27
  146.8 9.9 %collective-permute-start.43 = (bf16[576,128]{1,0:T(8,128)(2,1)S(1)}, bf16[576,128]{1,0:T(8,128)(2,1)S(1)}, u32[]{:S(2)}, u32[]{:S(2)}) collective-permute-start(bf16[576,128]{1,0:T(8,128)(2,1)S(1)} %pad_maximum_fusion.7), channel_id=1, source_target_pairs={{0,96},{32,64},{64,32},{96,0},{1,97},{33,65},{65,33},{97,1},{2,98}... | collective-permute-start | bytes 442376 | tf_op jit(solution)/shard_map/ppermute | solution.py:27
  150.3 6.4 %collective-permute-start.36 = (bf16[576,128]{1,0:T(8,128)(2,1)S(1)}, bf16[576,128]{1,0:T(8,128)(2,1)S(1)}, u32[]{:S(2)}, u32[]{:S(2)}) collective-permute-start(bf16[576,128]{1,0:T(8,128)(2,1)S(1)} %pad_maximum_fusion.6), channel_id=1, source_target_pairs={{0,12},{4,8},{8,4},{12,0},{1,13},{5,9},{9,5},{13,1},{2,14},{6,10},... | collective-permute-start | bytes 442376 | tf_op jit(solution)/shard_map/ppermute | solution.py:27
  152.7 8.0 %collective-permute-start.28 = (bf16[960,128]{1,0:T(8,128)(2,1)S(1)}, bf16[960,128]{1,0:T(8,128)(2,1)S(1)}, u32[]{:S(2)}, u32[]{:S(2)}) collective-permute-start(bf16[960,128]{1,0:T(8,128)(2,1)S(1)} %pad_maximum_fusion.5), channel_id=1, source_target_pairs={{0,96},{32,64},{64,32},{96,0},{1,97},{33,65},{65,33},{97,1},{2,98}... | collective-permute-start | bytes 737288 | tf_op jit(solution)/shard_map/ppermute | solution.py:27
  155.5 7.5 %collective-permute-start.22 = (bf16[960,128]{1,0:T(8,128)(2,1)S(1)}, bf16[960,128]{1,0:T(8,128)(2,1)S(1)}, u32[]{:S(2)}, u32[]{:S(2)}) collective-permute-start(bf16[960,128]{1,0:T(8,128)(2,1)S(1)} %pad_maximum_fusion.4), channel_id=1, source_target_pairs={{0,12},{4,8},{8,4},{12,0},{1,13},{5,9},{9,5},{13,1},{2,14},{6,10},... | collective-permute-start | bytes 737288 | tf_op jit(solution)/shard_map/ppermute | solution.py:27
  156.9 15.0 %collective-permute-start.45 = (bf16[576,128]{1,0:T(8,128)(2,1)S(1)}, bf16[576,128]{1,0:T(8,128)(2,1)S(1)}, u32[]{:S(2)}, u32[]{:S(2)}) collective-permute-start(bf16[576,128]{1,0:T(8,128)(2,1)S(1)} %fusion.3), channel_id=1, source_target_pairs={{0,16},{16,0},{1,17},{17,1},{2,18},{18,2},{3,19},{19,3},{4,20},{20... | collective-permute-start | bytes 442376 | tf_op jit(solution)/shard_map/ppermute | solution.py:27
  160.8 5.0 %collective-permute-start.29 = (bf16[480,128]{1,0:T(8,128)(2,1)S(1)}, bf16[480,128]{1,0:T(8,128)(2,1)S(1)}, u32[]{:S(2)}, u32[]{:S(2)}) collective-permute-start(bf16[480,128]{1,0:T(8,128)(2,1)S(1)} %pad_maximum_fusion.9), channel_id=1, source_target_pairs={{0,32},{32,0},{64,96},{96,64},{1,33},{33,1},{65,97},{97,65},{2,34}... | collective-permute-start | bytes 368648 | tf_op jit(solution)/shard_map/ppermute | solution.py:27
  163.1 5.0 %collective-permute-start.23 = (bf16[480,128]{1,0:T(8,128)(2,1)S(1)}, bf16[480,128]{1,0:T(8,128)(2,1)S(1)}, u32[]{:S(2)}, u32[]{:S(2)}) collective-permute-start(bf16[480,128]{1,0:T(8,128)(2,1)S(1)} %pad_maximum_fusion.8), channel_id=1, source_target_pairs={{0,4},{4,0},{8,12},{12,8},{1,5},{5,1},{9,13},{13,9},{2,6},{6,2},{1... | collective-permute-start | bytes 368648 | tf_op jit(solution)/shard_map/ppermute | solution.py:27
  168.2 6.3 %collective-permute-start.44 = (bf16[384,128]{1,0:T(8,128)(2,1)S(1)}, bf16[384,128]{1,0:T(8,128)(2,1)S(1)}, u32[]{:S(2)}, u32[]{:S(2)}) collective-permute-start(bf16[384,128]{1,0:T(8,128)(2,1)S(1)} %pad_maximum_fusion.10), channel_id=1, source_target_pairs={{0,16},{16,0},{1,17},{17,1},{2,18},{18,2},{3,19},{19,3},{4,20},{20... | collective-permute-start | bytes 294920 | tf_op jit(solution)/shard_map/ppermute | solution.py:27
  (8 other events, 16.3 us)

commit v3 on v2

--- a/solution.py
+++ b/solution.py
@@ -75,14 +75,6 @@
         chosen = ids[...] == (mine ^ m)
         row = jnp.sum(jnp.where(chosen, combine[...], 0.0), axis=0, keepdims=True)
         out[...] = jnp.broadcast_to(row, out.shape)
-
-
-def combine_body(ids, c0, c1, c2, c3, out):
-    mine = group_index()
-    total = jnp.zeros(out.shape, F32)
-    for m, c in enumerate((c0, c1, c2, c3)):
-        total = total + jnp.where(ids[...] == (mine ^ m), c[0:1, :], 0.0)
-    out[...] = total
 
 
 def forward_body(x0, x1, c0, c1, wg, wu, slope, act_out, hid, cht, xt, xs):
@@ -198,7 +190,8 @@
 
 TILE = 256
 EARLY = ((2, 0, 3), (3, 0, 3))
-LATER = ((0, 0, 2), (1, 0, 2), (0, 2, 3), (1, 2, 3))
+LATER = ((0, 0, 3), (1, 0, 3))
+EXTRA = 128
 
 
 def gate_body(first, specs, xta, xtb, gda, gdb, uda, udb, *refs):
@@ -246,17 +239,34 @@
     )
 
 
-def rows_body(gda, gdb, uda, udb, wg, wu, r0, r1, r2, r3, gd, ud):
+def rows_body(gda, gdb, uda, udb, wg, wu, *refs):
+    combs, (own, side, across, gd, ud) = refs[:4], refs[4:]
     half = gda.shape[0]
     for scratch, pair in ((gd, (gda, gdb)), (ud, (uda, udb))):
         for j, ref in enumerate(pair):
             scratch[pl.ds(j * half, half), :] = ref[...]
+    places = ((own, 0), (side, 0), (across, 0), (side, PIECE))
     tile = 512
     for n in range(wg.shape[0] // tile):
         at = pl.ds(n * tile, tile)
         total = (nt(gd[...], wg[at, :]) + nt(ud[...], wu[at, :])).astype(BF16)
-        for j, r in enumerate((r0, r1, r2, r3)):
-            r[:, at] = total[j * PIECE : (j + 1) * PIECE, :]
+        for j, (out, row) in enumerate(places):
+            out[pl.ds(row, PIECE), at] = total[j * PIECE : (j + 1) * PIECE, :]
+    mine = lax.broadcasted_iota(jnp.int32, (PIECE, EXTRA), 1) == group_index()
+    for comb, (out, row) in zip(combs, places):
+        value = jnp.where(mine, as_column(comb[...]), 0.0)
+        out[pl.ds(row, PIECE), pl.ds(wg.shape[0], EXTRA)] = value.astype(BF16)
+
+
+def tokens_body(ids, own, side, across, grad, combine):
+    total = own[...].astype(F32) + side[pl.ds(0, PIECE), :].astype(F32) + across[...].astype(F32)
+    d = grad.shape[1]
+    grad[...] = total[:, :d].astype(BF16)
+    lanes = total[:, d:].T
+    picked = jnp.zeros(combine.shape, F32)
+    for e in range(4):
+        picked = picked + jnp.where(ids[...] == e, lanes[e : e + 1, :], 0.0)
+    combine[...] = picked
 
 
 def finish_body(*refs):
@@ -267,8 +277,8 @@
     done = []
     for n, base in enumerate(bases):
         rows = base.shape[0]
-        p = (EARLY + LATER)[n][0] if n < 6 else n - 6
-        if n < 6 or p < 2:
+        p = (EARLY + LATER)[n][0] if n < 4 else n - 4
+        if n < 4 or p < 2:
             array, at = recv[p // 2 * 2]
             done.append(base[...] + array[at : at + rows])
             recv[p // 2 * 2] = (array, at + rows)
@@ -279,7 +289,7 @@
         for k in range(total.shape[0] // half):
             to = first * TILE + k * LANES
             out[pl.ds(p % 2 * half, half), pl.ds(to, LANES)] = total[k * half : (k + 1) * half].astype(BF16)
-    for p, total in enumerate(done[6:]):
+    for p, total in enumerate(done[4:]):
         for k in range(cols // LANES):
             down[:, pl.ds(p * cols + k * LANES, LANES)] = total[k * low : (k + 1) * low].astype(BF16)
 
@@ -320,10 +330,10 @@
     gate_send += gate_half(HALF, LATER, xts, gds, uds)
     down_keep = [a for k in range(2) for a in down_half(0, k, hts, pieces[k])]
     gate_keep = gate_half(0, EARLY + LATER, xts, gds, uds)
-    grads = kernel(
+    own_rows, side_rows, far_rows = kernel(
         rows_body,
-        (*gds, *uds, wg, wu),
-        [((PIECE, d), BF16)] * 4,
+        (*gds, *uds, wg, wu, ha[2], ha[3], hb[2], hb[3]),
+        [((n * PIECE, d + EXTRA), BF16) for n in (1, 2, 1)],
         12,
         4 * rows * d * ff,
         scratch=(pltpu.VMEM((rows, ff), BF16),) * 2,
@@ -350,14 +360,12 @@
             at += send.shape[0]
         return got
 
-    for p in (0, 1):
-        exchange(have[p][:1], ORDERS[p][1])
     for p in (2, 3):
         exchange(have[p][:1], ORDERS[p][1])
     for p in (2, 3):
         exchange(downs[p : p + 1], DOWN_ORDERS[p][1])
     for p in (0, 1):
-        exchange(have[p][1:], ORDERS[p][1])
+        exchange(have[p], ORDERS[p][1])
     for p in (2, 3):
         exchange(downs[p : p + 1], DOWN_ORDERS[p][2])
     for step in (2, 3):
@@ -374,14 +382,13 @@
         1 << 20,
     )
 
-    near = moved(grads[1], "c", 1)
-    far = (grads[2].astype(F32) + moved(grads[3], "c", 1).astype(F32)).astype(BF16)
-    far = moved(far, "zl", 1)
-    input_grad = (grads[0].astype(F32) + near.astype(F32) + far.astype(F32)).astype(BF16)
-
-    comb = [ha[2], ha[3], hb[2], hb[3]]
-    given = [comb[0]] + [moved(comb[m], GROUP, m) for m in (1, 2, 3)]
-    combine_grad = kernel(combine_body, (expert_ids.T, *given), [((2, PIECE), F32)], 2, 1 << 10)[0].T
+    side_rows = moved(side_rows, "c", 1)
+    far_rows = (far_rows.astype(F32) + side_rows[PIECE:].astype(F32)).astype(BF16)
+    far_rows = moved(far_rows, "zl", 1)
+    input_grad, combine_grad = kernel(
+        tokens_body, (expert_ids.T, own_rows, side_rows, far_rows), [((PIECE, d), BF16), ((2, PIECE), F32)], 8, 1 << 20
+    )
+    combine_grad = combine_grad.T
     return (input_grad, combine_grad, gate_grad[None], up_grad[None], down_grad[None])
 
 

time: 175 us -> 166 us (0.949)
  starting transfers between devices: 63.5 us -> 56 us
    ppermute x46 -> x38, starting transfers between devices: 63.5 us -> 56 us  [moved(): lax.ppermute(array, axis, [(i, i ^ mask) for i in range(lax.axis_size(axi...]
    ppermute x46 -> x38, waiting for transfers between devices: 82.5 us -> 82.3 us  [moved(): lax.ppermute(array, axis, [(i, i ^ mask) for i in range(lax.axis_size(axi...]
  transfers between devices with their start and end apart: 46 -> 38, of which waited for: 17 -> 18; matrix products, arithmetic and copies ran while one was open for 3% -> 2% of each run, Pallas kernels for 9% -> 8%
where the time goes in v3:
time: 166 us
  waiting for transfers between devices  82.3 us (50%)
  starting transfers between devices  56 us (34%)
  Pallas kernels  17.8 us (11%)
  local copies, waits for them, and re-layouts  6.48 us (4%)
  other arithmetic  2.3 us (1%)
    ppermute x38, waiting for transfers between devices, moved(): lax.ppermute(array, axis, [(i, i ^ mask) for i in range(lax.axis_size(axi...  82.3 us
    ppermute x38, starting transfers between devices, moved(): lax.ppermute(array, axis, [(i, i ^ mask) for i in range(lax.axis_size(axi...  56 us
    pallas_call x15, Pallas kernels, kernel(): pl.pallas_call(body, in_specs=[vmem] * len(ins), out_specs=[vmem] * len(o...  17.8 us
    unnamed x20, local copies, waits for them, and re-layouts  5.37 us
  transfers between devices with their start and end apart: 38, of which 18 were waited for; matrix products, arithmetic and copies ran while one was open for 2% of the time, Pallas kernels for 8%

profile of v3, /device:TPU:0, one launch (start us, length us, event | category | flops | bytes accessed | tf_op | source)
XLA Modules:
  0.0 166.0 jit_solution(7043674610333548958)
XLA Ops:
  0.6 2.1 %collective-permute-start.9 = (bf16[128,2048]{1,0:T(8,128)(2,1)}, bf16[128,2048]{1,0:T(8,128)(2,1)S(1)}, u32[]{:S(2)}, u32[]{:S(2)}) collective-permute-start(bf16[128,2048]{1,0:T(8,128)(2,1)} %x0.1), channel_id=1, source_target_pairs={{0,2},{2,0},{1,3},{3,1},{4,6},{6,4},{5,7},{7,5},{8,10},{10,8},{9,1... | collective-permute-start | bytes 1572872 | tf_op jit(solution)/shard_map/ppermute | solution.py:27
  4.8 10.1 %collective-permute-done.9.x0 = bf16[128,2048]{1,0:T(8,128)(2,1)S(1)} collective-permute-done((bf16[128,2048]{1,0:T(8,128)(2,1)}, bf16[128,2048]{1,0:T(8,128)(2,1)S(1)}, u32[]{:S(2)}, u32[]{:S(2)}) %collective-permute-start.9) | collective-permute-done | bytes 524320 | tf_op jit(solution)/shard_map/ppermute | solution.py:27
  14.9 1.1 fusion.1
  16.0 1.8 %collective-permute-start.3 = (bf16[128,1024]{1,0:T(8,128)(2,1)S(1)}, bf16[128,1024]{1,0:T(8,128)(2,1)S(1)}, u32[]{:S(2)}, u32[]{:S(2)}) collective-permute-start(bf16[128,1024]{1,0:T(8,128)(2,1)S(1)} %get-tuple-element.108), channel_id=1, source_target_pairs={{0,2},{2,0},{1,3},{3,1},{4,6},{6,4},{5,7},{7,5},{8,10},{10,8},{9,1... | collective-permute-start | bytes 786440 | tf_op jit(solution)/shard_map/ppermute | solution.py:27
  18.1 7.1 %collective-permute-done.3.refs_0_.refs_4_ = bf16[128,1024]{1,0:T(8,128)(2,1)S(1)} collective-permute-done((bf16[128,1024]{1,0:T(8,128)(2,1)S(1)}, bf16[128,1024]{1,0:T(8,128)(2,1)S(1)}, u32[]{:S(2)}, u32[]{:S(2)}) %collective-permute-start.3) | collective-permute-done | bytes 262176 | tf_op jit(solution)/shard_map/ppermute | solution.py:27
  25.2 1.7 %collective-permute-start.7 = (f32[8,128]{1,0:T(8,128)S(1)}, f32[8,128]{1,0:T(8,128)S(1)}, u32[]{:S(2)}, u32[]{:S(2)}) collective-permute-start(f32[8,128]{1,0:T(8,128)S(1)} %get-tuple-element.55), channel_id=1, source_target_pairs={{0,2},{1,3},{2,0},{3,1},{4,6},{5,7},{6,4},{7,5},{8,10},{9,11},{10,... | collective-permute-start | bytes 12296 | tf_op jit(solution)/shard_map/ppermute | solution.py:27
  27.0 3.5 %collective-permute-done.4.refs_1_.refs_4_ = bf16[128,1024]{1,0:T(8,128)(2,1)S(1)} collective-permute-done((bf16[128,1024]{1,0:T(8,128)(2,1)S(1)}, bf16[128,1024]{1,0:T(8,128)(2,1)S(1)}, u32[]{:S(2)}, u32[]{:S(2)}) %collective-permute-start.4) | collective-permute-done | bytes 262176 | tf_op jit(solution)/shard_map/ppermute | solution.py:27
  30.9 1.9 %copy-done.2 = bf16[1,2048,768]{2,1,0:T(8,128)(2,1)S(1)} copy-done((bf16[1,2048,768]{2,1,0:T(8,128)(2,1)S(1)}, bf16[1,2048,768]{2,1,0:T(8,128)(2,1)}, u32[]{:S(2)}) %copy-start.2) | copy-done | bytes 3145752
  32.8 1.9 %copy-done.4 = bf16[1,2048,768]{2,1,0:T(8,128)(2,1)S(1)} copy-done((bf16[1,2048,768]{2,1,0:T(8,128)(2,1)S(1)}, bf16[1,2048,768]{2,1,0:T(8,128)(2,1)}, u32[]{:S(2)}) %copy-start.4) | copy-done | bytes 3145752
  34.7 2.0 %shard_map.111 = (f32[256,768]{1,0:T(8,128)S(1)}, f32[256,768]{1,0:T(8,128)S(1)}, bf16[256,768]{1,0:T(8,128)(2,1)S(1)}, f32[768,256]{1,0:T(8,128)S(1)}, bf16[2048,256]{1,0:T(8,128)(2,1)S(1)}) custom-call(bf16[128,2048]{1,0:T(8,128)(2,1)S(1)} %copy-done.6, bf16[128,2048]{1,0:T(8,128)(2,1)S(1)} %collective-permute-done.2.x1, ...), custom_call_target="tpu_custom_call" | custom-call | flops 1610612736 | bytes 1048576 | tf_op jit(solution)/shard_map/pallas_call | solution.py:61
  36.7 1.4 collective-permute-start.8
  38.2 1.2 shard_map.112
  40.0 2.0 %shard_map.113 = (f32[256,768]{1,0:T(8,128)S(1)}, f32[256,768]{1,0:T(8,128)S(1)}, bf16[256,768]{1,0:T(8,128)(2,1)S(1)}, f32[768,256]{1,0:T(8,128)S(1)}, bf16[2048,256]{1,0:T(8,128)(2,1)S(1)}) custom-call(bf16[128,2048]{1,0:T(8,128)(2,1)S(1)} %collective-permute-done.9.x0, bf16[128,2048]{1,0:T(8,128)(2,1)S(1)} %collective-permute-done.10.x1, ...), custom_call_target="tpu_custom_call" | custom-call | flops 1610612736 | bytes 1048576 | tf_op jit(solution)/shard_map/pallas_call | solution.py:61
  42.0 1.2 shard_map.114
  43.3 1.0 shard_map.121
  44.2 1.0 shard_map.118
  45.2 1.7 %collective-permute-start.31 = (bf16[3072,128]{1,0:T(8,128)(2,1)S(1)}, bf16[3072,128]{1,0:T(8,128)(2,1)S(1)}, u32[]{:S(2)}, u32[]{:S(2)}) collective-permute-start(bf16[3072,128]{1,0:T(8,128)(2,1)S(1)} %get-tuple-element.87), channel_id=1, source_target_pairs={{0,4},{4,0},{8,12},{12,8},{1,5},{5,1},{9,13},{13,9},{2,6},{6,2},{1... | collective-permute-start | bytes 2359304 | tf_op jit(solution)/shard_map/ppermute | solution.py:27
  48.0 1.5 collective-permute-start.26
  50.0 3.0 %collective-permute-start.20 = (bf16[3072,128]{1,0:T(8,128)(2,1)S(1)}, bf16[3072,128]{1,0:T(8,128)(2,1)S(1)}, u32[]{:S(2)}, u32[]{:S(2)}) collective-permute-start(bf16[3072,128]{1,0:T(8,128)(2,1)S(1)} %get-tuple-element.80), channel_id=1, source_target_pairs={{0,12},{4,8},{8,4},{12,0},{1,13},{5,9},{9,5},{13,1},{2,14},{6,10},... | collective-permute-start | bytes 2359304 | tf_op jit(solution)/shard_map/ppermute | solution.py:27
  53.1 3.4 %shard_map.115 = (bf16[128,2176]{1,0:T(8,128)(2,1)S(1)}, bf16[256,2176]{1,0:T(8,128)(2,1)S(1)}, bf16[128,2176]{1,0:T(8,128)(2,1)S(1)}) custom-call(bf16[256,768]{1,0:T(8,128)(2,1)S(1)} %get-tuple-element.54.gda.refs_2_, bf16[256,768]{1,0:T(8,128)(2,1)S(1)} %get-tuple-element.60.gdb.refs_3_, bf16[256,768]{1,0:T(8,128)(2,1)S(1)} %get-tuple-element.61.uda.refs_4_, ...), custom_call_target="tpu_custom_call" | custom-call | flops 3221225472 | bytes 1048576 | tf_op jit(solution)/shard_map/pallas_call | solution.py:61
  58.3 1.8 %shard_map.117 = (bf16[3072,128]{1,0:T(8,128)(2,1)S(1)}, bf16[3072,128]{1,0:T(8,128)(2,1)S(1)}, bf16[3072,128]{1,0:T(8,128)(2,1)S(1)}, bf16[3072,128]{1,0:T(8,128)(2,1)S(1)}) custom-call(bf16[2048,256]{1,0:T(8,128)(2,1)S(1)} %get-tuple-element.72.refs_0_, bf16[2048,256]{1,0:T(8,128)(2,1)S(1)} %get-tuple-element.73.refs_1_, ...), custom_call_target="tpu_custom_call" | custom-call | flops 1610612736 | bytes 1048576 | tf_op jit(solution)/shard_map/pallas_call | solution.py:61
  60.1 13.6 %collective-permute-done.32 = bf16[1536,128]{1,0:T(8,128)(2,1)S(1)} collective-permute-done((bf16[1536,128]{1,0:T(8,128)(2,1)S(1)}, bf16[1536,128]{1,0:T(8,128)(2,1)S(1)}, u32[]{:S(2)}, u32[]{:S(2)}) %collective-permute-start.32) | collective-permute-done | bytes 393248 | tf_op jit(solution)/shard_map/ppermute | solution.py:27
  73.7 3.6 %collective-permute-start.15 = (bf16[3072,128]{1,0:T(8,128)(2,1)S(1)}, bf16[3072,128]{1,0:T(8,128)(2,1)S(1)}, u32[]{:S(2)}, u32[]{:S(2)}) collective-permute-start(bf16[3072,128]{1,0:T(8,128)(2,1)S(1)} %shard_map.120), channel_id=1, source_target_pairs={{0,16},{16,0},{1,17},{17,1},{2,18},{18,2},{3,19},{19,3},{4,20},{20... | collective-permute-start | bytes 2359304 | tf_op jit(solution)/shard_map/ppermute | solution.py:27
  77.4 2.8 %collective-permute-start.13 = (bf16[3072,128]{1,0:T(8,128)(2,1)S(1)}, bf16[3072,128]{1,0:T(8,128)(2,1)S(1)}, u32[]{:S(2)}, u32[]{:S(2)}) collective-permute-start(bf16[3072,128]{1,0:T(8,128)(2,1)S(1)} %get-tuple-element.75), channel_id=1, source_target_pairs={{0,96},{32,64},{64,32},{96,0},{1,97},{33,65},{65,33},{97,1},{2,98}... | collective-permute-start | bytes 2359304 | tf_op jit(solution)/shard_map/ppermute | solution.py:27
  80.5 3.1 %collective-permute-start.33 = (bf16[2304,128]{1,0:T(8,128)(2,1)S(1)}, bf16[2304,128]{1,0:T(8,128)(2,1)S(1)}, u32[]{:S(2)}, u32[]{:S(2)}) collective-permute-start(bf16[2304,128]{1,0:T(8,128)(2,1)S(1)} %pad_maximum_fusion.1), channel_id=1, source_target_pairs={{0,12},{4,8},{8,4},{12,0},{1,13},{5,9},{9,5},{13,1},{2,14},{6,10},... | collective-permute-start | bytes 1769480 | tf_op jit(solution)/shard_map/ppermute | solution.py:27
  84.5 10.2 %collective-permute-done.15 = bf16[3072,128]{1,0:T(8,128)(2,1)S(1)} collective-permute-done((bf16[3072,128]{1,0:T(8,128)(2,1)S(1)}, bf16[3072,128]{1,0:T(8,128)(2,1)S(1)}, u32[]{:S(2)}, u32[]{:S(2)}) %collective-permute-start.15) | collective-permute-done | bytes 786464 | tf_op jit(solution)/shard_map/ppermute | solution.py:27
  94.6 1.6 collective-permute-start.21
  96.3 2.7 %collective-permute-done.13 = bf16[3072,128]{1,0:T(8,128)(2,1)S(1)} collective-permute-done((bf16[3072,128]{1,0:T(8,128)(2,1)S(1)}, bf16[3072,128]{1,0:T(8,128)(2,1)S(1)}, u32[]{:S(2)}, u32[]{:S(2)}) %collective-permute-start.13) | collective-permute-done | bytes 786464 | tf_op jit(solution)/shard_map/ppermute | solution.py:27
  99.1 3.0 %collective-permute-start.22 = (bf16[768,128]{1,0:T(8,128)(2,1)S(1)}, bf16[768,128]{1,0:T(8,128)(2,1)S(1)}, u32[]{:S(2)}, u32[]{:S(2)}) collective-permute-start(bf16[768,128]{1,0:T(8,128)(2,1)S(1)} %add_convert_fusion.9), channel_id=1, source_target_pairs={{0,12},{4,8},{8,4},{12,0},{1,13},{5,9},{9,5},{13,1},{2,14},{6,10},... | collective-permute-start | bytes 589832 | tf_op jit(solution)/shard_map/ppermute | solution.py:27
  102.2 3.7 %collective-permute-done.22 = bf16[768,128]{1,0:T(8,128)(2,1)S(1)} collective-permute-done((bf16[768,128]{1,0:T(8,128)(2,1)S(1)}, bf16[768,128]{1,0:T(8,128)(2,1)S(1)}, u32[]{:S(2)}, u32[]{:S(2)}) %collective-permute-start.22) | collective-permute-done | bytes 196640 | tf_op jit(solution)/shard_map/ppermute | solution.py:27
  105.9 2.8 %collective-permute-start.16 = (bf16[768,128]{1,0:T(8,128)(2,1)S(1)}, bf16[768,128]{1,0:T(8,128)(2,1)S(1)}, u32[]{:S(2)}, u32[]{:S(2)}) collective-permute-start(bf16[768,128]{1,0:T(8,128)(2,1)S(1)} %add_convert_fusion.11), channel_id=1, source_target_pairs={{0,96},{32,64},{64,32},{96,0},{1,97},{33,65},{65,33},{97,1},{2,98}... | collective-permute-start | bytes 589832 | tf_op jit(solution)/shard_map/ppermute | solution.py:27
  108.7 5.6 %collective-permute-done.16 = bf16[768,128]{1,0:T(8,128)(2,1)S(1)} collective-permute-done((bf16[768,128]{1,0:T(8,128)(2,1)S(1)}, bf16[768,128]{1,0:T(8,128)(2,1)S(1)}, u32[]{:S(2)}, u32[]{:S(2)}) %collective-permute-start.16) | collective-permute-done | bytes 196640 | tf_op jit(solution)/shard_map/ppermute | solution.py:27
  114.3 1.6 collective-permute-start.23
  115.9 3.0 %collective-permute-done.23 = bf16[384,128]{1,0:T(8,128)(2,1)S(1)} collective-permute-done((bf16[384,128]{1,0:T(8,128)(2,1)S(1)}, bf16[384,128]{1,0:T(8,128)(2,1)S(1)}, u32[]{:S(2)}, u32[]{:S(2)}) %collective-permute-start.23) | collective-permute-done | bytes 98336 | tf_op jit(solution)/shard_map/ppermute | solution.py:27
  119.2 5.4 %collective-permute-done.17 = bf16[384,128]{1,0:T(8,128)(2,1)S(1)} collective-permute-done((bf16[384,128]{1,0:T(8,128)(2,1)S(1)}, bf16[384,128]{1,0:T(8,128)(2,1)S(1)}, u32[]{:S(2)}, u32[]{:S(2)}) %collective-permute-start.17) | collective-permute-done | bytes 98336 | tf_op jit(solution)/shard_map/ppermute | solution.py:27
  125.4 2.5 %collective-permute-start.24 = (bf16[960,128]{1,0:T(8,128)(2,1)S(1)}, bf16[960,128]{1,0:T(8,128)(2,1)S(1)}, u32[]{:S(2)}, u32[]{:S(2)}) collective-permute-start(bf16[960,128]{1,0:T(8,128)(2,1)S(1)} %pad_maximum_fusion.5), channel_id=1, source_target_pairs={{0,96},{32,64},{64,32},{96,0},{1,97},{33,65},{65,33},{97,1},{2,98}... | collective-permute-start | bytes 737288 | tf_op jit(solution)/shard_map/ppermute | solution.py:27
  128.0 4.4 %collective-permute-done.14 = bf16[1536,128]{1,0:T(8,128)(2,1)S(1)} collective-permute-done((bf16[1536,128]{1,0:T(8,128)(2,1)S(1)}, bf16[1536,128]{1,0:T(8,128)(2,1)S(1)}, u32[]{:S(2)}, u32[]{:S(2)}) %collective-permute-start.14) | collective-permute-done | bytes 393248 | tf_op jit(solution)/shard_map/ppermute | solution.py:27
  132.5 5.0 %collective-permute-start.18 = (bf16[960,128]{1,0:T(8,128)(2,1)S(1)}, bf16[960,128]{1,0:T(8,128)(2,1)S(1)}, u32[]{:S(2)}, u32[]{:S(2)}) collective-permute-start(bf16[960,128]{1,0:T(8,128)(2,1)S(1)} %pad_maximum_fusion.4), channel_id=1, source_target_pairs={{0,12},{4,8},{8,4},{12,0},{1,13},{5,9},{9,5},{13,1},{2,14},{6,10},... | collective-permute-start | bytes 737288 | tf_op jit(solution)/shard_map/ppermute | solution.py:27
  138.4 1.8 %collective-permute-start.25 = (bf16[480,128]{1,0:T(8,128)(2,1)S(1)}, bf16[480,128]{1,0:T(8,128)(2,1)S(1)}, u32[]{:S(2)}, u32[]{:S(2)}) collective-permute-start(bf16[480,128]{1,0:T(8,128)(2,1)S(1)} %pad_maximum_fusion.10), channel_id=1, source_target_pairs={{0,32},{32,0},{64,96},{96,64},{1,33},{33,1},{65,97},{97,65},{2,34}... | collective-permute-start | bytes 368648 | tf_op jit(solution)/shard_map/ppermute | solution.py:27
  140.2 1.4 collective-permute-done.18
  142.4 3.4 %collective-permute-done.25 = bf16[480,128]{1,0:T(8,128)(2,1)S(1)} collective-permute-done((bf16[480,128]{1,0:T(8,128)(2,1)S(1)}, bf16[480,128]{1,0:T(8,128)(2,1)S(1)}, u32[]{:S(2)}, u32[]{:S(2)}) %collective-permute-start.25) | collective-permute-done | bytes 122912 | tf_op jit(solution)/shard_map/ppermute | solution.py:27
  146.8 2.1 %collective-permute-start.36 = (bf16[384,128]{1,0:T(8,128)(2,1)S(1)}, bf16[384,128]{1,0:T(8,128)(2,1)S(1)}, u32[]{:S(2)}, u32[]{:S(2)}) collective-permute-start(bf16[384,128]{1,0:T(8,128)(2,1)S(1)} %pad_maximum_fusion.11), channel_id=1, source_target_pairs={{0,16},{16,0},{1,17},{17,1},{2,18},{18,2},{3,19},{19,3},{4,20},{20... | collective-permute-start | bytes 294920 | tf_op jit(solution)/shard_map/ppermute | solution.py:27
  149.0 2.8 %collective-permute-start.35 = (bf16[576,128]{1,0:T(8,128)(2,1)S(1)}, bf16[576,128]{1,0:T(8,128)(2,1)S(1)}, u32[]{:S(2)}, u32[]{:S(2)}) collective-permute-start(bf16[576,128]{1,0:T(8,128)(2,1)S(1)} %pad_maximum_fusion.7), channel_id=1, source_target_pairs={{0,96},{32,64},{64,32},{96,0},{1,97},{33,65},{65,33},{97,1},{2,98}... | collective-permute-start | bytes 442376 | tf_op jit(solution)/shard_map/ppermute | solution.py:27
  152.0 3.3 %collective-permute-start.30 = (bf16[576,128]{1,0:T(8,128)(2,1)S(1)}, bf16[576,128]{1,0:T(8,128)(2,1)S(1)}, u32[]{:S(2)}, u32[]{:S(2)}) collective-permute-start(bf16[576,128]{1,0:T(8,128)(2,1)S(1)} %pad_maximum_fusion.6), channel_id=1, source_target_pairs={{0,12},{4,8},{8,4},{12,0},{1,13},{5,9},{9,5},{13,1},{2,14},{6,10},... | collective-permute-start | bytes 442376 | tf_op jit(solution)/shard_map/ppermute | solution.py:27
  155.6 2.9 %collective-permute-done.30 = bf16[576,128]{1,0:T(8,128)(2,1)S(1)} collective-permute-done((bf16[576,128]{1,0:T(8,128)(2,1)S(1)}, bf16[576,128]{1,0:T(8,128)(2,1)S(1)}, u32[]{:S(2)}, u32[]{:S(2)}) %collective-permute-start.30) | collective-permute-done | bytes 147488 | tf_op jit(solution)/shard_map/ppermute | solution.py:27
  158.6 1.6 collective-permute-start.37
  160.2 1.2 shard_map.116
  161.4 3.9 %collective-permute-done.37.refs_9_ = bf16[576,128]{1,0:T(8,128)(2,1)S(1)} collective-permute-done((bf16[576,128]{1,0:T(8,128)(2,1)S(1)}, bf16[576,128]{1,0:T(8,128)(2,1)S(1)}, u32[]{:S(2)}, u32[]{:S(2)}) %collective-permute-start.37) | collective-permute-done | bytes 147488 | tf_op jit(solution)/shard_map/ppermute | solution.py:27
  (112 shorter events, 13.6 us)
Async XLA Ops:
  0.6 30.3 %copy-start.6 = (bf16[128,2048]{1,0:T(8,128)(2,1)S(1)}, bf16[128,2048]{1,0:T(8,128)(2,1)}, u32[]{:S(2)}) copy-start(bf16[128,2048]{1,0:T(8,128)(2,1)} %x0.1) | copy-start | bytes 1572868
  0.6 14.2 %collective-permute-start.9 = (bf16[128,2048]{1,0:T(8,128)(2,1)}, bf16[128,2048]{1,0:T(8,128)(2,1)S(1)}, u32[]{:S(2)}, u32[]{:S(2)}) collective-permute-start(bf16[128,2048]{1,0:T(8,128)(2,1)} %x0.1), channel_id=1, source_target_pairs={{0,2},{2,0},{1,3},{3,1},{4,6},{6,4},{5,7},{7,5},{8,10},{10,8},{9,1... | collective-permute-start | bytes 1572872 | tf_op jit(solution)/shard_map/ppermute | solution.py:27
  2.7 27.7 %collective-permute-start.2 = (bf16[128,2048]{1,0:T(8,128)(2,1)}, bf16[128,2048]{1,0:T(8,128)(2,1)S(1)}, u32[]{:S(2)}, u32[]{:S(2)}) collective-permute-start(bf16[128,2048]{1,0:T(8,128)(2,1)} %x0.1), channel_id=1, source_target_pairs={{0,1},{1,0},{2,3},{3,2},{4,5},{5,4},{6,7},{7,6},{8,9},{9,8},{10,11... | collective-permute-start | bytes 1572872 | tf_op jit(solution)/shard_map/ppermute | solution.py:27
  2.8 0.7 copy-start.7
  3.4 0.7 copy-start.9
  4.1 13.6 %collective-permute-start.1 = (f32[8,128]{1,0:T(8,128)S(1)}, f32[8,128]{1,0:T(8,128)S(1)}, u32[]{:S(2)}, u32[]{:S(2)}) collective-permute-start(f32[8,128]{1,0:T(8,128)S(1)} %get-tuple-element.50), channel_id=1, source_target_pairs={{0,1},{1,0},{2,3},{3,2},{4,5},{5,4},{6,7},{7,6},{8,9},{9,8},{10,11... | collective-permute-start | bytes 12296 | tf_op jit(solution)/shard_map/ppermute | solution.py:27
  4.7 32.0 %collective-permute-start = (bf16[128,2048]{1,0:T(8,128)(2,1)}, bf16[128,2048]{1,0:T(8,128)(2,1)S(1)}, u32[]{:S(2)}, u32[]{:S(2)}) collective-permute-start(bf16[128,2048]{1,0:T(8,128)(2,1)} %refs_2_.7), channel_id=1, source_target_pairs={{0,1},{1,0},{2,3},{3,2},{4,5},{5,4},{6,7},{7,6},{8,9},{9,8},{10,11... | collective-permute-start | bytes 1572872 | tf_op jit(solution)/shard_map/ppermute | solution.py:27
  14.9 24.9 %collective-permute-start.10 = (bf16[128,2048]{1,0:T(8,128)(2,1)S(1)}, bf16[128,2048]{1,0:T(8,128)(2,1)S(1)}, u32[]{:S(2)}, u32[]{:S(2)}) collective-permute-start(bf16[128,2048]{1,0:T(8,128)(2,1)S(1)} %collective-permute-done.9.x0), channel_id=1, source_target_pairs={{0,1},{1,0},{2,3},{3,2},{4,5},{5,4},{6,7},{7,6},{8,9},{9,8},{10,11... | collective-permute-start | bytes 1572872 | tf_op jit(solution)/shard_map/ppermute | solution.py:27
  16.0 9.3 %collective-permute-start.3 = (bf16[128,1024]{1,0:T(8,128)(2,1)S(1)}, bf16[128,1024]{1,0:T(8,128)(2,1)S(1)}, u32[]{:S(2)}, u32[]{:S(2)}) collective-permute-start(bf16[128,1024]{1,0:T(8,128)(2,1)S(1)} %get-tuple-element.108), channel_id=1, source_target_pairs={{0,2},{2,0},{1,3},{3,1},{4,6},{6,4},{5,7},{7,5},{8,10},{10,8},{9,1... | collective-permute-start | bytes 786440 | tf_op jit(solution)/shard_map/ppermute | solution.py:27
  17.8 12.6 %collective-permute-start.4 = (bf16[128,1024]{1,0:T(8,128)(2,1)S(1)}, bf16[128,1024]{1,0:T(8,128)(2,1)S(1)}, u32[]{:S(2)}, u32[]{:S(2)}) collective-permute-start(bf16[128,1024]{1,0:T(8,128)(2,1)S(1)} %get-tuple-element.107), channel_id=1, source_target_pairs={{0,2},{2,0},{1,3},{3,1},{4,6},{6,4},{5,7},{7,5},{8,10},{10,8},{9,1... | collective-permute-start | bytes 786440 | tf_op jit(solution)/shard_map/ppermute | solution.py:27
  25.2 14.1 %collective-permute-start.7 = (f32[8,128]{1,0:T(8,128)S(1)}, f32[8,128]{1,0:T(8,128)S(1)}, u32[]{:S(2)}, u32[]{:S(2)}) collective-permute-start(f32[8,128]{1,0:T(8,128)S(1)} %get-tuple-element.55), channel_id=1, source_target_pairs={{0,2},{1,3},{2,0},{3,1},{4,6},{5,7},{6,4},{7,5},{8,10},{9,11},{10,... | collective-permute-start | bytes 12296 | tf_op jit(solution)/shard_map/ppermute | solution.py:27
  30.4 11.6 %collective-permute-start.5 = (bf16[128,1024]{1,0:T(8,128)(2,1)S(1)}, bf16[128,1024]{1,0:T(8,128)(2,1)S(1)}, u32[]{:S(2)}, u32[]{:S(2)}) collective-permute-start(bf16[128,1024]{1,0:T(8,128)(2,1)S(1)} %collective-permute-done.3.refs_0_.refs_4_), channel_id=1, source_target_pairs={{0,1},{1,0},{2,3},{3,2},{4,5},{5,4},{6,7},{7,6},{8,9},{9,8},{10,11... | collective-permute-start | bytes 786440 | tf_op jit(solution)/shard_map/ppermute | solution.py:27
  30.4 11.6 %collective-permute-start.6 = (bf16[128,1024]{1,0:T(8,128)(2,1)S(1)}, bf16[128,1024]{1,0:T(8,128)(2,1)S(1)}, u32[]{:S(2)}, u32[]{:S(2)}) collective-permute-start(bf16[128,1024]{1,0:T(8,128)(2,1)S(1)} %collective-permute-done.4.refs_1_.refs_4_), channel_id=1, source_target_pairs={{0,1},{1,0},{2,3},{3,2},{4,5},{5,4},{6,7},{7,6},{8,9},{9,8},{10,11... | collective-permute-start | bytes 786440 | tf_op jit(solution)/shard_map/ppermute | solution.py:27
  30.9 1.9 %copy-start.2 = (bf16[1,2048,768]{2,1,0:T(8,128)(2,1)S(1)}, bf16[1,2048,768]{2,1,0:T(8,128)(2,1)}, u32[]{:S(2)}) copy-start(bf16[1,2048,768]{2,1,0:T(8,128)(2,1)} %param.11) | copy-start | bytes 9437188
  32.8 1.9 %copy-start.4 = (bf16[1,2048,768]{2,1,0:T(8,128)(2,1)S(1)}, bf16[1,2048,768]{2,1,0:T(8,128)(2,1)}, u32[]{:S(2)}) copy-start(bf16[1,2048,768]{2,1,0:T(8,128)(2,1)} %param.12) | copy-start | bytes 9437188
  34.7 3.4 %copy-start = (bf16[128,2048]{1,0:T(8,128)(2,1)S(1)}, bf16[128,2048]{1,0:T(8,128)(2,1)}, u32[]{:S(2)}) copy-start(bf16[128,2048]{1,0:T(8,128)(2,1)} %refs_2_.7) | copy-start | bytes 1572868
  34.7 3.4 %copy-start.1 = (bf16[1,768,2048]{2,1,0:T(8,128)(2,1)S(1)}, bf16[1,768,2048]{2,1,0:T(8,128)(2,1)}, u32[]{:S(2)}) copy-start(bf16[1,768,2048]{2,1,0:T(8,128)(2,1)} %param.13) | copy-start | bytes 9437188
  34.7 5.1 %copy-start.5 = (bf16[1,2048,768]{2,1,0:T(8,128)(2,1)S(1)}, bf16[1,2048,768]{2,1,0:T(8,128)(2,1)}, u32[]{:S(2)}) copy-start(bf16[1,2048,768]{2,1,0:T(8,128)(2,1)} %param.12) | copy-start | bytes 9437188
  36.7 3.1 %collective-permute-start.8 = (f32[8,128]{1,0:T(8,128)S(1)}, f32[8,128]{1,0:T(8,128)S(1)}, u32[]{:S(2)}, u32[]{:S(2)}) collective-permute-start(f32[8,128]{1,0:T(8,128)S(1)} %get-tuple-element.56), channel_id=1, source_target_pairs={{0,3},{1,2},{2,1},{3,0},{4,7},{5,6},{6,5},{7,4},{8,11},{9,10},{10,... | collective-permute-start | bytes 12296 | tf_op jit(solution)/shard_map/ppermute | solution.py:27
  38.2 1.9 %copy-start.3 = (bf16[1,2048,768]{2,1,0:T(8,128)(2,1)S(1)}, bf16[1,2048,768]{2,1,0:T(8,128)(2,1)}, u32[]{:S(2)}) copy-start(bf16[1,2048,768]{2,1,0:T(8,128)(2,1)} %param.11) | copy-start | bytes 9437188
  45.2 35.0 %collective-permute-start.31 = (bf16[3072,128]{1,0:T(8,128)(2,1)S(1)}, bf16[3072,128]{1,0:T(8,128)(2,1)S(1)}, u32[]{:S(2)}, u32[]{:S(2)}) collective-permute-start(bf16[3072,128]{1,0:T(8,128)(2,1)S(1)} %get-tuple-element.87), channel_id=1, source_target_pairs={{0,4},{4,0},{8,12},{12,8},{1,5},{5,1},{9,13},{13,9},{2,6},{6,2},{1... | collective-permute-start | bytes 2359304 | tf_op jit(solution)/shard_map/ppermute | solution.py:27
  47.5 26.2 %collective-permute-start.32 = (bf16[1536,128]{1,0:T(8,128)(2,1)S(1)}, bf16[1536,128]{1,0:T(8,128)(2,1)S(1)}, u32[]{:S(2)}, u32[]{:S(2)}) collective-permute-start(bf16[1536,128]{1,0:T(8,128)(2,1)S(1)} %get-tuple-element.89), channel_id=1, source_target_pairs={{0,4},{4,0},{8,12},{12,8},{1,5},{5,1},{9,13},{13,9},{2,6},{6,2},{1... | collective-permute-start | bytes 1179656 | tf_op jit(solution)/shard_map/ppermute | solution.py:27
  48.0 32.5 %collective-permute-start.26 = (bf16[3072,128]{1,0:T(8,128)(2,1)S(1)}, bf16[3072,128]{1,0:T(8,128)(2,1)S(1)}, u32[]{:S(2)}, u32[]{:S(2)}) collective-permute-start(bf16[3072,128]{1,0:T(8,128)(2,1)S(1)} %get-tuple-element.83), channel_id=1, source_target_pairs={{0,32},{32,0},{64,96},{96,64},{1,33},{33,1},{65,97},{97,65},{2,34}... | collective-permute-start | bytes 2359304 | tf_op jit(solution)/shard_map/ppermute | solution.py:27
  49.5 27.8 %collective-permute-start.27 = (bf16[1536,128]{1,0:T(8,128)(2,1)S(1)}, bf16[1536,128]{1,0:T(8,128)(2,1)S(1)}, u32[]{:S(2)}, u32[]{:S(2)}) collective-permute-start(bf16[1536,128]{1,0:T(8,128)(2,1)S(1)} %get-tuple-element.85), channel_id=1, source_target_pairs={{0,32},{32,0},{64,96},{96,64},{1,33},{33,1},{65,97},{97,65},{2,34}... | collective-permute-start | bytes 1179656 | tf_op jit(solution)/shard_map/ppermute | solution.py:27
  50.0 33.7 %collective-permute-start.20 = (bf16[3072,128]{1,0:T(8,128)(2,1)S(1)}, bf16[3072,128]{1,0:T(8,128)(2,1)S(1)}, u32[]{:S(2)}, u32[]{:S(2)}) collective-permute-start(bf16[3072,128]{1,0:T(8,128)(2,1)S(1)} %get-tuple-element.80), channel_id=1, source_target_pairs={{0,12},{4,8},{8,4},{12,0},{1,13},{5,9},{9,5},{13,1},{2,14},{6,10},... | collective-permute-start | bytes 2359304 | tf_op jit(solution)/shard_map/ppermute | solution.py:27
  73.7 20.9 %collective-permute-start.15 = (bf16[3072,128]{1,0:T(8,128)(2,1)S(1)}, bf16[3072,128]{1,0:T(8,128)(2,1)S(1)}, u32[]{:S(2)}, u32[]{:S(2)}) collective-permute-start(bf16[3072,128]{1,0:T(8,128)(2,1)S(1)} %shard_map.120), channel_id=1, source_target_pairs={{0,16},{16,0},{1,17},{17,1},{2,18},{18,2},{3,19},{19,3},{4,20},{20... | collective-permute-start | bytes 2359304 | tf_op jit(solution)/shard_map/ppermute | solution.py:27
  77.4 21.7 %collective-permute-start.13 = (bf16[3072,128]{1,0:T(8,128)(2,1)S(1)}, bf16[3072,128]{1,0:T(8,128)(2,1)S(1)}, u32[]{:S(2)}, u32[]{:S(2)}) collective-permute-start(bf16[3072,128]{1,0:T(8,128)(2,1)S(1)} %get-tuple-element.75), channel_id=1, source_target_pairs={{0,96},{32,64},{64,32},{96,0},{1,97},{33,65},{65,33},{97,1},{2,98}... | collective-permute-start | bytes 2359304 | tf_op jit(solution)/shard_map/ppermute | solution.py:27
  80.3 44.7 %collective-permute-start.11 = (bf16[256,2176]{1,0:T(8,128)(2,1)S(1)}, bf16[256,2176]{1,0:T(8,128)(2,1)S(1)}, u32[]{:S(2)}, u32[]{:S(2)}) collective-permute-start(bf16[256,2176]{1,0:T(8,128)(2,1)S(1)} %get-tuple-element.68), channel_id=1, source_target_pairs={{0,1},{1,0},{2,3},{3,2},{4,5},{5,4},{6,7},{7,6},{8,9},{9,8},{10,11... | collective-permute-start | bytes 3342344 | tf_op jit(solution)/shard_map/ppermute | solution.py:27
  80.5 56.9 %collective-permute-start.33 = (bf16[2304,128]{1,0:T(8,128)(2,1)S(1)}, bf16[2304,128]{1,0:T(8,128)(2,1)S(1)}, u32[]{:S(2)}, u32[]{:S(2)}) collective-permute-start(bf16[2304,128]{1,0:T(8,128)(2,1)S(1)} %pad_maximum_fusion.1), channel_id=1, source_target_pairs={{0,12},{4,8},{8,4},{12,0},{1,13},{5,9},{9,5},{13,1},{2,14},{6,10},... | collective-permute-start | bytes 1769480 | tf_op jit(solution)/shard_map/ppermute | solution.py:27
  83.8 54.2 %collective-permute-start.28 = (bf16[2304,128]{1,0:T(8,128)(2,1)S(1)}, bf16[2304,128]{1,0:T(8,128)(2,1)S(1)}, u32[]{:S(2)}, u32[]{:S(2)}) collective-permute-start(bf16[2304,128]{1,0:T(8,128)(2,1)S(1)} %pad_maximum_fusion), channel_id=1, source_target_pairs={{0,96},{32,64},{64,32},{96,0},{1,97},{33,65},{65,33},{97,1},{2,98}... | collective-permute-start | bytes 1769480 | tf_op jit(solution)/shard_map/ppermute | solution.py:27
  94.6 30.7 %collective-permute-start.21 = (bf16[1536,128]{1,0:T(8,128)(2,1)S(1)}, bf16[1536,128]{1,0:T(8,128)(2,1)S(1)}, u32[]{:S(2)}, u32[]{:S(2)}) collective-permute-start(bf16[1536,128]{1,0:T(8,128)(2,1)S(1)} %add_convert_fusion.3), channel_id=1, source_target_pairs={{0,4},{4,0},{8,12},{12,8},{1,5},{5,1},{9,13},{13,9},{2,6},{6,2},{1... | collective-permute-start | bytes 1179656 | tf_op jit(solution)/shard_map/ppermute | solution.py:27
  99.1 6.9 %collective-permute-start.22 = (bf16[768,128]{1,0:T(8,128)(2,1)S(1)}, bf16[768,128]{1,0:T(8,128)(2,1)S(1)}, u32[]{:S(2)}, u32[]{:S(2)}) collective-permute-start(bf16[768,128]{1,0:T(8,128)(2,1)S(1)} %add_convert_fusion.9), channel_id=1, source_target_pairs={{0,12},{4,8},{8,4},{12,0},{1,13},{5,9},{9,5},{13,1},{2,14},{6,10},... | collective-permute-start | bytes 589832 | tf_op jit(solution)/shard_map/ppermute | solution.py:27
  105.9 8.4 %collective-permute-start.16 = (bf16[768,128]{1,0:T(8,128)(2,1)S(1)}, bf16[768,128]{1,0:T(8,128)(2,1)S(1)}, u32[]{:S(2)}, u32[]{:S(2)}) collective-permute-start(bf16[768,128]{1,0:T(8,128)(2,1)S(1)} %add_convert_fusion.11), channel_id=1, source_target_pairs={{0,96},{32,64},{64,32},{96,0},{1,97},{33,65},{65,33},{97,1},{2,98}... | collective-permute-start | bytes 589832 | tf_op jit(solution)/shard_map/ppermute | solution.py:27
  114.3 4.6 %collective-permute-start.23 = (bf16[384,128]{1,0:T(8,128)(2,1)S(1)}, bf16[384,128]{1,0:T(8,128)(2,1)S(1)}, u32[]{:S(2)}, u32[]{:S(2)}) collective-permute-start(bf16[384,128]{1,0:T(8,128)(2,1)S(1)} %add_convert_fusion.18), channel_id=1, source_target_pairs={{0,4},{4,0},{8,12},{12,8},{1,5},{5,1},{9,13},{13,9},{2,6},{6,2},{1... | collective-permute-start | bytes 294920 | tf_op jit(solution)/shard_map/ppermute | solution.py:27
  118.9 5.7 %collective-permute-start.17 = (bf16[384,128]{1,0:T(8,128)(2,1)S(1)}, bf16[384,128]{1,0:T(8,128)(2,1)S(1)}, u32[]{:S(2)}, u32[]{:S(2)}) collective-permute-start(bf16[384,128]{1,0:T(8,128)(2,1)S(1)} %add_convert_fusion.20), channel_id=1, source_target_pairs={{0,32},{32,0},{64,96},{96,64},{1,33},{33,1},{65,97},{97,65},{2,34}... | collective-permute-start | bytes 294920 | tf_op jit(solution)/shard_map/ppermute | solution.py:27
  124.6 7.8 %collective-permute-start.14 = (bf16[1536,128]{1,0:T(8,128)(2,1)S(1)}, bf16[1536,128]{1,0:T(8,128)(2,1)S(1)}, u32[]{:S(2)}, u32[]{:S(2)}) collective-permute-start(bf16[1536,128]{1,0:T(8,128)(2,1)S(1)} %add_convert_fusion.4), channel_id=1, source_target_pairs={{0,32},{32,0},{64,96},{96,64},{1,33},{33,1},{65,97},{97,65},{2,34}... | collective-permute-start | bytes 1179656 | tf_op jit(solution)/shard_map/ppermute | solution.py:27
  125.1 35.2 %collective-permute-start.12 = (bf16[128,2176]{1,0:T(8,128)(2,1)S(1)}, bf16[128,2176]{1,0:T(8,128)(2,1)S(1)}, u32[]{:S(2)}, u32[]{:S(2)}) collective-permute-start(bf16[128,2176]{1,0:T(8,128)(2,1)S(1)} %add_convert_fusion), channel_id=1, source_target_pairs={{0,2},{2,0},{1,3},{3,1},{4,6},{6,4},{5,7},{7,5},{8,10},{10,8},{9,1... | collective-permute-start | bytes 1671176 | tf_op jit(solution)/shard_map/ppermute | solution.py:27
  125.4 12.8 %collective-permute-start.24 = (bf16[960,128]{1,0:T(8,128)(2,1)S(1)}, bf16[960,128]{1,0:T(8,128)(2,1)S(1)}, u32[]{:S(2)}, u32[]{:S(2)}) collective-permute-start(bf16[960,128]{1,0:T(8,128)(2,1)S(1)} %pad_maximum_fusion.5), channel_id=1, source_target_pairs={{0,96},{32,64},{64,32},{96,0},{1,97},{33,65},{65,33},{97,1},{2,98}... | collective-permute-start | bytes 737288 | tf_op jit(solution)/shard_map/ppermute | solution.py:27
  132.5 9.1 %collective-permute-start.18 = (bf16[960,128]{1,0:T(8,128)(2,1)S(1)}, bf16[960,128]{1,0:T(8,128)(2,1)S(1)}, u32[]{:S(2)}, u32[]{:S(2)}) collective-permute-start(bf16[960,128]{1,0:T(8,128)(2,1)S(1)} %pad_maximum_fusion.4), channel_id=1, source_target_pairs={{0,12},{4,8},{8,4},{12,0},{1,13},{5,9},{9,5},{13,1},{2,14},{6,10},... | collective-permute-start | bytes 737288 | tf_op jit(solution)/shard_map/ppermute | solution.py:27
  137.6 11.3 %collective-permute-start.34 = (bf16[1152,128]{1,0:T(8,128)(2,1)S(1)}, bf16[1152,128]{1,0:T(8,128)(2,1)S(1)}, u32[]{:S(2)}, u32[]{:S(2)}) collective-permute-start(bf16[1152,128]{1,0:T(8,128)(2,1)S(1)} %pad_maximum_fusion.3), channel_id=1, source_target_pairs={{0,32},{32,0},{64,96},{96,64},{1,33},{33,1},{65,97},{97,65},{2,34}... | collective-permute-start | bytes 884744 | tf_op jit(solution)/shard_map/ppermute | solution.py:27
  138.2 13.7 %collective-permute-start.29 = (bf16[1152,128]{1,0:T(8,128)(2,1)S(1)}, bf16[1152,128]{1,0:T(8,128)(2,1)S(1)}, u32[]{:S(2)}, u32[]{:S(2)}) collective-permute-start(bf16[1152,128]{1,0:T(8,128)(2,1)S(1)} %pad_maximum_fusion.2), channel_id=1, source_target_pairs={{0,4},{4,0},{8,12},{12,8},{1,5},{5,1},{9,13},{13,9},{2,6},{6,2},{1... | collective-permute-start | bytes 884744 | tf_op jit(solution)/shard_map/ppermute | solution.py:27
  138.4 7.4 %collective-permute-start.25 = (bf16[480,128]{1,0:T(8,128)(2,1)S(1)}, bf16[480,128]{1,0:T(8,128)(2,1)S(1)}, u32[]{:S(2)}, u32[]{:S(2)}) collective-permute-start(bf16[480,128]{1,0:T(8,128)(2,1)S(1)} %pad_maximum_fusion.10), channel_id=1, source_target_pairs={{0,32},{32,0},{64,96},{96,64},{1,33},{33,1},{65,97},{97,65},{2,34}... | collective-permute-start | bytes 368648 | tf_op jit(solution)/shard_map/ppermute | solution.py:27
  141.7 5.0 %collective-permute-start.19 = (bf16[480,128]{1,0:T(8,128)(2,1)S(1)}, bf16[480,128]{1,0:T(8,128)(2,1)S(1)}, u32[]{:S(2)}, u32[]{:S(2)}) collective-permute-start(bf16[480,128]{1,0:T(8,128)(2,1)S(1)} %pad_maximum_fusion.9), channel_id=1, source_target_pairs={{0,4},{4,0},{8,12},{12,8},{1,5},{5,1},{9,13},{13,9},{2,6},{6,2},{1... | collective-permute-start | bytes 368648 | tf_op jit(solution)/shard_map/ppermute | solution.py:27
  146.8 14.6 %collective-permute-start.36 = (bf16[384,128]{1,0:T(8,128)(2,1)S(1)}, bf16[384,128]{1,0:T(8,128)(2,1)S(1)}, u32[]{:S(2)}, u32[]{:S(2)}) collective-permute-start(bf16[384,128]{1,0:T(8,128)(2,1)S(1)} %pad_maximum_fusion.11), channel_id=1, source_target_pairs={{0,16},{16,0},{1,17},{17,1},{2,18},{18,2},{3,19},{19,3},{4,20},{20... | collective-permute-start | bytes 294920 | tf_op jit(solution)/shard_map/ppermute | solution.py:27
  149.0 6.4 %collective-permute-start.35 = (bf16[576,128]{1,0:T(8,128)(2,1)S(1)}, bf16[576,128]{1,0:T(8,128)(2,1)S(1)}, u32[]{:S(2)}, u32[]{:S(2)}) collective-permute-start(bf16[576,128]{1,0:T(8,128)(2,1)S(1)} %pad_maximum_fusion.7), channel_id=1, source_target_pairs={{0,96},{32,64},{64,32},{96,0},{1,97},{33,65},{65,33},{97,1},{2,98}... | collective-permute-start | bytes 442376 | tf_op jit(solution)/shard_map/ppermute | solution.py:27
  152.0 8.2 %copy-start.8 = (s32[128,2]{0,1:T(2,128)S(1)}, s32[128,2]{0,1:T(2,128)}, u32[]{:S(2)}) copy-start(s32[128,2]{0,1:T(2,128)} %param.9) | copy-start | bytes 3076
  152.0 6.4 %collective-permute-start.30 = (bf16[576,128]{1,0:T(8,128)(2,1)S(1)}, bf16[576,128]{1,0:T(8,128)(2,1)S(1)}, u32[]{:S(2)}, u32[]{:S(2)}) collective-permute-start(bf16[576,128]{1,0:T(8,128)(2,1)S(1)} %pad_maximum_fusion.6), channel_id=1, source_target_pairs={{0,12},{4,8},{8,4},{12,0},{1,13},{5,9},{9,5},{13,1},{2,14},{6,10},... | collective-permute-start | bytes 442376 | tf_op jit(solution)/shard_map/ppermute | solution.py:27
  158.6 6.7 %collective-permute-start.37 = (bf16[576,128]{1,0:T(8,128)(2,1)S(1)}, bf16[576,128]{1,0:T(8,128)(2,1)S(1)}, u32[]{:S(2)}, u32[]{:S(2)}) collective-permute-start(bf16[576,128]{1,0:T(8,128)(2,1)S(1)} %pad_maximum_fusion.8), channel_id=1, source_target_pairs={{0,16},{16,0},{1,17},{17,1},{2,18},{18,2},{3,19},{19,3},{4,20},{20... | collective-permute-start | bytes 442376 | tf_op jit(solution)/shard_map/ppermute | solution.py:27

commit v4 on v3

--- a/solution.py
+++ b/solution.py
@@ -14,7 +14,7 @@
 EVERY = ("x", "zh", "y", "zl", "c")
 XA, XB, YA, YB, Z = ("x", 1), ("x", 3), ("y", 1), ("y", 3), ("zh", 1)
 ORDERS = ((XA, XB, YA, YB, Z), (YA, YB, XA, XB, Z), (XB, XA, YB, YA, Z), (YB, YA, XB, XA, Z))
-DOWN_ORDERS = ORDERS[:2] + ((Z, XB, XA, YB, YA), (Z, YB, YA, XB, XA))
+DOWN_ORDERS = ORDERS[:2] + ((Z, XA, YB, YA, XB), (Z, YA, XB, XA, YB))
 CHAINS = (2, 3, 0, 1)
 BLOCKS = 32
 HALF = BLOCKS // 2
@@ -270,20 +270,15 @@
 
 
 def finish_body(*refs):
-    bases, (last_a, last_b), (gate, up, down) = refs[:-5], refs[-5:-3], refs[-3:]
-    recv = {0: (last_b[...].astype(F32), 0), 2: (last_a[...].astype(F32), 0)}
+    bases, (last_a, last_b, end2, end3), (gate, up, down) = refs[:8], refs[8:12], refs[12:]
     half, low = gate.shape[0] // 2, down.shape[0]
     cols = down.shape[1] // 4
-    done = []
-    for n, base in enumerate(bases):
-        rows = base.shape[0]
-        p = (EARLY + LATER)[n][0] if n < 4 else n - 4
-        if n < 4 or p < 2:
-            array, at = recv[p // 2 * 2]
-            done.append(base[...] + array[at : at + rows])
-            recv[p // 2 * 2] = (array, at + rows)
-        else:
-            done.append(base[...])
+    received = [r[...].astype(F32) for r in (last_a, last_b, end2, end3)]
+    received = jnp.concatenate(received, axis=0)
+    done, at = [], 0
+    for base in bases:
+        done.append(base[...] + received[at : at + base.shape[0]])
+        at += base.shape[0]
     for (p, first, _), total in zip(EARLY + LATER, done):
         out = gate if p < 2 else up
         for k in range(total.shape[0] // half):
@@ -360,23 +355,20 @@
             at += send.shape[0]
         return got
 
-    for p in (2, 3):
-        exchange(have[p][:1], ORDERS[p][1])
+    for p in CHAINS:
+        exchange(have[p][: 2 if p < 2 else 1], ORDERS[p][1])
     for p in (2, 3):
         exchange(downs[p : p + 1], DOWN_ORDERS[p][1])
-    for p in (0, 1):
-        exchange(have[p], ORDERS[p][1])
-    for p in (2, 3):
-        exchange(downs[p : p + 1], DOWN_ORDERS[p][2])
     for step in (2, 3):
         for p in CHAINS:
             exchange(have[p], ORDERS[p][step])
     last_a = exchange(gates[:2], Z)
     last_b = exchange(gates[2:] + downs[:2], Z)
-    bases = [summed(h[:-1], 0, 1, F32) for h in gates + downs[:2]] + [summed(h, 0, 1, F32) for h in downs[2:]]
+    ends = [exchange(downs[p : p + 1], DOWN_ORDERS[p][4]) for p in (2, 3)]
+    bases = [summed(h[:-1], 0, 1, F32) for h in gates + downs]
     gate_grad, up_grad, down_grad = kernel(
         finish_body,
-        (*bases, last_a, last_b),
+        (*bases, last_a, last_b, *ends),
         [((d // BLOCKS, ff), BF16), ((d // BLOCKS, ff), BF16), ((ff // BLOCKS, d), BF16)],
         4,
         1 << 20,

time: 166 us -> 161 us (0.970)
  starting transfers between devices: 56 us -> 51.2 us
    ppermute x38, starting transfers between devices: 56 us -> 51.2 us  [moved(): lax.ppermute(array, axis, [(i, i ^ mask) for i in range(lax.axis_size(axi...]
  transfers between devices with their start and end apart: 38 -> 38, of which waited for: 18 -> 17; matrix products, arithmetic and copies ran while one was open for 2% -> 2% of each run, Pallas kernels for 8% -> 9%
where the time goes in v4:
time: 161 us
  waiting for transfers between devices  82 us (51%)
  starting transfers between devices  51.2 us (32%)
  Pallas kernels  17.8 us (11%)
  local copies, waits for them, and re-layouts  6.48 us (4%)
  other arithmetic  2.29 us (1%)
    ppermute x38, waiting for transfers between devices, moved(): lax.ppermute(array, axis, [(i, i ^ mask) for i in range(lax.axis_size(axi...  82 us
    ppermute x38, starting transfers between devices, moved(): lax.ppermute(array, axis, [(i, i ^ mask) for i in range(lax.axis_size(axi...  51.2 us
    pallas_call x15, Pallas kernels, kernel(): pl.pallas_call(body, in_specs=[vmem] * len(ins), out_specs=[vmem] * len(o...  17.8 us
    unnamed x20, local copies, waits for them, and re-layouts  5.37 us
  transfers between devices with their start and end apart: 38, of which 17 were waited for; matrix products, arithmetic and copies ran while one was open for 2% of the time, Pallas kernels for 9%

profile of v4, /device:TPU:0, one launch (start us, length us, event | category | flops | bytes accessed | tf_op | source)
XLA Modules:
  0.0 160.9 jit_solution(3707590029974636037)
XLA Ops:
  0.6 2.1 %collective-permute-start.9 = (bf16[128,2048]{1,0:T(8,128)(2,1)}, bf16[128,2048]{1,0:T(8,128)(2,1)S(1)}, u32[]{:S(2)}, u32[]{:S(2)}) collective-permute-start(bf16[128,2048]{1,0:T(8,128)(2,1)} %x0.1), channel_id=1, source_target_pairs={{0,2},{2,0},{1,3},{3,1},{4,6},{6,4},{5,7},{7,5},{8,10},{10,8},{9,1... | collective-permute-start | bytes 1572872 | tf_op jit(solution)/shard_map/ppermute | solution.py:27
  4.8 10.1 %collective-permute-done.9.x0 = bf16[128,2048]{1,0:T(8,128)(2,1)S(1)} collective-permute-done((bf16[128,2048]{1,0:T(8,128)(2,1)}, bf16[128,2048]{1,0:T(8,128)(2,1)S(1)}, u32[]{:S(2)}, u32[]{:S(2)}) %collective-permute-start.9) | collective-permute-done | bytes 524320 | tf_op jit(solution)/shard_map/ppermute | solution.py:27
  14.9 1.1 fusion.1
  16.0 1.8 %collective-permute-start.3 = (bf16[128,1024]{1,0:T(8,128)(2,1)S(1)}, bf16[128,1024]{1,0:T(8,128)(2,1)S(1)}, u32[]{:S(2)}, u32[]{:S(2)}) collective-permute-start(bf16[128,1024]{1,0:T(8,128)(2,1)S(1)} %get-tuple-element.112), channel_id=1, source_target_pairs={{0,2},{2,0},{1,3},{3,1},{4,6},{6,4},{5,7},{7,5},{8,10},{10,8},{9,1... | collective-permute-start | bytes 786440 | tf_op jit(solution)/shard_map/ppermute | solution.py:27
  18.1 7.1 %collective-permute-done.3.refs_0_.refs_4_ = bf16[128,1024]{1,0:T(8,128)(2,1)S(1)} collective-permute-done((bf16[128,1024]{1,0:T(8,128)(2,1)S(1)}, bf16[128,1024]{1,0:T(8,128)(2,1)S(1)}, u32[]{:S(2)}, u32[]{:S(2)}) %collective-permute-start.3) | collective-permute-done | bytes 262176 | tf_op jit(solution)/shard_map/ppermute | solution.py:27
  25.2 1.7 %collective-permute-start.7 = (f32[8,128]{1,0:T(8,128)S(1)}, f32[8,128]{1,0:T(8,128)S(1)}, u32[]{:S(2)}, u32[]{:S(2)}) collective-permute-start(f32[8,128]{1,0:T(8,128)S(1)} %get-tuple-element.55), channel_id=1, source_target_pairs={{0,2},{1,3},{2,0},{3,1},{4,6},{5,7},{6,4},{7,5},{8,10},{9,11},{10,... | collective-permute-start | bytes 12296 | tf_op jit(solution)/shard_map/ppermute | solution.py:27
  27.0 3.5 %collective-permute-done.4.refs_1_.refs_4_ = bf16[128,1024]{1,0:T(8,128)(2,1)S(1)} collective-permute-done((bf16[128,1024]{1,0:T(8,128)(2,1)S(1)}, bf16[128,1024]{1,0:T(8,128)(2,1)S(1)}, u32[]{:S(2)}, u32[]{:S(2)}) %collective-permute-start.4) | collective-permute-done | bytes 262176 | tf_op jit(solution)/shard_map/ppermute | solution.py:27
  30.9 1.9 %copy-done.2 = bf16[1,2048,768]{2,1,0:T(8,128)(2,1)S(1)} copy-done((bf16[1,2048,768]{2,1,0:T(8,128)(2,1)S(1)}, bf16[1,2048,768]{2,1,0:T(8,128)(2,1)}, u32[]{:S(2)}) %copy-start.2) | copy-done | bytes 3145752
  32.8 1.9 %copy-done.4 = bf16[1,2048,768]{2,1,0:T(8,128)(2,1)S(1)} copy-done((bf16[1,2048,768]{2,1,0:T(8,128)(2,1)S(1)}, bf16[1,2048,768]{2,1,0:T(8,128)(2,1)}, u32[]{:S(2)}) %copy-start.4) | copy-done | bytes 3145752
  34.7 2.0 %shard_map.111 = (f32[256,768]{1,0:T(8,128)S(1)}, f32[256,768]{1,0:T(8,128)S(1)}, bf16[256,768]{1,0:T(8,128)(2,1)S(1)}, f32[768,256]{1,0:T(8,128)S(1)}, bf16[2048,256]{1,0:T(8,128)(2,1)S(1)}) custom-call(bf16[128,2048]{1,0:T(8,128)(2,1)S(1)} %copy-done.6, bf16[128,2048]{1,0:T(8,128)(2,1)S(1)} %collective-permute-done.2.x1, ...), custom_call_target="tpu_custom_call" | custom-call | flops 1610612736 | bytes 1048576 | tf_op jit(solution)/shard_map/pallas_call | solution.py:61
  36.7 1.4 collective-permute-start.8
  38.2 1.2 shard_map.112
  40.0 2.0 %shard_map.113 = (f32[256,768]{1,0:T(8,128)S(1)}, f32[256,768]{1,0:T(8,128)S(1)}, bf16[256,768]{1,0:T(8,128)(2,1)S(1)}, f32[768,256]{1,0:T(8,128)S(1)}, bf16[2048,256]{1,0:T(8,128)(2,1)S(1)}) custom-call(bf16[128,2048]{1,0:T(8,128)(2,1)S(1)} %collective-permute-done.9.x0, bf16[128,2048]{1,0:T(8,128)(2,1)S(1)} %collective-permute-done.10.x1, ...), custom_call_target="tpu_custom_call" | custom-call | flops 1610612736 | bytes 1048576 | tf_op jit(solution)/shard_map/pallas_call | solution.py:61
  42.0 1.2 shard_map.114
  43.3 1.0 shard_map.121
  44.2 1.0 shard_map.118
  45.2 1.7 %collective-permute-start.29 = (bf16[3072,128]{1,0:T(8,128)(2,1)S(1)}, bf16[3072,128]{1,0:T(8,128)(2,1)S(1)}, u32[]{:S(2)}, u32[]{:S(2)}) collective-permute-start(bf16[3072,128]{1,0:T(8,128)(2,1)S(1)} %get-tuple-element.87), channel_id=1, source_target_pairs={{0,4},{4,0},{8,12},{12,8},{1,5},{5,1},{9,13},{13,9},{2,6},{6,2},{1... | collective-permute-start | bytes 2359304 | tf_op jit(solution)/shard_map/ppermute | solution.py:27
  48.0 1.5 collective-permute-start.24
  50.0 3.0 %collective-permute-start.19 = (bf16[3072,128]{1,0:T(8,128)(2,1)S(1)}, bf16[3072,128]{1,0:T(8,128)(2,1)S(1)}, u32[]{:S(2)}, u32[]{:S(2)}) collective-permute-start(bf16[3072,128]{1,0:T(8,128)(2,1)S(1)} %get-tuple-element.80), channel_id=1, source_target_pairs={{0,12},{4,8},{8,4},{12,0},{1,13},{5,9},{9,5},{13,1},{2,14},{6,10},... | collective-permute-start | bytes 2359304 | tf_op jit(solution)/shard_map/ppermute | solution.py:27
  53.1 3.4 %shard_map.115 = (bf16[128,2176]{1,0:T(8,128)(2,1)S(1)}, bf16[256,2176]{1,0:T(8,128)(2,1)S(1)}, bf16[128,2176]{1,0:T(8,128)(2,1)S(1)}) custom-call(bf16[256,768]{1,0:T(8,128)(2,1)S(1)} %get-tuple-element.54.gda.refs_2_, bf16[256,768]{1,0:T(8,128)(2,1)S(1)} %get-tuple-element.60.gdb.refs_3_, bf16[256,768]{1,0:T(8,128)(2,1)S(1)} %get-tuple-element.61.uda.refs_4_, ...), custom_call_target="tpu_custom_call" | custom-call | flops 3221225472 | bytes 1048576 | tf_op jit(solution)/shard_map/pallas_call | solution.py:61
  58.3 1.8 %shard_map.117 = (bf16[3072,128]{1,0:T(8,128)(2,1)S(1)}, bf16[3072,128]{1,0:T(8,128)(2,1)S(1)}, bf16[3072,128]{1,0:T(8,128)(2,1)S(1)}, bf16[3072,128]{1,0:T(8,128)(2,1)S(1)}) custom-call(bf16[2048,256]{1,0:T(8,128)(2,1)S(1)} %get-tuple-element.72.refs_0_, bf16[2048,256]{1,0:T(8,128)(2,1)S(1)} %get-tuple-element.73.refs_1_, ...), custom_call_target="tpu_custom_call" | custom-call | flops 1610612736 | bytes 1048576 | tf_op jit(solution)/shard_map/pallas_call | solution.py:61
  60.1 13.6 %collective-permute-done.30 = bf16[1536,128]{1,0:T(8,128)(2,1)S(1)} collective-permute-done((bf16[1536,128]{1,0:T(8,128)(2,1)S(1)}, bf16[1536,128]{1,0:T(8,128)(2,1)S(1)}, u32[]{:S(2)}, u32[]{:S(2)}) %collective-permute-start.30) | collective-permute-done | bytes 393248 | tf_op jit(solution)/shard_map/ppermute | solution.py:27
  73.7 3.6 %collective-permute-start.15 = (bf16[3072,128]{1,0:T(8,128)(2,1)S(1)}, bf16[3072,128]{1,0:T(8,128)(2,1)S(1)}, u32[]{:S(2)}, u32[]{:S(2)}) collective-permute-start(bf16[3072,128]{1,0:T(8,128)(2,1)S(1)} %shard_map.120), channel_id=1, source_target_pairs={{0,16},{16,0},{1,17},{17,1},{2,18},{18,2},{3,19},{19,3},{4,20},{20... | collective-permute-start | bytes 2359304 | tf_op jit(solution)/shard_map/ppermute | solution.py:27
  77.4 2.8 %collective-permute-start.13 = (bf16[3072,128]{1,0:T(8,128)(2,1)S(1)}, bf16[3072,128]{1,0:T(8,128)(2,1)S(1)}, u32[]{:S(2)}, u32[]{:S(2)}) collective-permute-start(bf16[3072,128]{1,0:T(8,128)(2,1)S(1)} %get-tuple-element.75), channel_id=1, source_target_pairs={{0,96},{32,64},{64,32},{96,0},{1,97},{33,65},{65,33},{97,1},{2,98}... | collective-permute-start | bytes 2359304 | tf_op jit(solution)/shard_map/ppermute | solution.py:27
  80.5 3.1 %collective-permute-start.31 = (bf16[2304,128]{1,0:T(8,128)(2,1)S(1)}, bf16[2304,128]{1,0:T(8,128)(2,1)S(1)}, u32[]{:S(2)}, u32[]{:S(2)}) collective-permute-start(bf16[2304,128]{1,0:T(8,128)(2,1)S(1)} %pad_maximum_fusion.1), channel_id=1, source_target_pairs={{0,12},{4,8},{8,4},{12,0},{1,13},{5,9},{9,5},{13,1},{2,14},{6,10},... | collective-permute-start | bytes 1769480 | tf_op jit(solution)/shard_map/ppermute | solution.py:27
  84.5 10.2 %collective-permute-done.15 = bf16[3072,128]{1,0:T(8,128)(2,1)S(1)} collective-permute-done((bf16[3072,128]{1,0:T(8,128)(2,1)S(1)}, bf16[3072,128]{1,0:T(8,128)(2,1)S(1)}, u32[]{:S(2)}, u32[]{:S(2)}) %collective-permute-start.15) | collective-permute-done | bytes 786464 | tf_op jit(solution)/shard_map/ppermute | solution.py:27
  94.6 1.6 collective-permute-start.20
  96.3 2.7 %collective-permute-done.13 = bf16[3072,128]{1,0:T(8,128)(2,1)S(1)} collective-permute-done((bf16[3072,128]{1,0:T(8,128)(2,1)S(1)}, bf16[3072,128]{1,0:T(8,128)(2,1)S(1)}, u32[]{:S(2)}, u32[]{:S(2)}) %collective-permute-start.13) | collective-permute-done | bytes 786464 | tf_op jit(solution)/shard_map/ppermute | solution.py:27
  99.1 1.6 collective-permute-start.21
  100.8 8.1 %collective-permute-done.21 = bf16[768,128]{1,0:T(8,128)(2,1)S(1)} collective-permute-done((bf16[768,128]{1,0:T(8,128)(2,1)S(1)}, bf16[768,128]{1,0:T(8,128)(2,1)S(1)}, u32[]{:S(2)}, u32[]{:S(2)}) %collective-permute-start.21) | collective-permute-done | bytes 196640 | tf_op jit(solution)/shard_map/ppermute | solution.py:27
  108.9 1.5 collective-permute-start.16
  110.5 4.5 %collective-permute-done.16 = bf16[768,128]{1,0:T(8,128)(2,1)S(1)} collective-permute-done((bf16[768,128]{1,0:T(8,128)(2,1)S(1)}, bf16[768,128]{1,0:T(8,128)(2,1)S(1)}, u32[]{:S(2)}, u32[]{:S(2)}) %collective-permute-start.16) | collective-permute-done | bytes 196640 | tf_op jit(solution)/shard_map/ppermute | solution.py:27
  114.9 1.5 collective-permute-start.14
  117.3 2.2 %collective-permute-start.22 = (bf16[1152,128]{1,0:T(8,128)(2,1)S(1)}, bf16[1152,128]{1,0:T(8,128)(2,1)S(1)}, u32[]{:S(2)}, u32[]{:S(2)}) collective-permute-start(bf16[1152,128]{1,0:T(8,128)(2,1)S(1)} %pad_maximum_fusion.3), channel_id=1, source_target_pairs={{0,96},{32,64},{64,32},{96,0},{1,97},{33,65},{65,33},{97,1},{2,98}... | collective-permute-start | bytes 884744 | tf_op jit(solution)/shard_map/ppermute | solution.py:27
  119.4 3.6 %collective-permute-done.14 = bf16[1536,128]{1,0:T(8,128)(2,1)S(1)} collective-permute-done((bf16[1536,128]{1,0:T(8,128)(2,1)S(1)}, bf16[1536,128]{1,0:T(8,128)(2,1)S(1)}, u32[]{:S(2)}, u32[]{:S(2)}) %collective-permute-start.14) | collective-permute-done | bytes 393248 | tf_op jit(solution)/shard_map/ppermute | solution.py:27
  123.1 3.8 %collective-permute-start.17 = (bf16[1152,128]{1,0:T(8,128)(2,1)S(1)}, bf16[1152,128]{1,0:T(8,128)(2,1)S(1)}, u32[]{:S(2)}, u32[]{:S(2)}) collective-permute-start(bf16[1152,128]{1,0:T(8,128)(2,1)S(1)} %pad_maximum_fusion.2), channel_id=1, source_target_pairs={{0,12},{4,8},{8,4},{12,0},{1,13},{5,9},{9,5},{13,1},{2,14},{6,10},... | collective-permute-start | bytes 884744 | tf_op jit(solution)/shard_map/ppermute | solution.py:27
  127.1 1.6 collective-permute-start.32
  129.7 2.0 %collective-permute-done.17 = bf16[1152,128]{1,0:T(8,128)(2,1)S(1)} collective-permute-done((bf16[1152,128]{1,0:T(8,128)(2,1)S(1)}, bf16[1152,128]{1,0:T(8,128)(2,1)S(1)}, u32[]{:S(2)}, u32[]{:S(2)}) %collective-permute-start.17) | collective-permute-done | bytes 294944 | tf_op jit(solution)/shard_map/ppermute | solution.py:27
  131.9 3.6 %collective-permute-done.23 = bf16[576,128]{1,0:T(8,128)(2,1)S(1)} collective-permute-done((bf16[576,128]{1,0:T(8,128)(2,1)S(1)}, bf16[576,128]{1,0:T(8,128)(2,1)S(1)}, u32[]{:S(2)}, u32[]{:S(2)}) %collective-permute-start.23) | collective-permute-done | bytes 147488 | tf_op jit(solution)/shard_map/ppermute | solution.py:27
  135.6 1.7 %collective-permute-done.18 = bf16[576,128]{1,0:T(8,128)(2,1)S(1)} collective-permute-done((bf16[576,128]{1,0:T(8,128)(2,1)S(1)}, bf16[576,128]{1,0:T(8,128)(2,1)S(1)}, u32[]{:S(2)}, u32[]{:S(2)}) %collective-permute-start.18) | collective-permute-done | bytes 147488 | tf_op jit(solution)/shard_map/ppermute | solution.py:27
  137.3 3.3 %collective-permute-start.34 = (bf16[384,128]{1,0:T(8,128)(2,1)S(1)}, bf16[384,128]{1,0:T(8,128)(2,1)S(1)}, u32[]{:S(2)}, u32[]{:S(2)}) collective-permute-start(bf16[384,128]{1,0:T(8,128)(2,1)S(1)} %pad_maximum_fusion.11), channel_id=1, source_target_pairs={{0,16},{16,0},{1,17},{17,1},{2,18},{18,2},{3,19},{19,3},{4,20},{20... | collective-permute-start | bytes 294920 | tf_op jit(solution)/shard_map/ppermute | solution.py:27
  140.7 3.1 %collective-permute-start.37 = (bf16[96,128]{1,0:T(8,128)(2,1)S(1)}, bf16[96,128]{1,0:T(8,128)(2,1)S(1)}, u32[]{:S(2)}, u32[]{:S(2)}) collective-permute-start(bf16[96,128]{1,0:T(8,128)(2,1)S(1)} %get-tuple-element.105), channel_id=1, source_target_pairs={{0,12},{4,8},{8,4},{12,0},{1,13},{5,9},{9,5},{13,1},{2,14},{6,10},... | collective-permute-start | bytes 73736 | tf_op jit(solution)/shard_map/ppermute | solution.py:27
  143.9 2.9 %collective-permute-start.33 = (bf16[576,128]{1,0:T(8,128)(2,1)S(1)}, bf16[576,128]{1,0:T(8,128)(2,1)S(1)}, u32[]{:S(2)}, u32[]{:S(2)}) collective-permute-start(bf16[576,128]{1,0:T(8,128)(2,1)S(1)} %pad_maximum_fusion.9), channel_id=1, source_target_pairs={{0,96},{32,64},{64,32},{96,0},{1,97},{33,65},{65,33},{97,1},{2,98}... | collective-permute-start | bytes 442376 | tf_op jit(solution)/shard_map/ppermute | solution.py:27
  147.0 3.3 %collective-permute-done.33 = bf16[576,128]{1,0:T(8,128)(2,1)S(1)} collective-permute-done((bf16[576,128]{1,0:T(8,128)(2,1)S(1)}, bf16[576,128]{1,0:T(8,128)(2,1)S(1)}, u32[]{:S(2)}, u32[]{:S(2)}) %collective-permute-start.33) | collective-permute-done | bytes 147488 | tf_op jit(solution)/shard_map/ppermute | solution.py:27
  150.4 2.9 %collective-permute-done.28 = bf16[576,128]{1,0:T(8,128)(2,1)S(1)} collective-permute-done((bf16[576,128]{1,0:T(8,128)(2,1)S(1)}, bf16[576,128]{1,0:T(8,128)(2,1)S(1)}, u32[]{:S(2)}, u32[]{:S(2)}) %collective-permute-start.28) | collective-permute-done | bytes 147488 | tf_op jit(solution)/shard_map/ppermute | solution.py:27
  154.4 1.2 shard_map.116
  155.6 3.4 %collective-permute-done.36.refs_10_ = bf16[96,128]{1,0:T(8,128)(2,1)S(1)} collective-permute-done((bf16[96,128]{1,0:T(8,128)(2,1)S(1)}, bf16[96,128]{1,0:T(8,128)(2,1)S(1)}, u32[]{:S(2)}, u32[]{:S(2)}) %collective-permute-start.36) | collective-permute-done | bytes 24608 | tf_op jit(solution)/shard_map/ppermute | solution.py:27
  159.0 1.2 collective-permute-done.35.refs_9_
  (110 shorter events, 13.1 us)
Async XLA Ops:
  0.6 30.3 %copy-start.6 = (bf16[128,2048]{1,0:T(8,128)(2,1)S(1)}, bf16[128,2048]{1,0:T(8,128)(2,1)}, u32[]{:S(2)}) copy-start(bf16[128,2048]{1,0:T(8,128)(2,1)} %x0.1) | copy-start | bytes 1572868
  0.6 14.2 %collective-permute-start.9 = (bf16[128,2048]{1,0:T(8,128)(2,1)}, bf16[128,2048]{1,0:T(8,128)(2,1)S(1)}, u32[]{:S(2)}, u32[]{:S(2)}) collective-permute-start(bf16[128,2048]{1,0:T(8,128)(2,1)} %x0.1), channel_id=1, source_target_pairs={{0,2},{2,0},{1,3},{3,1},{4,6},{6,4},{5,7},{7,5},{8,10},{10,8},{9,1... | collective-permute-start | bytes 1572872 | tf_op jit(solution)/shard_map/ppermute | solution.py:27
  2.7 27.7 %collective-permute-start.2 = (bf16[128,2048]{1,0:T(8,128)(2,1)}, bf16[128,2048]{1,0:T(8,128)(2,1)S(1)}, u32[]{:S(2)}, u32[]{:S(2)}) collective-permute-start(bf16[128,2048]{1,0:T(8,128)(2,1)} %x0.1), channel_id=1, source_target_pairs={{0,1},{1,0},{2,3},{3,2},{4,5},{5,4},{6,7},{7,6},{8,9},{9,8},{10,11... | collective-permute-start | bytes 1572872 | tf_op jit(solution)/shard_map/ppermute | solution.py:27
  2.8 0.7 copy-start.7
  3.4 0.7 copy-start.9
  4.1 13.6 %collective-permute-start.1 = (f32[8,128]{1,0:T(8,128)S(1)}, f32[8,128]{1,0:T(8,128)S(1)}, u32[]{:S(2)}, u32[]{:S(2)}) collective-permute-start(f32[8,128]{1,0:T(8,128)S(1)} %get-tuple-element.50), channel_id=1, source_target_pairs={{0,1},{1,0},{2,3},{3,2},{4,5},{5,4},{6,7},{7,6},{8,9},{9,8},{10,11... | collective-permute-start | bytes 12296 | tf_op jit(solution)/shard_map/ppermute | solution.py:27
  4.7 32.0 %collective-permute-start = (bf16[128,2048]{1,0:T(8,128)(2,1)}, bf16[128,2048]{1,0:T(8,128)(2,1)S(1)}, u32[]{:S(2)}, u32[]{:S(2)}) collective-permute-start(bf16[128,2048]{1,0:T(8,128)(2,1)} %refs_2_.7), channel_id=1, source_target_pairs={{0,1},{1,0},{2,3},{3,2},{4,5},{5,4},{6,7},{7,6},{8,9},{9,8},{10,11... | collective-permute-start | bytes 1572872 | tf_op jit(solution)/shard_map/ppermute | solution.py:27
  14.9 24.9 %collective-permute-start.10 = (bf16[128,2048]{1,0:T(8,128)(2,1)S(1)}, bf16[128,2048]{1,0:T(8,128)(2,1)S(1)}, u32[]{:S(2)}, u32[]{:S(2)}) collective-permute-start(bf16[128,2048]{1,0:T(8,128)(2,1)S(1)} %collective-permute-done.9.x0), channel_id=1, source_target_pairs={{0,1},{1,0},{2,3},{3,2},{4,5},{5,4},{6,7},{7,6},{8,9},{9,8},{10,11... | collective-permute-start | bytes 1572872 | tf_op jit(solution)/shard_map/ppermute | solution.py:27
  16.0 9.3 %collective-permute-start.3 = (bf16[128,1024]{1,0:T(8,128)(2,1)S(1)}, bf16[128,1024]{1,0:T(8,128)(2,1)S(1)}, u32[]{:S(2)}, u32[]{:S(2)}) collective-permute-start(bf16[128,1024]{1,0:T(8,128)(2,1)S(1)} %get-tuple-element.112), channel_id=1, source_target_pairs={{0,2},{2,0},{1,3},{3,1},{4,6},{6,4},{5,7},{7,5},{8,10},{10,8},{9,1... | collective-permute-start | bytes 786440 | tf_op jit(solution)/shard_map/ppermute | solution.py:27
  17.8 12.6 %collective-permute-start.4 = (bf16[128,1024]{1,0:T(8,128)(2,1)S(1)}, bf16[128,1024]{1,0:T(8,128)(2,1)S(1)}, u32[]{:S(2)}, u32[]{:S(2)}) collective-permute-start(bf16[128,1024]{1,0:T(8,128)(2,1)S(1)} %get-tuple-element.111), channel_id=1, source_target_pairs={{0,2},{2,0},{1,3},{3,1},{4,6},{6,4},{5,7},{7,5},{8,10},{10,8},{9,1... | collective-permute-start | bytes 786440 | tf_op jit(solution)/shard_map/ppermute | solution.py:27
  25.2 14.1 %collective-permute-start.7 = (f32[8,128]{1,0:T(8,128)S(1)}, f32[8,128]{1,0:T(8,128)S(1)}, u32[]{:S(2)}, u32[]{:S(2)}) collective-permute-start(f32[8,128]{1,0:T(8,128)S(1)} %get-tuple-element.55), channel_id=1, source_target_pairs={{0,2},{1,3},{2,0},{3,1},{4,6},{5,7},{6,4},{7,5},{8,10},{9,11},{10,... | collective-permute-start | bytes 12296 | tf_op jit(solution)/shard_map/ppermute | solution.py:27
  30.4 11.6 %collective-permute-start.5 = (bf16[128,1024]{1,0:T(8,128)(2,1)S(1)}, bf16[128,1024]{1,0:T(8,128)(2,1)S(1)}, u32[]{:S(2)}, u32[]{:S(2)}) collective-permute-start(bf16[128,1024]{1,0:T(8,128)(2,1)S(1)} %collective-permute-done.3.refs_0_.refs_4_), channel_id=1, source_target_pairs={{0,1},{1,0},{2,3},{3,2},{4,5},{5,4},{6,7},{7,6},{8,9},{9,8},{10,11... | collective-permute-start | bytes 786440 | tf_op jit(solution)/shard_map/ppermute | solution.py:27
  30.4 11.6 %collective-permute-start.6 = (bf16[128,1024]{1,0:T(8,128)(2,1)S(1)}, bf16[128,1024]{1,0:T(8,128)(2,1)S(1)}, u32[]{:S(2)}, u32[]{:S(2)}) collective-permute-start(bf16[128,1024]{1,0:T(8,128)(2,1)S(1)} %collective-permute-done.4.refs_1_.refs_4_), channel_id=1, source_target_pairs={{0,1},{1,0},{2,3},{3,2},{4,5},{5,4},{6,7},{7,6},{8,9},{9,8},{10,11... | collective-permute-start | bytes 786440 | tf_op jit(solution)/shard_map/ppermute | solution.py:27
  30.9 1.9 %copy-start.2 = (bf16[1,2048,768]{2,1,0:T(8,128)(2,1)S(1)}, bf16[1,2048,768]{2,1,0:T(8,128)(2,1)}, u32[]{:S(2)}) copy-start(bf16[1,2048,768]{2,1,0:T(8,128)(2,1)} %param.11) | copy-start | bytes 9437188
  32.8 1.9 %copy-start.4 = (bf16[1,2048,768]{2,1,0:T(8,128)(2,1)S(1)}, bf16[1,2048,768]{2,1,0:T(8,128)(2,1)}, u32[]{:S(2)}) copy-start(bf16[1,2048,768]{2,1,0:T(8,128)(2,1)} %param.12) | copy-start | bytes 9437188
  34.7 3.4 %copy-start = (bf16[128,2048]{1,0:T(8,128)(2,1)S(1)}, bf16[128,2048]{1,0:T(8,128)(2,1)}, u32[]{:S(2)}) copy-start(bf16[128,2048]{1,0:T(8,128)(2,1)} %refs_2_.7) | copy-start | bytes 1572868
  34.7 3.4 %copy-start.1 = (bf16[1,768,2048]{2,1,0:T(8,128)(2,1)S(1)}, bf16[1,768,2048]{2,1,0:T(8,128)(2,1)}, u32[]{:S(2)}) copy-start(bf16[1,768,2048]{2,1,0:T(8,128)(2,1)} %param.13) | copy-start | bytes 9437188
  34.7 5.1 %copy-start.5 = (bf16[1,2048,768]{2,1,0:T(8,128)(2,1)S(1)}, bf16[1,2048,768]{2,1,0:T(8,128)(2,1)}, u32[]{:S(2)}) copy-start(bf16[1,2048,768]{2,1,0:T(8,128)(2,1)} %param.12) | copy-start | bytes 9437188
  36.7 3.1 %collective-permute-start.8 = (f32[8,128]{1,0:T(8,128)S(1)}, f32[8,128]{1,0:T(8,128)S(1)}, u32[]{:S(2)}, u32[]{:S(2)}) collective-permute-start(f32[8,128]{1,0:T(8,128)S(1)} %get-tuple-element.56), channel_id=1, source_target_pairs={{0,3},{1,2},{2,1},{3,0},{4,7},{5,6},{6,5},{7,4},{8,11},{9,10},{10,... | collective-permute-start | bytes 12296 | tf_op jit(solution)/shard_map/ppermute | solution.py:27
  38.2 1.9 %copy-start.3 = (bf16[1,2048,768]{2,1,0:T(8,128)(2,1)S(1)}, bf16[1,2048,768]{2,1,0:T(8,128)(2,1)}, u32[]{:S(2)}) copy-start(bf16[1,2048,768]{2,1,0:T(8,128)(2,1)} %param.11) | copy-start | bytes 9437188
  45.2 35.0 %collective-permute-start.29 = (bf16[3072,128]{1,0:T(8,128)(2,1)S(1)}, bf16[3072,128]{1,0:T(8,128)(2,1)S(1)}, u32[]{:S(2)}, u32[]{:S(2)}) collective-permute-start(bf16[3072,128]{1,0:T(8,128)(2,1)S(1)} %get-tuple-element.87), channel_id=1, source_target_pairs={{0,4},{4,0},{8,12},{12,8},{1,5},{5,1},{9,13},{13,9},{2,6},{6,2},{1... | collective-permute-start | bytes 2359304 | tf_op jit(solution)/shard_map/ppermute | solution.py:27
  47.5 26.2 %collective-permute-start.30 = (bf16[1536,128]{1,0:T(8,128)(2,1)S(1)}, bf16[1536,128]{1,0:T(8,128)(2,1)S(1)}, u32[]{:S(2)}, u32[]{:S(2)}) collective-permute-start(bf16[1536,128]{1,0:T(8,128)(2,1)S(1)} %get-tuple-element.89), channel_id=1, source_target_pairs={{0,4},{4,0},{8,12},{12,8},{1,5},{5,1},{9,13},{13,9},{2,6},{6,2},{1... | collective-permute-start | bytes 1179656 | tf_op jit(solution)/shard_map/ppermute | solution.py:27
  48.0 32.5 %collective-permute-start.24 = (bf16[3072,128]{1,0:T(8,128)(2,1)S(1)}, bf16[3072,128]{1,0:T(8,128)(2,1)S(1)}, u32[]{:S(2)}, u32[]{:S(2)}) collective-permute-start(bf16[3072,128]{1,0:T(8,128)(2,1)S(1)} %get-tuple-element.83), channel_id=1, source_target_pairs={{0,32},{32,0},{64,96},{96,64},{1,33},{33,1},{65,97},{97,65},{2,34}... | collective-permute-start | bytes 2359304 | tf_op jit(solution)/shard_map/ppermute | solution.py:27
  49.5 27.8 %collective-permute-start.25 = (bf16[1536,128]{1,0:T(8,128)(2,1)S(1)}, bf16[1536,128]{1,0:T(8,128)(2,1)S(1)}, u32[]{:S(2)}, u32[]{:S(2)}) collective-permute-start(bf16[1536,128]{1,0:T(8,128)(2,1)S(1)} %get-tuple-element.85), channel_id=1, source_target_pairs={{0,32},{32,0},{64,96},{96,64},{1,33},{33,1},{65,97},{97,65},{2,34}... | collective-permute-start | bytes 1179656 | tf_op jit(solution)/shard_map/ppermute | solution.py:27
  50.0 33.7 %collective-permute-start.19 = (bf16[3072,128]{1,0:T(8,128)(2,1)S(1)}, bf16[3072,128]{1,0:T(8,128)(2,1)S(1)}, u32[]{:S(2)}, u32[]{:S(2)}) collective-permute-start(bf16[3072,128]{1,0:T(8,128)(2,1)S(1)} %get-tuple-element.80), channel_id=1, source_target_pairs={{0,12},{4,8},{8,4},{12,0},{1,13},{5,9},{9,5},{13,1},{2,14},{6,10},... | collective-permute-start | bytes 2359304 | tf_op jit(solution)/shard_map/ppermute | solution.py:27
  73.7 20.9 %collective-permute-start.15 = (bf16[3072,128]{1,0:T(8,128)(2,1)S(1)}, bf16[3072,128]{1,0:T(8,128)(2,1)S(1)}, u32[]{:S(2)}, u32[]{:S(2)}) collective-permute-start(bf16[3072,128]{1,0:T(8,128)(2,1)S(1)} %shard_map.120), channel_id=1, source_target_pairs={{0,16},{16,0},{1,17},{17,1},{2,18},{18,2},{3,19},{19,3},{4,20},{20... | collective-permute-start | bytes 2359304 | tf_op jit(solution)/shard_map/ppermute | solution.py:27
  77.4 21.7 %collective-permute-start.13 = (bf16[3072,128]{1,0:T(8,128)(2,1)S(1)}, bf16[3072,128]{1,0:T(8,128)(2,1)S(1)}, u32[]{:S(2)}, u32[]{:S(2)}) collective-permute-start(bf16[3072,128]{1,0:T(8,128)(2,1)S(1)} %get-tuple-element.75), channel_id=1, source_target_pairs={{0,96},{32,64},{64,32},{96,0},{1,97},{33,65},{65,33},{97,1},{2,98}... | collective-permute-start | bytes 2359304 | tf_op jit(solution)/shard_map/ppermute | solution.py:27
  80.3 36.2 %collective-permute-start.11 = (bf16[256,2176]{1,0:T(8,128)(2,1)S(1)}, bf16[256,2176]{1,0:T(8,128)(2,1)S(1)}, u32[]{:S(2)}, u32[]{:S(2)}) collective-permute-start(bf16[256,2176]{1,0:T(8,128)(2,1)S(1)} %get-tuple-element.68), channel_id=1, source_target_pairs={{0,1},{1,0},{2,3},{3,2},{4,5},{5,4},{6,7},{7,6},{8,9},{9,8},{10,11... | collective-permute-start | bytes 3342344 | tf_op jit(solution)/shard_map/ppermute | solution.py:27
  80.5 46.4 %collective-permute-start.31 = (bf16[2304,128]{1,0:T(8,128)(2,1)S(1)}, bf16[2304,128]{1,0:T(8,128)(2,1)S(1)}, u32[]{:S(2)}, u32[]{:S(2)}) collective-permute-start(bf16[2304,128]{1,0:T(8,128)(2,1)S(1)} %pad_maximum_fusion.1), channel_id=1, source_target_pairs={{0,12},{4,8},{8,4},{12,0},{1,13},{5,9},{9,5},{13,1},{2,14},{6,10},... | collective-permute-start | bytes 1769480 | tf_op jit(solution)/shard_map/ppermute | solution.py:27
  83.8 44.9 %collective-permute-start.26 = (bf16[2304,128]{1,0:T(8,128)(2,1)S(1)}, bf16[2304,128]{1,0:T(8,128)(2,1)S(1)}, u32[]{:S(2)}, u32[]{:S(2)}) collective-permute-start(bf16[2304,128]{1,0:T(8,128)(2,1)S(1)} %pad_maximum_fusion), channel_id=1, source_target_pairs={{0,96},{32,64},{64,32},{96,0},{1,97},{33,65},{65,33},{97,1},{2,98}... | collective-permute-start | bytes 1769480 | tf_op jit(solution)/shard_map/ppermute | solution.py:27
  94.6 22.5 %collective-permute-start.20 = (bf16[1536,128]{1,0:T(8,128)(2,1)S(1)}, bf16[1536,128]{1,0:T(8,128)(2,1)S(1)}, u32[]{:S(2)}, u32[]{:S(2)}) collective-permute-start(bf16[1536,128]{1,0:T(8,128)(2,1)S(1)} %add_convert_fusion.3), channel_id=1, source_target_pairs={{0,4},{4,0},{8,12},{12,8},{1,5},{5,1},{9,13},{13,9},{2,6},{6,2},{1... | collective-permute-start | bytes 1179656 | tf_op jit(solution)/shard_map/ppermute | solution.py:27
  99.1 9.9 %collective-permute-start.21 = (bf16[768,128]{1,0:T(8,128)(2,1)S(1)}, bf16[768,128]{1,0:T(8,128)(2,1)S(1)}, u32[]{:S(2)}, u32[]{:S(2)}) collective-permute-start(bf16[768,128]{1,0:T(8,128)(2,1)S(1)} %add_convert_fusion.9), channel_id=1, source_target_pairs={{0,4},{4,0},{8,12},{12,8},{1,5},{5,1},{9,13},{13,9},{2,6},{6,2},{1... | collective-permute-start | bytes 589832 | tf_op jit(solution)/shard_map/ppermute | solution.py:27
  108.9 6.0 %collective-permute-start.16 = (bf16[768,128]{1,0:T(8,128)(2,1)S(1)}, bf16[768,128]{1,0:T(8,128)(2,1)S(1)}, u32[]{:S(2)}, u32[]{:S(2)}) collective-permute-start(bf16[768,128]{1,0:T(8,128)(2,1)S(1)} %add_convert_fusion.11), channel_id=1, source_target_pairs={{0,32},{32,0},{64,96},{96,64},{1,33},{33,1},{65,97},{97,65},{2,34}... | collective-permute-start | bytes 589832 | tf_op jit(solution)/shard_map/ppermute | solution.py:27
  114.9 8.1 %collective-permute-start.14 = (bf16[1536,128]{1,0:T(8,128)(2,1)S(1)}, bf16[1536,128]{1,0:T(8,128)(2,1)S(1)}, u32[]{:S(2)}, u32[]{:S(2)}) collective-permute-start(bf16[1536,128]{1,0:T(8,128)(2,1)S(1)} %add_convert_fusion.4), channel_id=1, source_target_pairs={{0,32},{32,0},{64,96},{96,64},{1,33},{33,1},{65,97},{97,65},{2,34}... | collective-permute-start | bytes 1179656 | tf_op jit(solution)/shard_map/ppermute | solution.py:27
  116.6 37.8 %collective-permute-start.12 = (bf16[128,2176]{1,0:T(8,128)(2,1)S(1)}, bf16[128,2176]{1,0:T(8,128)(2,1)S(1)}, u32[]{:S(2)}, u32[]{:S(2)}) collective-permute-start(bf16[128,2176]{1,0:T(8,128)(2,1)S(1)} %add_convert_fusion), channel_id=1, source_target_pairs={{0,2},{2,0},{1,3},{3,1},{4,6},{6,4},{5,7},{7,5},{8,10},{10,8},{9,1... | collective-permute-start | bytes 1671176 | tf_op jit(solution)/shard_map/ppermute | solution.py:27
  117.3 11.7 %collective-permute-start.22 = (bf16[1152,128]{1,0:T(8,128)(2,1)S(1)}, bf16[1152,128]{1,0:T(8,128)(2,1)S(1)}, u32[]{:S(2)}, u32[]{:S(2)}) collective-permute-start(bf16[1152,128]{1,0:T(8,128)(2,1)S(1)} %pad_maximum_fusion.3), channel_id=1, source_target_pairs={{0,96},{32,64},{64,32},{96,0},{1,97},{33,65},{65,33},{97,1},{2,98}... | collective-permute-start | bytes 884744 | tf_op jit(solution)/shard_map/ppermute | solution.py:27
  123.1 8.5 %collective-permute-start.17 = (bf16[1152,128]{1,0:T(8,128)(2,1)S(1)}, bf16[1152,128]{1,0:T(8,128)(2,1)S(1)}, u32[]{:S(2)}, u32[]{:S(2)}) collective-permute-start(bf16[1152,128]{1,0:T(8,128)(2,1)S(1)} %pad_maximum_fusion.2), channel_id=1, source_target_pairs={{0,12},{4,8},{8,4},{12,0},{1,13},{5,9},{9,5},{13,1},{2,14},{6,10},... | collective-permute-start | bytes 884744 | tf_op jit(solution)/shard_map/ppermute | solution.py:27
  127.1 16.6 %collective-permute-start.32 = (bf16[1152,128]{1,0:T(8,128)(2,1)S(1)}, bf16[1152,128]{1,0:T(8,128)(2,1)S(1)}, u32[]{:S(2)}, u32[]{:S(2)}) collective-permute-start(bf16[1152,128]{1,0:T(8,128)(2,1)S(1)} %pad_maximum_fusion.5), channel_id=1, source_target_pairs={{0,32},{32,0},{64,96},{96,64},{1,33},{33,1},{65,97},{97,65},{2,34}... | collective-permute-start | bytes 884744 | tf_op jit(solution)/shard_map/ppermute | solution.py:27
  128.9 17.9 %collective-permute-start.27 = (bf16[1152,128]{1,0:T(8,128)(2,1)S(1)}, bf16[1152,128]{1,0:T(8,128)(2,1)S(1)}, u32[]{:S(2)}, u32[]{:S(2)}) collective-permute-start(bf16[1152,128]{1,0:T(8,128)(2,1)S(1)} %pad_maximum_fusion.4), channel_id=1, source_target_pairs={{0,4},{4,0},{8,12},{12,8},{1,5},{5,1},{9,13},{13,9},{2,6},{6,2},{1... | collective-permute-start | bytes 884744 | tf_op jit(solution)/shard_map/ppermute | solution.py:27
  129.1 6.4 %collective-permute-start.23 = (bf16[576,128]{1,0:T(8,128)(2,1)S(1)}, bf16[576,128]{1,0:T(8,128)(2,1)S(1)}, u32[]{:S(2)}, u32[]{:S(2)}) collective-permute-start(bf16[576,128]{1,0:T(8,128)(2,1)S(1)} %pad_maximum_fusion.7), channel_id=1, source_target_pairs={{0,32},{32,0},{64,96},{96,64},{1,33},{33,1},{65,97},{97,65},{2,34}... | collective-permute-start | bytes 442376 | tf_op jit(solution)/shard_map/ppermute | solution.py:27
  131.8 5.5 %collective-permute-start.18 = (bf16[576,128]{1,0:T(8,128)(2,1)S(1)}, bf16[576,128]{1,0:T(8,128)(2,1)S(1)}, u32[]{:S(2)}, u32[]{:S(2)}) collective-permute-start(bf16[576,128]{1,0:T(8,128)(2,1)S(1)} %pad_maximum_fusion.6), channel_id=1, source_target_pairs={{0,4},{4,0},{8,12},{12,8},{1,5},{5,1},{9,13},{13,9},{2,6},{6,2},{1... | collective-permute-start | bytes 442376 | tf_op jit(solution)/shard_map/ppermute | solution.py:27
  137.3 21.6 %collective-permute-start.34 = (bf16[384,128]{1,0:T(8,128)(2,1)S(1)}, bf16[384,128]{1,0:T(8,128)(2,1)S(1)}, u32[]{:S(2)}, u32[]{:S(2)}) collective-permute-start(bf16[384,128]{1,0:T(8,128)(2,1)S(1)} %pad_maximum_fusion.11), channel_id=1, source_target_pairs={{0,16},{16,0},{1,17},{17,1},{2,18},{18,2},{3,19},{19,3},{4,20},{20... | collective-permute-start | bytes 294920 | tf_op jit(solution)/shard_map/ppermute | solution.py:27
  140.7 14.9 %collective-permute-start.37 = (bf16[96,128]{1,0:T(8,128)(2,1)S(1)}, bf16[96,128]{1,0:T(8,128)(2,1)S(1)}, u32[]{:S(2)}, u32[]{:S(2)}) collective-permute-start(bf16[96,128]{1,0:T(8,128)(2,1)S(1)} %get-tuple-element.105), channel_id=1, source_target_pairs={{0,12},{4,8},{8,4},{12,0},{1,13},{5,9},{9,5},{13,1},{2,14},{6,10},... | collective-permute-start | bytes 73736 | tf_op jit(solution)/shard_map/ppermute | solution.py:27
  143.9 6.4 %collective-permute-start.33 = (bf16[576,128]{1,0:T(8,128)(2,1)S(1)}, bf16[576,128]{1,0:T(8,128)(2,1)S(1)}, u32[]{:S(2)}, u32[]{:S(2)}) collective-permute-start(bf16[576,128]{1,0:T(8,128)(2,1)S(1)} %pad_maximum_fusion.9), channel_id=1, source_target_pairs={{0,96},{32,64},{64,32},{96,0},{1,97},{33,65},{65,33},{97,1},{2,98}... | collective-permute-start | bytes 442376 | tf_op jit(solution)/shard_map/ppermute | solution.py:27
  146.9 7.5 %copy-start.8 = (s32[128,2]{0,1:T(2,128)S(1)}, s32[128,2]{0,1:T(2,128)}, u32[]{:S(2)}) copy-start(s32[128,2]{0,1:T(2,128)} %param.9) | copy-start | bytes 3076
  146.9 6.4 %collective-permute-start.28 = (bf16[576,128]{1,0:T(8,128)(2,1)S(1)}, bf16[576,128]{1,0:T(8,128)(2,1)S(1)}, u32[]{:S(2)}, u32[]{:S(2)}) collective-permute-start(bf16[576,128]{1,0:T(8,128)(2,1)S(1)} %pad_maximum_fusion.8), channel_id=1, source_target_pairs={{0,12},{4,8},{8,4},{12,0},{1,13},{5,9},{9,5},{13,1},{2,14},{6,10},... | collective-permute-start | bytes 442376 | tf_op jit(solution)/shard_map/ppermute | solution.py:27
  153.5 6.7 %collective-permute-start.35 = (bf16[576,128]{1,0:T(8,128)(2,1)S(1)}, bf16[576,128]{1,0:T(8,128)(2,1)S(1)}, u32[]{:S(2)}, u32[]{:S(2)}) collective-permute-start(bf16[576,128]{1,0:T(8,128)(2,1)S(1)} %pad_maximum_fusion.10), channel_id=1, source_target_pairs={{0,16},{16,0},{1,17},{17,1},{2,18},{18,2},{3,19},{19,3},{4,20},{20... | collective-permute-start | bytes 442376 | tf_op jit(solution)/shard_map/ppermute | solution.py:27
  153.9 5.1 %collective-permute-start.36 = (bf16[96,128]{1,0:T(8,128)(2,1)S(1)}, bf16[96,128]{1,0:T(8,128)(2,1)S(1)}, u32[]{:S(2)}, u32[]{:S(2)}) collective-permute-start(bf16[96,128]{1,0:T(8,128)(2,1)S(1)} %get-tuple-element.107), channel_id=1, source_target_pairs={{0,96},{32,64},{64,32},{96,0},{1,97},{33,65},{65,33},{97,1},{2,98}... | collective-permute-start | bytes 73736 | tf_op jit(solution)/shard_map/ppermute | solution.py:27

commit v5 on v4

--- a/solution.py
+++ b/solution.py
@@ -56,7 +56,7 @@
     return jnp.dot(a, b, preferred_element_type=F32)
 
 
-def kernel(body, ins, outs, limit, flops, scratch=()):
+def kernel(body, ins, outs, limit, flops, scratch=(), aliases=None):
     vmem = pl.BlockSpec(memory_space=pltpu.VMEM)
     return pl.pallas_call(
         body,
@@ -64,6 +64,7 @@
         out_specs=[vmem] * len(outs),
         out_shape=[jax.ShapeDtypeStruct(s, t) for s, t in outs],
         scratch_shapes=list(scratch),
+        input_output_aliases=aliases or {},
         compiler_params=pltpu.CompilerParams(vmem_limit_bytes=limit << 20),
         cost_estimate=pl.CostEstimate(flops=flops, transcendentals=0, bytes_accessed=1 << 20),
     )(*ins)
@@ -75,6 +76,19 @@
         chosen = ids[...] == (mine ^ m)
         row = jnp.sum(jnp.where(chosen, combine[...], 0.0), axis=0, keepdims=True)
         out[...] = jnp.broadcast_to(row, out.shape)
+
+
+def in_turn(body, ins, outs, limit, flops, scratch=()):
+    def first(*refs):
+        pl.when(lax.axis_index("c") != LEADER)(lambda: body(*refs))
+
+    def second(*refs):
+        kept = refs[: len(ins)] + refs[len(ins) + len(outs) :]
+        pl.when(lax.axis_index("c") == LEADER)(lambda: body(*kept))
+
+    early = kernel(first, ins, outs, limit, flops, scratch)
+    aliases = {len(ins) + k: k for k in range(len(outs))}
+    return kernel(second, (*ins, *early), outs, limit, flops, scratch, aliases)
 
 
 def forward_body(x0, x1, c0, c1, wg, wu, slope, act_out, hid, cht, xt, xs):
@@ -191,6 +205,7 @@
 TILE = 256
 EARLY = ((2, 0, 3), (3, 0, 3))
 LATER = ((0, 0, 3), (1, 0, 3))
+LEADER = 1
 EXTRA = 128
 
 
@@ -325,7 +340,7 @@
     gate_send += gate_half(HALF, LATER, xts, gds, uds)
     down_keep = [a for k in range(2) for a in down_half(0, k, hts, pieces[k])]
     gate_keep = gate_half(0, EARLY + LATER, xts, gds, uds)
-    own_rows, side_rows, far_rows = kernel(
+    own_rows, side_rows, far_rows = in_turn(
         rows_body,
         (*gds, *uds, wg, wu, ha[2], ha[3], hb[2], hb[3]),
         [((n * PIECE, d + EXTRA), BF16) for n in (1, 2, 1)],

time: 161 us -> 161 us (level)
    pallas_call x15 -> x16, Pallas kernels: 17.8 us -> 17.9 us  [kernel(): pl.pallas_call(body, in_specs=[vmem] * len(ins), out_specs=[vmem] * len(o...]
where the time goes in v5:
time: 161 us
  waiting for transfers between devices  81.7 us (51%)
  starting transfers between devices  51.2 us (32%)
  Pallas kernels  17.9 us (11%)
  local copies, waits for them, and re-layouts  6.48 us (4%)
  other arithmetic  2.29 us (1%)
    ppermute x38, waiting for transfers between devices, moved(): lax.ppermute(array, axis, [(i, i ^ mask) for i in range(lax.axis_size(axi...  81.7 us
    ppermute x38, starting transfers between devices, moved(): lax.ppermute(array, axis, [(i, i ^ mask) for i in range(lax.axis_size(axi...  51.2 us
    pallas_call x16, Pallas kernels, kernel(): pl.pallas_call(body, in_specs=[vmem] * len(ins), out_specs=[vmem] * len(o...  17.9 us
    unnamed x20, local copies, waits for them, and re-layouts  5.37 us
  transfers between devices with their start and end apart: 38, of which 17 were waited for; matrix products, arithmetic and copies ran while one was open for 2% of the time, Pallas kernels for 9%

profile of v5, /device:TPU:0, one launch (start us, length us, event | category | flops | bytes accessed | tf_op | source)
XLA Modules:
  0.0 160.7 jit_solution(13046201431026498128)
XLA Ops:
  0.6 2.1 %collective-permute-start.9 = (bf16[128,2048]{1,0:T(8,128)(2,1)}, bf16[128,2048]{1,0:T(8,128)(2,1)S(1)}, u32[]{:S(2)}, u32[]{:S(2)}) collective-permute-start(bf16[128,2048]{1,0:T(8,128)(2,1)} %x0.1), channel_id=1, source_target_pairs={{0,2},{2,0},{1,3},{3,1},{4,6},{6,4},{5,7},{7,5},{8,10},{10,8},{9,1... | collective-permute-start | bytes 1572872 | tf_op jit(solution)/shard_map/ppermute | solution.py:27
  4.8 10.1 %collective-permute-done.9.x0 = bf16[128,2048]{1,0:T(8,128)(2,1)S(1)} collective-permute-done((bf16[128,2048]{1,0:T(8,128)(2,1)}, bf16[128,2048]{1,0:T(8,128)(2,1)S(1)}, u32[]{:S(2)}, u32[]{:S(2)}) %collective-permute-start.9) | collective-permute-done | bytes 524320 | tf_op jit(solution)/shard_map/ppermute | solution.py:27
  14.9 1.1 fusion.1
  16.0 1.8 %collective-permute-start.3 = (bf16[128,1024]{1,0:T(8,128)(2,1)S(1)}, bf16[128,1024]{1,0:T(8,128)(2,1)S(1)}, u32[]{:S(2)}, u32[]{:S(2)}) collective-permute-start(bf16[128,1024]{1,0:T(8,128)(2,1)S(1)} %get-tuple-element.118), channel_id=1, source_target_pairs={{0,2},{2,0},{1,3},{3,1},{4,6},{6,4},{5,7},{7,5},{8,10},{10,8},{9,1... | collective-permute-start | bytes 786440 | tf_op jit(solution)/shard_map/ppermute | solution.py:27
  18.1 7.1 %collective-permute-done.3.refs_0_.refs_4_ = bf16[128,1024]{1,0:T(8,128)(2,1)S(1)} collective-permute-done((bf16[128,1024]{1,0:T(8,128)(2,1)S(1)}, bf16[128,1024]{1,0:T(8,128)(2,1)S(1)}, u32[]{:S(2)}, u32[]{:S(2)}) %collective-permute-start.3) | collective-permute-done | bytes 262176 | tf_op jit(solution)/shard_map/ppermute | solution.py:27
  25.2 1.7 %collective-permute-start.7 = (f32[8,128]{1,0:T(8,128)S(1)}, f32[8,128]{1,0:T(8,128)S(1)}, u32[]{:S(2)}, u32[]{:S(2)}) collective-permute-start(f32[8,128]{1,0:T(8,128)S(1)} %get-tuple-element.58), channel_id=1, source_target_pairs={{0,2},{1,3},{2,0},{3,1},{4,6},{5,7},{6,4},{7,5},{8,10},{9,11},{10,... | collective-permute-start | bytes 12296 | tf_op jit(solution)/shard_map/ppermute | solution.py:27
  27.0 3.5 %collective-permute-done.4.refs_1_.refs_4_ = bf16[128,1024]{1,0:T(8,128)(2,1)S(1)} collective-permute-done((bf16[128,1024]{1,0:T(8,128)(2,1)S(1)}, bf16[128,1024]{1,0:T(8,128)(2,1)S(1)}, u32[]{:S(2)}, u32[]{:S(2)}) %collective-permute-start.4) | collective-permute-done | bytes 262176 | tf_op jit(solution)/shard_map/ppermute | solution.py:27
  30.9 1.9 %copy-done.2 = bf16[1,2048,768]{2,1,0:T(8,128)(2,1)S(1)} copy-done((bf16[1,2048,768]{2,1,0:T(8,128)(2,1)S(1)}, bf16[1,2048,768]{2,1,0:T(8,128)(2,1)}, u32[]{:S(2)}) %copy-start.2) | copy-done | bytes 3145752
  32.8 1.9 %copy-done.4 = bf16[1,2048,768]{2,1,0:T(8,128)(2,1)S(1)} copy-done((bf16[1,2048,768]{2,1,0:T(8,128)(2,1)S(1)}, bf16[1,2048,768]{2,1,0:T(8,128)(2,1)}, u32[]{:S(2)}) %copy-start.4) | copy-done | bytes 3145752
  34.7 2.0 %shard_map.111 = (f32[256,768]{1,0:T(8,128)S(1)}, f32[256,768]{1,0:T(8,128)S(1)}, bf16[256,768]{1,0:T(8,128)(2,1)S(1)}, f32[768,256]{1,0:T(8,128)S(1)}, bf16[2048,256]{1,0:T(8,128)(2,1)S(1)}) custom-call(bf16[128,2048]{1,0:T(8,128)(2,1)S(1)} %copy-done.6, bf16[128,2048]{1,0:T(8,128)(2,1)S(1)} %collective-permute-done.2.x1, ...), custom_call_target="tpu_custom_call" | custom-call | flops 1610612736 | bytes 1048576 | tf_op jit(solution)/shard_map/pallas_call | solution.py:61
  36.7 1.4 collective-permute-start.8
  38.2 1.2 shard_map.112
  40.0 2.0 %shard_map.113 = (f32[256,768]{1,0:T(8,128)S(1)}, f32[256,768]{1,0:T(8,128)S(1)}, bf16[256,768]{1,0:T(8,128)(2,1)S(1)}, f32[768,256]{1,0:T(8,128)S(1)}, bf16[2048,256]{1,0:T(8,128)(2,1)S(1)}) custom-call(bf16[128,2048]{1,0:T(8,128)(2,1)S(1)} %collective-permute-done.9.x0, bf16[128,2048]{1,0:T(8,128)(2,1)S(1)} %collective-permute-done.10.x1, ...), custom_call_target="tpu_custom_call" | custom-call | flops 1610612736 | bytes 1048576 | tf_op jit(solution)/shard_map/pallas_call | solution.py:61
  42.0 1.2 shard_map.114
  43.3 1.0 shard_map.122
  44.2 1.0 shard_map.119
  45.2 1.7 %collective-permute-start.29 = (bf16[3072,128]{1,0:T(8,128)(2,1)S(1)}, bf16[3072,128]{1,0:T(8,128)(2,1)S(1)}, u32[]{:S(2)}, u32[]{:S(2)}) collective-permute-start(bf16[3072,128]{1,0:T(8,128)(2,1)S(1)} %get-tuple-element.93), channel_id=1, source_target_pairs={{0,4},{4,0},{8,12},{12,8},{1,5},{5,1},{9,13},{13,9},{2,6},{6,2},{1... | collective-permute-start | bytes 2359304 | tf_op jit(solution)/shard_map/ppermute | solution.py:27
  48.0 1.5 collective-permute-start.24
  50.0 3.0 %collective-permute-start.19 = (bf16[3072,128]{1,0:T(8,128)(2,1)S(1)}, bf16[3072,128]{1,0:T(8,128)(2,1)S(1)}, u32[]{:S(2)}, u32[]{:S(2)}) collective-permute-start(bf16[3072,128]{1,0:T(8,128)(2,1)S(1)} %get-tuple-element.86), channel_id=1, source_target_pairs={{0,12},{4,8},{8,4},{12,0},{1,13},{5,9},{9,5},{13,1},{2,14},{6,10},... | collective-permute-start | bytes 2359304 | tf_op jit(solution)/shard_map/ppermute | solution.py:27
  53.1 3.4 %shard_map.115 = (bf16[128,2176]{1,0:T(8,128)(2,1)S(1)}, bf16[256,2176]{1,0:T(8,128)(2,1)S(1)}, bf16[128,2176]{1,0:T(8,128)(2,1)S(1)}) custom-call(bf16[256,768]{1,0:T(8,128)(2,1)S(1)} %get-tuple-element.57.refs_0_.refs_2_, bf16[256,768]{1,0:T(8,128)(2,1)S(1)} %get-tuple-element.63.refs_1_.refs_3_, bf16[256,768]{1,0:T(8,128)(2,1)S(1)} %get-tuple-element.64.refs_2_.refs_4_, ...), custom_call_target="tpu_custom_call" | custom-call | flops 3221225472 | bytes 1048576 | tf_op jit(solution)/shard_map/pallas_call | solution.py:61
  58.3 1.8 %shard_map.118 = (bf16[3072,128]{1,0:T(8,128)(2,1)S(1)}, bf16[3072,128]{1,0:T(8,128)(2,1)S(1)}, bf16[3072,128]{1,0:T(8,128)(2,1)S(1)}, bf16[3072,128]{1,0:T(8,128)(2,1)S(1)}) custom-call(bf16[2048,256]{1,0:T(8,128)(2,1)S(1)} %get-tuple-element.78.refs_0_, bf16[2048,256]{1,0:T(8,128)(2,1)S(1)} %get-tuple-element.79.refs_1_, ...), custom_call_target="tpu_custom_call" | custom-call | flops 1610612736 | bytes 1048576 | tf_op jit(solution)/shard_map/pallas_call | solution.py:61
  60.1 13.6 %collective-permute-done.30 = bf16[1536,128]{1,0:T(8,128)(2,1)S(1)} collective-permute-done((bf16[1536,128]{1,0:T(8,128)(2,1)S(1)}, bf16[1536,128]{1,0:T(8,128)(2,1)S(1)}, u32[]{:S(2)}, u32[]{:S(2)}) %collective-permute-start.30) | collective-permute-done | bytes 393248 | tf_op jit(solution)/shard_map/ppermute | solution.py:27
  73.7 3.6 %collective-permute-start.15 = (bf16[3072,128]{1,0:T(8,128)(2,1)S(1)}, bf16[3072,128]{1,0:T(8,128)(2,1)S(1)}, u32[]{:S(2)}, u32[]{:S(2)}) collective-permute-start(bf16[3072,128]{1,0:T(8,128)(2,1)S(1)} %shard_map.121), channel_id=1, source_target_pairs={{0,16},{16,0},{1,17},{17,1},{2,18},{18,2},{3,19},{19,3},{4,20},{20... | collective-permute-start | bytes 2359304 | tf_op jit(solution)/shard_map/ppermute | solution.py:27
  77.4 2.8 %collective-permute-start.13 = (bf16[3072,128]{1,0:T(8,128)(2,1)S(1)}, bf16[3072,128]{1,0:T(8,128)(2,1)S(1)}, u32[]{:S(2)}, u32[]{:S(2)}) collective-permute-start(bf16[3072,128]{1,0:T(8,128)(2,1)S(1)} %get-tuple-element.81), channel_id=1, source_target_pairs={{0,96},{32,64},{64,32},{96,0},{1,97},{33,65},{65,33},{97,1},{2,98}... | collective-permute-start | bytes 2359304 | tf_op jit(solution)/shard_map/ppermute | solution.py:27
  80.5 3.1 %collective-permute-start.31 = (bf16[2304,128]{1,0:T(8,128)(2,1)S(1)}, bf16[2304,128]{1,0:T(8,128)(2,1)S(1)}, u32[]{:S(2)}, u32[]{:S(2)}) collective-permute-start(bf16[2304,128]{1,0:T(8,128)(2,1)S(1)} %pad_maximum_fusion.1), channel_id=1, source_target_pairs={{0,12},{4,8},{8,4},{12,0},{1,13},{5,9},{9,5},{13,1},{2,14},{6,10},... | collective-permute-start | bytes 1769480 | tf_op jit(solution)/shard_map/ppermute | solution.py:27
  84.5 10.2 %collective-permute-done.15 = bf16[3072,128]{1,0:T(8,128)(2,1)S(1)} collective-permute-done((bf16[3072,128]{1,0:T(8,128)(2,1)S(1)}, bf16[3072,128]{1,0:T(8,128)(2,1)S(1)}, u32[]{:S(2)}, u32[]{:S(2)}) %collective-permute-start.15) | collective-permute-done | bytes 786464 | tf_op jit(solution)/shard_map/ppermute | solution.py:27
  94.6 1.6 collective-permute-start.20
  96.3 2.7 %collective-permute-done.13 = bf16[3072,128]{1,0:T(8,128)(2,1)S(1)} collective-permute-done((bf16[3072,128]{1,0:T(8,128)(2,1)S(1)}, bf16[3072,128]{1,0:T(8,128)(2,1)S(1)}, u32[]{:S(2)}, u32[]{:S(2)}) %collective-permute-start.13) | collective-permute-done | bytes 786464 | tf_op jit(solution)/shard_map/ppermute | solution.py:27
  99.1 1.6 collective-permute-start.21
  100.8 8.1 %collective-permute-done.21 = bf16[768,128]{1,0:T(8,128)(2,1)S(1)} collective-permute-done((bf16[768,128]{1,0:T(8,128)(2,1)S(1)}, bf16[768,128]{1,0:T(8,128)(2,1)S(1)}, u32[]{:S(2)}, u32[]{:S(2)}) %collective-permute-start.21) | collective-permute-done | bytes 196640 | tf_op jit(solution)/shard_map/ppermute | solution.py:27
  108.9 1.5 collective-permute-start.16
  110.5 4.5 %collective-permute-done.16 = bf16[768,128]{1,0:T(8,128)(2,1)S(1)} collective-permute-done((bf16[768,128]{1,0:T(8,128)(2,1)S(1)}, bf16[768,128]{1,0:T(8,128)(2,1)S(1)}, u32[]{:S(2)}, u32[]{:S(2)}) %collective-permute-start.16) | collective-permute-done | bytes 196640 | tf_op jit(solution)/shard_map/ppermute | solution.py:27
  114.9 1.5 collective-permute-start.14
  117.3 2.2 %collective-permute-start.22 = (bf16[1152,128]{1,0:T(8,128)(2,1)S(1)}, bf16[1152,128]{1,0:T(8,128)(2,1)S(1)}, u32[]{:S(2)}, u32[]{:S(2)}) collective-permute-start(bf16[1152,128]{1,0:T(8,128)(2,1)S(1)} %pad_maximum_fusion.3), channel_id=1, source_target_pairs={{0,96},{32,64},{64,32},{96,0},{1,97},{33,65},{65,33},{97,1},{2,98}... | collective-permute-start | bytes 884744 | tf_op jit(solution)/shard_map/ppermute | solution.py:27
  119.4 3.6 %collective-permute-done.14 = bf16[1536,128]{1,0:T(8,128)(2,1)S(1)} collective-permute-done((bf16[1536,128]{1,0:T(8,128)(2,1)S(1)}, bf16[1536,128]{1,0:T(8,128)(2,1)S(1)}, u32[]{:S(2)}, u32[]{:S(2)}) %collective-permute-start.14) | collective-permute-done | bytes 393248 | tf_op jit(solution)/shard_map/ppermute | solution.py:27
  123.1 3.6 %collective-permute-start.17 = (bf16[1152,128]{1,0:T(8,128)(2,1)S(1)}, bf16[1152,128]{1,0:T(8,128)(2,1)S(1)}, u32[]{:S(2)}, u32[]{:S(2)}) collective-permute-start(bf16[1152,128]{1,0:T(8,128)(2,1)S(1)} %pad_maximum_fusion.2), channel_id=1, source_target_pairs={{0,12},{4,8},{8,4},{12,0},{1,13},{5,9},{9,5},{13,1},{2,14},{6,10},... | collective-permute-start | bytes 884744 | tf_op jit(solution)/shard_map/ppermute | solution.py:27
  126.9 1.8 %collective-permute-start.32 = (bf16[1152,128]{1,0:T(8,128)(2,1)S(1)}, bf16[1152,128]{1,0:T(8,128)(2,1)S(1)}, u32[]{:S(2)}, u32[]{:S(2)}) collective-permute-start(bf16[1152,128]{1,0:T(8,128)(2,1)S(1)} %pad_maximum_fusion.5), channel_id=1, source_target_pairs={{0,32},{32,0},{64,96},{96,64},{1,33},{33,1},{65,97},{97,65},{2,34}... | collective-permute-start | bytes 884744 | tf_op jit(solution)/shard_map/ppermute | solution.py:27
  129.7 1.7 %collective-permute-done.17 = bf16[1152,128]{1,0:T(8,128)(2,1)S(1)} collective-permute-done((bf16[1152,128]{1,0:T(8,128)(2,1)S(1)}, bf16[1152,128]{1,0:T(8,128)(2,1)S(1)}, u32[]{:S(2)}, u32[]{:S(2)}) %collective-permute-start.17) | collective-permute-done | bytes 294944 | tf_op jit(solution)/shard_map/ppermute | solution.py:27
  131.9 3.6 %collective-permute-done.23 = bf16[576,128]{1,0:T(8,128)(2,1)S(1)} collective-permute-done((bf16[576,128]{1,0:T(8,128)(2,1)S(1)}, bf16[576,128]{1,0:T(8,128)(2,1)S(1)}, u32[]{:S(2)}, u32[]{:S(2)}) %collective-permute-start.23) | collective-permute-done | bytes 147488 | tf_op jit(solution)/shard_map/ppermute | solution.py:27
  135.6 1.7 %collective-permute-done.18 = bf16[576,128]{1,0:T(8,128)(2,1)S(1)} collective-permute-done((bf16[576,128]{1,0:T(8,128)(2,1)S(1)}, bf16[576,128]{1,0:T(8,128)(2,1)S(1)}, u32[]{:S(2)}, u32[]{:S(2)}) %collective-permute-start.18) | collective-permute-done | bytes 147488 | tf_op jit(solution)/shard_map/ppermute | solution.py:27
  137.4 3.3 %collective-permute-start.34 = (bf16[384,128]{1,0:T(8,128)(2,1)S(1)}, bf16[384,128]{1,0:T(8,128)(2,1)S(1)}, u32[]{:S(2)}, u32[]{:S(2)}) collective-permute-start(bf16[384,128]{1,0:T(8,128)(2,1)S(1)} %pad_maximum_fusion.11), channel_id=1, source_target_pairs={{0,16},{16,0},{1,17},{17,1},{2,18},{18,2},{3,19},{19,3},{4,20},{20... | collective-permute-start | bytes 294920 | tf_op jit(solution)/shard_map/ppermute | solution.py:27
  140.7 2.8 %collective-permute-start.37 = (bf16[96,128]{1,0:T(8,128)(2,1)S(1)}, bf16[96,128]{1,0:T(8,128)(2,1)S(1)}, u32[]{:S(2)}, u32[]{:S(2)}) collective-permute-start(bf16[96,128]{1,0:T(8,128)(2,1)S(1)} %get-tuple-element.111), channel_id=1, source_target_pairs={{0,12},{4,8},{8,4},{12,0},{1,13},{5,9},{9,5},{13,1},{2,14},{6,10},... | collective-permute-start | bytes 73736 | tf_op jit(solution)/shard_map/ppermute | solution.py:27
  143.7 2.9 %collective-permute-start.33 = (bf16[576,128]{1,0:T(8,128)(2,1)S(1)}, bf16[576,128]{1,0:T(8,128)(2,1)S(1)}, u32[]{:S(2)}, u32[]{:S(2)}) collective-permute-start(bf16[576,128]{1,0:T(8,128)(2,1)S(1)} %pad_maximum_fusion.9), channel_id=1, source_target_pairs={{0,96},{32,64},{64,32},{96,0},{1,97},{33,65},{65,33},{97,1},{2,98}... | collective-permute-start | bytes 442376 | tf_op jit(solution)/shard_map/ppermute | solution.py:27
  146.8 3.3 %collective-permute-done.33 = bf16[576,128]{1,0:T(8,128)(2,1)S(1)} collective-permute-done((bf16[576,128]{1,0:T(8,128)(2,1)S(1)}, bf16[576,128]{1,0:T(8,128)(2,1)S(1)}, u32[]{:S(2)}, u32[]{:S(2)}) %collective-permute-start.33) | collective-permute-done | bytes 147488 | tf_op jit(solution)/shard_map/ppermute | solution.py:27
  150.2 2.9 %collective-permute-done.28 = bf16[576,128]{1,0:T(8,128)(2,1)S(1)} collective-permute-done((bf16[576,128]{1,0:T(8,128)(2,1)S(1)}, bf16[576,128]{1,0:T(8,128)(2,1)S(1)}, u32[]{:S(2)}, u32[]{:S(2)}) %collective-permute-start.28) | collective-permute-done | bytes 147488 | tf_op jit(solution)/shard_map/ppermute | solution.py:27
  154.2 1.2 shard_map.117
  155.4 3.4 %collective-permute-done.36.refs_10_ = bf16[96,128]{1,0:T(8,128)(2,1)S(1)} collective-permute-done((bf16[96,128]{1,0:T(8,128)(2,1)S(1)}, bf16[96,128]{1,0:T(8,128)(2,1)S(1)}, u32[]{:S(2)}, u32[]{:S(2)}) %collective-permute-start.36) | collective-permute-done | bytes 24608 | tf_op jit(solution)/shard_map/ppermute | solution.py:27
  158.8 1.2 collective-permute-done.35.refs_9_
  (111 shorter events, 13.3 us)
Async XLA Ops:
  0.6 30.3 %copy-start.6 = (bf16[128,2048]{1,0:T(8,128)(2,1)S(1)}, bf16[128,2048]{1,0:T(8,128)(2,1)}, u32[]{:S(2)}) copy-start(bf16[128,2048]{1,0:T(8,128)(2,1)} %x0.1) | copy-start | bytes 1572868
  0.6 14.2 %collective-permute-start.9 = (bf16[128,2048]{1,0:T(8,128)(2,1)}, bf16[128,2048]{1,0:T(8,128)(2,1)S(1)}, u32[]{:S(2)}, u32[]{:S(2)}) collective-permute-start(bf16[128,2048]{1,0:T(8,128)(2,1)} %x0.1), channel_id=1, source_target_pairs={{0,2},{2,0},{1,3},{3,1},{4,6},{6,4},{5,7},{7,5},{8,10},{10,8},{9,1... | collective-permute-start | bytes 1572872 | tf_op jit(solution)/shard_map/ppermute | solution.py:27
  2.7 27.7 %collective-permute-start.2 = (bf16[128,2048]{1,0:T(8,128)(2,1)}, bf16[128,2048]{1,0:T(8,128)(2,1)S(1)}, u32[]{:S(2)}, u32[]{:S(2)}) collective-permute-start(bf16[128,2048]{1,0:T(8,128)(2,1)} %x0.1), channel_id=1, source_target_pairs={{0,1},{1,0},{2,3},{3,2},{4,5},{5,4},{6,7},{7,6},{8,9},{9,8},{10,11... | collective-permute-start | bytes 1572872 | tf_op jit(solution)/shard_map/ppermute | solution.py:27
  2.8 0.7 copy-start.7
  3.4 0.7 copy-start.9
  4.1 13.6 %collective-permute-start.1 = (f32[8,128]{1,0:T(8,128)S(1)}, f32[8,128]{1,0:T(8,128)S(1)}, u32[]{:S(2)}, u32[]{:S(2)}) collective-permute-start(f32[8,128]{1,0:T(8,128)S(1)} %get-tuple-element.53), channel_id=1, source_target_pairs={{0,1},{1,0},{2,3},{3,2},{4,5},{5,4},{6,7},{7,6},{8,9},{9,8},{10,11... | collective-permute-start | bytes 12296 | tf_op jit(solution)/shard_map/ppermute | solution.py:27
  4.7 32.0 %collective-permute-start = (bf16[128,2048]{1,0:T(8,128)(2,1)}, bf16[128,2048]{1,0:T(8,128)(2,1)S(1)}, u32[]{:S(2)}, u32[]{:S(2)}) collective-permute-start(bf16[128,2048]{1,0:T(8,128)(2,1)} %refs_2_.7), channel_id=1, source_target_pairs={{0,1},{1,0},{2,3},{3,2},{4,5},{5,4},{6,7},{7,6},{8,9},{9,8},{10,11... | collective-permute-start | bytes 1572872 | tf_op jit(solution)/shard_map/ppermute | solution.py:27
  14.9 24.9 %collective-permute-start.10 = (bf16[128,2048]{1,0:T(8,128)(2,1)S(1)}, bf16[128,2048]{1,0:T(8,128)(2,1)S(1)}, u32[]{:S(2)}, u32[]{:S(2)}) collective-permute-start(bf16[128,2048]{1,0:T(8,128)(2,1)S(1)} %collective-permute-done.9.x0), channel_id=1, source_target_pairs={{0,1},{1,0},{2,3},{3,2},{4,5},{5,4},{6,7},{7,6},{8,9},{9,8},{10,11... | collective-permute-start | bytes 1572872 | tf_op jit(solution)/shard_map/ppermute | solution.py:27
  16.0 9.3 %collective-permute-start.3 = (bf16[128,1024]{1,0:T(8,128)(2,1)S(1)}, bf16[128,1024]{1,0:T(8,128)(2,1)S(1)}, u32[]{:S(2)}, u32[]{:S(2)}) collective-permute-start(bf16[128,1024]{1,0:T(8,128)(2,1)S(1)} %get-tuple-element.118), channel_id=1, source_target_pairs={{0,2},{2,0},{1,3},{3,1},{4,6},{6,4},{5,7},{7,5},{8,10},{10,8},{9,1... | collective-permute-start | bytes 786440 | tf_op jit(solution)/shard_map/ppermute | solution.py:27
  17.8 12.6 %collective-permute-start.4 = (bf16[128,1024]{1,0:T(8,128)(2,1)S(1)}, bf16[128,1024]{1,0:T(8,128)(2,1)S(1)}, u32[]{:S(2)}, u32[]{:S(2)}) collective-permute-start(bf16[128,1024]{1,0:T(8,128)(2,1)S(1)} %get-tuple-element.117), channel_id=1, source_target_pairs={{0,2},{2,0},{1,3},{3,1},{4,6},{6,4},{5,7},{7,5},{8,10},{10,8},{9,1... | collective-permute-start | bytes 786440 | tf_op jit(solution)/shard_map/ppermute | solution.py:27
  25.2 14.1 %collective-permute-start.7 = (f32[8,128]{1,0:T(8,128)S(1)}, f32[8,128]{1,0:T(8,128)S(1)}, u32[]{:S(2)}, u32[]{:S(2)}) collective-permute-start(f32[8,128]{1,0:T(8,128)S(1)} %get-tuple-element.58), channel_id=1, source_target_pairs={{0,2},{1,3},{2,0},{3,1},{4,6},{5,7},{6,4},{7,5},{8,10},{9,11},{10,... | collective-permute-start | bytes 12296 | tf_op jit(solution)/shard_map/ppermute | solution.py:27
  30.4 11.6 %collective-permute-start.5 = (bf16[128,1024]{1,0:T(8,128)(2,1)S(1)}, bf16[128,1024]{1,0:T(8,128)(2,1)S(1)}, u32[]{:S(2)}, u32[]{:S(2)}) collective-permute-start(bf16[128,1024]{1,0:T(8,128)(2,1)S(1)} %collective-permute-done.3.refs_0_.refs_4_), channel_id=1, source_target_pairs={{0,1},{1,0},{2,3},{3,2},{4,5},{5,4},{6,7},{7,6},{8,9},{9,8},{10,11... | collective-permute-start | bytes 786440 | tf_op jit(solution)/shard_map/ppermute | solution.py:27
  30.4 11.6 %collective-permute-start.6 = (bf16[128,1024]{1,0:T(8,128)(2,1)S(1)}, bf16[128,1024]{1,0:T(8,128)(2,1)S(1)}, u32[]{:S(2)}, u32[]{:S(2)}) collective-permute-start(bf16[128,1024]{1,0:T(8,128)(2,1)S(1)} %collective-permute-done.4.refs_1_.refs_4_), channel_id=1, source_target_pairs={{0,1},{1,0},{2,3},{3,2},{4,5},{5,4},{6,7},{7,6},{8,9},{9,8},{10,11... | collective-permute-start | bytes 786440 | tf_op jit(solution)/shard_map/ppermute | solution.py:27
  30.9 1.9 %copy-start.2 = (bf16[1,2048,768]{2,1,0:T(8,128)(2,1)S(1)}, bf16[1,2048,768]{2,1,0:T(8,128)(2,1)}, u32[]{:S(2)}) copy-start(bf16[1,2048,768]{2,1,0:T(8,128)(2,1)} %param.11) | copy-start | bytes 9437188
  32.8 1.9 %copy-start.4 = (bf16[1,2048,768]{2,1,0:T(8,128)(2,1)S(1)}, bf16[1,2048,768]{2,1,0:T(8,128)(2,1)}, u32[]{:S(2)}) copy-start(bf16[1,2048,768]{2,1,0:T(8,128)(2,1)} %param.12) | copy-start | bytes 9437188
  34.7 3.4 %copy-start = (bf16[128,2048]{1,0:T(8,128)(2,1)S(1)}, bf16[128,2048]{1,0:T(8,128)(2,1)}, u32[]{:S(2)}) copy-start(bf16[128,2048]{1,0:T(8,128)(2,1)} %refs_2_.7) | copy-start | bytes 1572868
  34.7 3.4 %copy-start.1 = (bf16[1,768,2048]{2,1,0:T(8,128)(2,1)S(1)}, bf16[1,768,2048]{2,1,0:T(8,128)(2,1)}, u32[]{:S(2)}) copy-start(bf16[1,768,2048]{2,1,0:T(8,128)(2,1)} %param.13) | copy-start | bytes 9437188
  34.7 5.1 %copy-start.5 = (bf16[1,2048,768]{2,1,0:T(8,128)(2,1)S(1)}, bf16[1,2048,768]{2,1,0:T(8,128)(2,1)}, u32[]{:S(2)}) copy-start(bf16[1,2048,768]{2,1,0:T(8,128)(2,1)} %param.12) | copy-start | bytes 9437188
  36.7 3.1 %collective-permute-start.8 = (f32[8,128]{1,0:T(8,128)S(1)}, f32[8,128]{1,0:T(8,128)S(1)}, u32[]{:S(2)}, u32[]{:S(2)}) collective-permute-start(f32[8,128]{1,0:T(8,128)S(1)} %get-tuple-element.59), channel_id=1, source_target_pairs={{0,3},{1,2},{2,1},{3,0},{4,7},{5,6},{6,5},{7,4},{8,11},{9,10},{10,... | collective-permute-start | bytes 12296 | tf_op jit(solution)/shard_map/ppermute | solution.py:27
  38.2 1.9 %copy-start.3 = (bf16[1,2048,768]{2,1,0:T(8,128)(2,1)S(1)}, bf16[1,2048,768]{2,1,0:T(8,128)(2,1)}, u32[]{:S(2)}) copy-start(bf16[1,2048,768]{2,1,0:T(8,128)(2,1)} %param.11) | copy-start | bytes 9437188
  45.2 35.0 %collective-permute-start.29 = (bf16[3072,128]{1,0:T(8,128)(2,1)S(1)}, bf16[3072,128]{1,0:T(8,128)(2,1)S(1)}, u32[]{:S(2)}, u32[]{:S(2)}) collective-permute-start(bf16[3072,128]{1,0:T(8,128)(2,1)S(1)} %get-tuple-element.93), channel_id=1, source_target_pairs={{0,4},{4,0},{8,12},{12,8},{1,5},{5,1},{9,13},{13,9},{2,6},{6,2},{1... | collective-permute-start | bytes 2359304 | tf_op jit(solution)/shard_map/ppermute | solution.py:27
  47.5 26.2 %collective-permute-start.30 = (bf16[1536,128]{1,0:T(8,128)(2,1)S(1)}, bf16[1536,128]{1,0:T(8,128)(2,1)S(1)}, u32[]{:S(2)}, u32[]{:S(2)}) collective-permute-start(bf16[1536,128]{1,0:T(8,128)(2,1)S(1)} %get-tuple-element.95), channel_id=1, source_target_pairs={{0,4},{4,0},{8,12},{12,8},{1,5},{5,1},{9,13},{13,9},{2,6},{6,2},{1... | collective-permute-start | bytes 1179656 | tf_op jit(solution)/shard_map/ppermute | solution.py:27
  48.0 32.5 %collective-permute-start.24 = (bf16[3072,128]{1,0:T(8,128)(2,1)S(1)}, bf16[3072,128]{1,0:T(8,128)(2,1)S(1)}, u32[]{:S(2)}, u32[]{:S(2)}) collective-permute-start(bf16[3072,128]{1,0:T(8,128)(2,1)S(1)} %get-tuple-element.89), channel_id=1, source_target_pairs={{0,32},{32,0},{64,96},{96,64},{1,33},{33,1},{65,97},{97,65},{2,34}... | collective-permute-start | bytes 2359304 | tf_op jit(solution)/shard_map/ppermute | solution.py:27
  49.5 27.8 %collective-permute-start.25 = (bf16[1536,128]{1,0:T(8,128)(2,1)S(1)}, bf16[1536,128]{1,0:T(8,128)(2,1)S(1)}, u32[]{:S(2)}, u32[]{:S(2)}) collective-permute-start(bf16[1536,128]{1,0:T(8,128)(2,1)S(1)} %get-tuple-element.91), channel_id=1, source_target_pairs={{0,32},{32,0},{64,96},{96,64},{1,33},{33,1},{65,97},{97,65},{2,34}... | collective-permute-start | bytes 1179656 | tf_op jit(solution)/shard_map/ppermute | solution.py:27
  50.0 33.7 %collective-permute-start.19 = (bf16[3072,128]{1,0:T(8,128)(2,1)S(1)}, bf16[3072,128]{1,0:T(8,128)(2,1)S(1)}, u32[]{:S(2)}, u32[]{:S(2)}) collective-permute-start(bf16[3072,128]{1,0:T(8,128)(2,1)S(1)} %get-tuple-element.86), channel_id=1, source_target_pairs={{0,12},{4,8},{8,4},{12,0},{1,13},{5,9},{9,5},{13,1},{2,14},{6,10},... | collective-permute-start | bytes 2359304 | tf_op jit(solution)/shard_map/ppermute | solution.py:27
  73.7 20.9 %collective-permute-start.15 = (bf16[3072,128]{1,0:T(8,128)(2,1)S(1)}, bf16[3072,128]{1,0:T(8,128)(2,1)S(1)}, u32[]{:S(2)}, u32[]{:S(2)}) collective-permute-start(bf16[3072,128]{1,0:T(8,128)(2,1)S(1)} %shard_map.121), channel_id=1, source_target_pairs={{0,16},{16,0},{1,17},{17,1},{2,18},{18,2},{3,19},{19,3},{4,20},{20... | collective-permute-start | bytes 2359304 | tf_op jit(solution)/shard_map/ppermute | solution.py:27
  77.4 21.7 %collective-permute-start.13 = (bf16[3072,128]{1,0:T(8,128)(2,1)S(1)}, bf16[3072,128]{1,0:T(8,128)(2,1)S(1)}, u32[]{:S(2)}, u32[]{:S(2)}) collective-permute-start(bf16[3072,128]{1,0:T(8,128)(2,1)S(1)} %get-tuple-element.81), channel_id=1, source_target_pairs={{0,96},{32,64},{64,32},{96,0},{1,97},{33,65},{65,33},{97,1},{2,98}... | collective-permute-start | bytes 2359304 | tf_op jit(solution)/shard_map/ppermute | solution.py:27
  80.3 36.2 %collective-permute-start.11 = (bf16[256,2176]{1,0:T(8,128)(2,1)S(1)}, bf16[256,2176]{1,0:T(8,128)(2,1)S(1)}, u32[]{:S(2)}, u32[]{:S(2)}) collective-permute-start(bf16[256,2176]{1,0:T(8,128)(2,1)S(1)} %get-tuple-element.74), channel_id=1, source_target_pairs={{0,1},{1,0},{2,3},{3,2},{4,5},{5,4},{6,7},{7,6},{8,9},{9,8},{10,11... | collective-permute-start | bytes 3342344 | tf_op jit(solution)/shard_map/ppermute | solution.py:27
  80.5 46.2 %collective-permute-start.31 = (bf16[2304,128]{1,0:T(8,128)(2,1)S(1)}, bf16[2304,128]{1,0:T(8,128)(2,1)S(1)}, u32[]{:S(2)}, u32[]{:S(2)}) collective-permute-start(bf16[2304,128]{1,0:T(8,128)(2,1)S(1)} %pad_maximum_fusion.1), channel_id=1, source_target_pairs={{0,12},{4,8},{8,4},{12,0},{1,13},{5,9},{9,5},{13,1},{2,14},{6,10},... | collective-permute-start | bytes 1769480 | tf_op jit(solution)/shard_map/ppermute | solution.py:27
  83.8 44.9 %collective-permute-start.26 = (bf16[2304,128]{1,0:T(8,128)(2,1)S(1)}, bf16[2304,128]{1,0:T(8,128)(2,1)S(1)}, u32[]{:S(2)}, u32[]{:S(2)}) collective-permute-start(bf16[2304,128]{1,0:T(8,128)(2,1)S(1)} %pad_maximum_fusion), channel_id=1, source_target_pairs={{0,96},{32,64},{64,32},{96,0},{1,97},{33,65},{65,33},{97,1},{2,98}... | collective-permute-start | bytes 1769480 | tf_op jit(solution)/shard_map/ppermute | solution.py:27
  94.6 22.5 %collective-permute-start.20 = (bf16[1536,128]{1,0:T(8,128)(2,1)S(1)}, bf16[1536,128]{1,0:T(8,128)(2,1)S(1)}, u32[]{:S(2)}, u32[]{:S(2)}) collective-permute-start(bf16[1536,128]{1,0:T(8,128)(2,1)S(1)} %add_convert_fusion.3), channel_id=1, source_target_pairs={{0,4},{4,0},{8,12},{12,8},{1,5},{5,1},{9,13},{13,9},{2,6},{6,2},{1... | collective-permute-start | bytes 1179656 | tf_op jit(solution)/shard_map/ppermute | solution.py:27
  99.1 9.9 %collective-permute-start.21 = (bf16[768,128]{1,0:T(8,128)(2,1)S(1)}, bf16[768,128]{1,0:T(8,128)(2,1)S(1)}, u32[]{:S(2)}, u32[]{:S(2)}) collective-permute-start(bf16[768,128]{1,0:T(8,128)(2,1)S(1)} %add_convert_fusion.9), channel_id=1, source_target_pairs={{0,4},{4,0},{8,12},{12,8},{1,5},{5,1},{9,13},{13,9},{2,6},{6,2},{1... | collective-permute-start | bytes 589832 | tf_op jit(solution)/shard_map/ppermute | solution.py:27
  108.9 6.0 %collective-permute-start.16 = (bf16[768,128]{1,0:T(8,128)(2,1)S(1)}, bf16[768,128]{1,0:T(8,128)(2,1)S(1)}, u32[]{:S(2)}, u32[]{:S(2)}) collective-permute-start(bf16[768,128]{1,0:T(8,128)(2,1)S(1)} %add_convert_fusion.11), channel_id=1, source_target_pairs={{0,32},{32,0},{64,96},{96,64},{1,33},{33,1},{65,97},{97,65},{2,34}... | collective-permute-start | bytes 589832 | tf_op jit(solution)/shard_map/ppermute | solution.py:27
  114.9 8.1 %collective-permute-start.14 = (bf16[1536,128]{1,0:T(8,128)(2,1)S(1)}, bf16[1536,128]{1,0:T(8,128)(2,1)S(1)}, u32[]{:S(2)}, u32[]{:S(2)}) collective-permute-start(bf16[1536,128]{1,0:T(8,128)(2,1)S(1)} %add_convert_fusion.4), channel_id=1, source_target_pairs={{0,32},{32,0},{64,96},{96,64},{1,33},{33,1},{65,97},{97,65},{2,34}... | collective-permute-start | bytes 1179656 | tf_op jit(solution)/shard_map/ppermute | solution.py:27
  116.6 37.5 %collective-permute-start.12 = (bf16[128,2176]{1,0:T(8,128)(2,1)S(1)}, bf16[128,2176]{1,0:T(8,128)(2,1)S(1)}, u32[]{:S(2)}, u32[]{:S(2)}) collective-permute-start(bf16[128,2176]{1,0:T(8,128)(2,1)S(1)} %add_convert_fusion), channel_id=1, source_target_pairs={{0,2},{2,0},{1,3},{3,1},{4,6},{6,4},{5,7},{7,5},{8,10},{10,8},{9,1... | collective-permute-start | bytes 1671176 | tf_op jit(solution)/shard_map/ppermute | solution.py:27
  117.3 11.7 %collective-permute-start.22 = (bf16[1152,128]{1,0:T(8,128)(2,1)S(1)}, bf16[1152,128]{1,0:T(8,128)(2,1)S(1)}, u32[]{:S(2)}, u32[]{:S(2)}) collective-permute-start(bf16[1152,128]{1,0:T(8,128)(2,1)S(1)} %pad_maximum_fusion.3), channel_id=1, source_target_pairs={{0,96},{32,64},{64,32},{96,0},{1,97},{33,65},{65,33},{97,1},{2,98}... | collective-permute-start | bytes 884744 | tf_op jit(solution)/shard_map/ppermute | solution.py:27
  123.1 8.3 %collective-permute-start.17 = (bf16[1152,128]{1,0:T(8,128)(2,1)S(1)}, bf16[1152,128]{1,0:T(8,128)(2,1)S(1)}, u32[]{:S(2)}, u32[]{:S(2)}) collective-permute-start(bf16[1152,128]{1,0:T(8,128)(2,1)S(1)} %pad_maximum_fusion.2), channel_id=1, source_target_pairs={{0,12},{4,8},{8,4},{12,0},{1,13},{5,9},{9,5},{13,1},{2,14},{6,10},... | collective-permute-start | bytes 884744 | tf_op jit(solution)/shard_map/ppermute | solution.py:27
  126.9 16.6 %collective-permute-start.32 = (bf16[1152,128]{1,0:T(8,128)(2,1)S(1)}, bf16[1152,128]{1,0:T(8,128)(2,1)S(1)}, u32[]{:S(2)}, u32[]{:S(2)}) collective-permute-start(bf16[1152,128]{1,0:T(8,128)(2,1)S(1)} %pad_maximum_fusion.5), channel_id=1, source_target_pairs={{0,32},{32,0},{64,96},{96,64},{1,33},{33,1},{65,97},{97,65},{2,34}... | collective-permute-start | bytes 884744 | tf_op jit(solution)/shard_map/ppermute | solution.py:27
  128.9 17.7 %collective-permute-start.27 = (bf16[1152,128]{1,0:T(8,128)(2,1)S(1)}, bf16[1152,128]{1,0:T(8,128)(2,1)S(1)}, u32[]{:S(2)}, u32[]{:S(2)}) collective-permute-start(bf16[1152,128]{1,0:T(8,128)(2,1)S(1)} %pad_maximum_fusion.4), channel_id=1, source_target_pairs={{0,4},{4,0},{8,12},{12,8},{1,5},{5,1},{9,13},{13,9},{2,6},{6,2},{1... | collective-permute-start | bytes 884744 | tf_op jit(solution)/shard_map/ppermute | solution.py:27
  129.1 6.4 %collective-permute-start.23 = (bf16[576,128]{1,0:T(8,128)(2,1)S(1)}, bf16[576,128]{1,0:T(8,128)(2,1)S(1)}, u32[]{:S(2)}, u32[]{:S(2)}) collective-permute-start(bf16[576,128]{1,0:T(8,128)(2,1)S(1)} %pad_maximum_fusion.7), channel_id=1, source_target_pairs={{0,32},{32,0},{64,96},{96,64},{1,33},{33,1},{65,97},{97,65},{2,34}... | collective-permute-start | bytes 442376 | tf_op jit(solution)/shard_map/ppermute | solution.py:27
  131.6 5.7 %collective-permute-start.18 = (bf16[576,128]{1,0:T(8,128)(2,1)S(1)}, bf16[576,128]{1,0:T(8,128)(2,1)S(1)}, u32[]{:S(2)}, u32[]{:S(2)}) collective-permute-start(bf16[576,128]{1,0:T(8,128)(2,1)S(1)} %pad_maximum_fusion.6), channel_id=1, source_target_pairs={{0,4},{4,0},{8,12},{12,8},{1,5},{5,1},{9,13},{13,9},{2,6},{6,2},{1... | collective-permute-start | bytes 442376 | tf_op jit(solution)/shard_map/ppermute | solution.py:27
  137.4 21.4 %collective-permute-start.34 = (bf16[384,128]{1,0:T(8,128)(2,1)S(1)}, bf16[384,128]{1,0:T(8,128)(2,1)S(1)}, u32[]{:S(2)}, u32[]{:S(2)}) collective-permute-start(bf16[384,128]{1,0:T(8,128)(2,1)S(1)} %pad_maximum_fusion.11), channel_id=1, source_target_pairs={{0,16},{16,0},{1,17},{17,1},{2,18},{18,2},{3,19},{19,3},{4,20},{20... | collective-permute-start | bytes 294920 | tf_op jit(solution)/shard_map/ppermute | solution.py:27
  140.7 14.7 %collective-permute-start.37 = (bf16[96,128]{1,0:T(8,128)(2,1)S(1)}, bf16[96,128]{1,0:T(8,128)(2,1)S(1)}, u32[]{:S(2)}, u32[]{:S(2)}) collective-permute-start(bf16[96,128]{1,0:T(8,128)(2,1)S(1)} %get-tuple-element.111), channel_id=1, source_target_pairs={{0,12},{4,8},{8,4},{12,0},{1,13},{5,9},{9,5},{13,1},{2,14},{6,10},... | collective-permute-start | bytes 73736 | tf_op jit(solution)/shard_map/ppermute | solution.py:27
  143.7 6.4 %collective-permute-start.33 = (bf16[576,128]{1,0:T(8,128)(2,1)S(1)}, bf16[576,128]{1,0:T(8,128)(2,1)S(1)}, u32[]{:S(2)}, u32[]{:S(2)}) collective-permute-start(bf16[576,128]{1,0:T(8,128)(2,1)S(1)} %pad_maximum_fusion.9), channel_id=1, source_target_pairs={{0,96},{32,64},{64,32},{96,0},{1,97},{33,65},{65,33},{97,1},{2,98}... | collective-permute-start | bytes 442376 | tf_op jit(solution)/shard_map/ppermute | solution.py:27
  146.7 7.5 %copy-start.8 = (s32[128,2]{0,1:T(2,128)S(1)}, s32[128,2]{0,1:T(2,128)}, u32[]{:S(2)}) copy-start(s32[128,2]{0,1:T(2,128)} %param.9) | copy-start | bytes 3076
  146.7 6.4 %collective-permute-start.28 = (bf16[576,128]{1,0:T(8,128)(2,1)S(1)}, bf16[576,128]{1,0:T(8,128)(2,1)S(1)}, u32[]{:S(2)}, u32[]{:S(2)}) collective-permute-start(bf16[576,128]{1,0:T(8,128)(2,1)S(1)} %pad_maximum_fusion.8), channel_id=1, source_target_pairs={{0,12},{4,8},{8,4},{12,0},{1,13},{5,9},{9,5},{13,1},{2,14},{6,10},... | collective-permute-start | bytes 442376 | tf_op jit(solution)/shard_map/ppermute | solution.py:27
  153.2 6.7 %collective-permute-start.35 = (bf16[576,128]{1,0:T(8,128)(2,1)S(1)}, bf16[576,128]{1,0:T(8,128)(2,1)S(1)}, u32[]{:S(2)}, u32[]{:S(2)}) collective-permute-start(bf16[576,128]{1,0:T(8,128)(2,1)S(1)} %pad_maximum_fusion.10), channel_id=1, source_target_pairs={{0,16},{16,0},{1,17},{17,1},{2,18},{18,2},{3,19},{19,3},{4,20},{20... | collective-permute-start | bytes 442376 | tf_op jit(solution)/shard_map/ppermute | solution.py:27
  153.6 5.1 %collective-permute-start.36 = (bf16[96,128]{1,0:T(8,128)(2,1)S(1)}, bf16[96,128]{1,0:T(8,128)(2,1)S(1)}, u32[]{:S(2)}, u32[]{:S(2)}) collective-permute-start(bf16[96,128]{1,0:T(8,128)(2,1)S(1)} %get-tuple-element.113), channel_id=1, source_target_pairs={{0,96},{32,64},{64,32},{96,0},{1,97},{33,65},{65,33},{97,1},{2,98}... | collective-permute-start | bytes 73736 | tf_op jit(solution)/shard_map/ppermute | solution.py:27

commit v6 on v4

--- a/solution.py
+++ b/solution.py
@@ -14,8 +14,7 @@
 EVERY = ("x", "zh", "y", "zl", "c")
 XA, XB, YA, YB, Z = ("x", 1), ("x", 3), ("y", 1), ("y", 3), ("zh", 1)
 ORDERS = ((XA, XB, YA, YB, Z), (YA, YB, XA, XB, Z), (XB, XA, YB, YA, Z), (YB, YA, XB, XA, Z))
-DOWN_ORDERS = ORDERS[:2] + ((Z, XA, YB, YA, XB), (Z, YA, XB, XA, YB))
-CHAINS = (2, 3, 0, 1)
+CHAINS = (0, 1, 2, 3)
 BLOCKS = 32
 HALF = BLOCKS // 2
 PIECE = 128
@@ -116,10 +115,9 @@
     size = hta.shape[0] // BLOCKS
     rows = hta.shape[1]
     for q in range(2):
-        out = outs[q % len(outs)]
-        base = q * (out.shape[0] // 2) if len(outs) == 1 else 0
+        out = outs[q]
         for b in range(HALF):
-            start = pl.multiple_of(block_at(DOWN_ORDERS[2 * chunk + q], first + b) * size, 8)
+            start = pl.multiple_of(block_at(ORDERS[2 * chunk + q], first + b) * size, 8)
             mixed[q, pl.ds(b * size, size), pl.ds(0, rows)] = hta[pl.ds(start, size), :]
             mixed[q, pl.ds(b * size, size), pl.ds(rows, rows)] = htb[pl.ds(start, size), :]
         part = nn(mixed[q].astype(BF16), gs[:, pl.ds(q * cols, cols)])
@@ -127,14 +125,13 @@
             block = part[b * size : (b + 1) * size]
             stack = [block[:, k * LANES : (k + 1) * LANES] for k in range(cols // LANES)]
             tall = size * len(stack)
-            out[pl.ds(base + b * tall, tall), :] = jnp.concatenate(stack, axis=0).astype(BF16)
-
-
-def down_half(first, chunk, hts, pieces, joint=False):
+            out[pl.ds(b * tall, tall), :] = jnp.concatenate(stack, axis=0).astype(BF16)
+
+
+def down_half(first, chunk, hts, pieces):
     ff, rows = hts[0].shape
     width = pieces[2].shape[1]
-    count = 1 if joint else 2
-    out = ((2 // count * HALF * ff // BLOCKS * (width // 2 // LANES), LANES), BF16)
+    out = ((HALF * ff // BLOCKS * (width // 2 // LANES), LANES), BF16)
 
     def body(*refs):
         down_body(first, chunk, *refs)
@@ -142,7 +139,7 @@
     return kernel(
         body,
         (*hts, *pieces),
-        [out] * count,
+        [out] * 2,
         12,
         2 * rows * ff * width,
         scratch=(pltpu.VMEM((2, ff // 2, 2 * rows), F32), pltpu.VMEM((2 * rows, width), BF16)),
@@ -189,8 +186,8 @@
 
 
 TILE = 256
-EARLY = ((2, 0, 3), (3, 0, 3))
-LATER = ((0, 0, 3), (1, 0, 3))
+EARLY = ((0, 0, 3), (1, 0, 3))
+LATER = ((2, 0, 3), (3, 0, 3))
 EXTRA = 128
 
 
@@ -270,11 +267,10 @@
 
 
 def finish_body(*refs):
-    bases, (last_a, last_b, end2, end3), (gate, up, down) = refs[:8], refs[8:12], refs[12:]
+    bases, last, (gate, up, down) = refs[:8], refs[8], refs[9:]
     half, low = gate.shape[0] // 2, down.shape[0]
     cols = down.shape[1] // 4
-    received = [r[...].astype(F32) for r in (last_a, last_b, end2, end3)]
-    received = jnp.concatenate(received, axis=0)
+    received = last[...].astype(F32)
     done, at = [], 0
     for base in bases:
         done.append(base[...] + received[at : at + base.shape[0]])
@@ -316,8 +312,7 @@
     fb = forward(tok_far, tok_both, cwb, wg, wu)
     hts, xts = (fa[3], fb[3]), (fa[4], fb[4])
     pieces = [(cotangent, cot_near, cot_far[k], cot_both[k]) for k in range(2)]
-    down_send = down_half(HALF, 0, hts, pieces[0])
-    down_z = down_half(HALF, 1, hts, pieces[1], joint=True)[0]
+    down_send = [a for k in range(2) for a in down_half(HALF, k, hts, pieces[k])]
     ha = hidden_part(((cotangent,), (cot_near,)), cwa, wd, *fa[:3])
     hb = hidden_part((cot_far, cot_both), cwb, wd, *fb[:3])
     gds, uds = (ha[0], hb[0]), (ha[1], hb[1])
@@ -334,10 +329,7 @@
         scratch=(pltpu.VMEM((rows, ff), BF16),) * 2,
     )
 
-    down_z = moved(down_z, *Z)
-    size = down_z.shape[0] // 2
-    down_got = [moved(down_send[p], *ORDERS[p][0]) for p in (0, 1)]
-    down_got += [lax.optimization_barrier(a) for a in (down_z[:size], down_z[size:])]
+    down_got = [moved(down_send[p], *ORDERS[p][0]) for p in range(4)]
     gates, downs = [], [[(HALF, down_keep[p]), (HALF, down_got[p])] for p in range(4)]
     for spec, keep, send in zip(EARLY + LATER, gate_keep, gate_send):
         gates.append([(HALF, keep), (HALF, moved(send, *ORDERS[spec[0]][0]))])
@@ -355,20 +347,14 @@
             at += send.shape[0]
         return got
 
-    for p in CHAINS:
-        exchange(have[p][: 2 if p < 2 else 1], ORDERS[p][1])
-    for p in (2, 3):
-        exchange(downs[p : p + 1], DOWN_ORDERS[p][1])
-    for step in (2, 3):
+    for step in (1, 2, 3):
         for p in CHAINS:
             exchange(have[p], ORDERS[p][step])
-    last_a = exchange(gates[:2], Z)
-    last_b = exchange(gates[2:] + downs[:2], Z)
-    ends = [exchange(downs[p : p + 1], DOWN_ORDERS[p][4]) for p in (2, 3)]
+    last = exchange(gates + downs, Z)
     bases = [summed(h[:-1], 0, 1, F32) for h in gates + downs]
     gate_grad, up_grad, down_grad = kernel(
         finish_body,
-        (*bases, last_a, last_b, *ends),
+        (*bases, last),
         [((d // BLOCKS, ff), BF16), ((d // BLOCKS, ff), BF16), ((ff // BLOCKS, d), BF16)],
         4,
         1 << 20,

time: 161 us -> 128 us (0.80)
  waiting for transfers between devices: 82 us -> 58.2 us
  starting transfers between devices: 51.2 us -> 41.6 us
    ppermute x38 -> x34, waiting for transfers between devices: 82 us -> 58.2 us  [moved(): lax.ppermute(array, axis, [(i, i ^ mask) for i in range(lax.axis_size(axi...]
    ppermute x38 -> x34, starting transfers between devices: 51.2 us -> 41.6 us  [moved(): lax.ppermute(array, axis, [(i, i ^ mask) for i in range(lax.axis_size(axi...]
  transfers between devices with their start and end apart: 38 -> 34, of which waited for: 17 -> 14; matrix products, arithmetic and copies ran while one was open for 2% -> 3% of each run, Pallas kernels for 9% -> 10%
where the time goes in v6:
time: 128 us
  waiting for transfers between devices  58.2 us (45%)
  starting transfers between devices  41.6 us (32%)
  Pallas kernels  17.8 us (14%)
  local copies, waits for them, and re-layouts  6.43 us (5%)
  other arithmetic  2.48 us (2%)
    ppermute x34, waiting for transfers between devices, moved(): lax.ppermute(array, axis, [(i, i ^ mask) for i in range(lax.axis_size(axi...  58.2 us
    ppermute x34, starting transfers between devices, moved(): lax.ppermute(array, axis, [(i, i ^ mask) for i in range(lax.axis_size(axi...  41.6 us
    pallas_call x15, Pallas kernels, kernel(): pl.pallas_call(body, in_specs=[vmem] * len(ins), out_specs=[vmem] * len(o...  17.8 us
    unnamed x20, local copies, waits for them, and re-layouts  5.37 us
  transfers between devices with their start and end apart: 34, of which 14 were waited for; matrix products, arithmetic and copies ran while one was open for 3% of the time, Pallas kernels for 10%

profile of v6, /device:TPU:0, one launch (start us, length us, event | category | flops | bytes accessed | tf_op | source)
XLA Modules:
  0.0 127.7 jit_solution(15714960378585214476)
XLA Ops:
  0.6 2.1 %collective-permute-start.9 = (bf16[128,2048]{1,0:T(8,128)(2,1)}, bf16[128,2048]{1,0:T(8,128)(2,1)S(1)}, u32[]{:S(2)}, u32[]{:S(2)}) collective-permute-start(bf16[128,2048]{1,0:T(8,128)(2,1)} %x0.1), channel_id=1, source_target_pairs={{0,2},{2,0},{1,3},{3,1},{4,6},{6,4},{5,7},{7,5},{8,10},{10,8},{9,1... | collective-permute-start | bytes 1572872 | tf_op jit(solution)/shard_map/ppermute | solution.py:26
  2.8 0.7 copy-done.7
  3.4 0.7 copy-done.9
  4.1 0.6 collective-permute-start.1
  4.8 10.1 %collective-permute-done.9.x0 = bf16[128,2048]{1,0:T(8,128)(2,1)S(1)} collective-permute-done((bf16[128,2048]{1,0:T(8,128)(2,1)}, bf16[128,2048]{1,0:T(8,128)(2,1)S(1)}, u32[]{:S(2)}, u32[]{:S(2)}) %collective-permute-start.9) | collective-permute-done | bytes 524320 | tf_op jit(solution)/shard_map/ppermute | solution.py:26
  14.9 1.1 fusion.8
  16.0 1.8 %collective-permute-start.4 = (bf16[128,1024]{1,0:T(8,128)(2,1)S(1)}, bf16[128,1024]{1,0:T(8,128)(2,1)S(1)}, u32[]{:S(2)}, u32[]{:S(2)}) collective-permute-start(bf16[128,1024]{1,0:T(8,128)(2,1)S(1)} %get-tuple-element.97), channel_id=1, source_target_pairs={{0,2},{2,0},{1,3},{3,1},{4,6},{6,4},{5,7},{7,5},{8,10},{10,8},{9,1... | collective-permute-start | bytes 786440 | tf_op jit(solution)/shard_map/ppermute | solution.py:26
  18.1 7.1 %collective-permute-done.4.refs_1_.refs_4_ = bf16[128,1024]{1,0:T(8,128)(2,1)S(1)} collective-permute-done((bf16[128,1024]{1,0:T(8,128)(2,1)S(1)}, bf16[128,1024]{1,0:T(8,128)(2,1)S(1)}, u32[]{:S(2)}, u32[]{:S(2)}) %collective-permute-start.4) | collective-permute-done | bytes 262176 | tf_op jit(solution)/shard_map/ppermute | solution.py:26
  25.2 1.7 %collective-permute-start.7 = (f32[8,128]{1,0:T(8,128)S(1)}, f32[8,128]{1,0:T(8,128)S(1)}, u32[]{:S(2)}, u32[]{:S(2)}) collective-permute-start(f32[8,128]{1,0:T(8,128)S(1)} %get-tuple-element.57), channel_id=1, source_target_pairs={{0,2},{1,3},{2,0},{3,1},{4,6},{5,7},{6,4},{7,5},{8,10},{9,11},{10,... | collective-permute-start | bytes 12296 | tf_op jit(solution)/shard_map/ppermute | solution.py:26
  27.0 3.5 %collective-permute-done.3.refs_0_.refs_4_ = bf16[128,1024]{1,0:T(8,128)(2,1)S(1)} collective-permute-done((bf16[128,1024]{1,0:T(8,128)(2,1)S(1)}, bf16[128,1024]{1,0:T(8,128)(2,1)S(1)}, u32[]{:S(2)}, u32[]{:S(2)}) %collective-permute-start.3) | collective-permute-done | bytes 262176 | tf_op jit(solution)/shard_map/ppermute | solution.py:26
  30.9 1.9 %copy-done.2 = bf16[1,2048,768]{2,1,0:T(8,128)(2,1)S(1)} copy-done((bf16[1,2048,768]{2,1,0:T(8,128)(2,1)S(1)}, bf16[1,2048,768]{2,1,0:T(8,128)(2,1)}, u32[]{:S(2)}) %copy-start.2) | copy-done | bytes 3145752
  32.8 1.9 %copy-done.4 = bf16[1,2048,768]{2,1,0:T(8,128)(2,1)S(1)} copy-done((bf16[1,2048,768]{2,1,0:T(8,128)(2,1)S(1)}, bf16[1,2048,768]{2,1,0:T(8,128)(2,1)}, u32[]{:S(2)}) %copy-start.4) | copy-done | bytes 3145752
  34.7 2.0 %shard_map.111 = (f32[256,768]{1,0:T(8,128)S(1)}, f32[256,768]{1,0:T(8,128)S(1)}, bf16[256,768]{1,0:T(8,128)(2,1)S(1)}, f32[768,256]{1,0:T(8,128)S(1)}, bf16[2048,256]{1,0:T(8,128)(2,1)S(1)}) custom-call(bf16[128,2048]{1,0:T(8,128)(2,1)S(1)} %copy-done.6, bf16[128,2048]{1,0:T(8,128)(2,1)S(1)} %collective-permute-done.2.x1, ...), custom_call_target="tpu_custom_call" | custom-call | flops 1610612736 | bytes 1048576 | tf_op jit(solution)/shard_map/pallas_call | solution.py:60
  36.7 1.4 %collective-permute-start.8 = (f32[8,128]{1,0:T(8,128)S(1)}, f32[8,128]{1,0:T(8,128)S(1)}, u32[]{:S(2)}, u32[]{:S(2)}) collective-permute-start(f32[8,128]{1,0:T(8,128)S(1)} %get-tuple-element.58), channel_id=1, source_target_pairs={{0,3},{1,2},{2,1},{3,0},{4,7},{5,6},{6,5},{7,4},{8,11},{9,10},{10,... | collective-permute-start | bytes 12296 | tf_op jit(solution)/shard_map/ppermute | solution.py:26
  38.2 1.2 shard_map.112
  40.0 2.0 %shard_map.113 = (f32[256,768]{1,0:T(8,128)S(1)}, f32[256,768]{1,0:T(8,128)S(1)}, bf16[256,768]{1,0:T(8,128)(2,1)S(1)}, f32[768,256]{1,0:T(8,128)S(1)}, bf16[2048,256]{1,0:T(8,128)(2,1)S(1)}) custom-call(bf16[128,2048]{1,0:T(8,128)(2,1)S(1)} %collective-permute-done.9.x0, bf16[128,2048]{1,0:T(8,128)(2,1)S(1)} %collective-permute-done.10.x1, ...), custom_call_target="tpu_custom_call" | custom-call | flops 1610612736 | bytes 1048576 | tf_op jit(solution)/shard_map/pallas_call | solution.py:60
  42.0 1.2 shard_map.114
  43.2 1.0 shard_map.121
  44.2 1.0 shard_map.118
  45.2 0.6 shard_map.123
  45.8 2.8 %collective-permute-start.24 = (bf16[1536,128]{1,0:T(8,128)(2,1)S(1)}, bf16[1536,128]{1,0:T(8,128)(2,1)S(1)}, u32[]{:S(2)}, u32[]{:S(2)}) collective-permute-start(bf16[1536,128]{1,0:T(8,128)(2,1)S(1)} %get-tuple-element.89), channel_id=1, source_target_pairs={{0,96},{32,64},{64,32},{96,0},{1,97},{33,65},{65,33},{97,1},{2,98}... | collective-permute-start | bytes 1179656 | tf_op jit(solution)/shard_map/ppermute | solution.py:26
  48.7 3.0 %collective-permute-start.29 = (bf16[1536,128]{1,0:T(8,128)(2,1)S(1)}, bf16[1536,128]{1,0:T(8,128)(2,1)S(1)}, u32[]{:S(2)}, u32[]{:S(2)}) collective-permute-start(bf16[1536,128]{1,0:T(8,128)(2,1)S(1)} %get-tuple-element.93), channel_id=1, source_target_pairs={{0,12},{4,8},{8,4},{12,0},{1,13},{5,9},{9,5},{13,1},{2,14},{6,10},... | collective-permute-start | bytes 1179656 | tf_op jit(solution)/shard_map/ppermute | solution.py:26
  52.7 1.1 collective-permute-start.23
  54.4 3.4 %shard_map.115 = (bf16[128,2176]{1,0:T(8,128)(2,1)S(1)}, bf16[256,2176]{1,0:T(8,128)(2,1)S(1)}, bf16[128,2176]{1,0:T(8,128)(2,1)S(1)}) custom-call(bf16[256,768]{1,0:T(8,128)(2,1)S(1)} %get-tuple-element.56.gda.refs_2_, bf16[256,768]{1,0:T(8,128)(2,1)S(1)} %get-tuple-element.62.gdb.refs_3_, bf16[256,768]{1,0:T(8,128)(2,1)S(1)} %get-tuple-element.63.uda.refs_4_, ...), custom_call_target="tpu_custom_call" | custom-call | flops 3221225472 | bytes 1048576 | tf_op jit(solution)/shard_map/pallas_call | solution.py:60
  57.9 0.6 shard_map.119
  58.5 1.8 %shard_map.117 = (bf16[3072,128]{1,0:T(8,128)(2,1)S(1)}, bf16[3072,128]{1,0:T(8,128)(2,1)S(1)}, bf16[3072,128]{1,0:T(8,128)(2,1)S(1)}, bf16[3072,128]{1,0:T(8,128)(2,1)S(1)}) custom-call(bf16[2048,256]{1,0:T(8,128)(2,1)S(1)} %get-tuple-element.74.refs_0_, bf16[2048,256]{1,0:T(8,128)(2,1)S(1)} %get-tuple-element.75.refs_1_, ...), custom_call_target="tpu_custom_call" | custom-call | flops 1610612736 | bytes 1048576 | tf_op jit(solution)/shard_map/pallas_call | solution.py:60
  60.3 1.8 %collective-permute-start.28 = (bf16[3072,128]{1,0:T(8,128)(2,1)S(1)}, bf16[3072,128]{1,0:T(8,128)(2,1)S(1)}, u32[]{:S(2)}, u32[]{:S(2)}) collective-permute-start(bf16[3072,128]{1,0:T(8,128)(2,1)S(1)} %get-tuple-element.91), channel_id=1, source_target_pairs={{0,12},{4,8},{8,4},{12,0},{1,13},{5,9},{9,5},{13,1},{2,14},{6,10},... | collective-permute-start | bytes 2359304 | tf_op jit(solution)/shard_map/ppermute | solution.py:26
  62.6 0.7 collective-permute-done.14
  63.7 16.6 %collective-permute-done.28 = bf16[3072,128]{1,0:T(8,128)(2,1)S(1)} collective-permute-done((bf16[3072,128]{1,0:T(8,128)(2,1)S(1)}, bf16[3072,128]{1,0:T(8,128)(2,1)S(1)}, u32[]{:S(2)}, u32[]{:S(2)}) %collective-permute-start.28) | collective-permute-done | bytes 786464 | tf_op jit(solution)/shard_map/ppermute | solution.py:26
  80.4 0.6 collective-permute-start.30
  81.2 1.0 collective-permute-start.25
  82.4 1.0 collective-permute-start.20
  83.5 2.4 %collective-permute-start.15 = (bf16[2304,128]{1,0:T(8,128)(2,1)S(1)}, bf16[2304,128]{1,0:T(8,128)(2,1)S(1)}, u32[]{:S(2)}, u32[]{:S(2)}) collective-permute-start(bf16[2304,128]{1,0:T(8,128)(2,1)S(1)} %pad_maximum_fusion), channel_id=1, source_target_pairs={{0,96},{32,64},{64,32},{96,0},{1,97},{33,65},{65,33},{97,1},{2,98}... | collective-permute-start | bytes 1769480 | tf_op jit(solution)/shard_map/ppermute | solution.py:26
  86.1 1.7 %collective-permute-start.12 = (bf16[128,2176]{1,0:T(8,128)(2,1)S(1)}, bf16[128,2176]{1,0:T(8,128)(2,1)S(1)}, u32[]{:S(2)}, u32[]{:S(2)}) collective-permute-start(bf16[128,2176]{1,0:T(8,128)(2,1)S(1)} %add_convert_fusion), channel_id=1, source_target_pairs={{0,2},{2,0},{1,3},{3,1},{4,6},{6,4},{5,7},{7,5},{8,10},{10,8},{9,1... | collective-permute-start | bytes 1671176 | tf_op jit(solution)/shard_map/ppermute | solution.py:26
  87.8 6.7 %collective-permute-done.30 = bf16[2304,128]{1,0:T(8,128)(2,1)S(1)} collective-permute-done((bf16[2304,128]{1,0:T(8,128)(2,1)S(1)}, bf16[2304,128]{1,0:T(8,128)(2,1)S(1)}, u32[]{:S(2)}, u32[]{:S(2)}) %collective-permute-start.30) | collective-permute-done | bytes 589856 | tf_op jit(solution)/shard_map/ppermute | solution.py:26
  94.6 2.7 %collective-permute-start.31 = (bf16[1152,128]{1,0:T(8,128)(2,1)S(1)}, bf16[1152,128]{1,0:T(8,128)(2,1)S(1)}, u32[]{:S(2)}, u32[]{:S(2)}) collective-permute-start(bf16[1152,128]{1,0:T(8,128)(2,1)S(1)} %pad_maximum_fusion.7), channel_id=1, source_target_pairs={{0,96},{32,64},{64,32},{96,0},{1,97},{33,65},{65,33},{97,1},{2,98}... | collective-permute-start | bytes 884744 | tf_op jit(solution)/shard_map/ppermute | solution.py:26
  97.5 1.5 %collective-permute-start.26 = (bf16[1152,128]{1,0:T(8,128)(2,1)S(1)}, bf16[1152,128]{1,0:T(8,128)(2,1)S(1)}, u32[]{:S(2)}, u32[]{:S(2)}) collective-permute-start(bf16[1152,128]{1,0:T(8,128)(2,1)S(1)} %pad_maximum_fusion.6), channel_id=1, source_target_pairs={{0,12},{4,8},{8,4},{12,0},{1,13},{5,9},{9,5},{13,1},{2,14},{6,10},... | collective-permute-start | bytes 884744 | tf_op jit(solution)/shard_map/ppermute | solution.py:26
  99.8 1.6 %collective-permute-start.16 = (bf16[1152,128]{1,0:T(8,128)(2,1)S(1)}, bf16[1152,128]{1,0:T(8,128)(2,1)S(1)}, u32[]{:S(2)}, u32[]{:S(2)}) collective-permute-start(bf16[1152,128]{1,0:T(8,128)(2,1)S(1)} %pad_maximum_fusion.4), channel_id=1, source_target_pairs={{0,4},{4,0},{8,12},{12,8},{1,5},{5,1},{9,13},{13,9},{2,6},{6,2},{1... | collective-permute-start | bytes 884744 | tf_op jit(solution)/shard_map/ppermute | solution.py:26
  101.4 2.9 %collective-permute-done.31 = bf16[1152,128]{1,0:T(8,128)(2,1)S(1)} collective-permute-done((bf16[1152,128]{1,0:T(8,128)(2,1)S(1)}, bf16[1152,128]{1,0:T(8,128)(2,1)S(1)}, u32[]{:S(2)}, u32[]{:S(2)}) %collective-permute-start.31) | collective-permute-done | bytes 294944 | tf_op jit(solution)/shard_map/ppermute | solution.py:26
  105.6 0.6 collective-permute-start.27
  106.2 1.1 collective-permute-done.16
  107.5 4.2 %collective-permute-start.17 = (bf16[576,128]{1,0:T(8,128)(2,1)S(1)}, bf16[576,128]{1,0:T(8,128)(2,1)S(1)}, u32[]{:S(2)}, u32[]{:S(2)}) collective-permute-start(bf16[576,128]{1,0:T(8,128)(2,1)S(1)} %pad_maximum_fusion.8), channel_id=1, source_target_pairs={{0,12},{4,8},{8,4},{12,0},{1,13},{5,9},{9,5},{13,1},{2,14},{6,10},... | collective-permute-start | bytes 442376 | tf_op jit(solution)/shard_map/ppermute | solution.py:26
  111.8 1.4 %collective-permute-start.22 = (bf16[576,128]{1,0:T(8,128)(2,1)S(1)}, bf16[576,128]{1,0:T(8,128)(2,1)S(1)}, u32[]{:S(2)}, u32[]{:S(2)}) collective-permute-start(bf16[576,128]{1,0:T(8,128)(2,1)S(1)} %pad_maximum_fusion.9), channel_id=1, source_target_pairs={{0,96},{32,64},{64,32},{96,0},{1,97},{33,65},{65,33},{97,1},{2,98}... | collective-permute-start | bytes 442376 | tf_op jit(solution)/shard_map/ppermute | solution.py:26
  113.2 1.2 shard_map.116
  114.8 3.4 %collective-permute-done.22 = bf16[576,128]{1,0:T(8,128)(2,1)S(1)} collective-permute-done((bf16[576,128]{1,0:T(8,128)(2,1)S(1)}, bf16[576,128]{1,0:T(8,128)(2,1)S(1)}, u32[]{:S(2)}, u32[]{:S(2)}) %collective-permute-start.22) | collective-permute-done | bytes 147488 | tf_op jit(solution)/shard_map/ppermute | solution.py:26
  118.5 3.7 %collective-permute-start.33 = (bf16[1152,128]{1,0:T(8,128)(2,1)S(1)}, bf16[1152,128]{1,0:T(8,128)(2,1)S(1)}, u32[]{:S(2)}, u32[]{:S(2)}) collective-permute-start(bf16[1152,128]{1,0:T(8,128)(2,1)S(1)} %fusion.7), channel_id=1, source_target_pairs={{0,16},{16,0},{1,17},{17,1},{2,18},{18,2},{3,19},{19,3},{4,20},{20... | collective-permute-start | bytes 884744 | tf_op jit(solution)/shard_map/ppermute | solution.py:26
  122.5 4.4 %collective-permute-done.33.refs_8_ = bf16[1152,128]{1,0:T(8,128)(2,1)S(1)} collective-permute-done((bf16[1152,128]{1,0:T(8,128)(2,1)S(1)}, bf16[1152,128]{1,0:T(8,128)(2,1)S(1)}, u32[]{:S(2)}, u32[]{:S(2)}) %collective-permute-start.33) | collective-permute-done | bytes 294944 | tf_op jit(solution)/shard_map/ppermute | solution.py:26
  126.9 0.8 shard_map.124
  (109 shorter events, 8.2 us)
Async XLA Ops:
  0.6 30.3 %copy-start.6 = (bf16[128,2048]{1,0:T(8,128)(2,1)S(1)}, bf16[128,2048]{1,0:T(8,128)(2,1)}, u32[]{:S(2)}) copy-start(bf16[128,2048]{1,0:T(8,128)(2,1)} %x0.1) | copy-start | bytes 1572868
  0.6 14.2 %collective-permute-start.9 = (bf16[128,2048]{1,0:T(8,128)(2,1)}, bf16[128,2048]{1,0:T(8,128)(2,1)S(1)}, u32[]{:S(2)}, u32[]{:S(2)}) collective-permute-start(bf16[128,2048]{1,0:T(8,128)(2,1)} %x0.1), channel_id=1, source_target_pairs={{0,2},{2,0},{1,3},{3,1},{4,6},{6,4},{5,7},{7,5},{8,10},{10,8},{9,1... | collective-permute-start | bytes 1572872 | tf_op jit(solution)/shard_map/ppermute | solution.py:26
  2.7 27.7 %collective-permute-start.2 = (bf16[128,2048]{1,0:T(8,128)(2,1)}, bf16[128,2048]{1,0:T(8,128)(2,1)S(1)}, u32[]{:S(2)}, u32[]{:S(2)}) collective-permute-start(bf16[128,2048]{1,0:T(8,128)(2,1)} %x0.1), channel_id=1, source_target_pairs={{0,1},{1,0},{2,3},{3,2},{4,5},{5,4},{6,7},{7,6},{8,9},{9,8},{10,11... | collective-permute-start | bytes 1572872 | tf_op jit(solution)/shard_map/ppermute | solution.py:26
  2.8 0.7 copy-start.7
  3.4 0.7 copy-start.9
  4.1 13.6 %collective-permute-start.1 = (f32[8,128]{1,0:T(8,128)S(1)}, f32[8,128]{1,0:T(8,128)S(1)}, u32[]{:S(2)}, u32[]{:S(2)}) collective-permute-start(f32[8,128]{1,0:T(8,128)S(1)} %get-tuple-element.52), channel_id=1, source_target_pairs={{0,1},{1,0},{2,3},{3,2},{4,5},{5,4},{6,7},{7,6},{8,9},{9,8},{10,11... | collective-permute-start | bytes 12296 | tf_op jit(solution)/shard_map/ppermute | solution.py:26
  4.7 32.0 %collective-permute-start = (bf16[128,2048]{1,0:T(8,128)(2,1)}, bf16[128,2048]{1,0:T(8,128)(2,1)S(1)}, u32[]{:S(2)}, u32[]{:S(2)}) collective-permute-start(bf16[128,2048]{1,0:T(8,128)(2,1)} %refs_2_.7), channel_id=1, source_target_pairs={{0,1},{1,0},{2,3},{3,2},{4,5},{5,4},{6,7},{7,6},{8,9},{9,8},{10,11... | collective-permute-start | bytes 1572872 | tf_op jit(solution)/shard_map/ppermute | solution.py:26
  14.9 24.9 %collective-permute-start.10 = (bf16[128,2048]{1,0:T(8,128)(2,1)S(1)}, bf16[128,2048]{1,0:T(8,128)(2,1)S(1)}, u32[]{:S(2)}, u32[]{:S(2)}) collective-permute-start(bf16[128,2048]{1,0:T(8,128)(2,1)S(1)} %collective-permute-done.9.x0), channel_id=1, source_target_pairs={{0,1},{1,0},{2,3},{3,2},{4,5},{5,4},{6,7},{7,6},{8,9},{9,8},{10,11... | collective-permute-start | bytes 1572872 | tf_op jit(solution)/shard_map/ppermute | solution.py:26
  16.0 9.3 %collective-permute-start.4 = (bf16[128,1024]{1,0:T(8,128)(2,1)S(1)}, bf16[128,1024]{1,0:T(8,128)(2,1)S(1)}, u32[]{:S(2)}, u32[]{:S(2)}) collective-permute-start(bf16[128,1024]{1,0:T(8,128)(2,1)S(1)} %get-tuple-element.97), channel_id=1, source_target_pairs={{0,2},{2,0},{1,3},{3,1},{4,6},{6,4},{5,7},{7,5},{8,10},{10,8},{9,1... | collective-permute-start | bytes 786440 | tf_op jit(solution)/shard_map/ppermute | solution.py:26
  17.8 12.6 %collective-permute-start.3 = (bf16[128,1024]{1,0:T(8,128)(2,1)S(1)}, bf16[128,1024]{1,0:T(8,128)(2,1)S(1)}, u32[]{:S(2)}, u32[]{:S(2)}) collective-permute-start(bf16[128,1024]{1,0:T(8,128)(2,1)S(1)} %get-tuple-element.98), channel_id=1, source_target_pairs={{0,2},{2,0},{1,3},{3,1},{4,6},{6,4},{5,7},{7,5},{8,10},{10,8},{9,1... | collective-permute-start | bytes 786440 | tf_op jit(solution)/shard_map/ppermute | solution.py:26
  25.2 14.1 %collective-permute-start.7 = (f32[8,128]{1,0:T(8,128)S(1)}, f32[8,128]{1,0:T(8,128)S(1)}, u32[]{:S(2)}, u32[]{:S(2)}) collective-permute-start(f32[8,128]{1,0:T(8,128)S(1)} %get-tuple-element.57), channel_id=1, source_target_pairs={{0,2},{1,3},{2,0},{3,1},{4,6},{5,7},{6,4},{7,5},{8,10},{9,11},{10,... | collective-permute-start | bytes 12296 | tf_op jit(solution)/shard_map/ppermute | solution.py:26
  30.4 11.6 %collective-permute-start.6 = (bf16[128,1024]{1,0:T(8,128)(2,1)S(1)}, bf16[128,1024]{1,0:T(8,128)(2,1)S(1)}, u32[]{:S(2)}, u32[]{:S(2)}) collective-permute-start(bf16[128,1024]{1,0:T(8,128)(2,1)S(1)} %collective-permute-done.4.refs_1_.refs_4_), channel_id=1, source_target_pairs={{0,1},{1,0},{2,3},{3,2},{4,5},{5,4},{6,7},{7,6},{8,9},{9,8},{10,11... | collective-permute-start | bytes 786440 | tf_op jit(solution)/shard_map/ppermute | solution.py:26
  30.4 11.6 %collective-permute-start.5 = (bf16[128,1024]{1,0:T(8,128)(2,1)S(1)}, bf16[128,1024]{1,0:T(8,128)(2,1)S(1)}, u32[]{:S(2)}, u32[]{:S(2)}) collective-permute-start(bf16[128,1024]{1,0:T(8,128)(2,1)S(1)} %collective-permute-done.3.refs_0_.refs_4_), channel_id=1, source_target_pairs={{0,1},{1,0},{2,3},{3,2},{4,5},{5,4},{6,7},{7,6},{8,9},{9,8},{10,11... | collective-permute-start | bytes 786440 | tf_op jit(solution)/shard_map/ppermute | solution.py:26
  30.9 1.9 %copy-start.2 = (bf16[1,2048,768]{2,1,0:T(8,128)(2,1)S(1)}, bf16[1,2048,768]{2,1,0:T(8,128)(2,1)}, u32[]{:S(2)}) copy-start(bf16[1,2048,768]{2,1,0:T(8,128)(2,1)} %param.11) | copy-start | bytes 9437188
  32.8 1.9 %copy-start.4 = (bf16[1,2048,768]{2,1,0:T(8,128)(2,1)S(1)}, bf16[1,2048,768]{2,1,0:T(8,128)(2,1)}, u32[]{:S(2)}) copy-start(bf16[1,2048,768]{2,1,0:T(8,128)(2,1)} %param.12) | copy-start | bytes 9437188
  34.7 3.4 %copy-start = (bf16[128,2048]{1,0:T(8,128)(2,1)S(1)}, bf16[128,2048]{1,0:T(8,128)(2,1)}, u32[]{:S(2)}) copy-start(bf16[128,2048]{1,0:T(8,128)(2,1)} %refs_2_.7) | copy-start | bytes 1572868
  34.7 3.4 %copy-start.1 = (bf16[1,768,2048]{2,1,0:T(8,128)(2,1)S(1)}, bf16[1,768,2048]{2,1,0:T(8,128)(2,1)}, u32[]{:S(2)}) copy-start(bf16[1,768,2048]{2,1,0:T(8,128)(2,1)} %param.13) | copy-start | bytes 9437188
  34.7 5.1 %copy-start.5 = (bf16[1,2048,768]{2,1,0:T(8,128)(2,1)S(1)}, bf16[1,2048,768]{2,1,0:T(8,128)(2,1)}, u32[]{:S(2)}) copy-start(bf16[1,2048,768]{2,1,0:T(8,128)(2,1)} %param.12) | copy-start | bytes 9437188
  36.7 3.1 %collective-permute-start.8 = (f32[8,128]{1,0:T(8,128)S(1)}, f32[8,128]{1,0:T(8,128)S(1)}, u32[]{:S(2)}, u32[]{:S(2)}) collective-permute-start(f32[8,128]{1,0:T(8,128)S(1)} %get-tuple-element.58), channel_id=1, source_target_pairs={{0,3},{1,2},{2,1},{3,0},{4,7},{5,6},{6,5},{7,4},{8,11},{9,10},{10,... | collective-permute-start | bytes 12296 | tf_op jit(solution)/shard_map/ppermute | solution.py:26
  38.2 1.9 %copy-start.3 = (bf16[1,2048,768]{2,1,0:T(8,128)(2,1)S(1)}, bf16[1,2048,768]{2,1,0:T(8,128)(2,1)}, u32[]{:S(2)}) copy-start(bf16[1,2048,768]{2,1,0:T(8,128)(2,1)} %param.11) | copy-start | bytes 9437188
  45.8 14.5 %collective-permute-start.24 = (bf16[1536,128]{1,0:T(8,128)(2,1)S(1)}, bf16[1536,128]{1,0:T(8,128)(2,1)S(1)}, u32[]{:S(2)}, u32[]{:S(2)}) collective-permute-start(bf16[1536,128]{1,0:T(8,128)(2,1)S(1)} %get-tuple-element.89), channel_id=1, source_target_pairs={{0,96},{32,64},{64,32},{96,0},{1,97},{33,65},{65,33},{97,1},{2,98}... | collective-permute-start | bytes 1179656 | tf_op jit(solution)/shard_map/ppermute | solution.py:26
  48.7 13.5 %collective-permute-start.29 = (bf16[1536,128]{1,0:T(8,128)(2,1)S(1)}, bf16[1536,128]{1,0:T(8,128)(2,1)S(1)}, u32[]{:S(2)}, u32[]{:S(2)}) collective-permute-start(bf16[1536,128]{1,0:T(8,128)(2,1)S(1)} %get-tuple-element.93), channel_id=1, source_target_pairs={{0,12},{4,8},{8,4},{12,0},{1,13},{5,9},{9,5},{13,1},{2,14},{6,10},... | collective-permute-start | bytes 1179656 | tf_op jit(solution)/shard_map/ppermute | solution.py:26
  52.3 11.0 %collective-permute-start.14 = (bf16[1536,128]{1,0:T(8,128)(2,1)S(1)}, bf16[1536,128]{1,0:T(8,128)(2,1)S(1)}, u32[]{:S(2)}, u32[]{:S(2)}) collective-permute-start(bf16[1536,128]{1,0:T(8,128)(2,1)S(1)} %get-tuple-element.81), channel_id=1, source_target_pairs={{0,32},{32,0},{64,96},{96,64},{1,33},{33,1},{65,97},{97,65},{2,34}... | collective-permute-start | bytes 1179656 | tf_op jit(solution)/shard_map/ppermute | solution.py:26
  52.6 10.9 %collective-permute-start.19 = (bf16[1536,128]{1,0:T(8,128)(2,1)S(1)}, bf16[1536,128]{1,0:T(8,128)(2,1)S(1)}, u32[]{:S(2)}, u32[]{:S(2)}) collective-permute-start(bf16[1536,128]{1,0:T(8,128)(2,1)S(1)} %get-tuple-element.85), channel_id=1, source_target_pairs={{0,4},{4,0},{8,12},{12,8},{1,5},{5,1},{9,13},{13,9},{2,6},{6,2},{1... | collective-permute-start | bytes 1179656 | tf_op jit(solution)/shard_map/ppermute | solution.py:26
  52.7 28.3 %collective-permute-start.23 = (bf16[3072,128]{1,0:T(8,128)(2,1)S(1)}, bf16[3072,128]{1,0:T(8,128)(2,1)S(1)}, u32[]{:S(2)}, u32[]{:S(2)}) collective-permute-start(bf16[3072,128]{1,0:T(8,128)(2,1)S(1)} %get-tuple-element.87), channel_id=1, source_target_pairs={{0,96},{32,64},{64,32},{96,0},{1,97},{33,65},{65,33},{97,1},{2,98}... | collective-permute-start | bytes 2359304 | tf_op jit(solution)/shard_map/ppermute | solution.py:26
  60.3 20.0 %collective-permute-start.28 = (bf16[3072,128]{1,0:T(8,128)(2,1)S(1)}, bf16[3072,128]{1,0:T(8,128)(2,1)S(1)}, u32[]{:S(2)}, u32[]{:S(2)}) collective-permute-start(bf16[3072,128]{1,0:T(8,128)(2,1)S(1)} %get-tuple-element.91), channel_id=1, source_target_pairs={{0,12},{4,8},{8,4},{12,0},{1,13},{5,9},{9,5},{13,1},{2,14},{6,10},... | collective-permute-start | bytes 2359304 | tf_op jit(solution)/shard_map/ppermute | solution.py:26
  62.2 21.2 %collective-permute-start.13 = (bf16[3072,128]{1,0:T(8,128)(2,1)S(1)}, bf16[3072,128]{1,0:T(8,128)(2,1)S(1)}, u32[]{:S(2)}, u32[]{:S(2)}) collective-permute-start(bf16[3072,128]{1,0:T(8,128)(2,1)S(1)} %get-tuple-element.77), channel_id=1, source_target_pairs={{0,32},{32,0},{64,96},{96,64},{1,33},{33,1},{65,97},{97,65},{2,34}... | collective-permute-start | bytes 2359304 | tf_op jit(solution)/shard_map/ppermute | solution.py:26
  63.3 18.9 %collective-permute-start.18 = (bf16[3072,128]{1,0:T(8,128)(2,1)S(1)}, bf16[3072,128]{1,0:T(8,128)(2,1)S(1)}, u32[]{:S(2)}, u32[]{:S(2)}) collective-permute-start(bf16[3072,128]{1,0:T(8,128)(2,1)S(1)} %get-tuple-element.83), channel_id=1, source_target_pairs={{0,4},{4,0},{8,12},{12,8},{1,5},{5,1},{9,13},{13,9},{2,6},{6,2},{1... | collective-permute-start | bytes 2359304 | tf_op jit(solution)/shard_map/ppermute | solution.py:26
  63.5 22.4 %collective-permute-start.11 = (bf16[256,2176]{1,0:T(8,128)(2,1)S(1)}, bf16[256,2176]{1,0:T(8,128)(2,1)S(1)}, u32[]{:S(2)}, u32[]{:S(2)}) collective-permute-start(bf16[256,2176]{1,0:T(8,128)(2,1)S(1)} %get-tuple-element.70), channel_id=1, source_target_pairs={{0,1},{1,0},{2,3},{3,2},{4,5},{5,4},{6,7},{7,6},{8,9},{9,8},{10,11... | collective-permute-start | bytes 3342344 | tf_op jit(solution)/shard_map/ppermute | solution.py:26
  80.4 14.0 %collective-permute-start.30 = (bf16[2304,128]{1,0:T(8,128)(2,1)S(1)}, bf16[2304,128]{1,0:T(8,128)(2,1)S(1)}, u32[]{:S(2)}, u32[]{:S(2)}) collective-permute-start(bf16[2304,128]{1,0:T(8,128)(2,1)S(1)} %pad_maximum_fusion.3), channel_id=1, source_target_pairs={{0,4},{4,0},{8,12},{12,8},{1,5},{5,1},{9,13},{13,9},{2,6},{6,2},{1... | collective-permute-start | bytes 1769480 | tf_op jit(solution)/shard_map/ppermute | solution.py:26
  81.2 16.1 %collective-permute-start.25 = (bf16[2304,128]{1,0:T(8,128)(2,1)S(1)}, bf16[2304,128]{1,0:T(8,128)(2,1)S(1)}, u32[]{:S(2)}, u32[]{:S(2)}) collective-permute-start(bf16[2304,128]{1,0:T(8,128)(2,1)S(1)} %pad_maximum_fusion.2), channel_id=1, source_target_pairs={{0,32},{32,0},{64,96},{96,64},{1,33},{33,1},{65,97},{97,65},{2,34}... | collective-permute-start | bytes 1769480 | tf_op jit(solution)/shard_map/ppermute | solution.py:26
  82.4 16.6 %collective-permute-start.20 = (bf16[2304,128]{1,0:T(8,128)(2,1)S(1)}, bf16[2304,128]{1,0:T(8,128)(2,1)S(1)}, u32[]{:S(2)}, u32[]{:S(2)}) collective-permute-start(bf16[2304,128]{1,0:T(8,128)(2,1)S(1)} %pad_maximum_fusion.1), channel_id=1, source_target_pairs={{0,12},{4,8},{8,4},{12,0},{1,13},{5,9},{9,5},{13,1},{2,14},{6,10},... | collective-permute-start | bytes 1769480 | tf_op jit(solution)/shard_map/ppermute | solution.py:26
  83.5 16.1 %collective-permute-start.15 = (bf16[2304,128]{1,0:T(8,128)(2,1)S(1)}, bf16[2304,128]{1,0:T(8,128)(2,1)S(1)}, u32[]{:S(2)}, u32[]{:S(2)}) collective-permute-start(bf16[2304,128]{1,0:T(8,128)(2,1)S(1)} %pad_maximum_fusion), channel_id=1, source_target_pairs={{0,96},{32,64},{64,32},{96,0},{1,97},{33,65},{65,33},{97,1},{2,98}... | collective-permute-start | bytes 1769480 | tf_op jit(solution)/shard_map/ppermute | solution.py:26
  86.1 27.1 %collective-permute-start.12 = (bf16[128,2176]{1,0:T(8,128)(2,1)S(1)}, bf16[128,2176]{1,0:T(8,128)(2,1)S(1)}, u32[]{:S(2)}, u32[]{:S(2)}) collective-permute-start(bf16[128,2176]{1,0:T(8,128)(2,1)S(1)} %add_convert_fusion), channel_id=1, source_target_pairs={{0,2},{2,0},{1,3},{3,1},{4,6},{6,4},{5,7},{7,5},{8,10},{10,8},{9,1... | collective-permute-start | bytes 1671176 | tf_op jit(solution)/shard_map/ppermute | solution.py:26
  94.6 9.7 %collective-permute-start.31 = (bf16[1152,128]{1,0:T(8,128)(2,1)S(1)}, bf16[1152,128]{1,0:T(8,128)(2,1)S(1)}, u32[]{:S(2)}, u32[]{:S(2)}) collective-permute-start(bf16[1152,128]{1,0:T(8,128)(2,1)S(1)} %pad_maximum_fusion.7), channel_id=1, source_target_pairs={{0,96},{32,64},{64,32},{96,0},{1,97},{33,65},{65,33},{97,1},{2,98}... | collective-permute-start | bytes 884744 | tf_op jit(solution)/shard_map/ppermute | solution.py:26
  97.5 8.0 %collective-permute-start.26 = (bf16[1152,128]{1,0:T(8,128)(2,1)S(1)}, bf16[1152,128]{1,0:T(8,128)(2,1)S(1)}, u32[]{:S(2)}, u32[]{:S(2)}) collective-permute-start(bf16[1152,128]{1,0:T(8,128)(2,1)S(1)} %pad_maximum_fusion.6), channel_id=1, source_target_pairs={{0,12},{4,8},{8,4},{12,0},{1,13},{5,9},{9,5},{13,1},{2,14},{6,10},... | collective-permute-start | bytes 884744 | tf_op jit(solution)/shard_map/ppermute | solution.py:26
  99.2 12.5 %collective-permute-start.21 = (bf16[1152,128]{1,0:T(8,128)(2,1)S(1)}, bf16[1152,128]{1,0:T(8,128)(2,1)S(1)}, u32[]{:S(2)}, u32[]{:S(2)}) collective-permute-start(bf16[1152,128]{1,0:T(8,128)(2,1)S(1)} %pad_maximum_fusion.5), channel_id=1, source_target_pairs={{0,32},{32,0},{64,96},{96,64},{1,33},{33,1},{65,97},{97,65},{2,34}... | collective-permute-start | bytes 884744 | tf_op jit(solution)/shard_map/ppermute | solution.py:26
  99.8 7.6 %collective-permute-start.16 = (bf16[1152,128]{1,0:T(8,128)(2,1)S(1)}, bf16[1152,128]{1,0:T(8,128)(2,1)S(1)}, u32[]{:S(2)}, u32[]{:S(2)}) collective-permute-start(bf16[1152,128]{1,0:T(8,128)(2,1)S(1)} %pad_maximum_fusion.4), channel_id=1, source_target_pairs={{0,4},{4,0},{8,12},{12,8},{1,5},{5,1},{9,13},{13,9},{2,6},{6,2},{1... | collective-permute-start | bytes 884744 | tf_op jit(solution)/shard_map/ppermute | solution.py:26
  104.5 13.9 %collective-permute-start.32 = (bf16[576,128]{1,0:T(8,128)(2,1)S(1)}, bf16[576,128]{1,0:T(8,128)(2,1)S(1)}, u32[]{:S(2)}, u32[]{:S(2)}) collective-permute-start(bf16[576,128]{1,0:T(8,128)(2,1)S(1)} %pad_maximum_fusion.11), channel_id=1, source_target_pairs={{0,32},{32,0},{64,96},{96,64},{1,33},{33,1},{65,97},{97,65},{2,34}... | collective-permute-start | bytes 442376 | tf_op jit(solution)/shard_map/ppermute | solution.py:26
  105.6 7.6 %copy-start.8 = (s32[128,2]{0,1:T(2,128)S(1)}, s32[128,2]{0,1:T(2,128)}, u32[]{:S(2)}) copy-start(s32[128,2]{0,1:T(2,128)} %param.9) | copy-start | bytes 3076
  105.6 12.7 %collective-permute-start.27 = (bf16[576,128]{1,0:T(8,128)(2,1)S(1)}, bf16[576,128]{1,0:T(8,128)(2,1)S(1)}, u32[]{:S(2)}, u32[]{:S(2)}) collective-permute-start(bf16[576,128]{1,0:T(8,128)(2,1)S(1)} %pad_maximum_fusion.10), channel_id=1, source_target_pairs={{0,4},{4,0},{8,12},{12,8},{1,5},{5,1},{9,13},{13,9},{2,6},{6,2},{1... | collective-permute-start | bytes 442376 | tf_op jit(solution)/shard_map/ppermute | solution.py:26
  107.5 7.3 %collective-permute-start.17 = (bf16[576,128]{1,0:T(8,128)(2,1)S(1)}, bf16[576,128]{1,0:T(8,128)(2,1)S(1)}, u32[]{:S(2)}, u32[]{:S(2)}) collective-permute-start(bf16[576,128]{1,0:T(8,128)(2,1)S(1)} %pad_maximum_fusion.8), channel_id=1, source_target_pairs={{0,12},{4,8},{8,4},{12,0},{1,13},{5,9},{9,5},{13,1},{2,14},{6,10},... | collective-permute-start | bytes 442376 | tf_op jit(solution)/shard_map/ppermute | solution.py:26
  111.8 6.4 %collective-permute-start.22 = (bf16[576,128]{1,0:T(8,128)(2,1)S(1)}, bf16[576,128]{1,0:T(8,128)(2,1)S(1)}, u32[]{:S(2)}, u32[]{:S(2)}) collective-permute-start(bf16[576,128]{1,0:T(8,128)(2,1)S(1)} %pad_maximum_fusion.9), channel_id=1, source_target_pairs={{0,96},{32,64},{64,32},{96,0},{1,97},{33,65},{65,33},{97,1},{2,98}... | collective-permute-start | bytes 442376 | tf_op jit(solution)/shard_map/ppermute | solution.py:26
  118.5 8.4 %collective-permute-start.33 = (bf16[1152,128]{1,0:T(8,128)(2,1)S(1)}, bf16[1152,128]{1,0:T(8,128)(2,1)S(1)}, u32[]{:S(2)}, u32[]{:S(2)}) collective-permute-start(bf16[1152,128]{1,0:T(8,128)(2,1)S(1)} %fusion.7), channel_id=1, source_target_pairs={{0,16},{16,0},{1,17},{17,1},{2,18},{18,2},{3,19},{19,3},{4,20},{20... | collective-permute-start | bytes 884744 | tf_op jit(solution)/shard_map/ppermute | solution.py:26

commit v7 on v6

--- a/solution.py
+++ b/solution.py
@@ -347,9 +347,12 @@
             at += send.shape[0]
         return got
 
+    for p in (2, 3):
+        exchange(downs[p : p + 1], ORDERS[p][1])
     for step in (1, 2, 3):
         for p in CHAINS:
-            exchange(have[p], ORDERS[p][step])
+            pieces = have[p][:1] if step == 1 and p > 1 else have[p]
+            exchange(pieces, ORDERS[p][step])
     last = exchange(gates + downs, Z)
     bases = [summed(h[:-1], 0, 1, F32) for h in gates + downs]
     gate_grad, up_grad, down_grad = kernel(

time: 128 us -> 141 us (1.10)
  waiting for transfers between devices: 58.2 us -> 69.9 us
    ppermute x34 -> x36, waiting for transfers between devices: 58.2 us -> 69.9 us  [moved(): lax.ppermute(array, axis, [(i, i ^ mask) for i in range(lax.axis_size(axi...]
    ppermute x34 -> x36, starting transfers between devices: 41.6 us -> 42.8 us  [moved(): lax.ppermute(array, axis, [(i, i ^ mask) for i in range(lax.axis_size(axi...]
  transfers between devices with their start and end apart: 34 -> 36, of which waited for: 14 -> 16; matrix products, arithmetic and copies ran while one was open for 3% -> 2% of each run, Pallas kernels for 10% -> 9%
where the time goes in v7:
time: 141 us; the launch traced here: 140 us
  waiting for transfers between devices  69.9 us (50%)
  starting transfers between devices  42.8 us (30%)
  Pallas kernels  17.8 us (13%)
  local copies, waits for them, and re-layouts  6.43 us (5%)
  other arithmetic  2.38 us (2%)
    ppermute x36, waiting for transfers between devices, moved(): lax.ppermute(array, axis, [(i, i ^ mask) for i in range(lax.axis_size(axi...  69.9 us
    ppermute x36, starting transfers between devices, moved(): lax.ppermute(array, axis, [(i, i ^ mask) for i in range(lax.axis_size(axi...  42.8 us
    pallas_call x15, Pallas kernels, kernel(): pl.pallas_call(body, in_specs=[vmem] * len(ins), out_specs=[vmem] * len(o...  17.8 us
    unnamed x20, local copies, waits for them, and re-layouts  5.37 us
  transfers between devices with their start and end apart: 36, of which 16 were waited for; matrix products, arithmetic and copies ran while one was open for 2% of the time, Pallas kernels for 9%

profile of v7, /device:TPU:0, one launch (start us, length us, event | category | flops | bytes accessed | tf_op | source)
XLA Modules:
  0.0 140.5 jit_solution(4858688258570227989)
XLA Ops:
  0.6 2.1 %collective-permute-start.9 = (bf16[128,2048]{1,0:T(8,128)(2,1)}, bf16[128,2048]{1,0:T(8,128)(2,1)S(1)}, u32[]{:S(2)}, u32[]{:S(2)}) collective-permute-start(bf16[128,2048]{1,0:T(8,128)(2,1)} %x0.1), channel_id=1, source_target_pairs={{0,2},{2,0},{1,3},{3,1},{4,6},{6,4},{5,7},{7,5},{8,10},{10,8},{9,1... | collective-permute-start | bytes 1572872 | tf_op jit(solution)/shard_map/ppermute | solution.py:26
  2.8 0.7 copy-done.7
  4.8 10.1 %collective-permute-done.9.x0 = bf16[128,2048]{1,0:T(8,128)(2,1)S(1)} collective-permute-done((bf16[128,2048]{1,0:T(8,128)(2,1)}, bf16[128,2048]{1,0:T(8,128)(2,1)S(1)}, u32[]{:S(2)}, u32[]{:S(2)}) %collective-permute-start.9) | collective-permute-done | bytes 524320 | tf_op jit(solution)/shard_map/ppermute | solution.py:26
  14.9 1.1 fusion.8
  16.0 1.8 %collective-permute-start.4 = (bf16[128,1024]{1,0:T(8,128)(2,1)S(1)}, bf16[128,1024]{1,0:T(8,128)(2,1)S(1)}, u32[]{:S(2)}, u32[]{:S(2)}) collective-permute-start(bf16[128,1024]{1,0:T(8,128)(2,1)S(1)} %get-tuple-element.97), channel_id=1, source_target_pairs={{0,2},{2,0},{1,3},{3,1},{4,6},{6,4},{5,7},{7,5},{8,10},{10,8},{9,1... | collective-permute-start | bytes 786440 | tf_op jit(solution)/shard_map/ppermute | solution.py:26
  18.1 7.1 %collective-permute-done.4.refs_1_.refs_4_ = bf16[128,1024]{1,0:T(8,128)(2,1)S(1)} collective-permute-done((bf16[128,1024]{1,0:T(8,128)(2,1)S(1)}, bf16[128,1024]{1,0:T(8,128)(2,1)S(1)}, u32[]{:S(2)}, u32[]{:S(2)}) %collective-permute-start.4) | collective-permute-done | bytes 262176 | tf_op jit(solution)/shard_map/ppermute | solution.py:26
  25.2 1.7 %collective-permute-start.7 = (f32[8,128]{1,0:T(8,128)S(1)}, f32[8,128]{1,0:T(8,128)S(1)}, u32[]{:S(2)}, u32[]{:S(2)}) collective-permute-start(f32[8,128]{1,0:T(8,128)S(1)} %get-tuple-element.57), channel_id=1, source_target_pairs={{0,2},{1,3},{2,0},{3,1},{4,6},{5,7},{6,4},{7,5},{8,10},{9,11},{10,... | collective-permute-start | bytes 12296 | tf_op jit(solution)/shard_map/ppermute | solution.py:26
  27.0 3.5 %collective-permute-done.3.refs_0_.refs_4_ = bf16[128,1024]{1,0:T(8,128)(2,1)S(1)} collective-permute-done((bf16[128,1024]{1,0:T(8,128)(2,1)S(1)}, bf16[128,1024]{1,0:T(8,128)(2,1)S(1)}, u32[]{:S(2)}, u32[]{:S(2)}) %collective-permute-start.3) | collective-permute-done | bytes 262176 | tf_op jit(solution)/shard_map/ppermute | solution.py:26
  30.9 1.9 %copy-done.2 = bf16[1,2048,768]{2,1,0:T(8,128)(2,1)S(1)} copy-done((bf16[1,2048,768]{2,1,0:T(8,128)(2,1)S(1)}, bf16[1,2048,768]{2,1,0:T(8,128)(2,1)}, u32[]{:S(2)}) %copy-start.2) | copy-done | bytes 3145752
  32.8 1.9 %copy-done.4 = bf16[1,2048,768]{2,1,0:T(8,128)(2,1)S(1)} copy-done((bf16[1,2048,768]{2,1,0:T(8,128)(2,1)S(1)}, bf16[1,2048,768]{2,1,0:T(8,128)(2,1)}, u32[]{:S(2)}) %copy-start.4) | copy-done | bytes 3145752
  34.7 2.0 %shard_map.111 = (f32[256,768]{1,0:T(8,128)S(1)}, f32[256,768]{1,0:T(8,128)S(1)}, bf16[256,768]{1,0:T(8,128)(2,1)S(1)}, f32[768,256]{1,0:T(8,128)S(1)}, bf16[2048,256]{1,0:T(8,128)(2,1)S(1)}) custom-call(bf16[128,2048]{1,0:T(8,128)(2,1)S(1)} %copy-done.6, bf16[128,2048]{1,0:T(8,128)(2,1)S(1)} %collective-permute-done.2.x1, ...), custom_call_target="tpu_custom_call" | custom-call | flops 1610612736 | bytes 1048576 | tf_op jit(solution)/shard_map/pallas_call | solution.py:60
  36.7 1.4 %collective-permute-start.8 = (f32[8,128]{1,0:T(8,128)S(1)}, f32[8,128]{1,0:T(8,128)S(1)}, u32[]{:S(2)}, u32[]{:S(2)}) collective-permute-start(f32[8,128]{1,0:T(8,128)S(1)} %get-tuple-element.58), channel_id=1, source_target_pairs={{0,3},{1,2},{2,1},{3,0},{4,7},{5,6},{6,5},{7,4},{8,11},{9,10},{10,... | collective-permute-start | bytes 12296 | tf_op jit(solution)/shard_map/ppermute | solution.py:26
  38.2 1.2 shard_map.112
  40.0 2.0 %shard_map.113 = (f32[256,768]{1,0:T(8,128)S(1)}, f32[256,768]{1,0:T(8,128)S(1)}, bf16[256,768]{1,0:T(8,128)(2,1)S(1)}, f32[768,256]{1,0:T(8,128)S(1)}, bf16[2048,256]{1,0:T(8,128)(2,1)S(1)}) custom-call(bf16[128,2048]{1,0:T(8,128)(2,1)S(1)} %collective-permute-done.9.x0, bf16[128,2048]{1,0:T(8,128)(2,1)S(1)} %collective-permute-done.10.x1, ...), custom_call_target="tpu_custom_call" | custom-call | flops 1610612736 | bytes 1048576 | tf_op jit(solution)/shard_map/pallas_call | solution.py:60
  42.0 1.2 shard_map.114
  43.2 1.0 shard_map.121
  44.2 1.0 shard_map.118
  45.8 2.8 %collective-permute-start.25 = (bf16[1536,128]{1,0:T(8,128)(2,1)S(1)}, bf16[1536,128]{1,0:T(8,128)(2,1)S(1)}, u32[]{:S(2)}, u32[]{:S(2)}) collective-permute-start(bf16[1536,128]{1,0:T(8,128)(2,1)S(1)} %get-tuple-element.89), channel_id=1, source_target_pairs={{0,96},{32,64},{64,32},{96,0},{1,97},{33,65},{65,33},{97,1},{2,98}... | collective-permute-start | bytes 1179656 | tf_op jit(solution)/shard_map/ppermute | solution.py:26
  48.7 3.0 %collective-permute-start.31 = (bf16[1536,128]{1,0:T(8,128)(2,1)S(1)}, bf16[1536,128]{1,0:T(8,128)(2,1)S(1)}, u32[]{:S(2)}, u32[]{:S(2)}) collective-permute-start(bf16[1536,128]{1,0:T(8,128)(2,1)S(1)} %get-tuple-element.93), channel_id=1, source_target_pairs={{0,12},{4,8},{8,4},{12,0},{1,13},{5,9},{9,5},{13,1},{2,14},{6,10},... | collective-permute-start | bytes 1179656 | tf_op jit(solution)/shard_map/ppermute | solution.py:26
  52.7 1.1 collective-permute-start.23
  54.4 3.4 %shard_map.115 = (bf16[128,2176]{1,0:T(8,128)(2,1)S(1)}, bf16[256,2176]{1,0:T(8,128)(2,1)S(1)}, bf16[128,2176]{1,0:T(8,128)(2,1)S(1)}) custom-call(bf16[256,768]{1,0:T(8,128)(2,1)S(1)} %get-tuple-element.56.gda.refs_2_, bf16[256,768]{1,0:T(8,128)(2,1)S(1)} %get-tuple-element.62.gdb.refs_3_, bf16[256,768]{1,0:T(8,128)(2,1)S(1)} %get-tuple-element.63.uda.refs_4_, ...), custom_call_target="tpu_custom_call" | custom-call | flops 3221225472 | bytes 1048576 | tf_op jit(solution)/shard_map/pallas_call | solution.py:60
  58.5 1.8 %shard_map.117 = (bf16[3072,128]{1,0:T(8,128)(2,1)S(1)}, bf16[3072,128]{1,0:T(8,128)(2,1)S(1)}, bf16[3072,128]{1,0:T(8,128)(2,1)S(1)}, bf16[3072,128]{1,0:T(8,128)(2,1)S(1)}) custom-call(bf16[2048,256]{1,0:T(8,128)(2,1)S(1)} %get-tuple-element.74.refs_0_, bf16[2048,256]{1,0:T(8,128)(2,1)S(1)} %get-tuple-element.75.refs_1_, ...), custom_call_target="tpu_custom_call" | custom-call | flops 1610612736 | bytes 1048576 | tf_op jit(solution)/shard_map/pallas_call | solution.py:60
  60.3 1.8 %collective-permute-start.29 = (bf16[3072,128]{1,0:T(8,128)(2,1)S(1)}, bf16[3072,128]{1,0:T(8,128)(2,1)S(1)}, u32[]{:S(2)}, u32[]{:S(2)}) collective-permute-start(bf16[3072,128]{1,0:T(8,128)(2,1)S(1)} %get-tuple-element.91), channel_id=1, source_target_pairs={{0,12},{4,8},{8,4},{12,0},{1,13},{5,9},{9,5},{13,1},{2,14},{6,10},... | collective-permute-start | bytes 2359304 | tf_op jit(solution)/shard_map/ppermute | solution.py:26
  62.6 0.7 collective-permute-done.14
  63.5 1.5 %collective-permute-start.26 = (bf16[768,128]{1,0:T(8,128)(2,1)S(1)}, bf16[768,128]{1,0:T(8,128)(2,1)S(1)}, u32[]{:S(2)}, u32[]{:S(2)}) collective-permute-start(bf16[768,128]{1,0:T(8,128)(2,1)S(1)} %add_convert_fusion.7), channel_id=1, source_target_pairs={{0,32},{32,0},{64,96},{96,64},{1,33},{33,1},{65,97},{97,65},{2,34}... | collective-permute-start | bytes 589832 | tf_op jit(solution)/shard_map/ppermute | solution.py:26
  65.1 19.7 %collective-permute-done.26 = bf16[768,128]{1,0:T(8,128)(2,1)S(1)} collective-permute-done((bf16[768,128]{1,0:T(8,128)(2,1)S(1)}, bf16[768,128]{1,0:T(8,128)(2,1)S(1)}, u32[]{:S(2)}, u32[]{:S(2)}) %collective-permute-start.26) | collective-permute-done | bytes 196640 | tf_op jit(solution)/shard_map/ppermute | solution.py:26
  85.2 5.2 %collective-permute-done.32 = bf16[768,128]{1,0:T(8,128)(2,1)S(1)} collective-permute-done((bf16[768,128]{1,0:T(8,128)(2,1)S(1)}, bf16[768,128]{1,0:T(8,128)(2,1)S(1)}, u32[]{:S(2)}, u32[]{:S(2)}) %collective-permute-start.32) | collective-permute-done | bytes 196640 | tf_op jit(solution)/shard_map/ppermute | solution.py:26
  91.2 1.0 collective-permute-start.24
  92.4 2.4 %collective-permute-start.20 = (bf16[2304,128]{1,0:T(8,128)(2,1)S(1)}, bf16[2304,128]{1,0:T(8,128)(2,1)S(1)}, u32[]{:S(2)}, u32[]{:S(2)}) collective-permute-start(bf16[2304,128]{1,0:T(8,128)(2,1)S(1)} %pad_maximum_fusion.1), channel_id=1, source_target_pairs={{0,12},{4,8},{8,4},{12,0},{1,13},{5,9},{9,5},{13,1},{2,14},{6,10},... | collective-permute-start | bytes 1769480 | tf_op jit(solution)/shard_map/ppermute | solution.py:26
  95.0 2.4 %collective-permute-start.15 = (bf16[2304,128]{1,0:T(8,128)(2,1)S(1)}, bf16[2304,128]{1,0:T(8,128)(2,1)S(1)}, u32[]{:S(2)}, u32[]{:S(2)}) collective-permute-start(bf16[2304,128]{1,0:T(8,128)(2,1)S(1)} %pad_maximum_fusion), channel_id=1, source_target_pairs={{0,96},{32,64},{64,32},{96,0},{1,97},{33,65},{65,33},{97,1},{2,98}... | collective-permute-start | bytes 1769480 | tf_op jit(solution)/shard_map/ppermute | solution.py:26
  97.6 1.2 collective-permute-start.12
  98.8 3.5 %collective-permute-done.30 = bf16[1536,128]{1,0:T(8,128)(2,1)S(1)} collective-permute-done((bf16[1536,128]{1,0:T(8,128)(2,1)S(1)}, bf16[1536,128]{1,0:T(8,128)(2,1)S(1)}, u32[]{:S(2)}, u32[]{:S(2)}) %collective-permute-start.30) | collective-permute-done | bytes 393248 | tf_op jit(solution)/shard_map/ppermute | solution.py:26
  102.4 2.8 %collective-permute-start.33 = (bf16[1152,128]{1,0:T(8,128)(2,1)S(1)}, bf16[1152,128]{1,0:T(8,128)(2,1)S(1)}, u32[]{:S(2)}, u32[]{:S(2)}) collective-permute-start(bf16[1152,128]{1,0:T(8,128)(2,1)S(1)} %pad_maximum_fusion.5), channel_id=1, source_target_pairs={{0,96},{32,64},{64,32},{96,0},{1,97},{33,65},{65,33},{97,1},{2,98}... | collective-permute-start | bytes 884744 | tf_op jit(solution)/shard_map/ppermute | solution.py:26
  105.3 1.4 collective-permute-start.27
  106.7 2.4 %collective-permute-done.20 = bf16[2304,128]{1,0:T(8,128)(2,1)S(1)} collective-permute-done((bf16[2304,128]{1,0:T(8,128)(2,1)S(1)}, bf16[2304,128]{1,0:T(8,128)(2,1)S(1)}, u32[]{:S(2)}, u32[]{:S(2)}) %collective-permute-start.20) | collective-permute-done | bytes 589856 | tf_op jit(solution)/shard_map/ppermute | solution.py:26
  109.3 1.9 %collective-permute-start.21 = (bf16[1152,128]{1,0:T(8,128)(2,1)S(1)}, bf16[1152,128]{1,0:T(8,128)(2,1)S(1)}, u32[]{:S(2)}, u32[]{:S(2)}) collective-permute-start(bf16[1152,128]{1,0:T(8,128)(2,1)S(1)} %pad_maximum_fusion.3), channel_id=1, source_target_pairs={{0,32},{32,0},{64,96},{96,64},{1,33},{33,1},{65,97},{97,65},{2,34}... | collective-permute-start | bytes 884744 | tf_op jit(solution)/shard_map/ppermute | solution.py:26
  111.2 1.2 collective-permute-done.15
  113.1 4.4 %collective-permute-done.33 = bf16[1152,128]{1,0:T(8,128)(2,1)S(1)} collective-permute-done((bf16[1152,128]{1,0:T(8,128)(2,1)S(1)}, bf16[1152,128]{1,0:T(8,128)(2,1)S(1)}, u32[]{:S(2)}, u32[]{:S(2)}) %collective-permute-start.33) | collective-permute-done | bytes 294944 | tf_op jit(solution)/shard_map/ppermute | solution.py:26
  117.8 1.0 collective-permute-start.28
  118.8 4.0 %collective-permute-done.34 = bf16[576,128]{1,0:T(8,128)(2,1)S(1)} collective-permute-done((bf16[576,128]{1,0:T(8,128)(2,1)S(1)}, bf16[576,128]{1,0:T(8,128)(2,1)S(1)}, u32[]{:S(2)}, u32[]{:S(2)}) %collective-permute-start.34) | collective-permute-done | bytes 147488 | tf_op jit(solution)/shard_map/ppermute | solution.py:26
  123.3 1.2 collective-permute-start.17
  124.6 2.4 %collective-permute-start.22 = (bf16[576,128]{1,0:T(8,128)(2,1)S(1)}, bf16[576,128]{1,0:T(8,128)(2,1)S(1)}, u32[]{:S(2)}, u32[]{:S(2)}) collective-permute-start(bf16[576,128]{1,0:T(8,128)(2,1)S(1)} %pad_maximum_fusion.7), channel_id=1, source_target_pairs={{0,96},{32,64},{64,32},{96,0},{1,97},{33,65},{65,33},{97,1},{2,98}... | collective-permute-start | bytes 442376 | tf_op jit(solution)/shard_map/ppermute | solution.py:26
  127.0 1.2 shard_map.116
  128.2 1.5 %collective-permute-done.17 = bf16[576,128]{1,0:T(8,128)(2,1)S(1)} collective-permute-done((bf16[576,128]{1,0:T(8,128)(2,1)S(1)}, bf16[576,128]{1,0:T(8,128)(2,1)S(1)}, u32[]{:S(2)}, u32[]{:S(2)}) %collective-permute-start.17) | collective-permute-done | bytes 147488 | tf_op jit(solution)/shard_map/ppermute | solution.py:26
  129.8 1.3 collective-permute-done.22
  131.3 3.7 %collective-permute-start.35 = (bf16[1152,128]{1,0:T(8,128)(2,1)S(1)}, bf16[1152,128]{1,0:T(8,128)(2,1)S(1)}, u32[]{:S(2)}, u32[]{:S(2)}) collective-permute-start(bf16[1152,128]{1,0:T(8,128)(2,1)S(1)} %fusion.7), channel_id=1, source_target_pairs={{0,16},{16,0},{1,17},{17,1},{2,18},{18,2},{3,19},{19,3},{4,20},{20... | collective-permute-start | bytes 884744 | tf_op jit(solution)/shard_map/ppermute | solution.py:26
  135.1 4.6 %collective-permute-done.35.refs_8_ = bf16[1152,128]{1,0:T(8,128)(2,1)S(1)} collective-permute-done((bf16[1152,128]{1,0:T(8,128)(2,1)S(1)}, bf16[1152,128]{1,0:T(8,128)(2,1)S(1)}, u32[]{:S(2)}, u32[]{:S(2)}) %collective-permute-start.35) | collective-permute-done | bytes 294944 | tf_op jit(solution)/shard_map/ppermute | solution.py:26
  139.7 0.8 shard_map.124
  (111 shorter events, 10.1 us)
Async XLA Ops:
  0.6 30.3 %copy-start.6 = (bf16[128,2048]{1,0:T(8,128)(2,1)S(1)}, bf16[128,2048]{1,0:T(8,128)(2,1)}, u32[]{:S(2)}) copy-start(bf16[128,2048]{1,0:T(8,128)(2,1)} %x0.1) | copy-start | bytes 1572868
  0.6 14.2 %collective-permute-start.9 = (bf16[128,2048]{1,0:T(8,128)(2,1)}, bf16[128,2048]{1,0:T(8,128)(2,1)S(1)}, u32[]{:S(2)}, u32[]{:S(2)}) collective-permute-start(bf16[128,2048]{1,0:T(8,128)(2,1)} %x0.1), channel_id=1, source_target_pairs={{0,2},{2,0},{1,3},{3,1},{4,6},{6,4},{5,7},{7,5},{8,10},{10,8},{9,1... | collective-permute-start | bytes 1572872 | tf_op jit(solution)/shard_map/ppermute | solution.py:26
  2.7 27.7 %collective-permute-start.2 = (bf16[128,2048]{1,0:T(8,128)(2,1)}, bf16[128,2048]{1,0:T(8,128)(2,1)S(1)}, u32[]{:S(2)}, u32[]{:S(2)}) collective-permute-start(bf16[128,2048]{1,0:T(8,128)(2,1)} %x0.1), channel_id=1, source_target_pairs={{0,1},{1,0},{2,3},{3,2},{4,5},{5,4},{6,7},{7,6},{8,9},{9,8},{10,11... | collective-permute-start | bytes 1572872 | tf_op jit(solution)/shard_map/ppermute | solution.py:26
  2.8 0.7 copy-start.7
  3.4 0.7 copy-start.9
  4.1 13.6 %collective-permute-start.1 = (f32[8,128]{1,0:T(8,128)S(1)}, f32[8,128]{1,0:T(8,128)S(1)}, u32[]{:S(2)}, u32[]{:S(2)}) collective-permute-start(f32[8,128]{1,0:T(8,128)S(1)} %get-tuple-element.52), channel_id=1, source_target_pairs={{0,1},{1,0},{2,3},{3,2},{4,5},{5,4},{6,7},{7,6},{8,9},{9,8},{10,11... | collective-permute-start | bytes 12296 | tf_op jit(solution)/shard_map/ppermute | solution.py:26
  4.7 32.0 %collective-permute-start = (bf16[128,2048]{1,0:T(8,128)(2,1)}, bf16[128,2048]{1,0:T(8,128)(2,1)S(1)}, u32[]{:S(2)}, u32[]{:S(2)}) collective-permute-start(bf16[128,2048]{1,0:T(8,128)(2,1)} %refs_2_.7), channel_id=1, source_target_pairs={{0,1},{1,0},{2,3},{3,2},{4,5},{5,4},{6,7},{7,6},{8,9},{9,8},{10,11... | collective-permute-start | bytes 1572872 | tf_op jit(solution)/shard_map/ppermute | solution.py:26
  14.9 24.9 %collective-permute-start.10 = (bf16[128,2048]{1,0:T(8,128)(2,1)S(1)}, bf16[128,2048]{1,0:T(8,128)(2,1)S(1)}, u32[]{:S(2)}, u32[]{:S(2)}) collective-permute-start(bf16[128,2048]{1,0:T(8,128)(2,1)S(1)} %collective-permute-done.9.x0), channel_id=1, source_target_pairs={{0,1},{1,0},{2,3},{3,2},{4,5},{5,4},{6,7},{7,6},{8,9},{9,8},{10,11... | collective-permute-start | bytes 1572872 | tf_op jit(solution)/shard_map/ppermute | solution.py:26
  16.0 9.3 %collective-permute-start.4 = (bf16[128,1024]{1,0:T(8,128)(2,1)S(1)}, bf16[128,1024]{1,0:T(8,128)(2,1)S(1)}, u32[]{:S(2)}, u32[]{:S(2)}) collective-permute-start(bf16[128,1024]{1,0:T(8,128)(2,1)S(1)} %get-tuple-element.97), channel_id=1, source_target_pairs={{0,2},{2,0},{1,3},{3,1},{4,6},{6,4},{5,7},{7,5},{8,10},{10,8},{9,1... | collective-permute-start | bytes 786440 | tf_op jit(solution)/shard_map/ppermute | solution.py:26
  17.8 12.6 %collective-permute-start.3 = (bf16[128,1024]{1,0:T(8,128)(2,1)S(1)}, bf16[128,1024]{1,0:T(8,128)(2,1)S(1)}, u32[]{:S(2)}, u32[]{:S(2)}) collective-permute-start(bf16[128,1024]{1,0:T(8,128)(2,1)S(1)} %get-tuple-element.98), channel_id=1, source_target_pairs={{0,2},{2,0},{1,3},{3,1},{4,6},{6,4},{5,7},{7,5},{8,10},{10,8},{9,1... | collective-permute-start | bytes 786440 | tf_op jit(solution)/shard_map/ppermute | solution.py:26
  25.2 14.1 %collective-permute-start.7 = (f32[8,128]{1,0:T(8,128)S(1)}, f32[8,128]{1,0:T(8,128)S(1)}, u32[]{:S(2)}, u32[]{:S(2)}) collective-permute-start(f32[8,128]{1,0:T(8,128)S(1)} %get-tuple-element.57), channel_id=1, source_target_pairs={{0,2},{1,3},{2,0},{3,1},{4,6},{5,7},{6,4},{7,5},{8,10},{9,11},{10,... | collective-permute-start | bytes 12296 | tf_op jit(solution)/shard_map/ppermute | solution.py:26
  30.4 11.6 %collective-permute-start.6 = (bf16[128,1024]{1,0:T(8,128)(2,1)S(1)}, bf16[128,1024]{1,0:T(8,128)(2,1)S(1)}, u32[]{:S(2)}, u32[]{:S(2)}) collective-permute-start(bf16[128,1024]{1,0:T(8,128)(2,1)S(1)} %collective-permute-done.4.refs_1_.refs_4_), channel_id=1, source_target_pairs={{0,1},{1,0},{2,3},{3,2},{4,5},{5,4},{6,7},{7,6},{8,9},{9,8},{10,11... | collective-permute-start | bytes 786440 | tf_op jit(solution)/shard_map/ppermute | solution.py:26
  30.4 11.6 %collective-permute-start.5 = (bf16[128,1024]{1,0:T(8,128)(2,1)S(1)}, bf16[128,1024]{1,0:T(8,128)(2,1)S(1)}, u32[]{:S(2)}, u32[]{:S(2)}) collective-permute-start(bf16[128,1024]{1,0:T(8,128)(2,1)S(1)} %collective-permute-done.3.refs_0_.refs_4_), channel_id=1, source_target_pairs={{0,1},{1,0},{2,3},{3,2},{4,5},{5,4},{6,7},{7,6},{8,9},{9,8},{10,11... | collective-permute-start | bytes 786440 | tf_op jit(solution)/shard_map/ppermute | solution.py:26
  30.9 1.9 %copy-start.2 = (bf16[1,2048,768]{2,1,0:T(8,128)(2,1)S(1)}, bf16[1,2048,768]{2,1,0:T(8,128)(2,1)}, u32[]{:S(2)}) copy-start(bf16[1,2048,768]{2,1,0:T(8,128)(2,1)} %param.11) | copy-start | bytes 9437188
  32.8 1.9 %copy-start.4 = (bf16[1,2048,768]{2,1,0:T(8,128)(2,1)S(1)}, bf16[1,2048,768]{2,1,0:T(8,128)(2,1)}, u32[]{:S(2)}) copy-start(bf16[1,2048,768]{2,1,0:T(8,128)(2,1)} %param.12) | copy-start | bytes 9437188
  34.7 3.4 %copy-start = (bf16[128,2048]{1,0:T(8,128)(2,1)S(1)}, bf16[128,2048]{1,0:T(8,128)(2,1)}, u32[]{:S(2)}) copy-start(bf16[128,2048]{1,0:T(8,128)(2,1)} %refs_2_.7) | copy-start | bytes 1572868
  34.7 3.4 %copy-start.1 = (bf16[1,768,2048]{2,1,0:T(8,128)(2,1)S(1)}, bf16[1,768,2048]{2,1,0:T(8,128)(2,1)}, u32[]{:S(2)}) copy-start(bf16[1,768,2048]{2,1,0:T(8,128)(2,1)} %param.13) | copy-start | bytes 9437188
  34.7 5.1 %copy-start.5 = (bf16[1,2048,768]{2,1,0:T(8,128)(2,1)S(1)}, bf16[1,2048,768]{2,1,0:T(8,128)(2,1)}, u32[]{:S(2)}) copy-start(bf16[1,2048,768]{2,1,0:T(8,128)(2,1)} %param.12) | copy-start | bytes 9437188
  36.7 3.1 %collective-permute-start.8 = (f32[8,128]{1,0:T(8,128)S(1)}, f32[8,128]{1,0:T(8,128)S(1)}, u32[]{:S(2)}, u32[]{:S(2)}) collective-permute-start(f32[8,128]{1,0:T(8,128)S(1)} %get-tuple-element.58), channel_id=1, source_target_pairs={{0,3},{1,2},{2,1},{3,0},{4,7},{5,6},{6,5},{7,4},{8,11},{9,10},{10,... | collective-permute-start | bytes 12296 | tf_op jit(solution)/shard_map/ppermute | solution.py:26
  38.2 1.9 %copy-start.3 = (bf16[1,2048,768]{2,1,0:T(8,128)(2,1)S(1)}, bf16[1,2048,768]{2,1,0:T(8,128)(2,1)}, u32[]{:S(2)}) copy-start(bf16[1,2048,768]{2,1,0:T(8,128)(2,1)} %param.11) | copy-start | bytes 9437188
  45.8 14.5 %collective-permute-start.25 = (bf16[1536,128]{1,0:T(8,128)(2,1)S(1)}, bf16[1536,128]{1,0:T(8,128)(2,1)S(1)}, u32[]{:S(2)}, u32[]{:S(2)}) collective-permute-start(bf16[1536,128]{1,0:T(8,128)(2,1)S(1)} %get-tuple-element.89), channel_id=1, source_target_pairs={{0,96},{32,64},{64,32},{96,0},{1,97},{33,65},{65,33},{97,1},{2,98}... | collective-permute-start | bytes 1179656 | tf_op jit(solution)/shard_map/ppermute | solution.py:26
  48.7 13.5 %collective-permute-start.31 = (bf16[1536,128]{1,0:T(8,128)(2,1)S(1)}, bf16[1536,128]{1,0:T(8,128)(2,1)S(1)}, u32[]{:S(2)}, u32[]{:S(2)}) collective-permute-start(bf16[1536,128]{1,0:T(8,128)(2,1)S(1)} %get-tuple-element.93), channel_id=1, source_target_pairs={{0,12},{4,8},{8,4},{12,0},{1,13},{5,9},{9,5},{13,1},{2,14},{6,10},... | collective-permute-start | bytes 1179656 | tf_op jit(solution)/shard_map/ppermute | solution.py:26
  52.3 11.0 %collective-permute-start.14 = (bf16[1536,128]{1,0:T(8,128)(2,1)S(1)}, bf16[1536,128]{1,0:T(8,128)(2,1)S(1)}, u32[]{:S(2)}, u32[]{:S(2)}) collective-permute-start(bf16[1536,128]{1,0:T(8,128)(2,1)S(1)} %get-tuple-element.81), channel_id=1, source_target_pairs={{0,32},{32,0},{64,96},{96,64},{1,33},{33,1},{65,97},{97,65},{2,34}... | collective-permute-start | bytes 1179656 | tf_op jit(solution)/shard_map/ppermute | solution.py:26
  52.6 10.9 %collective-permute-start.19 = (bf16[1536,128]{1,0:T(8,128)(2,1)S(1)}, bf16[1536,128]{1,0:T(8,128)(2,1)S(1)}, u32[]{:S(2)}, u32[]{:S(2)}) collective-permute-start(bf16[1536,128]{1,0:T(8,128)(2,1)S(1)} %get-tuple-element.85), channel_id=1, source_target_pairs={{0,4},{4,0},{8,12},{12,8},{1,5},{5,1},{9,13},{13,9},{2,6},{6,2},{1... | collective-permute-start | bytes 1179656 | tf_op jit(solution)/shard_map/ppermute | solution.py:26
  52.7 38.4 %collective-permute-start.23 = (bf16[3072,128]{1,0:T(8,128)(2,1)S(1)}, bf16[3072,128]{1,0:T(8,128)(2,1)S(1)}, u32[]{:S(2)}, u32[]{:S(2)}) collective-permute-start(bf16[3072,128]{1,0:T(8,128)(2,1)S(1)} %get-tuple-element.87), channel_id=1, source_target_pairs={{0,96},{32,64},{64,32},{96,0},{1,97},{33,65},{65,33},{97,1},{2,98}... | collective-permute-start | bytes 2359304 | tf_op jit(solution)/shard_map/ppermute | solution.py:26
  60.3 30.2 %collective-permute-start.29 = (bf16[3072,128]{1,0:T(8,128)(2,1)S(1)}, bf16[3072,128]{1,0:T(8,128)(2,1)S(1)}, u32[]{:S(2)}, u32[]{:S(2)}) collective-permute-start(bf16[3072,128]{1,0:T(8,128)(2,1)S(1)} %get-tuple-element.91), channel_id=1, source_target_pairs={{0,12},{4,8},{8,4},{12,0},{1,13},{5,9},{9,5},{13,1},{2,14},{6,10},... | collective-permute-start | bytes 2359304 | tf_op jit(solution)/shard_map/ppermute | solution.py:26
  62.2 32.6 %collective-permute-start.13 = (bf16[3072,128]{1,0:T(8,128)(2,1)S(1)}, bf16[3072,128]{1,0:T(8,128)(2,1)S(1)}, u32[]{:S(2)}, u32[]{:S(2)}) collective-permute-start(bf16[3072,128]{1,0:T(8,128)(2,1)S(1)} %get-tuple-element.77), channel_id=1, source_target_pairs={{0,32},{32,0},{64,96},{96,64},{1,33},{33,1},{65,97},{97,65},{2,34}... | collective-permute-start | bytes 2359304 | tf_op jit(solution)/shard_map/ppermute | solution.py:26
  63.3 29.0 %collective-permute-start.18 = (bf16[3072,128]{1,0:T(8,128)(2,1)S(1)}, bf16[3072,128]{1,0:T(8,128)(2,1)S(1)}, u32[]{:S(2)}, u32[]{:S(2)}) collective-permute-start(bf16[3072,128]{1,0:T(8,128)(2,1)S(1)} %get-tuple-element.83), channel_id=1, source_target_pairs={{0,4},{4,0},{8,12},{12,8},{1,5},{5,1},{9,13},{13,9},{2,6},{6,2},{1... | collective-permute-start | bytes 2359304 | tf_op jit(solution)/shard_map/ppermute | solution.py:26
  63.5 21.3 %collective-permute-start.26 = (bf16[768,128]{1,0:T(8,128)(2,1)S(1)}, bf16[768,128]{1,0:T(8,128)(2,1)S(1)}, u32[]{:S(2)}, u32[]{:S(2)}) collective-permute-start(bf16[768,128]{1,0:T(8,128)(2,1)S(1)} %add_convert_fusion.7), channel_id=1, source_target_pairs={{0,32},{32,0},{64,96},{96,64},{1,33},{33,1},{65,97},{97,65},{2,34}... | collective-permute-start | bytes 589832 | tf_op jit(solution)/shard_map/ppermute | solution.py:26
  84.8 5.7 %collective-permute-start.32 = (bf16[768,128]{1,0:T(8,128)(2,1)S(1)}, bf16[768,128]{1,0:T(8,128)(2,1)S(1)}, u32[]{:S(2)}, u32[]{:S(2)}) collective-permute-start(bf16[768,128]{1,0:T(8,128)(2,1)S(1)} %add_convert_fusion.5), channel_id=1, source_target_pairs={{0,4},{4,0},{8,12},{12,8},{1,5},{5,1},{9,13},{13,9},{2,6},{6,2},{1... | collective-permute-start | bytes 589832 | tf_op jit(solution)/shard_map/ppermute | solution.py:26
  90.5 6.9 %collective-permute-start.11 = (bf16[256,2176]{1,0:T(8,128)(2,1)S(1)}, bf16[256,2176]{1,0:T(8,128)(2,1)S(1)}, u32[]{:S(2)}, u32[]{:S(2)}) collective-permute-start(bf16[256,2176]{1,0:T(8,128)(2,1)S(1)} %get-tuple-element.70), channel_id=1, source_target_pairs={{0,1},{1,0},{2,3},{3,2},{4,5},{5,4},{6,7},{7,6},{8,9},{9,8},{10,11... | collective-permute-start | bytes 3342344 | tf_op jit(solution)/shard_map/ppermute | solution.py:26
  90.7 11.6 %collective-permute-start.30 = (bf16[1536,128]{1,0:T(8,128)(2,1)S(1)}, bf16[1536,128]{1,0:T(8,128)(2,1)S(1)}, u32[]{:S(2)}, u32[]{:S(2)}) collective-permute-start(bf16[1536,128]{1,0:T(8,128)(2,1)S(1)} %add_convert_fusion.1), channel_id=1, source_target_pairs={{0,4},{4,0},{8,12},{12,8},{1,5},{5,1},{9,13},{13,9},{2,6},{6,2},{1... | collective-permute-start | bytes 1179656 | tf_op jit(solution)/shard_map/ppermute | solution.py:26
  91.2 14.0 %collective-permute-start.24 = (bf16[1536,128]{1,0:T(8,128)(2,1)S(1)}, bf16[1536,128]{1,0:T(8,128)(2,1)S(1)}, u32[]{:S(2)}, u32[]{:S(2)}) collective-permute-start(bf16[1536,128]{1,0:T(8,128)(2,1)S(1)} %add_convert_fusion.2), channel_id=1, source_target_pairs={{0,32},{32,0},{64,96},{96,64},{1,33},{33,1},{65,97},{97,65},{2,34}... | collective-permute-start | bytes 1179656 | tf_op jit(solution)/shard_map/ppermute | solution.py:26
  92.4 16.8 %collective-permute-start.20 = (bf16[2304,128]{1,0:T(8,128)(2,1)S(1)}, bf16[2304,128]{1,0:T(8,128)(2,1)S(1)}, u32[]{:S(2)}, u32[]{:S(2)}) collective-permute-start(bf16[2304,128]{1,0:T(8,128)(2,1)S(1)} %pad_maximum_fusion.1), channel_id=1, source_target_pairs={{0,12},{4,8},{8,4},{12,0},{1,13},{5,9},{9,5},{13,1},{2,14},{6,10},... | collective-permute-start | bytes 1769480 | tf_op jit(solution)/shard_map/ppermute | solution.py:26
  95.0 17.5 %collective-permute-start.15 = (bf16[2304,128]{1,0:T(8,128)(2,1)S(1)}, bf16[2304,128]{1,0:T(8,128)(2,1)S(1)}, u32[]{:S(2)}, u32[]{:S(2)}) collective-permute-start(bf16[2304,128]{1,0:T(8,128)(2,1)S(1)} %pad_maximum_fusion), channel_id=1, source_target_pairs={{0,96},{32,64},{64,32},{96,0},{1,97},{33,65},{65,33},{97,1},{2,98}... | collective-permute-start | bytes 1769480 | tf_op jit(solution)/shard_map/ppermute | solution.py:26
  97.6 29.5 %collective-permute-start.12 = (bf16[128,2176]{1,0:T(8,128)(2,1)S(1)}, bf16[128,2176]{1,0:T(8,128)(2,1)S(1)}, u32[]{:S(2)}, u32[]{:S(2)}) collective-permute-start(bf16[128,2176]{1,0:T(8,128)(2,1)S(1)} %add_convert_fusion), channel_id=1, source_target_pairs={{0,2},{2,0},{1,3},{3,1},{4,6},{6,4},{5,7},{7,5},{8,10},{10,8},{9,1... | collective-permute-start | bytes 1671176 | tf_op jit(solution)/shard_map/ppermute | solution.py:26
  102.4 15.1 %collective-permute-start.33 = (bf16[1152,128]{1,0:T(8,128)(2,1)S(1)}, bf16[1152,128]{1,0:T(8,128)(2,1)S(1)}, u32[]{:S(2)}, u32[]{:S(2)}) collective-permute-start(bf16[1152,128]{1,0:T(8,128)(2,1)S(1)} %pad_maximum_fusion.5), channel_id=1, source_target_pairs={{0,96},{32,64},{64,32},{96,0},{1,97},{33,65},{65,33},{97,1},{2,98}... | collective-permute-start | bytes 884744 | tf_op jit(solution)/shard_map/ppermute | solution.py:26
  105.3 12.4 %collective-permute-start.27 = (bf16[1152,128]{1,0:T(8,128)(2,1)S(1)}, bf16[1152,128]{1,0:T(8,128)(2,1)S(1)}, u32[]{:S(2)}, u32[]{:S(2)}) collective-permute-start(bf16[1152,128]{1,0:T(8,128)(2,1)S(1)} %pad_maximum_fusion.4), channel_id=1, source_target_pairs={{0,12},{4,8},{8,4},{12,0},{1,13},{5,9},{9,5},{13,1},{2,14},{6,10},... | collective-permute-start | bytes 884744 | tf_op jit(solution)/shard_map/ppermute | solution.py:26
  109.3 15.1 %collective-permute-start.21 = (bf16[1152,128]{1,0:T(8,128)(2,1)S(1)}, bf16[1152,128]{1,0:T(8,128)(2,1)S(1)}, u32[]{:S(2)}, u32[]{:S(2)}) collective-permute-start(bf16[1152,128]{1,0:T(8,128)(2,1)S(1)} %pad_maximum_fusion.3), channel_id=1, source_target_pairs={{0,32},{32,0},{64,96},{96,64},{1,33},{33,1},{65,97},{97,65},{2,34}... | collective-permute-start | bytes 884744 | tf_op jit(solution)/shard_map/ppermute | solution.py:26
  112.6 10.5 %collective-permute-start.16 = (bf16[1152,128]{1,0:T(8,128)(2,1)S(1)}, bf16[1152,128]{1,0:T(8,128)(2,1)S(1)}, u32[]{:S(2)}, u32[]{:S(2)}) collective-permute-start(bf16[1152,128]{1,0:T(8,128)(2,1)S(1)} %pad_maximum_fusion.2), channel_id=1, source_target_pairs={{0,4},{4,0},{8,12},{12,8},{1,5},{5,1},{9,13},{13,9},{2,6},{6,2},{1... | collective-permute-start | bytes 884744 | tf_op jit(solution)/shard_map/ppermute | solution.py:26
  117.6 5.2 %collective-permute-start.34 = (bf16[576,128]{1,0:T(8,128)(2,1)S(1)}, bf16[576,128]{1,0:T(8,128)(2,1)S(1)}, u32[]{:S(2)}, u32[]{:S(2)}) collective-permute-start(bf16[576,128]{1,0:T(8,128)(2,1)S(1)} %pad_maximum_fusion.9), channel_id=1, source_target_pairs={{0,32},{32,0},{64,96},{96,64},{1,33},{33,1},{65,97},{97,65},{2,34}... | collective-permute-start | bytes 442376 | tf_op jit(solution)/shard_map/ppermute | solution.py:26
  117.8 5.2 %collective-permute-start.28 = (bf16[576,128]{1,0:T(8,128)(2,1)S(1)}, bf16[576,128]{1,0:T(8,128)(2,1)S(1)}, u32[]{:S(2)}, u32[]{:S(2)}) collective-permute-start(bf16[576,128]{1,0:T(8,128)(2,1)S(1)} %pad_maximum_fusion.8), channel_id=1, source_target_pairs={{0,4},{4,0},{8,12},{12,8},{1,5},{5,1},{9,13},{13,9},{2,6},{6,2},{1... | collective-permute-start | bytes 442376 | tf_op jit(solution)/shard_map/ppermute | solution.py:26
  123.1 3.9 %copy-start.8 = (s32[128,2]{0,1:T(2,128)S(1)}, s32[128,2]{0,1:T(2,128)}, u32[]{:S(2)}) copy-start(s32[128,2]{0,1:T(2,128)} %param.9) | copy-start | bytes 3076
  123.3 6.4 %collective-permute-start.17 = (bf16[576,128]{1,0:T(8,128)(2,1)S(1)}, bf16[576,128]{1,0:T(8,128)(2,1)S(1)}, u32[]{:S(2)}, u32[]{:S(2)}) collective-permute-start(bf16[576,128]{1,0:T(8,128)(2,1)S(1)} %pad_maximum_fusion.6), channel_id=1, source_target_pairs={{0,12},{4,8},{8,4},{12,0},{1,13},{5,9},{9,5},{13,1},{2,14},{6,10},... | collective-permute-start | bytes 442376 | tf_op jit(solution)/shard_map/ppermute | solution.py:26
  124.6 6.4 %collective-permute-start.22 = (bf16[576,128]{1,0:T(8,128)(2,1)S(1)}, bf16[576,128]{1,0:T(8,128)(2,1)S(1)}, u32[]{:S(2)}, u32[]{:S(2)}) collective-permute-start(bf16[576,128]{1,0:T(8,128)(2,1)S(1)} %pad_maximum_fusion.7), channel_id=1, source_target_pairs={{0,96},{32,64},{64,32},{96,0},{1,97},{33,65},{65,33},{97,1},{2,98}... | collective-permute-start | bytes 442376 | tf_op jit(solution)/shard_map/ppermute | solution.py:26
  131.3 8.4 %collective-permute-start.35 = (bf16[1152,128]{1,0:T(8,128)(2,1)S(1)}, bf16[1152,128]{1,0:T(8,128)(2,1)S(1)}, u32[]{:S(2)}, u32[]{:S(2)}) collective-permute-start(bf16[1152,128]{1,0:T(8,128)(2,1)S(1)} %fusion.7), channel_id=1, source_target_pairs={{0,16},{16,0},{1,17},{17,1},{2,18},{18,2},{3,19},{19,3},{4,20},{20... | collective-permute-start | bytes 884744 | tf_op jit(solution)/shard_map/ppermute | solution.py:26

commit v8 on v6

--- a/solution.py
+++ b/solution.py
@@ -267,14 +267,15 @@
 
 
 def finish_body(*refs):
-    bases, last, (gate, up, down) = refs[:8], refs[8], refs[9:]
+    bases, lasts, (gate, up, down) = refs[:8], refs[8:10], refs[10:]
     half, low = gate.shape[0] // 2, down.shape[0]
     cols = down.shape[1] // 4
-    received = last[...].astype(F32)
-    done, at = [], 0
-    for base in bases:
-        done.append(base[...] + received[at : at + base.shape[0]])
-        at += base.shape[0]
+    received = [r[...].astype(F32) for r in lasts]
+    done, at = [], [0, 0]
+    for n, base in enumerate(bases):
+        k = n % 4 // 2
+        done.append(base[...] + received[k][at[k] : at[k] + base.shape[0]])
+        at[k] += base.shape[0]
     for (p, first, _), total in zip(EARLY + LATER, done):
         out = gate if p < 2 else up
         for k in range(total.shape[0] // half):
@@ -350,11 +351,12 @@
     for step in (1, 2, 3):
         for p in CHAINS:
             exchange(have[p], ORDERS[p][step])
-    last = exchange(gates + downs, Z)
+    last_a = exchange(gates[:2] + downs[:2], Z)
+    last_b = exchange(gates[2:] + downs[2:], Z)
     bases = [summed(h[:-1], 0, 1, F32) for h in gates + downs]
     gate_grad, up_grad, down_grad = kernel(
         finish_body,
-        (*bases, last),
+        (*bases, last_a, last_b),
         [((d // BLOCKS, ff), BF16), ((d // BLOCKS, ff), BF16), ((ff // BLOCKS, d), BF16)],
         4,
         1 << 20,

time: 128 us -> 124 us (0.969)
  waiting for transfers between devices: 58.2 us -> 51.2 us
  starting transfers between devices: 41.6 us -> 44.4 us
    ppermute x34 -> x35, waiting for transfers between devices: 58.2 us -> 51.2 us  [moved(): lax.ppermute(array, axis, [(i, i ^ mask) for i in range(lax.axis_size(axi...]
    ppermute x34 -> x35, starting transfers between devices: 41.6 us -> 44.4 us  [moved(): lax.ppermute(array, axis, [(i, i ^ mask) for i in range(lax.axis_size(axi...]
  transfers between devices with their start and end apart: 34 -> 35, of which waited for: 14 -> 12; matrix products, arithmetic and copies ran while one was open for 3% -> 3% of each run, Pallas kernels for 10% -> 11%
where the time goes in v8:
time: 124 us; the launch traced here: 123 us
  waiting for transfers between devices  51.2 us (41%)
  starting transfers between devices  44.4 us (36%)
  Pallas kernels  17.8 us (14%)
  local copies, waits for them, and re-layouts  6.43 us (5%)
  other arithmetic  2.37 us (2%)
    ppermute x35, waiting for transfers between devices, moved(): lax.ppermute(array, axis, [(i, i ^ mask) for i in range(lax.axis_size(axi...  51.2 us
    ppermute x35, starting transfers between devices, moved(): lax.ppermute(array, axis, [(i, i ^ mask) for i in range(lax.axis_size(axi...  44.4 us
    pallas_call x15, Pallas kernels, kernel(): pl.pallas_call(body, in_specs=[vmem] * len(ins), out_specs=[vmem] * len(o...  17.8 us
    unnamed x20, local copies, waits for them, and re-layouts  5.37 us
  transfers between devices with their start and end apart: 35, of which 12 were waited for; matrix products, arithmetic and copies ran while one was open for 3% of the time, Pallas kernels for 11%

profile of v8, /device:TPU:0, one launch (start us, length us, event | category | flops | bytes accessed | tf_op | source)
XLA Modules:
  0.0 123.3 jit_solution(321647914385851342)
XLA Ops:
  0.6 2.1 %collective-permute-start.9 = (bf16[128,2048]{1,0:T(8,128)(2,1)}, bf16[128,2048]{1,0:T(8,128)(2,1)S(1)}, u32[]{:S(2)}, u32[]{:S(2)}) collective-permute-start(bf16[128,2048]{1,0:T(8,128)(2,1)} %x0.1), channel_id=1, source_target_pairs={{0,2},{2,0},{1,3},{3,1},{4,6},{6,4},{5,7},{7,5},{8,10},{10,8},{9,1... | collective-permute-start | bytes 1572872 | tf_op jit(solution)/shard_map/ppermute | solution.py:26
  2.8 0.7 copy-done.7
  3.4 0.7 copy-done.9
  4.1 0.6 collective-permute-start.1
  4.8 10.1 %collective-permute-done.9.x0 = bf16[128,2048]{1,0:T(8,128)(2,1)S(1)} collective-permute-done((bf16[128,2048]{1,0:T(8,128)(2,1)}, bf16[128,2048]{1,0:T(8,128)(2,1)S(1)}, u32[]{:S(2)}, u32[]{:S(2)}) %collective-permute-start.9) | collective-permute-done | bytes 524320 | tf_op jit(solution)/shard_map/ppermute | solution.py:26
  14.9 1.1 fusion
  16.0 1.8 %collective-permute-start.4 = (bf16[128,1024]{1,0:T(8,128)(2,1)S(1)}, bf16[128,1024]{1,0:T(8,128)(2,1)S(1)}, u32[]{:S(2)}, u32[]{:S(2)}) collective-permute-start(bf16[128,1024]{1,0:T(8,128)(2,1)S(1)} %get-tuple-element.113), channel_id=1, source_target_pairs={{0,2},{2,0},{1,3},{3,1},{4,6},{6,4},{5,7},{7,5},{8,10},{10,8},{9,1... | collective-permute-start | bytes 786440 | tf_op jit(solution)/shard_map/ppermute | solution.py:26
  18.1 7.1 %collective-permute-done.4.refs_1_.refs_4_ = bf16[128,1024]{1,0:T(8,128)(2,1)S(1)} collective-permute-done((bf16[128,1024]{1,0:T(8,128)(2,1)S(1)}, bf16[128,1024]{1,0:T(8,128)(2,1)S(1)}, u32[]{:S(2)}, u32[]{:S(2)}) %collective-permute-start.4) | collective-permute-done | bytes 262176 | tf_op jit(solution)/shard_map/ppermute | solution.py:26
  25.2 1.7 %collective-permute-start.7 = (f32[8,128]{1,0:T(8,128)S(1)}, f32[8,128]{1,0:T(8,128)S(1)}, u32[]{:S(2)}, u32[]{:S(2)}) collective-permute-start(f32[8,128]{1,0:T(8,128)S(1)} %get-tuple-element.57), channel_id=1, source_target_pairs={{0,2},{1,3},{2,0},{3,1},{4,6},{5,7},{6,4},{7,5},{8,10},{9,11},{10,... | collective-permute-start | bytes 12296 | tf_op jit(solution)/shard_map/ppermute | solution.py:26
  27.0 3.5 %collective-permute-done.3.refs_0_.refs_4_ = bf16[128,1024]{1,0:T(8,128)(2,1)S(1)} collective-permute-done((bf16[128,1024]{1,0:T(8,128)(2,1)S(1)}, bf16[128,1024]{1,0:T(8,128)(2,1)S(1)}, u32[]{:S(2)}, u32[]{:S(2)}) %collective-permute-start.3) | collective-permute-done | bytes 262176 | tf_op jit(solution)/shard_map/ppermute | solution.py:26
  30.9 1.9 %copy-done.2 = bf16[1,2048,768]{2,1,0:T(8,128)(2,1)S(1)} copy-done((bf16[1,2048,768]{2,1,0:T(8,128)(2,1)S(1)}, bf16[1,2048,768]{2,1,0:T(8,128)(2,1)}, u32[]{:S(2)}) %copy-start.2) | copy-done | bytes 3145752
  32.8 1.9 %copy-done.4 = bf16[1,2048,768]{2,1,0:T(8,128)(2,1)S(1)} copy-done((bf16[1,2048,768]{2,1,0:T(8,128)(2,1)S(1)}, bf16[1,2048,768]{2,1,0:T(8,128)(2,1)}, u32[]{:S(2)}) %copy-start.4) | copy-done | bytes 3145752
  34.7 2.0 %shard_map.111 = (f32[256,768]{1,0:T(8,128)S(1)}, f32[256,768]{1,0:T(8,128)S(1)}, bf16[256,768]{1,0:T(8,128)(2,1)S(1)}, f32[768,256]{1,0:T(8,128)S(1)}, bf16[2048,256]{1,0:T(8,128)(2,1)S(1)}) custom-call(bf16[128,2048]{1,0:T(8,128)(2,1)S(1)} %copy-done.6, bf16[128,2048]{1,0:T(8,128)(2,1)S(1)} %collective-permute-done.2.x1, ...), custom_call_target="tpu_custom_call" | custom-call | flops 1610612736 | bytes 1048576 | tf_op jit(solution)/shard_map/pallas_call | solution.py:60
  36.7 1.4 %collective-permute-start.8 = (f32[8,128]{1,0:T(8,128)S(1)}, f32[8,128]{1,0:T(8,128)S(1)}, u32[]{:S(2)}, u32[]{:S(2)}) collective-permute-start(f32[8,128]{1,0:T(8,128)S(1)} %get-tuple-element.58), channel_id=1, source_target_pairs={{0,3},{1,2},{2,1},{3,0},{4,7},{5,6},{6,5},{7,4},{8,11},{9,10},{10,... | collective-permute-start | bytes 12296 | tf_op jit(solution)/shard_map/ppermute | solution.py:26
  38.2 1.2 shard_map.112
  40.0 2.0 %shard_map.113 = (f32[256,768]{1,0:T(8,128)S(1)}, f32[256,768]{1,0:T(8,128)S(1)}, bf16[256,768]{1,0:T(8,128)(2,1)S(1)}, f32[768,256]{1,0:T(8,128)S(1)}, bf16[2048,256]{1,0:T(8,128)(2,1)S(1)}) custom-call(bf16[128,2048]{1,0:T(8,128)(2,1)S(1)} %collective-permute-done.9.x0, bf16[128,2048]{1,0:T(8,128)(2,1)S(1)} %collective-permute-done.10.x1, ...), custom_call_target="tpu_custom_call" | custom-call | flops 1610612736 | bytes 1048576 | tf_op jit(solution)/shard_map/pallas_call | solution.py:60
  42.0 1.2 shard_map.114
  43.2 1.0 shard_map.121
  44.2 1.0 shard_map.118
  45.2 0.6 shard_map.123
  45.8 2.8 %collective-permute-start.24 = (bf16[1536,128]{1,0:T(8,128)(2,1)S(1)}, bf16[1536,128]{1,0:T(8,128)(2,1)S(1)}, u32[]{:S(2)}, u32[]{:S(2)}) collective-permute-start(bf16[1536,128]{1,0:T(8,128)(2,1)S(1)} %get-tuple-element.89), channel_id=1, source_target_pairs={{0,96},{32,64},{64,32},{96,0},{1,97},{33,65},{65,33},{97,1},{2,98}... | collective-permute-start | bytes 1179656 | tf_op jit(solution)/shard_map/ppermute | solution.py:26
  48.7 3.0 %collective-permute-start.29 = (bf16[1536,128]{1,0:T(8,128)(2,1)S(1)}, bf16[1536,128]{1,0:T(8,128)(2,1)S(1)}, u32[]{:S(2)}, u32[]{:S(2)}) collective-permute-start(bf16[1536,128]{1,0:T(8,128)(2,1)S(1)} %get-tuple-element.93), channel_id=1, source_target_pairs={{0,12},{4,8},{8,4},{12,0},{1,13},{5,9},{9,5},{13,1},{2,14},{6,10},... | collective-permute-start | bytes 1179656 | tf_op jit(solution)/shard_map/ppermute | solution.py:26
  52.7 1.1 collective-permute-start.23
  53.8 0.6 shard_map.122
  54.4 3.4 %shard_map.115 = (bf16[128,2176]{1,0:T(8,128)(2,1)S(1)}, bf16[256,2176]{1,0:T(8,128)(2,1)S(1)}, bf16[128,2176]{1,0:T(8,128)(2,1)S(1)}) custom-call(bf16[256,768]{1,0:T(8,128)(2,1)S(1)} %get-tuple-element.56.gda.refs_2_, bf16[256,768]{1,0:T(8,128)(2,1)S(1)} %get-tuple-element.62.gdb.refs_3_, bf16[256,768]{1,0:T(8,128)(2,1)S(1)} %get-tuple-element.63.uda.refs_4_, ...), custom_call_target="tpu_custom_call" | custom-call | flops 3221225472 | bytes 1048576 | tf_op jit(solution)/shard_map/pallas_call | solution.py:60
  57.9 0.6 shard_map.119
  58.5 1.8 %shard_map.117 = (bf16[3072,128]{1,0:T(8,128)(2,1)S(1)}, bf16[3072,128]{1,0:T(8,128)(2,1)S(1)}, bf16[3072,128]{1,0:T(8,128)(2,1)S(1)}, bf16[3072,128]{1,0:T(8,128)(2,1)S(1)}) custom-call(bf16[2048,256]{1,0:T(8,128)(2,1)S(1)} %get-tuple-element.74.refs_0_, bf16[2048,256]{1,0:T(8,128)(2,1)S(1)} %get-tuple-element.75.refs_1_, ...), custom_call_target="tpu_custom_call" | custom-call | flops 1610612736 | bytes 1048576 | tf_op jit(solution)/shard_map/pallas_call | solution.py:60
  60.3 1.8 %collective-permute-start.28 = (bf16[3072,128]{1,0:T(8,128)(2,1)S(1)}, bf16[3072,128]{1,0:T(8,128)(2,1)S(1)}, u32[]{:S(2)}, u32[]{:S(2)}) collective-permute-start(bf16[3072,128]{1,0:T(8,128)(2,1)S(1)} %get-tuple-element.91), channel_id=1, source_target_pairs={{0,12},{4,8},{8,4},{12,0},{1,13},{5,9},{9,5},{13,1},{2,14},{6,10},... | collective-permute-start | bytes 2359304 | tf_op jit(solution)/shard_map/ppermute | solution.py:26
  62.6 0.7 collective-permute-done.14
  63.7 16.6 %collective-permute-done.28 = bf16[3072,128]{1,0:T(8,128)(2,1)S(1)} collective-permute-done((bf16[3072,128]{1,0:T(8,128)(2,1)S(1)}, bf16[3072,128]{1,0:T(8,128)(2,1)S(1)}, u32[]{:S(2)}, u32[]{:S(2)}) %collective-permute-start.28) | collective-permute-done | bytes 786464 | tf_op jit(solution)/shard_map/ppermute | solution.py:26
  80.4 0.6 collective-permute-start.30
  81.2 1.0 collective-permute-start.25
  82.4 1.0 collective-permute-start.20
  83.5 2.4 %collective-permute-start.15 = (bf16[2304,128]{1,0:T(8,128)(2,1)S(1)}, bf16[2304,128]{1,0:T(8,128)(2,1)S(1)}, u32[]{:S(2)}, u32[]{:S(2)}) collective-permute-start(bf16[2304,128]{1,0:T(8,128)(2,1)S(1)} %pad_maximum_fusion), channel_id=1, source_target_pairs={{0,96},{32,64},{64,32},{96,0},{1,97},{33,65},{65,33},{97,1},{2,98}... | collective-permute-start | bytes 1769480 | tf_op jit(solution)/shard_map/ppermute | solution.py:26
  86.1 1.7 %collective-permute-start.12 = (bf16[128,2176]{1,0:T(8,128)(2,1)S(1)}, bf16[128,2176]{1,0:T(8,128)(2,1)S(1)}, u32[]{:S(2)}, u32[]{:S(2)}) collective-permute-start(bf16[128,2176]{1,0:T(8,128)(2,1)S(1)} %add_convert_fusion), channel_id=1, source_target_pairs={{0,2},{2,0},{1,3},{3,1},{4,6},{6,4},{5,7},{7,5},{8,10},{10,8},{9,1... | collective-permute-start | bytes 1671176 | tf_op jit(solution)/shard_map/ppermute | solution.py:26
  87.8 6.7 %collective-permute-done.30 = bf16[2304,128]{1,0:T(8,128)(2,1)S(1)} collective-permute-done((bf16[2304,128]{1,0:T(8,128)(2,1)S(1)}, bf16[2304,128]{1,0:T(8,128)(2,1)S(1)}, u32[]{:S(2)}, u32[]{:S(2)}) %collective-permute-start.30) | collective-permute-done | bytes 589856 | tf_op jit(solution)/shard_map/ppermute | solution.py:26
  94.6 2.7 %collective-permute-start.31 = (bf16[1152,128]{1,0:T(8,128)(2,1)S(1)}, bf16[1152,128]{1,0:T(8,128)(2,1)S(1)}, u32[]{:S(2)}, u32[]{:S(2)}) collective-permute-start(bf16[1152,128]{1,0:T(8,128)(2,1)S(1)} %pad_maximum_fusion.7), channel_id=1, source_target_pairs={{0,96},{32,64},{64,32},{96,0},{1,97},{33,65},{65,33},{97,1},{2,98}... | collective-permute-start | bytes 884744 | tf_op jit(solution)/shard_map/ppermute | solution.py:26
  97.5 1.5 %collective-permute-start.26 = (bf16[1152,128]{1,0:T(8,128)(2,1)S(1)}, bf16[1152,128]{1,0:T(8,128)(2,1)S(1)}, u32[]{:S(2)}, u32[]{:S(2)}) collective-permute-start(bf16[1152,128]{1,0:T(8,128)(2,1)S(1)} %pad_maximum_fusion.6), channel_id=1, source_target_pairs={{0,12},{4,8},{8,4},{12,0},{1,13},{5,9},{9,5},{13,1},{2,14},{6,10},... | collective-permute-start | bytes 884744 | tf_op jit(solution)/shard_map/ppermute | solution.py:26
  99.8 1.6 %collective-permute-start.16 = (bf16[1152,128]{1,0:T(8,128)(2,1)S(1)}, bf16[1152,128]{1,0:T(8,128)(2,1)S(1)}, u32[]{:S(2)}, u32[]{:S(2)}) collective-permute-start(bf16[1152,128]{1,0:T(8,128)(2,1)S(1)} %pad_maximum_fusion.4), channel_id=1, source_target_pairs={{0,4},{4,0},{8,12},{12,8},{1,5},{5,1},{9,13},{13,9},{2,6},{6,2},{1... | collective-permute-start | bytes 884744 | tf_op jit(solution)/shard_map/ppermute | solution.py:26
  101.4 2.9 %collective-permute-done.31 = bf16[1152,128]{1,0:T(8,128)(2,1)S(1)} collective-permute-done((bf16[1152,128]{1,0:T(8,128)(2,1)S(1)}, bf16[1152,128]{1,0:T(8,128)(2,1)S(1)}, u32[]{:S(2)}, u32[]{:S(2)}) %collective-permute-start.31) | collective-permute-done | bytes 294944 | tf_op jit(solution)/shard_map/ppermute | solution.py:26
  105.6 0.6 collective-permute-start.27
  106.4 2.3 %collective-permute-start.22 = (bf16[576,128]{1,0:T(8,128)(2,1)S(1)}, bf16[576,128]{1,0:T(8,128)(2,1)S(1)}, u32[]{:S(2)}, u32[]{:S(2)}) collective-permute-start(bf16[576,128]{1,0:T(8,128)(2,1)S(1)} %pad_maximum_fusion.9), channel_id=1, source_target_pairs={{0,96},{32,64},{64,32},{96,0},{1,97},{33,65},{65,33},{97,1},{2,98}... | collective-permute-start | bytes 442376 | tf_op jit(solution)/shard_map/ppermute | solution.py:26
  108.9 2.8 %collective-permute-start.17 = (bf16[576,128]{1,0:T(8,128)(2,1)S(1)}, bf16[576,128]{1,0:T(8,128)(2,1)S(1)}, u32[]{:S(2)}, u32[]{:S(2)}) collective-permute-start(bf16[576,128]{1,0:T(8,128)(2,1)S(1)} %pad_maximum_fusion.8), channel_id=1, source_target_pairs={{0,12},{4,8},{8,4},{12,0},{1,13},{5,9},{9,5},{13,1},{2,14},{6,10},... | collective-permute-start | bytes 442376 | tf_op jit(solution)/shard_map/ppermute | solution.py:26
  111.9 3.7 %collective-permute-start.34 = (bf16[576,128]{1,0:T(8,128)(2,1)S(1)}, bf16[576,128]{1,0:T(8,128)(2,1)S(1)}, u32[]{:S(2)}, u32[]{:S(2)}) collective-permute-start(bf16[576,128]{1,0:T(8,128)(2,1)S(1)} %pad_maximum_fusion.13), channel_id=1, source_target_pairs={{0,16},{16,0},{1,17},{17,1},{2,18},{18,2},{3,19},{19,3},{4,20},{20... | collective-permute-start | bytes 442376 | tf_op jit(solution)/shard_map/ppermute | solution.py:26
  115.9 3.3 %collective-permute-start.33 = (bf16[576,128]{1,0:T(8,128)(2,1)S(1)}, bf16[576,128]{1,0:T(8,128)(2,1)S(1)}, u32[]{:S(2)}, u32[]{:S(2)}) collective-permute-start(bf16[576,128]{1,0:T(8,128)(2,1)S(1)} %pad_maximum_fusion.12), channel_id=1, source_target_pairs={{0,16},{16,0},{1,17},{17,1},{2,18},{18,2},{3,19},{19,3},{4,20},{20... | collective-permute-start | bytes 442376 | tf_op jit(solution)/shard_map/ppermute | solution.py:26
  119.2 1.2 shard_map.116
  120.3 2.3 %collective-permute-done.33.refs_8_ = bf16[576,128]{1,0:T(8,128)(2,1)S(1)} collective-permute-done((bf16[576,128]{1,0:T(8,128)(2,1)S(1)}, bf16[576,128]{1,0:T(8,128)(2,1)S(1)}, u32[]{:S(2)}, u32[]{:S(2)}) %collective-permute-start.33) | collective-permute-done | bytes 147488 | tf_op jit(solution)/shard_map/ppermute | solution.py:26
  122.6 0.7 shard_map.124
  (105 shorter events, 7.3 us)
Async XLA Ops:
  0.6 30.3 %copy-start.6 = (bf16[128,2048]{1,0:T(8,128)(2,1)S(1)}, bf16[128,2048]{1,0:T(8,128)(2,1)}, u32[]{:S(2)}) copy-start(bf16[128,2048]{1,0:T(8,128)(2,1)} %x0.1) | copy-start | bytes 1572868
  0.6 14.2 %collective-permute-start.9 = (bf16[128,2048]{1,0:T(8,128)(2,1)}, bf16[128,2048]{1,0:T(8,128)(2,1)S(1)}, u32[]{:S(2)}, u32[]{:S(2)}) collective-permute-start(bf16[128,2048]{1,0:T(8,128)(2,1)} %x0.1), channel_id=1, source_target_pairs={{0,2},{2,0},{1,3},{3,1},{4,6},{6,4},{5,7},{7,5},{8,10},{10,8},{9,1... | collective-permute-start | bytes 1572872 | tf_op jit(solution)/shard_map/ppermute | solution.py:26
  2.7 27.7 %collective-permute-start.2 = (bf16[128,2048]{1,0:T(8,128)(2,1)}, bf16[128,2048]{1,0:T(8,128)(2,1)S(1)}, u32[]{:S(2)}, u32[]{:S(2)}) collective-permute-start(bf16[128,2048]{1,0:T(8,128)(2,1)} %x0.1), channel_id=1, source_target_pairs={{0,1},{1,0},{2,3},{3,2},{4,5},{5,4},{6,7},{7,6},{8,9},{9,8},{10,11... | collective-permute-start | bytes 1572872 | tf_op jit(solution)/shard_map/ppermute | solution.py:26
  2.8 0.7 copy-start.7
  3.4 0.7 copy-start.9
  4.1 13.6 %collective-permute-start.1 = (f32[8,128]{1,0:T(8,128)S(1)}, f32[8,128]{1,0:T(8,128)S(1)}, u32[]{:S(2)}, u32[]{:S(2)}) collective-permute-start(f32[8,128]{1,0:T(8,128)S(1)} %get-tuple-element.52), channel_id=1, source_target_pairs={{0,1},{1,0},{2,3},{3,2},{4,5},{5,4},{6,7},{7,6},{8,9},{9,8},{10,11... | collective-permute-start | bytes 12296 | tf_op jit(solution)/shard_map/ppermute | solution.py:26
  4.7 32.0 %collective-permute-start = (bf16[128,2048]{1,0:T(8,128)(2,1)}, bf16[128,2048]{1,0:T(8,128)(2,1)S(1)}, u32[]{:S(2)}, u32[]{:S(2)}) collective-permute-start(bf16[128,2048]{1,0:T(8,128)(2,1)} %refs_2_.7), channel_id=1, source_target_pairs={{0,1},{1,0},{2,3},{3,2},{4,5},{5,4},{6,7},{7,6},{8,9},{9,8},{10,11... | collective-permute-start | bytes 1572872 | tf_op jit(solution)/shard_map/ppermute | solution.py:26
  14.9 24.9 %collective-permute-start.10 = (bf16[128,2048]{1,0:T(8,128)(2,1)S(1)}, bf16[128,2048]{1,0:T(8,128)(2,1)S(1)}, u32[]{:S(2)}, u32[]{:S(2)}) collective-permute-start(bf16[128,2048]{1,0:T(8,128)(2,1)S(1)} %collective-permute-done.9.x0), channel_id=1, source_target_pairs={{0,1},{1,0},{2,3},{3,2},{4,5},{5,4},{6,7},{7,6},{8,9},{9,8},{10,11... | collective-permute-start | bytes 1572872 | tf_op jit(solution)/shard_map/ppermute | solution.py:26
  16.0 9.3 %collective-permute-start.4 = (bf16[128,1024]{1,0:T(8,128)(2,1)S(1)}, bf16[128,1024]{1,0:T(8,128)(2,1)S(1)}, u32[]{:S(2)}, u32[]{:S(2)}) collective-permute-start(bf16[128,1024]{1,0:T(8,128)(2,1)S(1)} %get-tuple-element.113), channel_id=1, source_target_pairs={{0,2},{2,0},{1,3},{3,1},{4,6},{6,4},{5,7},{7,5},{8,10},{10,8},{9,1... | collective-permute-start | bytes 786440 | tf_op jit(solution)/shard_map/ppermute | solution.py:26
  17.8 12.6 %collective-permute-start.3 = (bf16[128,1024]{1,0:T(8,128)(2,1)S(1)}, bf16[128,1024]{1,0:T(8,128)(2,1)S(1)}, u32[]{:S(2)}, u32[]{:S(2)}) collective-permute-start(bf16[128,1024]{1,0:T(8,128)(2,1)S(1)} %get-tuple-element.114), channel_id=1, source_target_pairs={{0,2},{2,0},{1,3},{3,1},{4,6},{6,4},{5,7},{7,5},{8,10},{10,8},{9,1... | collective-permute-start | bytes 786440 | tf_op jit(solution)/shard_map/ppermute | solution.py:26
  25.2 14.1 %collective-permute-start.7 = (f32[8,128]{1,0:T(8,128)S(1)}, f32[8,128]{1,0:T(8,128)S(1)}, u32[]{:S(2)}, u32[]{:S(2)}) collective-permute-start(f32[8,128]{1,0:T(8,128)S(1)} %get-tuple-element.57), channel_id=1, source_target_pairs={{0,2},{1,3},{2,0},{3,1},{4,6},{5,7},{6,4},{7,5},{8,10},{9,11},{10,... | collective-permute-start | bytes 12296 | tf_op jit(solution)/shard_map/ppermute | solution.py:26
  30.4 11.6 %collective-permute-start.6 = (bf16[128,1024]{1,0:T(8,128)(2,1)S(1)}, bf16[128,1024]{1,0:T(8,128)(2,1)S(1)}, u32[]{:S(2)}, u32[]{:S(2)}) collective-permute-start(bf16[128,1024]{1,0:T(8,128)(2,1)S(1)} %collective-permute-done.4.refs_1_.refs_4_), channel_id=1, source_target_pairs={{0,1},{1,0},{2,3},{3,2},{4,5},{5,4},{6,7},{7,6},{8,9},{9,8},{10,11... | collective-permute-start | bytes 786440 | tf_op jit(solution)/shard_map/ppermute | solution.py:26
  30.4 11.6 %collective-permute-start.5 = (bf16[128,1024]{1,0:T(8,128)(2,1)S(1)}, bf16[128,1024]{1,0:T(8,128)(2,1)S(1)}, u32[]{:S(2)}, u32[]{:S(2)}) collective-permute-start(bf16[128,1024]{1,0:T(8,128)(2,1)S(1)} %collective-permute-done.3.refs_0_.refs_4_), channel_id=1, source_target_pairs={{0,1},{1,0},{2,3},{3,2},{4,5},{5,4},{6,7},{7,6},{8,9},{9,8},{10,11... | collective-permute-start | bytes 786440 | tf_op jit(solution)/shard_map/ppermute | solution.py:26
  30.9 1.9 %copy-start.2 = (bf16[1,2048,768]{2,1,0:T(8,128)(2,1)S(1)}, bf16[1,2048,768]{2,1,0:T(8,128)(2,1)}, u32[]{:S(2)}) copy-start(bf16[1,2048,768]{2,1,0:T(8,128)(2,1)} %param.11) | copy-start | bytes 9437188
  32.8 1.9 %copy-start.4 = (bf16[1,2048,768]{2,1,0:T(8,128)(2,1)S(1)}, bf16[1,2048,768]{2,1,0:T(8,128)(2,1)}, u32[]{:S(2)}) copy-start(bf16[1,2048,768]{2,1,0:T(8,128)(2,1)} %param.12) | copy-start | bytes 9437188
  34.7 3.4 %copy-start = (bf16[128,2048]{1,0:T(8,128)(2,1)S(1)}, bf16[128,2048]{1,0:T(8,128)(2,1)}, u32[]{:S(2)}) copy-start(bf16[128,2048]{1,0:T(8,128)(2,1)} %refs_2_.7) | copy-start | bytes 1572868
  34.7 3.4 %copy-start.1 = (bf16[1,768,2048]{2,1,0:T(8,128)(2,1)S(1)}, bf16[1,768,2048]{2,1,0:T(8,128)(2,1)}, u32[]{:S(2)}) copy-start(bf16[1,768,2048]{2,1,0:T(8,128)(2,1)} %param.13) | copy-start | bytes 9437188
  34.7 5.1 %copy-start.5 = (bf16[1,2048,768]{2,1,0:T(8,128)(2,1)S(1)}, bf16[1,2048,768]{2,1,0:T(8,128)(2,1)}, u32[]{:S(2)}) copy-start(bf16[1,2048,768]{2,1,0:T(8,128)(2,1)} %param.12) | copy-start | bytes 9437188
  36.7 3.1 %collective-permute-start.8 = (f32[8,128]{1,0:T(8,128)S(1)}, f32[8,128]{1,0:T(8,128)S(1)}, u32[]{:S(2)}, u32[]{:S(2)}) collective-permute-start(f32[8,128]{1,0:T(8,128)S(1)} %get-tuple-element.58), channel_id=1, source_target_pairs={{0,3},{1,2},{2,1},{3,0},{4,7},{5,6},{6,5},{7,4},{8,11},{9,10},{10,... | collective-permute-start | bytes 12296 | tf_op jit(solution)/shard_map/ppermute | solution.py:26
  38.2 1.9 %copy-start.3 = (bf16[1,2048,768]{2,1,0:T(8,128)(2,1)S(1)}, bf16[1,2048,768]{2,1,0:T(8,128)(2,1)}, u32[]{:S(2)}) copy-start(bf16[1,2048,768]{2,1,0:T(8,128)(2,1)} %param.11) | copy-start | bytes 9437188
  45.8 14.5 %collective-permute-start.24 = (bf16[1536,128]{1,0:T(8,128)(2,1)S(1)}, bf16[1536,128]{1,0:T(8,128)(2,1)S(1)}, u32[]{:S(2)}, u32[]{:S(2)}) collective-permute-start(bf16[1536,128]{1,0:T(8,128)(2,1)S(1)} %get-tuple-element.89), channel_id=1, source_target_pairs={{0,96},{32,64},{64,32},{96,0},{1,97},{33,65},{65,33},{97,1},{2,98}... | collective-permute-start | bytes 1179656 | tf_op jit(solution)/shard_map/ppermute | solution.py:26
  48.7 13.5 %collective-permute-start.29 = (bf16[1536,128]{1,0:T(8,128)(2,1)S(1)}, bf16[1536,128]{1,0:T(8,128)(2,1)S(1)}, u32[]{:S(2)}, u32[]{:S(2)}) collective-permute-start(bf16[1536,128]{1,0:T(8,128)(2,1)S(1)} %get-tuple-element.93), channel_id=1, source_target_pairs={{0,12},{4,8},{8,4},{12,0},{1,13},{5,9},{9,5},{13,1},{2,14},{6,10},... | collective-permute-start | bytes 1179656 | tf_op jit(solution)/shard_map/ppermute | solution.py:26
  52.3 11.0 %collective-permute-start.14 = (bf16[1536,128]{1,0:T(8,128)(2,1)S(1)}, bf16[1536,128]{1,0:T(8,128)(2,1)S(1)}, u32[]{:S(2)}, u32[]{:S(2)}) collective-permute-start(bf16[1536,128]{1,0:T(8,128)(2,1)S(1)} %get-tuple-element.81), channel_id=1, source_target_pairs={{0,32},{32,0},{64,96},{96,64},{1,33},{33,1},{65,97},{97,65},{2,34}... | collective-permute-start | bytes 1179656 | tf_op jit(solution)/shard_map/ppermute | solution.py:26
  52.6 10.9 %collective-permute-start.19 = (bf16[1536,128]{1,0:T(8,128)(2,1)S(1)}, bf16[1536,128]{1,0:T(8,128)(2,1)S(1)}, u32[]{:S(2)}, u32[]{:S(2)}) collective-permute-start(bf16[1536,128]{1,0:T(8,128)(2,1)S(1)} %get-tuple-element.85), channel_id=1, source_target_pairs={{0,4},{4,0},{8,12},{12,8},{1,5},{5,1},{9,13},{13,9},{2,6},{6,2},{1... | collective-permute-start | bytes 1179656 | tf_op jit(solution)/shard_map/ppermute | solution.py:26
  52.7 28.3 %collective-permute-start.23 = (bf16[3072,128]{1,0:T(8,128)(2,1)S(1)}, bf16[3072,128]{1,0:T(8,128)(2,1)S(1)}, u32[]{:S(2)}, u32[]{:S(2)}) collective-permute-start(bf16[3072,128]{1,0:T(8,128)(2,1)S(1)} %get-tuple-element.87), channel_id=1, source_target_pairs={{0,96},{32,64},{64,32},{96,0},{1,97},{33,65},{65,33},{97,1},{2,98}... | collective-permute-start | bytes 2359304 | tf_op jit(solution)/shard_map/ppermute | solution.py:26
  60.3 20.0 %collective-permute-start.28 = (bf16[3072,128]{1,0:T(8,128)(2,1)S(1)}, bf16[3072,128]{1,0:T(8,128)(2,1)S(1)}, u32[]{:S(2)}, u32[]{:S(2)}) collective-permute-start(bf16[3072,128]{1,0:T(8,128)(2,1)S(1)} %get-tuple-element.91), channel_id=1, source_target_pairs={{0,12},{4,8},{8,4},{12,0},{1,13},{5,9},{9,5},{13,1},{2,14},{6,10},... | collective-permute-start | bytes 2359304 | tf_op jit(solution)/shard_map/ppermute | solution.py:26
  62.2 21.2 %collective-permute-start.13 = (bf16[3072,128]{1,0:T(8,128)(2,1)S(1)}, bf16[3072,128]{1,0:T(8,128)(2,1)S(1)}, u32[]{:S(2)}, u32[]{:S(2)}) collective-permute-start(bf16[3072,128]{1,0:T(8,128)(2,1)S(1)} %get-tuple-element.77), channel_id=1, source_target_pairs={{0,32},{32,0},{64,96},{96,64},{1,33},{33,1},{65,97},{97,65},{2,34}... | collective-permute-start | bytes 2359304 | tf_op jit(solution)/shard_map/ppermute | solution.py:26
  63.3 18.9 %collective-permute-start.18 = (bf16[3072,128]{1,0:T(8,128)(2,1)S(1)}, bf16[3072,128]{1,0:T(8,128)(2,1)S(1)}, u32[]{:S(2)}, u32[]{:S(2)}) collective-permute-start(bf16[3072,128]{1,0:T(8,128)(2,1)S(1)} %get-tuple-element.83), channel_id=1, source_target_pairs={{0,4},{4,0},{8,12},{12,8},{1,5},{5,1},{9,13},{13,9},{2,6},{6,2},{1... | collective-permute-start | bytes 2359304 | tf_op jit(solution)/shard_map/ppermute | solution.py:26
  63.5 22.4 %collective-permute-start.11 = (bf16[256,2176]{1,0:T(8,128)(2,1)S(1)}, bf16[256,2176]{1,0:T(8,128)(2,1)S(1)}, u32[]{:S(2)}, u32[]{:S(2)}) collective-permute-start(bf16[256,2176]{1,0:T(8,128)(2,1)S(1)} %get-tuple-element.70), channel_id=1, source_target_pairs={{0,1},{1,0},{2,3},{3,2},{4,5},{5,4},{6,7},{7,6},{8,9},{9,8},{10,11... | collective-permute-start | bytes 3342344 | tf_op jit(solution)/shard_map/ppermute | solution.py:26
  80.4 14.0 %collective-permute-start.30 = (bf16[2304,128]{1,0:T(8,128)(2,1)S(1)}, bf16[2304,128]{1,0:T(8,128)(2,1)S(1)}, u32[]{:S(2)}, u32[]{:S(2)}) collective-permute-start(bf16[2304,128]{1,0:T(8,128)(2,1)S(1)} %pad_maximum_fusion.3), channel_id=1, source_target_pairs={{0,4},{4,0},{8,12},{12,8},{1,5},{5,1},{9,13},{13,9},{2,6},{6,2},{1... | collective-permute-start | bytes 1769480 | tf_op jit(solution)/shard_map/ppermute | solution.py:26
  81.2 16.1 %collective-permute-start.25 = (bf16[2304,128]{1,0:T(8,128)(2,1)S(1)}, bf16[2304,128]{1,0:T(8,128)(2,1)S(1)}, u32[]{:S(2)}, u32[]{:S(2)}) collective-permute-start(bf16[2304,128]{1,0:T(8,128)(2,1)S(1)} %pad_maximum_fusion.2), channel_id=1, source_target_pairs={{0,32},{32,0},{64,96},{96,64},{1,33},{33,1},{65,97},{97,65},{2,34}... | collective-permute-start | bytes 1769480 | tf_op jit(solution)/shard_map/ppermute | solution.py:26
  82.4 16.6 %collective-permute-start.20 = (bf16[2304,128]{1,0:T(8,128)(2,1)S(1)}, bf16[2304,128]{1,0:T(8,128)(2,1)S(1)}, u32[]{:S(2)}, u32[]{:S(2)}) collective-permute-start(bf16[2304,128]{1,0:T(8,128)(2,1)S(1)} %pad_maximum_fusion.1), channel_id=1, source_target_pairs={{0,12},{4,8},{8,4},{12,0},{1,13},{5,9},{9,5},{13,1},{2,14},{6,10},... | collective-permute-start | bytes 1769480 | tf_op jit(solution)/shard_map/ppermute | solution.py:26
  83.5 16.1 %collective-permute-start.15 = (bf16[2304,128]{1,0:T(8,128)(2,1)S(1)}, bf16[2304,128]{1,0:T(8,128)(2,1)S(1)}, u32[]{:S(2)}, u32[]{:S(2)}) collective-permute-start(bf16[2304,128]{1,0:T(8,128)(2,1)S(1)} %pad_maximum_fusion), channel_id=1, source_target_pairs={{0,96},{32,64},{64,32},{96,0},{1,97},{33,65},{65,33},{97,1},{2,98}... | collective-permute-start | bytes 1769480 | tf_op jit(solution)/shard_map/ppermute | solution.py:26
  86.1 33.1 %collective-permute-start.12 = (bf16[128,2176]{1,0:T(8,128)(2,1)S(1)}, bf16[128,2176]{1,0:T(8,128)(2,1)S(1)}, u32[]{:S(2)}, u32[]{:S(2)}) collective-permute-start(bf16[128,2176]{1,0:T(8,128)(2,1)S(1)} %add_convert_fusion), channel_id=1, source_target_pairs={{0,2},{2,0},{1,3},{3,1},{4,6},{6,4},{5,7},{7,5},{8,10},{10,8},{9,1... | collective-permute-start | bytes 1671176 | tf_op jit(solution)/shard_map/ppermute | solution.py:26
  94.6 9.7 %collective-permute-start.31 = (bf16[1152,128]{1,0:T(8,128)(2,1)S(1)}, bf16[1152,128]{1,0:T(8,128)(2,1)S(1)}, u32[]{:S(2)}, u32[]{:S(2)}) collective-permute-start(bf16[1152,128]{1,0:T(8,128)(2,1)S(1)} %pad_maximum_fusion.7), channel_id=1, source_target_pairs={{0,96},{32,64},{64,32},{96,0},{1,97},{33,65},{65,33},{97,1},{2,98}... | collective-permute-start | bytes 884744 | tf_op jit(solution)/shard_map/ppermute | solution.py:26
  97.5 8.0 %collective-permute-start.26 = (bf16[1152,128]{1,0:T(8,128)(2,1)S(1)}, bf16[1152,128]{1,0:T(8,128)(2,1)S(1)}, u32[]{:S(2)}, u32[]{:S(2)}) collective-permute-start(bf16[1152,128]{1,0:T(8,128)(2,1)S(1)} %pad_maximum_fusion.6), channel_id=1, source_target_pairs={{0,12},{4,8},{8,4},{12,0},{1,13},{5,9},{9,5},{13,1},{2,14},{6,10},... | collective-permute-start | bytes 884744 | tf_op jit(solution)/shard_map/ppermute | solution.py:26
  99.2 7.2 %collective-permute-start.21 = (bf16[1152,128]{1,0:T(8,128)(2,1)S(1)}, bf16[1152,128]{1,0:T(8,128)(2,1)S(1)}, u32[]{:S(2)}, u32[]{:S(2)}) collective-permute-start(bf16[1152,128]{1,0:T(8,128)(2,1)S(1)} %pad_maximum_fusion.5), channel_id=1, source_target_pairs={{0,32},{32,0},{64,96},{96,64},{1,33},{33,1},{65,97},{97,65},{2,34}... | collective-permute-start | bytes 884744 | tf_op jit(solution)/shard_map/ppermute | solution.py:26
  99.8 9.0 %collective-permute-start.16 = (bf16[1152,128]{1,0:T(8,128)(2,1)S(1)}, bf16[1152,128]{1,0:T(8,128)(2,1)S(1)}, u32[]{:S(2)}, u32[]{:S(2)}) collective-permute-start(bf16[1152,128]{1,0:T(8,128)(2,1)S(1)} %pad_maximum_fusion.4), channel_id=1, source_target_pairs={{0,4},{4,0},{8,12},{12,8},{1,5},{5,1},{9,13},{13,9},{2,6},{6,2},{1... | collective-permute-start | bytes 884744 | tf_op jit(solution)/shard_map/ppermute | solution.py:26
  104.5 7.2 %collective-permute-start.32 = (bf16[576,128]{1,0:T(8,128)(2,1)S(1)}, bf16[576,128]{1,0:T(8,128)(2,1)S(1)}, u32[]{:S(2)}, u32[]{:S(2)}) collective-permute-start(bf16[576,128]{1,0:T(8,128)(2,1)S(1)} %pad_maximum_fusion.11), channel_id=1, source_target_pairs={{0,32},{32,0},{64,96},{96,64},{1,33},{33,1},{65,97},{97,65},{2,34}... | collective-permute-start | bytes 442376 | tf_op jit(solution)/shard_map/ppermute | solution.py:26
  105.6 6.2 %collective-permute-start.27 = (bf16[576,128]{1,0:T(8,128)(2,1)S(1)}, bf16[576,128]{1,0:T(8,128)(2,1)S(1)}, u32[]{:S(2)}, u32[]{:S(2)}) collective-permute-start(bf16[576,128]{1,0:T(8,128)(2,1)S(1)} %pad_maximum_fusion.10), channel_id=1, source_target_pairs={{0,4},{4,0},{8,12},{12,8},{1,5},{5,1},{9,13},{13,9},{2,6},{6,2},{1... | collective-permute-start | bytes 442376 | tf_op jit(solution)/shard_map/ppermute | solution.py:26
  106.4 9.2 %collective-permute-start.22 = (bf16[576,128]{1,0:T(8,128)(2,1)S(1)}, bf16[576,128]{1,0:T(8,128)(2,1)S(1)}, u32[]{:S(2)}, u32[]{:S(2)}) collective-permute-start(bf16[576,128]{1,0:T(8,128)(2,1)S(1)} %pad_maximum_fusion.9), channel_id=1, source_target_pairs={{0,96},{32,64},{64,32},{96,0},{1,97},{33,65},{65,33},{97,1},{2,98}... | collective-permute-start | bytes 442376 | tf_op jit(solution)/shard_map/ppermute | solution.py:26
  108.9 6.9 %collective-permute-start.17 = (bf16[576,128]{1,0:T(8,128)(2,1)S(1)}, bf16[576,128]{1,0:T(8,128)(2,1)S(1)}, u32[]{:S(2)}, u32[]{:S(2)}) collective-permute-start(bf16[576,128]{1,0:T(8,128)(2,1)S(1)} %pad_maximum_fusion.8), channel_id=1, source_target_pairs={{0,12},{4,8},{8,4},{12,0},{1,13},{5,9},{9,5},{13,1},{2,14},{6,10},... | collective-permute-start | bytes 442376 | tf_op jit(solution)/shard_map/ppermute | solution.py:26
  111.9 7.2 %copy-start.8 = (s32[128,2]{0,1:T(2,128)S(1)}, s32[128,2]{0,1:T(2,128)}, u32[]{:S(2)}) copy-start(s32[128,2]{0,1:T(2,128)} %param.9) | copy-start | bytes 3076
  111.9 8.4 %collective-permute-start.34 = (bf16[576,128]{1,0:T(8,128)(2,1)S(1)}, bf16[576,128]{1,0:T(8,128)(2,1)S(1)}, u32[]{:S(2)}, u32[]{:S(2)}) collective-permute-start(bf16[576,128]{1,0:T(8,128)(2,1)S(1)} %pad_maximum_fusion.13), channel_id=1, source_target_pairs={{0,16},{16,0},{1,17},{17,1},{2,18},{18,2},{3,19},{19,3},{4,20},{20... | collective-permute-start | bytes 442376 | tf_op jit(solution)/shard_map/ppermute | solution.py:26
  115.9 6.7 %collective-permute-start.33 = (bf16[576,128]{1,0:T(8,128)(2,1)S(1)}, bf16[576,128]{1,0:T(8,128)(2,1)S(1)}, u32[]{:S(2)}, u32[]{:S(2)}) collective-permute-start(bf16[576,128]{1,0:T(8,128)(2,1)S(1)} %pad_maximum_fusion.12), channel_id=1, source_target_pairs={{0,16},{16,0},{1,17},{17,1},{2,18},{18,2},{3,19},{19,3},{4,20},{20... | collective-permute-start | bytes 442376 | tf_op jit(solution)/shard_map/ppermute | solution.py:26
